TPU v7x, 16 devices: a whole 2x2x2 slice. The times are simulated.
16 devices in a mesh: tp: 4 (over z, y), cp: 4 (over x, core).
Axes of the slice: x: 2, y: 2, z: 2, core: 2. Of those that a mesh axis runs over, the one named last changes fastest.
Arguments:
- tokens: int32 [2048], P('cp')
- pos: int32 [2048], P('cp')
- doc_id: int32 [2048], P('cp')
- dy: bfloat16 [2048, 2560], P('cp')
- table: bfloat16 [32000, 2560], P('tp')
- w_q: bfloat16 [2560, 2560], P(None, 'tp')
- w_k: bfloat16 [2560, 2560], P(None, 'tp')
- w_v: bfloat16 [2560, 2560], P(None, 'tp')
- w_o: bfloat16 [2560, 2560], P('tp')
- w_gate: bfloat16 [2560, 6912], P(None, 'tp')
- w_up: bfloat16 [2560, 6912], P(None, 'tp')
- w_down: bfloat16 [6912, 2560], P('tp')
- gain_one: bfloat16 [2560], replicated
- gain_two: bfloat16 [2560], replicated
- inv_freq: float32 [64], replicated
Outputs:
- output 1: bfloat16 [2048, 2560], P('cp')
- output 2: float32 [32000, 2560], P('tp')
- output 3: float32 [2560, 2560], P(None, 'tp')
- output 4: float32 [2560, 2560], P(None, 'tp')
- output 5: float32 [2560, 2560], P(None, 'tp')
- output 6: float32 [2560, 2560], P('tp')
- output 7: float32 [2560, 6912], P(None, 'tp')
- output 8: float32 [2560, 6912], P(None, 'tp')
- output 9: float32 [6912, 2560], P('tp')
- output 10: float32 [2560], replicated
- output 11: float32 [2560], replicated
All inputs are finite; a program needn't handle non-finite values.
Results may differ from a plain program's by a relative error of at most 0.0149397.
Values are sent between devices in bfloat16 or wider.
A program may use at most 1 GiB of HBM per device.

v0:
```python
import jax
import jax.numpy as jnp
from jax import lax
from jax.sharding import PartitionSpec as P

NORM_EPS = 1e-5
NEG_BIG = -1e30


def rms_stats(feats):
    inv_rms = lax.rsqrt(jnp.mean(feats * feats, axis=-1, keepdims=True) + NORM_EPS)
    return feats * inv_rms, inv_rms


def rms_back(d_normed, normed, inv_rms):
    return inv_rms * (d_normed - normed * jnp.mean(d_normed * normed, axis=-1, keepdims=True))


def rotate(tensor_in, cosine, sine):
    half = tensor_in.shape[-1] // 2
    first = tensor_in[..., :half]
    second = tensor_in[..., half:]
    return jnp.concatenate([first * cosine - second * sine, second * cosine + first * sine], axis=-1)


def to_bf16(feats):
    return feats.astype(jnp.bfloat16).astype(jnp.float32)


def slot_sequence(slot, block_len, cp_count):
    shard = slot // (2 * block_len)
    within = slot % (2 * block_len)
    block_no = jnp.where(within < block_len, shard, 2 * cp_count - 1 - shard)
    return block_no * block_len + within % block_len


def solution(mesh):
    cp_count = mesh.shape["cp"]

    def device_step(tokens, pos, doc_id, dy, table, w_q, w_k, w_v, w_o, w_gate, w_up, w_down, gain_one, gain_two, inv_freq):
        span = tokens.shape[0]
        total = span * cp_count
        rows = table.shape[0]
        head_dim = 2 * inv_freq.shape[0]
        kv_local = w_k.shape[1] // head_dim
        q_local = w_q.shape[1] // head_dim
        group = q_local // kv_local
        scale = head_dim ** -0.5
        tp_rank = lax.axis_index("tp")
        cp_rank = lax.axis_index("cp")
        gain_a = gain_one.astype(jnp.float32)
        gain_b = gain_two.astype(jnp.float32)

        local_ids = tokens - tp_rank * rows
        owned = (local_ids >= 0) & (local_ids < rows)
        safe_ids = jnp.where(owned, local_ids, 0)
        picked = jnp.where(owned[:, None], jnp.take(table, safe_ids, axis=0), jnp.zeros((), jnp.bfloat16))
        embed = lax.psum(picked, "tp").astype(jnp.float32)

        normed_a, inv_a = rms_stats(embed)
        act_a = (normed_a * gain_a).astype(jnp.bfloat16)
        angle = pos.astype(jnp.float32)[:, None, None] * inv_freq
        cosine = jnp.cos(angle)
        sine = jnp.sin(angle)
        query = jnp.dot(act_a, w_q, preferred_element_type=jnp.float32).reshape(span, q_local, head_dim)
        query = rotate(query, cosine, sine).astype(jnp.bfloat16).reshape(span, kv_local, group, head_dim)
        key_loc = jnp.dot(act_a, w_k, preferred_element_type=jnp.float32).reshape(span, kv_local, head_dim)
        key_loc = rotate(key_loc, cosine, sine).astype(jnp.bfloat16)
        value_loc = jnp.dot(act_a, w_v, preferred_element_type=jnp.float32).astype(jnp.bfloat16).reshape(span, kv_local, head_dim)

        key_all = lax.all_gather(key_loc, "cp", axis=0, tiled=True)
        value_all = lax.all_gather(value_loc, "cp", axis=0, tiled=True)
        doc_all = lax.all_gather(doc_id, "cp", axis=0, tiled=True)
        q_seq = slot_sequence(cp_rank * span + jnp.arange(span), span // 2, cp_count)
        k_seq = slot_sequence(jnp.arange(total), span // 2, cp_count)
        allowed = (doc_id[:, None] == doc_all[None, :]) & (k_seq[None, :] <= q_seq[:, None])

        scores = jnp.einsum("qkgd,skd->kgqs", query, key_all, preferred_element_type=jnp.float32) * scale
        attn_prob = jax.nn.softmax(jnp.where(allowed, scores, NEG_BIG), axis=-1)
        prob_b = attn_prob.astype(jnp.bfloat16)
        attended = jnp.einsum("kgqs,skd->qkgd", prob_b, value_all, preferred_element_type=jnp.float32)
        attended = attended.astype(jnp.bfloat16).reshape(span, q_local * head_dim)
        residual = embed + lax.psum(jnp.dot(attended, w_o, preferred_element_type=jnp.float32), "tp")
        normed_b, inv_b = rms_stats(residual)
        act_b = (normed_b * gain_b).astype(jnp.bfloat16)
        gate = jnp.dot(act_b, w_gate, preferred_element_type=jnp.float32)
        up_val = jnp.dot(act_b, w_up, preferred_element_type=jnp.float32)
        gate_sig = jax.nn.sigmoid(gate)
        hidden = (gate * gate_sig * up_val).astype(jnp.bfloat16)
        layer_out = residual + lax.psum(jnp.dot(hidden, w_down, preferred_element_type=jnp.float32), "tp")

        grad_down = jnp.einsum("tf,td->fd", hidden, dy, preferred_element_type=jnp.float32)
        d_hidden = to_bf16(jnp.einsum("td,fd->tf", dy, w_down, preferred_element_type=jnp.float32))
        d_gate = (d_hidden * up_val * gate_sig * (1.0 + gate * (1.0 - gate_sig))).astype(jnp.bfloat16)
        d_up = (d_hidden * gate * gate_sig).astype(jnp.bfloat16)
        grad_gate = jnp.einsum("td,tf->df", act_b, d_gate, preferred_element_type=jnp.float32)
        grad_up = jnp.einsum("td,tf->df", act_b, d_up, preferred_element_type=jnp.float32)
        d_act_b = jnp.einsum("tf,df->td", d_gate, w_gate, preferred_element_type=jnp.float32)
        d_act_b = d_act_b + jnp.einsum("tf,df->td", d_up, w_up, preferred_element_type=jnp.float32)
        d_act_b = to_bf16(lax.psum(d_act_b, "tp"))
        grad_gain_b = jnp.sum(d_act_b * normed_b, axis=0)
        d_resid = dy.astype(jnp.float32) + rms_back(d_act_b * gain_b, normed_b, inv_b)
        d_resid_b = d_resid.astype(jnp.bfloat16)
        grad_out = jnp.einsum("tc,td->cd", attended, d_resid_b, preferred_element_type=jnp.float32)
        d_att = jnp.einsum("td,cd->tc", d_resid_b, w_o, preferred_element_type=jnp.float32)
        d_att = d_att.astype(jnp.bfloat16).reshape(span, kv_local, group, head_dim)
        d_prob = to_bf16(jnp.einsum("qkgd,skd->kgqs", d_att, value_all, preferred_element_type=jnp.float32))
        d_scores = attn_prob * (d_prob - jnp.sum(attn_prob * d_prob, axis=-1, keepdims=True))
        d_scores = (d_scores * scale).astype(jnp.bfloat16)
        d_query = jnp.einsum("kgqs,skd->qkgd", d_scores, key_all, preferred_element_type=jnp.float32)
        d_key_all = jnp.einsum("kgqs,qkgd->skd", d_scores, query, preferred_element_type=jnp.float32)
        d_value_all = jnp.einsum("kgqs,qkgd->skd", prob_b, d_att, preferred_element_type=jnp.float32)
        d_key = lax.psum_scatter(d_key_all, "cp", scatter_dimension=0, tiled=True)
        d_value = lax.psum_scatter(d_value_all, "cp", scatter_dimension=0, tiled=True)
        d_q_pre = rotate(to_bf16(d_query).reshape(span, q_local, head_dim), cosine, -sine)
        d_q_pre = d_q_pre.astype(jnp.bfloat16).reshape(span, q_local * head_dim)
        d_k_pre = rotate(to_bf16(d_key), cosine, -sine).astype(jnp.bfloat16).reshape(span, kv_local * head_dim)
        d_v_pre = d_value.astype(jnp.bfloat16).reshape(span, kv_local * head_dim)
        grad_q = jnp.einsum("td,tc->dc", act_a, d_q_pre, preferred_element_type=jnp.float32)
        grad_k = jnp.einsum("td,tc->dc", act_a, d_k_pre, preferred_element_type=jnp.float32)
        grad_v = jnp.einsum("td,tc->dc", act_a, d_v_pre, preferred_element_type=jnp.float32)
        d_act_a = jnp.einsum("tc,dc->td", d_q_pre, w_q, preferred_element_type=jnp.float32)
        d_act_a = d_act_a + jnp.einsum("tc,dc->td", d_k_pre, w_k, preferred_element_type=jnp.float32)
        d_act_a = d_act_a + jnp.einsum("tc,dc->td", d_v_pre, w_v, preferred_element_type=jnp.float32)
        d_act_a = to_bf16(lax.psum(d_act_a, "tp"))
        grad_gain_a = jnp.sum(d_act_a * normed_a, axis=0)
        d_embed = d_resid + rms_back(d_act_a * gain_a, normed_a, inv_a)
        table_part = jax.ops.segment_sum(jnp.where(owned[:, None], d_embed, 0.0), safe_ids, num_segments=rows)
        grad_table = lax.psum(table_part, "cp")
        weight_grads = lax.psum((grad_q, grad_k, grad_v, grad_out, grad_gate, grad_up, grad_down, grad_gain_a, grad_gain_b), "cp")
        return (layer_out.astype(jnp.bfloat16), grad_table) + tuple(weight_grads)

    col_spec = P(None, "tp")
    row_spec = P("tp", None)
    tok_spec = P("cp")
    rep_spec = P(None)
    in_specs = (tok_spec, tok_spec, tok_spec, P("cp", None), row_spec, col_spec, col_spec, col_spec, row_spec, col_spec, col_spec, row_spec, rep_spec, rep_spec, rep_spec)
    out_specs = (P("cp", None), row_spec, col_spec, col_spec, col_spec, row_spec, col_spec, col_spec, row_spec, rep_spec, rep_spec)
    return jax.shard_map(device_step, mesh=mesh, in_specs=in_specs, out_specs=out_specs, check_vma=False)
```

profile of v0, /device:TPU:0, one launch (start us, length us, event | category | flops | bytes accessed | tf_op | source)
XLA Modules:
  0.0 3525.4 jit_solution(9594050278906864061)
XLA Ops:
  8.6 19.9 gather_fusion
  34.2 88.7 %all-reduce.11.cloned.1.call-done = bf16[512,2560]{1,0:T(8,128)(2,1)} async-done(((bf16[512,2560]{1,0:T(8,128)(2,1)}), bf16[512,2560]{1,0:T(8,128)(2,1)}) %all-reduce.11.cloned.1.call-update) | async-done | bytes 2621456 | tf_op jit(solution)/shard_map/psum | solution.py:58
  176.6 14.0 fusion.8
  190.6 9.6 fusion.7
  202.1 11.1 fusion.41
  219.1 10.3 convolution_convert_fusion.1
  229.4 102.4 %all-reduce.13.cloned.1.call-done = f32[512,2560]{1,0:T(8,128)} async-done(((f32[512,2560]{1,0:T(8,128)}), f32[512,2560]{1,0:T(8,128)}) %all-reduce.13.cloned.1.call-update) | async-done | bytes 5242896 | tf_op jit(solution)/shard_map/psum | solution.py:83
  346.4 11.7 fusion.35
  374.6 10.3 convolution_add_fusion
  384.9 242.3 %all-reduce.20 = bf16[512,2560]{1,0:T(8,128)(2,1)} all-reduce(f32[512,2560]{1,0:T(8,128)} %convolution_add_fusion), channel_id=1, replica_groups=mesh['tp'=4,'cp'=4] {'tp'}, use_global_device_ids=true, to_apply=%region_7.8 | all-reduce | flops 1310720 | bytes 7864320 | tf_op jit(solution)/shard_map/psum | solution.py:100
  647.3 15.2 fusion.2
  662.5 13.7 fusion.9
  685.3 13.3 fusion.38
  700.4 10.6 fusion.92
  721.7 10.4 fusion.93
  750.6 31.1 reduce-scatter.5.cloned.1.call-done
  794.5 179.2 %all-reduce.21 = bf16[512,2560]{1,0:T(8,128)(2,1)} all-reduce(f32[512,2560]{1,0:T(8,128)} %add_add_fusion), channel_id=1, replica_groups=mesh['tp'=4,'cp'=4] {'tp'}, use_global_device_ids=true, to_apply=%region_12.13 | all-reduce | flops 1310720 | bytes 7864320 | tf_op jit(solution)/shard_map/psum | solution.py:125
  982.4 26.1 broadcast_in_dim.76
  1008.5 110.5 %scatter_fusion = f32[8000,2560]{1,0:T(8,128)} fusion(f32[8000,2560]{1,0:T(8,128)} %broadcast_in_dim.76, s32[512]{0:T(512)S(1)} %copy-done.31, f32[512,2560]{1,0:T(8,128)} %fusion.24), kind=kCustom, calls=%fused_computation.1 | custom fusion | flops 1310720 | bytes 15730688 | tf_op jit(solution)/shard_map/scatter-add | solution.py:128
  1136.5 12.3 all-reduce
  1148.8 220.1 %all-reduce.19.cloned.1.call-done = (f32[2560,1728]{0,1:T(8,128)}, f32[1728,2560]{1,0:T(8,128)}) async-done(((f32[2560,1728]{0,1:T(8,128)}, f32[1728,2560]{1,0:T(8,128)}), (f32[2560,1728]{0,1:T(8,128)}, f32[1728,2560]{1,0:T(8,128)})) %all-reduce.19.cloned.1.call-update) | async-done | bytes 35389456 | tf_op jit(solution)/shard_map/psum | solution.py:130
  1368.8 2041.6 %all-reduce.17.cloned.1.call-done = (f32[8000,2560]{1,0:T(8,128)}, f32[2560,640]{1,0:T(8,128)}, f32[2560,640]{1,0:T(8,128)}, f32[2560,640]{1,0:T(8,128)}, f32[640,2560]{1,0:T(8,128)}, /*index=5*/f32[2560,1728]{0,1:T(8,128)}) async-done(((f32[8000,2560]{1,0:T(8,128)}, f32[2560,640]{1,0:T(8,128)}, f32[2560,640]{1,0:T(8,128)}, f32[2560,640]{1,0:T(8,128)}, f32[640,2560]{1,0:T(8,128)}, ...) | async-done | bytes 125829136 | tf_op jit(solution)/shard_map/psum | solution.py:129
  3410.5 54.7 %copy.114 = f32[8000,2560]{1,0:T(8,128)} copy(f32[8000,2560]{1,0:T(8,128)} %get-tuple-element.60) | data formatting | bytes 163840000
  3497.9 13.7 copy.120
  (213 shorter events, 238.0 us)
Async XLA Ops:
  7.2 207.0 %copy-start = (bf16[640,2560]{1,0:T(8,128)(2,1)S(1)}, bf16[640,2560]{1,0:T(8,128)(2,1)}, u32[]{:S(2)}) copy-start(bf16[640,2560]{1,0:T(8,128)(2,1)} %param.23) | copy-start | bytes 9830404
  7.2 115.7 %all-reduce.11.cloned.1.call-start = ((), (), s32[]{:S(2)}) async-start(), calls=%async_computation.2 | async-start | bytes 5242880 | tf_op jit(solution)/shard_map/psum | solution.py:58
  8.1 20.5 copy-start.35
  32.3 144.4 %all-gather.6.cloned.1.call-start = ((), (), s32[]{:S(2)}) async-start(), calls=%async_computation.4 | async-start | bytes 3276800 | tf_op jit(solution)/shard_map/all_gather | solution.py:71
  32.3 120.8 %copy-start.25 = (f32[2560]{0:T(1024)}, f32[2560]{0:T(1024)S(1)}, u32[]{:S(2)}) copy-start(f32[2560]{0:T(1024)S(1)} %convert_element_type.126) | copy-start | bytes 30724
  34.2 113.1 %copy-start.23 = (f32[512,64]{1,0:T(8,128)}, f32[512,64]{1,0:T(8,128)S(1)}, u32[]{:S(2)}) copy-start(f32[512,64]{1,0:T(8,128)S(1)} %get-tuple-element.51) | copy-start | bytes 393220
  125.3 27.9 copy-start.27
  152.9 49.2 %all-gather.4.cloned.1.call-start = ((), (), s32[]{:S(2)}) async-start(), calls=%async_computation.3 | async-start | bytes 3276800 | tf_op jit(solution)/shard_map/all_gather | solution.py:72
  161.2 170.7 %all-reduce.13.cloned.1.call-start = ((), (), s32[]{:S(2)}) async-start(), calls=%async_computation.5 | async-start | bytes 10485760 | tf_op jit(solution)/shard_map/psum | solution.py:83
  218.8 413.8 %all-reduce.15.cloned.1.call-start = ((), (), s32[]{:S(2)}) async-start(), calls=%async_computation.6 | async-start | bytes 10485760 | tf_op jit(solution)/shard_map/psum | solution.py:90
  366.2 379.8 %reduce-scatter.3.cloned.1.call-start = ((), (), s32[]{:S(2)}) async-start(), calls=%async_computation.7 | async-start | bytes 6553600 | tf_op jit(solution)/shard_map/reduce_scatter | solution.py:113
  685.2 96.4 %reduce-scatter.5.cloned.1.call-start = ((), (), s32[]{:S(2)}) async-start(), calls=%async_computation.8 | async-start | bytes 6553600 | tf_op jit(solution)/shard_map/reduce_scatter | solution.py:114
  698.6 670.2 %all-reduce.19.cloned.1.call-start = ((), (), s32[]{:S(2)}) async-start(), calls=%async_computation.10 | async-start | bytes 70778880 | tf_op jit(solution)/shard_map/psum | solution.py:130
  720.0 2690.5 %all-reduce.17.cloned.1.call-start = ((), (), s32[]{:S(2)}) async-start(), calls=%async_computation.9 | async-start | bytes 251658240 | tf_op jit(solution)/shard_map/psum | solution.py:129
  750.3 37.1 %copy-start.15 = (bf16[512,5,128]{0,2,1:T(8,128)(2,1)}, bf16[512,5,128]{0,2,1:T(8,128)(2,1)S(1)}, u32[]{:S(2)}) copy-start(bf16[512,5,128]{0,2,1:T(8,128)(2,1)S(1)} %copy.76) | copy-start | bytes 1966084
  750.6 36.8 %copy-start.16 = (bf16[512,5,128]{0,2,1:T(8,128)(2,1)}, bf16[512,5,128]{0,2,1:T(8,128)(2,1)S(1)}, u32[]{:S(2)}) copy-start(bf16[512,5,128]{0,2,1:T(8,128)(2,1)S(1)} %copy.80) | copy-start | bytes 1966084
  794.5 179.2 %copy-start.2 = (bf16[512,2560]{1,0:T(8,128)(2,1)S(1)}, bf16[512,2560]{1,0:T(8,128)(2,1)}, u32[]{:S(2)}) copy-start(bf16[512,2560]{1,0:T(8,128)(2,1)} %all-reduce.11.cloned.1.call-done) | copy-start | bytes 7864324
  794.5 179.2 %copy-start.26 = (f32[2560]{0:T(1024)S(1)}, f32[2560]{0:T(1024)}, u32[]{:S(2)}) copy-start(f32[2560]{0:T(1024)} %copy-done.25) | copy-start | bytes 30724
  794.5 179.2 %copy-start.28 = (f32[512]{0:T(512)S(1)}, f32[512]{0:T(512)}, u32[]{:S(2)}) copy-start(f32[512]{0:T(512)} %copy-done.27) | copy-start | bytes 6148
  794.5 182.8 %copy-start.36 = (pred[512]{0:T(512)(128)(4,1)S(1)}, pred[512]{0:T(512)(128)(4,1)}, u32[]{:S(2)}) copy-start(pred[512]{0:T(512)(128)(4,1)} %copy-done.35) | copy-start | bytes 1540
  982.4 26.1 copy-start.31
  3488.9 22.7 slice-start
  3488.9 22.7 slice-start.1
  3488.9 22.7 slice-start.2
  (47 other events, 389.8 us)
Sparse Core Ops, SparseCore 0:
  32.4 90.5 all-reduce.10
  153.0 23.5 all-gather.5
  178.7 23.3 all-gather.3
  218.9 112.8 all-reduce.12
  366.3 177.0 all-reduce.14
  685.3 46.5 reduce-scatter.2
  735.0 46.6 reduce-scatter.4
  784.8 583.9 all-reduce.18
  1373.0 2037.4 all-reduce.16
where the time goes:
time: 3530 us
  waiting for transfers between devices  2490 us (71%)
  blocking collectives  439 us (12%)
  matrix products  208 us (6%)
  local copies, waits for them, and re-layouts  187 us (5%)
  other arithmetic  183 us (5%)
    psum x1, waiting for transfers between devices, device_step(): grad_table = lax.psum(table_part, 'cp')  2040 us
    psum x1, blocking collectives, device_step(): d_act_b = to_bf16(lax.psum(d_act_b, 'tp'))  242 us
    psum x1, waiting for transfers between devices, device_step(): lax.psum((grad_q, grad_k, grad_v, grad_out, grad_gate, grad_up, grad_down...  220 us
    psum x1, blocking collectives, device_step(): d_act_a = to_bf16(lax.psum(d_act_a, 'tp'))  179 us
    unnamed x136, local copies, waits for them, and re-layouts  135 us
    scatter-add x1, other arithmetic, device_step(): jax.ops.segment_sum(jnp.where(owned[:, None], d_embed, 0.0), safe_ids, nu...  110 us
    psum x1, waiting for transfers between devices, device_step(): lax.psum(jnp.dot(attended, w_o, preferred_element_type=jnp.float32), 'tp')  102 us
    psum x1, waiting for transfers between devices, device_step(): embed = lax.psum(picked, 'tp').astype(jnp.float32)  88.7 us
  transfers between devices with their start and end apart: 9, of which 7 were waited for; matrix products, arithmetic and copies ran while one was open for 9% of the time, Pallas kernels for 0%

commit v1 on v0

v1 whole, which is shorter than its diff:
```python
import functools
import jax
import jax.numpy as jnp
from jax import lax
from jax.experimental import pallas as pl
from jax.experimental.pallas import tpu as pltpu
from jax.sharding import PartitionSpec as P

NORM_EPS = 1e-5
NEG_BIG = -1e30
F32 = jnp.float32
BF16 = jnp.bfloat16


def rms_stats(feats):
    inv_rms = lax.rsqrt(jnp.mean(feats * feats, axis=-1, keepdims=True) + NORM_EPS)
    return feats * inv_rms, inv_rms


def rms_back(d_normed, normed, inv_rms):
    return inv_rms * (d_normed - normed * jnp.mean(d_normed * normed, axis=-1, keepdims=True))


def rotate(tensor_in, cosine, sine):
    half = tensor_in.shape[-1] // 2
    first = tensor_in[..., :half]
    second = tensor_in[..., half:]
    return jnp.concatenate([first * cosine - second * sine, second * cosine + first * sine], axis=-1)


def to_bf16(feats):
    return feats.astype(BF16).astype(F32)


def dot(a, b, ca, cb):
    return lax.dot_general(a, b, (((ca,), (cb,)), ((), ())), preferred_element_type=F32)


def slot_sequence(slot, block_len, cp_count):
    shard = slot // (2 * block_len)
    within = slot % (2 * block_len)
    block_no = jnp.where(within < block_len, shard, 2 * cp_count - 1 - shard)
    return block_no * block_len + within % block_len


def slot_block(j):
    return jnp.where(j < 4, 2 * j, 15 - 2 * j)


def qkv_kernel(x, gain, wq, wk, wv, cos, sin, act, q, k, v, *, head_dim):
    feats = x[...].astype(F32)
    inv = lax.rsqrt(jnp.mean(feats * feats, axis=-1, keepdims=True) + NORM_EPS)
    a = (feats * inv * gain[...]).astype(BF16)
    act[...] = a
    for w, out, turn in ((wq, q, True), (wk, k, True), (wv, v, False)):
        t = jnp.dot(a, w[...], preferred_element_type=F32)
        for h in range(w.shape[1] // head_dim):
            cols = slice(h * head_dim, (h + 1) * head_dim)
            th = t[:, cols]
            if turn:
                th = th * cos[...] + pltpu.roll(th, head_dim // 2, 1) * sin[...]
            out[:, cols] = th.astype(BF16)


def project_qkv(x_all, gain, wq, wk, wv, cos, sin, block=256):
    total, dim = x_all.shape
    width = wq.shape[1]
    head_dim = cos.shape[1]
    rows = lambda n: pl.BlockSpec((block, n), lambda i: (i, 0))
    whole = lambda a: pl.BlockSpec(a.shape, lambda i: (0, 0))
    return pl.pallas_call(
        functools.partial(qkv_kernel, head_dim=head_dim),
        out_shape=[jax.ShapeDtypeStruct((total, n), BF16) for n in (dim, width, width, width)],
        grid=(total // block,),
        in_specs=[rows(dim), whole(gain), whole(wq), whole(wk), whole(wv), rows(head_dim), rows(head_dim)],
        out_specs=[rows(dim), rows(width), rows(width), rows(width)],
        compiler_params=pltpu.CompilerParams(vmem_limit_bytes=48 * 1024 * 1024),
        cost_estimate=pl.CostEstimate(flops=6 * total * dim * width, bytes_accessed=4 * total * dim + 6 * dim * width + 6 * total * width, transcendentals=0),
        name="project_qkv",
    )(x_all, gain, wq, wk, wv, cos, sin)


def attend_kernel(info, q, k, v, doc_col, doc_row, out, lse, sc, *, heads, head_dim, scale):
    blk = q.shape[0]
    b = info[pl.program_id(0)]
    jmin = info[2 + pl.program_id(0)]
    row_n = lax.broadcasted_iota(jnp.int32, (blk, blk), 0) + b * blk
    col_n = lax.broadcasted_iota(jnp.int32, (blk, blk), 1)

    def score(j, peaks):
        sb = slot_block(j)
        off = pl.multiple_of(sb * blk, blk)
        allowed = (doc_col[...] == doc_row[sb]) & (col_n + j * blk <= row_n)
        new = []
        for h in range(heads):
            cols = slice(h * head_dim, (h + 1) * head_dim)
            s = dot(q[:, cols], k[pl.ds(off, blk), cols], 1, 1) * scale
            s = jnp.where(allowed, s, NEG_BIG)
            sc[j, h] = s
            new.append(jnp.maximum(peaks[h], jnp.max(s, axis=1, keepdims=True)))
        return tuple(new)

    peaks = lax.fori_loop(jmin, b + 1, score, tuple(jnp.full((blk, 1), NEG_BIG, F32) for _ in range(heads)))

    def weigh(j, sums):
        new = []
        for h in range(heads):
            p = jnp.exp(sc[j, h] - peaks[h])
            sc[j, h] = p
            new.append(sums[h] + jnp.sum(p, axis=1, keepdims=True))
        return tuple(new)

    sums = lax.fori_loop(jmin, b + 1, weigh, tuple(jnp.zeros((blk, 1), F32) for _ in range(heads)))
    inv = tuple(1.0 / t for t in sums)
    for h in range(heads):
        lse[:, h:h + 1] = peaks[h] + jnp.log(sums[h])

    def mix(j, acc):
        off = pl.multiple_of(slot_block(j) * blk, blk)
        new = []
        for h in range(heads):
            cols = slice(h * head_dim, (h + 1) * head_dim)
            new.append(acc[h] + jnp.dot((sc[j, h] * inv[h]).astype(BF16), v[pl.ds(off, blk), cols], preferred_element_type=F32))
        return tuple(new)

    acc = lax.fori_loop(jmin, b + 1, mix, tuple(jnp.zeros((blk, head_dim), F32) for _ in range(heads)))
    for h in range(heads):
        out[:, h * head_dim:(h + 1) * head_dim] = acc[h].astype(BF16)


def attend(info, q, k, v, doc_col, doc_row, head_dim, blk):
    total, width = k.shape
    heads = width // head_dim
    mine = lambda n: pl.BlockSpec((blk, n), lambda i, info: (2 * info[6] + i, 0))
    whole = lambda a: pl.BlockSpec(a.shape, lambda i, info: (0,) * a.ndim)
    return pl.pallas_call(
        functools.partial(attend_kernel, heads=heads, head_dim=head_dim, scale=head_dim ** -0.5),
        out_shape=[jax.ShapeDtypeStruct((2 * blk, width), BF16), jax.ShapeDtypeStruct((2 * blk, 8), F32)],
        grid_spec=pltpu.PrefetchScalarGridSpec(
            num_scalar_prefetch=1,
            grid=(2,),
            in_specs=[mine(width), whole(k), whole(v), mine(1), whole(doc_row)],
            out_specs=[pl.BlockSpec((blk, width), lambda i, info: (i, 0)), pl.BlockSpec((blk, 8), lambda i, info: (i, 0))],
            scratch_shapes=[pltpu.VMEM((total // blk, heads, blk, blk), F32)],
        ),
        compiler_params=pltpu.CompilerParams(vmem_limit_bytes=40 * 1024 * 1024),
        cost_estimate=pl.CostEstimate(flops=4 * 2 * blk * total * width, bytes_accessed=8 * total * width, transcendentals=heads * blk * total),
        name="attend",
    )(info, q, k, v, doc_col, doc_row)


def attend_back_kernel(info, q, k, v, do, doc_col, doc_row, lse_col, lse_row, del_col, del_row, cos, sin, out, acc, *, heads, head_dim, scale):
    blk = cos.shape[0]
    width = heads * head_dim
    i = pl.program_id(0)
    b = info[i]
    jmin = info[2 + i]
    imax = info[4 + i]
    me = pl.multiple_of((2 * info[6] + i) * blk, blk)
    mine = pl.ds(me, blk)
    iota_r = lax.broadcasted_iota(jnp.int32, (blk, blk), 0)
    iota_c = lax.broadcasted_iota(jnp.int32, (blk, blk), 1)
    acc[...] = jnp.zeros_like(acc)
    spans = [slice(h * head_dim, (h + 1) * head_dim) for h in range(heads)]

    def for_query(j, c):
        sb = slot_block(j)
        there = pl.ds(pl.multiple_of(sb * blk, blk), blk)
        allowed = (doc_col[mine, :] == doc_row[sb]) & (iota_c + j * blk <= iota_r + b * blk)
        for h, cols in enumerate(spans):
            s = jnp.where(allowed, dot(q[mine, cols], k[there, cols], 1, 1) * scale, NEG_BIG)
            p = jnp.exp(s - lse_col[mine, h:h + 1])
            dp = to_bf16(dot(do[mine, cols], v[there, cols], 1, 1))
            ds = (p * (dp - del_col[mine, h:h + 1]) * scale).astype(BF16)
            acc[0, :, cols] += jnp.dot(ds, k[there, cols], preferred_element_type=F32)
        return c

    lax.fori_loop(jmin, b + 1, for_query, 0)
    my_block = 2 * info[6] + i

    def for_key(j, c):
        sb = slot_block(j)
        there = pl.ds(pl.multiple_of(sb * blk, blk), blk)
        allowed = (doc_col[mine, :] == doc_row[sb]) & (iota_r + b * blk <= iota_c + j * blk)
        for h, cols in enumerate(spans):
            s = jnp.where(allowed, dot(k[mine, cols], q[there, cols], 1, 1) * scale, NEG_BIG)
            p = jnp.exp(s - lse_row[sb, h:h + 1, :])
            dp = to_bf16(dot(v[mine, cols], do[there, cols], 1, 1))
            ds = (p * (dp - del_row[sb, h:h + 1, :]) * scale).astype(BF16)
            acc[2, :, cols] += jnp.dot(p.astype(BF16), do[there, cols], preferred_element_type=F32)
            acc[1, :, cols] += jnp.dot(ds, q[there, cols], preferred_element_type=F32)
        return c

    lax.fori_loop(b, imax + 1, for_key, 0)
    for part in range(3):
        for h, cols in enumerate(spans):
            t = acc[part, :, cols]
            if part < 2:
                t = to_bf16(t)
                t = t * cos[...] - pltpu.roll(t, head_dim // 2, 1) * sin[...]
            out[:, part * width + h * head_dim:part * width + (h + 1) * head_dim] = t.astype(BF16)


def attend_back(info, q, k, v, do, doc_col, doc_row, lse_col, lse_row, del_col, del_row, cos, sin, blk):
    total, width = k.shape
    head_dim = cos.shape[1]
    heads = width // head_dim
    mine = lambda n: pl.BlockSpec((blk, n), lambda i, info: (2 * info[6] + i, 0))
    whole = lambda a: pl.BlockSpec(a.shape, lambda i, info: (0,) * a.ndim)
    arrays = (q, k, v, do, doc_col, doc_row, lse_col, lse_row, del_col, del_row)
    return pl.pallas_call(
        functools.partial(attend_back_kernel, heads=heads, head_dim=head_dim, scale=head_dim ** -0.5),
        out_shape=jax.ShapeDtypeStruct((2 * blk, 3 * width), BF16),
        grid_spec=pltpu.PrefetchScalarGridSpec(
            num_scalar_prefetch=1,
            grid=(2,),
            in_specs=[whole(a) for a in arrays] + [mine(head_dim), mine(head_dim)],
            out_specs=pl.BlockSpec((blk, 3 * width), lambda i, info: (i, 0)),
            scratch_shapes=[pltpu.VMEM((3, blk, width), F32)],
        ),
        compiler_params=pltpu.CompilerParams(vmem_limit_bytes=48 * 1024 * 1024),
        cost_estimate=pl.CostEstimate(flops=14 * 2 * blk * total * width // 2, bytes_accessed=12 * total * width, transcendentals=heads * blk * total),
        name="attend_back",
    )(info, *arrays, cos, sin)


def scatter_kernel(order, sid, bounds, d_hbm, base_hbm, out_hbm, rows, load_sem, row_sem):
    lo = bounds[0]
    hi = bounds[1]
    load = pltpu.make_async_copy(d_hbm, rows, load_sem)
    load.start()
    load.wait()

    def add_body(p, first):
        t = order[p]
        same = jnp.logical_and(p > lo, sid[p] == sid[jnp.maximum(p - 1, 0)])

        @pl.when(same)
        def _():
            rows[pl.ds(first, 1), :] = rows[pl.ds(first, 1), :] + rows[pl.ds(t, 1), :]

        return jnp.where(same, first, t)

    lax.fori_loop(lo, hi, add_body, 0)

    def send_body(p, count):
        new = jnp.logical_or(p == lo, sid[p] != sid[jnp.maximum(p - 1, 0)])

        @pl.when(new)
        def _():
            pltpu.make_async_copy(rows.at[pl.ds(order[p], 1), :], out_hbm.at[pl.ds(sid[p], 1), :], row_sem).start()

        return count + new.astype(jnp.int32)

    count = lax.fori_loop(lo, hi, send_body, 0)

    def wait_body(p, c):
        pltpu.make_async_copy(rows.at[pl.ds(0, 1), :], out_hbm.at[pl.ds(0, 1), :], row_sem).wait()
        return c

    lax.fori_loop(0, count, wait_body, 0)


def scatter_rows(order, sid, bounds, grads, rows):
    total, dim = grads.shape
    base = jnp.zeros((rows, dim), F32)
    return pl.pallas_call(
        scatter_kernel,
        out_shape=jax.ShapeDtypeStruct((rows, dim), F32),
        grid_spec=pltpu.PrefetchScalarGridSpec(
            num_scalar_prefetch=3,
            grid=(),
            in_specs=[pl.BlockSpec(memory_space=pl.ANY), pl.BlockSpec(memory_space=pl.ANY)],
            out_specs=pl.BlockSpec(memory_space=pl.ANY),
            scratch_shapes=[pltpu.VMEM((total, dim), F32), pltpu.SemaphoreType.DMA, pltpu.SemaphoreType.DMA],
        ),
        input_output_aliases={4: 0},
        compiler_params=pltpu.CompilerParams(vmem_limit_bytes=28 * 1024 * 1024),
        name="scatter_rows",
    )(order, sid, bounds, grads, base)


def solution(mesh):
    cp_count = mesh.shape["cp"]
    tp_count = mesh.shape["tp"]
    both = ("cp", "tp")
    x_swap = [(i, i ^ 2) for i in range(cp_count)]
    core_swap = [(i, i ^ 1) for i in range(cp_count)]

    def device_step(tokens, pos, doc_id, dy, table, w_q, w_k, w_v, w_o, w_gate, w_up, w_down, gain_one, gain_two, inv_freq):
        span = tokens.shape[0]
        total = span * cp_count
        part = span // tp_count
        rows, dim = table.shape
        head_dim = 2 * inv_freq.shape[0]
        heads = w_q.shape[1] // head_dim
        width = heads * head_dim
        scale = head_dim ** -0.5
        tp_rank = lax.axis_index("tp")
        cp_rank = lax.axis_index("cp")
        core = cp_rank % 2
        gain_a = gain_one.astype(F32)
        gain_b = gain_two.astype(F32)

        def own(arr):
            return lax.dynamic_slice_in_dim(arr, cp_rank * span, span, 0)

        local_ids = tokens - tp_rank * rows
        owned = (local_ids >= 0) & (local_ids < rows)
        safe_ids = jnp.where(owned, local_ids, 0)
        picked = jnp.where(owned[:, None], jnp.take(table, safe_ids, axis=0), jnp.zeros((), BF16))
        x_slice = lax.psum_scatter(picked, "tp", scatter_dimension=0, tiled=True)
        x_all = lax.all_gather(x_slice, both, axis=0, tiled=True)

        ints = lax.all_gather(jnp.stack([tokens, pos, doc_id]), "cp", axis=1, tiled=True)
        tok_all, pos_all, doc_all = ints[0], ints[1], ints[2]

        half = dim // 2
        wo_half = lax.dynamic_slice_in_dim(w_o, core * half, half, 1)
        wo_mine = lax.all_gather(wo_half, "tp", axis=0, tiled=True)
        wo_other = lax.ppermute(wo_mine, "cp", core_swap)
        wo_full = jnp.zeros((tp_count * width, dim), BF16)
        wo_full = lax.dynamic_update_slice_in_dim(wo_full, wo_mine, core * half, 1)
        wo_full = lax.dynamic_update_slice_in_dim(wo_full, wo_other, (1 - core) * half, 1)

        dy_x = lax.ppermute(dy, "cp", x_swap)
        dy_all = jnp.zeros((total, dim), BF16)
        for piece, who in ((dy, cp_rank), (dy_x, cp_rank ^ 2), (lax.ppermute(dy, "cp", core_swap), cp_rank ^ 1), (lax.ppermute(dy_x, "cp", core_swap), cp_rank ^ 3)):
            dy_all = lax.dynamic_update_slice_in_dim(dy_all, piece, who * span, 0)

        ids_all = tok_all
        slot_ids = jnp.arange(total, dtype=jnp.int32)
        before = (ids_all[None, :] < ids_all[:, None]) | ((ids_all[None, :] == ids_all[:, None]) & (slot_ids[None, :] < slot_ids[:, None]))
        rank = jnp.sum(before.astype(jnp.int32), axis=1)
        at_rank = rank[None, :] == slot_ids[:, None]
        order = jnp.sum(jnp.where(at_rank, slot_ids[None, :], 0), axis=1)
        sid = jnp.sum(jnp.where(at_rank, ids_all[None, :], 0), axis=1) - tp_rank * rows
        bounds = jnp.stack([jnp.sum((ids_all < tp_rank * rows).astype(jnp.int32)), jnp.sum((ids_all < (tp_rank + 1) * rows).astype(jnp.int32))])

        angle = pos_all.astype(F32)[:, None] * inv_freq[None, :]
        cos = jnp.cos(angle)
        sin = jnp.sin(angle)
        cos = jnp.concatenate([cos, cos], axis=1)
        sin = jnp.concatenate([-sin, sin], axis=1)
        act_a, query, key, value = project_qkv(x_all, gain_a[None, :], w_q, w_k, w_v, cos, sin)

        blk = span // 2
        blocks = total // blk
        doc_col = doc_all[:, None]
        doc_row = doc_all.reshape(blocks, 1, blk)
        seq_block = jnp.concatenate([jnp.arange(0, blocks, 2), jnp.arange(blocks - 1, 0, -2)])
        doc_seq = doc_all.reshape(blocks, blk)[seq_block]
        first_doc, last_doc = doc_seq[:, 0], doc_seq[:, -1]
        b_own = jnp.stack([cp_rank, blocks - 1 - cp_rank])
        first_own, last_own = first_doc[b_own], last_doc[b_own]
        jmin = jnp.sum((last_doc[None, :] < first_own[:, None]).astype(jnp.int32), axis=1)
        imax = jnp.sum((first_doc[None, :] <= last_own[:, None]).astype(jnp.int32), axis=1) - 1
        info = jnp.concatenate([b_own, jmin, imax, cp_rank[None]]).astype(jnp.int32)
        attended, lse = attend(info, query, key, value, doc_col, doc_row, head_dim, blk)

        att_parts = lax.all_gather(attended, both, axis=0, tiled=False).reshape(cp_count, tp_count, span, width)
        att_own = jnp.transpose(lax.dynamic_index_in_dim(att_parts, cp_rank, 0, keepdims=False), (1, 0, 2)).reshape(span, tp_count * width)
        x_own = own(x_all).astype(F32)
        residual = x_own + dot(att_own, wo_full, 1, 0)
        normed_o, inv_o = rms_stats(residual)
        act_b = (normed_o * gain_b).astype(BF16)

        def mlp(act, dyt):
            gate = dot(act, w_gate, 1, 0)
            up_val = dot(act, w_up, 1, 0)
            gate_sig = jax.nn.sigmoid(gate)
            hidden = (gate * gate_sig * up_val).astype(BF16)
            d_hidden = to_bf16(dot(dyt, w_down, 1, 1))
            d_gate = (d_hidden * up_val * gate_sig * (1.0 + gate * (1.0 - gate_sig))).astype(BF16)
            d_up = (d_hidden * gate * gate_sig).astype(BF16)
            return hidden, d_gate, d_up

        hidden, d_gate, d_up = mlp(act_b, dy)
        d_act_b = dot(d_gate, w_gate, 1, 1) + dot(d_up, w_up, 1, 1)
        d_act_b = to_bf16(lax.psum_scatter(d_act_b, "tp", scatter_dimension=0, tiled=True))

        def mine(arr):
            return lax.dynamic_slice_in_dim(arr, tp_rank * part, part, 0)

        res_part = mine(residual)
        normed_b, inv_b = rms_stats(res_part)
        grad_gain_b = jnp.sum(d_act_b * normed_b, axis=0)
        d_resid = mine(dy).astype(F32) + rms_back(d_act_b * gain_b, normed_b, inv_b)
        d_resid_all = lax.all_gather(d_resid.astype(BF16), both, axis=0, tiled=True)

        out_part = lax.psum_scatter(dot(hidden, w_down, 1, 0), "tp", scatter_dimension=0, tiled=True)
        layer_out = lax.all_gather((res_part + out_part).astype(BF16), "tp", axis=0, tiled=True)

        d_att = dot(d_resid_all, w_o, 1, 1)
        d_att_b = d_att.astype(BF16)
        att_heads = lax.dynamic_index_in_dim(att_parts, tp_rank, 1, keepdims=False).reshape(total, width)
        head_of = (jnp.arange(width)[None, :] // head_dim == jnp.arange(8)[:, None]).astype(F32)
        prod = att_heads.astype(F32) * d_att_b.astype(F32)
        delta = lax.dot_general(head_of, prod, (((1,), (1,)), ((), ())), precision=lax.Precision.HIGHEST, preferred_element_type=F32)
        lse_all = lax.all_gather(lse, "cp", axis=0, tiled=True)

        def by_block(arr):
            return jnp.transpose(arr.reshape(8, blocks, blk), (1, 0, 2))

        dqkv = attend_back(info, query, key, value, d_att_b, doc_col, doc_row, lse_all, by_block(lse_all.T), delta.T, by_block(delta), cos, sin, blk)
        d_q_pre, d_k_pre, d_v_pre = (dqkv[:, i * width:(i + 1) * width] for i in range(3))
        d_act_a = dot(d_q_pre, w_q, 1, 1) + dot(d_k_pre, w_k, 1, 1) + dot(d_v_pre, w_v, 1, 1)
        d_act_a = to_bf16(lax.psum_scatter(d_act_a, "tp", scatter_dimension=0, tiled=True))
        dqkv_all = lax.all_gather(dqkv, "cp", axis=0, tiled=True)
        normed_a, inv_a = rms_stats(x_slice.astype(F32))
        grad_gain_a = jnp.sum(d_act_a * normed_a, axis=0)
        d_embed = d_resid + rms_back(d_act_a * gain_a, normed_a, inv_a)
        d_embed_all = lax.all_gather(d_embed, both, axis=0, tiled=True)
        gain_grads = lax.psum(jnp.stack([grad_gain_a, grad_gain_b]), both)

        att_all = jnp.transpose(att_parts, (0, 2, 1, 3)).reshape(total, tp_count * width)
        resid_all = x_all.astype(F32) + dot(att_all, wo_full, 1, 0)
        act_b_all = (rms_stats(resid_all)[0] * gain_b).astype(BF16)
        hidden_all, d_gate_all, d_up_all = mlp(act_b_all, dy_all)
        grad_down = dot(hidden_all, dy_all, 0, 0)
        grad_gate = dot(act_b_all, d_gate_all, 0, 0)
        grad_up = dot(act_b_all, d_up_all, 0, 0)
        grad_out = dot(att_heads, d_resid_all, 0, 0)
        grad_qkv = [dot(act_a, dqkv_all[:, i * width:(i + 1) * width], 0, 0) for i in range(3)]

        grad_table = scatter_rows(order, sid, bounds, d_embed_all, rows)
        return (layer_out, grad_table, *grad_qkv, grad_out, grad_gate, grad_up, grad_down, gain_grads[0], gain_grads[1])

    col_spec = P(None, "tp")
    row_spec = P("tp", None)
    tok_spec = P("cp")
    rep_spec = P(None)
    in_specs = (tok_spec, tok_spec, tok_spec, P("cp", None), row_spec, col_spec, col_spec, col_spec, row_spec, col_spec, col_spec, row_spec, rep_spec, rep_spec, rep_spec)
    out_specs = (P("cp", None), row_spec, col_spec, col_spec, col_spec, row_spec, col_spec, col_spec, row_spec, rep_spec, rep_spec)
    return jax.shard_map(device_step, mesh=mesh, in_specs=in_specs, out_specs=out_specs, check_vma=False)
```

time: 3530 us -> 1020 us (0.29)
  waiting for transfers between devices: 2490 us -> 291 us
  blocking collectives: 439 us -> 48.3 us
  matrix products: 208 us -> 340 us
  other arithmetic: 183 us -> 53.5 us
  Pallas kernels: 0 us -> 118 us
  local copies, waits for them, and re-layouts: 187 us -> 134 us
    psum x5 -> x0, waiting for transfers between devices: 2450 us -> none  [the longest x1 2040 us: device_step(): grad_table = lax.psum(table_part, 'cp')]
    psum x3 -> x1, blocking collectives: 434 us -> 32.5 us  [device_step(): gain_grads = lax.psum(jnp.stack([grad_gain_a, grad_gain_b]), both)]
    dot_general x27 -> x23, matrix products: 208 us -> 340 us  [the longest x22 337 us: dot(): lax.dot_general(a, b, (((ca,), (cb,)), ((), ())), preferred_element_type=...]
    pallas_call x0 -> x4, Pallas kernels: none -> 118 us  [the longest x1 52.5 us: scatter_rows(): pl.pallas_call(scatter_kernel, out_shape=jax.ShapeDtypeStruct((rows, dim)...]
    scatter-add x1 -> x0, other arithmetic: 110 us -> none  [device_step(): jax.ops.segment_sum(jnp.where(owned[:, None], d_embed, 0.0), safe_ids, nu...]
    reduce_scatter x2 -> x4, waiting for transfers between devices: 31.1 us -> 137 us  [the longest x1 55.9 us: device_step(): lax.psum_scatter(d_act_b, 'tp', scatter_dimension=0, tiled=True)]
    all_gather x2 -> x7, waiting for transfers between devices: 9.41 us -> 115 us  [the longest x1 40.5 us: device_step(): x_all = lax.all_gather(x_slice, both, axis=0, tiled=True)]
    unnamed x136 -> x120, local copies, waits for them, and re-layouts: 135 us -> 30.8 us
  transfers between devices with their start and end apart: 9 -> 15, of which waited for: 7 -> 8; matrix products, arithmetic and copies ran while one was open for 9% -> 37% of each run, Pallas kernels for 0% -> 4%
where the time goes in v1:
time: 1020 us
  matrix products  340 us (33%)
  waiting for transfers between devices  291 us (29%)
  local copies, waits for them, and re-layouts  134 us (13%)
  Pallas kernels  118 us (12%)
  other arithmetic  53.5 us (5%)
  blocking collectives  48.3 us (5%)
  starting transfers between devices  22.9 us (2%)
  between operations  14.7 us (1%)
    dot_general x22, matrix products, dot(): lax.dot_general(a, b, (((ca,), (cb,)), ((), ())), preferred_element_type=...  337 us
    reduce_scatter x1, waiting for transfers between devices, device_step(): lax.psum_scatter(d_act_b, 'tp', scatter_dimension=0, tiled=True)  55.9 us
    pallas_call x1, Pallas kernels, scatter_rows(): pl.pallas_call(scatter_kernel, out_shape=jax.ShapeDtypeStruct((rows, dim)...  52.5 us
    reduce_scatter x1, waiting for transfers between devices, device_step(): x_slice = lax.psum_scatter(picked, 'tp', scatter_dimension=0, tiled=True)  46.5 us
    all_gather x1, waiting for transfers between devices, device_step(): x_all = lax.all_gather(x_slice, both, axis=0, tiled=True)  40.5 us
    all_gather x1, waiting for transfers between devices, device_step(): d_resid_all = lax.all_gather(d_resid.astype(BF16), both, axis=0, tiled=True)  40.4 us
    ppermute x1, waiting for transfers between devices, device_step(): dy_x = lax.ppermute(dy, 'cp', x_swap)  37.6 us
    reduce_scatter x1, waiting for transfers between devices, device_step(): lax.psum_scatter(dot(hidden, w_down, 1, 0), 'tp', scatter_dimension=0, ti...  34.6 us
  transfers between devices with their start and end apart: 15, of which 8 were waited for; matrix products, arithmetic and copies ran while one was open for 37% of the time, Pallas kernels for 4%

profile of v1, /device:TPU:0, one launch (start us, length us, event | category | flops | bytes accessed | tf_op | source)
XLA Modules:
  0.0 1022.1 jit_solution(17715420043482535794)
XLA Ops:
  8.1 13.1 %gather_fusion = bf16[512,2560]{1,0:T(8,128)(2,1)} fusion(bf16[8000,2560]{1,0:T(8,128)(2,1)} %param.19, s32[1024]{0:T(1024)S(1)} %pad_clamp_fusion.2), kind=kCustom, calls=%fused_computation | custom fusion | bytes 5244928 | tf_op jit(solution)/shard_map/jit(_take)/gather | solution.py:311
  24.9 46.5 %reduce-scatter.5.cloned.1.call-done = bf16[128,2560]{1,0:T(8,128)(2,1)} async-done(((bf16[512,2560]{1,0:T(8,128)(2,1)}), bf16[128,2560]{1,0:T(8,128)(2,1)}) %reduce-scatter.5.cloned.1.call-update) | async-done | bytes 655376 | tf_op jit(solution)/shard_map/reduce_scatter | solution.py:312
  88.8 40.5 %all-gather.9.cloned.1.call-done.x = bf16[2048,2560]{1,0:T(8,128)(2,1)} async-done(((bf16[128,2560]{1,0:T(8,128)(2,1)}), bf16[2048,2560]{1,0:T(8,128)(2,1)}) %all-gather.9.cloned.1.call-update) | async-done | bytes 10485776 | tf_op jit(solution)/shard_map/all_gather | solution.py:313
  131.7 33.7 %project_qkv.1 = (bf16[2048,2560]{1,0:T(8,128)(2,1)}, bf16[2048,640]{1,0:T(8,128)(2,1)S(1)}, bf16[2048,640]{1,0:T(8,128)(2,1)}, bf16[2048,640]{1,0:T(8,128)(2,1)}) custom-call(bf16[2048,2560]{1,0:T(8,128)(2,1)} %all-gather.9.cloned.1.call-done.x, f32[1,2560]{1,0:T(1,128)S(1)} %broadcast_in_dim.53.gain, bf16[2560,640]{1,0:T(8,128)(2,1)} %wq.1, ...), custom_call_target="tpu_custom_call" | custom-call | flops 20132659200 | bytes 38666240 | tf_op jit(solution)/shard_map/project_qkv/pallas_call | solution.py:71
  229.5 28.7 %all-gather.21.cloned.1.call-done = bf16[8192,640]{1,0:T(8,128)(2,1)} async-done(((bf16[512,640]{1,0:T(8,128)(2,1)}), bf16[8192,640]{1,0:T(8,128)(2,1)}) %all-gather.21.cloned.1.call-update) | async-done | bytes 10485776 | tf_op jit(solution)/shard_map/all_gather | solution.py:361
  315.7 55.9 %reduce-scatter.9.cloned.1.call-done = f32[128,2560]{1,0:T(8,128)} async-done(((f32[512,2560]{1,0:T(8,128)}), f32[128,2560]{1,0:T(8,128)}) %reduce-scatter.9.cloned.1.call-update) | async-done | bytes 1310736 | tf_op jit(solution)/shard_map/reduce_scatter | solution.py:380
  393.3 40.4 %all-gather.15.cloned.1.call-done = bf16[2048,2560]{1,0:T(8,128)(2,1)} async-done(((bf16[128,2560]{1,0:T(8,128)(2,1)}), bf16[2048,2560]{1,0:T(8,128)(2,1)}) %all-gather.15.cloned.1.call-update) | async-done | bytes 10485776 | tf_op jit(solution)/shard_map/all_gather | solution.py:389
  453.0 20.2 %attend_back.1 = bf16[512,1920]{1,0:T(8,128)(2,1)} custom-call(s32[7]{0:T(128)S(1)} %concatenate.58.info, bf16[2048,640]{1,0:T(8,128)(2,1)} %copy-done.11, bf16[2048,640]{1,0:T(8,128)(2,1)} %get-tuple-element.18.k, bf16[2048,640]{1,0:T(8,128)(2,1)} %get-tuple-element.19.v, bf16[2048,640]{1,0:T(8,128)(2,1)} %copy-done.19, s32[2048,1]{1,0:T(8,128)S(1)} %copy-done.9, ...), custom_call_target="tpu_custom_call" | custom-call | flops 4697620480 | bytes 15728640 | tf_op jit(solution)/shard_map/attend_back/pallas_call | solution.py:211
  484.9 13.0 %fusion.27 = f32[512,2560]{1,0:T(8,128)} fusion(bf16[1728,2560]{1,0:T(8,128)(2,1)} %param.26, f32[512,1728]{0,1:T(8,128)} %fusion.68, f32[512,1728]{0,1:T(8,128)} %fusion.69), kind=kOutput, calls=%fused_computation.54 | convolution fusion | flops 4535156736 | bytes 21168128 | tf_op jit(solution)/shard_map/dot_general | solution.py:36
  526.1 37.6 %collective-permute-done.1 = bf16[512,2560]{1,0:T(8,128)(2,1)} collective-permute-done((bf16[512,2560]{1,0:T(8,128)(2,1)}, bf16[512,2560]{1,0:T(8,128)(2,1)}, u32[]{:S(2)}, u32[]{:S(2)}) %collective-permute-start.1) | collective-permute-done | bytes 2621472 | tf_op jit(solution)/shard_map/ppermute | solution.py:326
  576.0 34.6 %reduce-scatter.7.cloned.1.call-done = f32[128,2560]{1,0:T(8,128)} async-done(((f32[512,2560]{1,0:T(8,128)}), f32[128,2560]{1,0:T(8,128)}) %reduce-scatter.7.cloned.1.call-update) | async-done | bytes 1310736 | tf_op jit(solution)/shard_map/reduce_scatter | solution.py:391
  618.9 25.0 %convolution_convert_fusion = bf16[2048,1728]{0,1:T(8,128)(2,1)} fusion(bf16[2048,2560]{1,0:T(8,128)(2,1)} %constant_dynamic-update-slice_fusion, bf16[1728,2560]{1,0:T(8,128)(2,1)} %param.26), kind=kOutput, calls=%fused_computation.23 | convolution fusion | flops 18122932224 | bytes 26411008 | tf_op jit(solution)/shard_map/dot_general | solution.py:36
  662.3 36.8 %multiply_reduce_fusion = (f32[2048]{0:T(1024)S(1)}, f32[2048,2560]{1,0:T(8,128)}) fusion(bf16[2048,2560]{1,0:T(8,128)(2,1)} %all-gather.9.cloned.1.call-done.x, bf16[2048,2560]{1,0:T(8,128)(2,1)} %bitcast.87, bf16[2560,2560]{1,0:T(8,128)(2,1)} %constant_dynamic-update-slice_fusion.4), kind=kOutput, calls=%fused_computation.5 | convolution fusion | flops 26864515072 | bytes 55058432 | tf_op jit(solution)/shard_map/dot_general | solution.py:36
  699.1 14.4 %multiply_convert_fusion = bf16[2048,2560]{1,0:T(8,128)(2,1)} fusion(f32[2048,2560]{1,0:T(8,128)} %get-tuple-element.51, bf16[2048,2560]{1,0:T(8,128)(2,1)S(1)} %bitcast.86, f32[2560]{0:T(1024)S(1)} %copy-done.26, f32[2048]{0:T(1024)S(1)} %add_rsqrt_fusion), kind=kLoop, calls=%fused_computation.4 | loop fusion | flops 26214400 | bytes 41961472 | tf_op jit(solution)/shard_map/convert_element_type | solution.py:418
  713.6 25.4 %fusion.73 = f32[2048,1728]{0,1:T(8,128)} fusion(bf16[2048,2560]{1,0:T(8,128)(2,1)} %multiply_convert_fusion, bf16[2560,1728]{0,1:T(8,128)(2,1)} %param.25), kind=kOutput, calls=%fused_computation.156 | convolution fusion | flops 18119393280 | bytes 33488896 | tf_op jit(solution)/shard_map/dot_general | solution.py:36
  739.0 23.0 %fusion.74 = f32[2048,1728]{0,1:T(8,128)} fusion(bf16[2048,2560]{1,0:T(8,128)(2,1)S(1)} %copy-done.18, bf16[2560,1728]{0,1:T(8,128)(2,1)} %param.24), kind=kOutput, calls=%fused_computation.157 | convolution fusion | flops 18119393280 | bytes 33488896 | tf_op jit(solution)/shard_map/dot_general | solution.py:36
  762.0 23.8 %fusion.8 = f32[2560,1728]{0,1:T(8,128)} fusion(bf16[2048,2560]{1,0:T(8,128)(2,1)S(1)} %copy-done.18, f32[2048,1728]{0,1:T(8,128)} %fusion.74, bf16[2048,1728]{0,1:T(8,128)(2,1)S(1)} %bitcast.105), kind=kOutput, calls=%fused_computation.25 | convolution fusion | flops 18144165888 | bytes 49414144 | tf_op jit(solution)/shard_map/dot_general | solution.py:36
  785.9 28.4 %fusion.7 = f32[1728,2560]{1,0:T(8,128)} fusion(bf16[2048,2560]{1,0:T(8,128)(2,1)} %constant_dynamic-update-slice_fusion, f32[2048,1728]{0,1:T(8,128)} %fusion.73, f32[2048,1728]{0,1:T(8,128)} %fusion.74), kind=kOutput, calls=%fused_computation.24 | convolution fusion | flops 18140626944 | bytes 56492032 | tf_op jit(solution)/shard_map/dot_general | solution.py:36
  814.3 31.6 %fusion.10 = f32[2560,1728]{0,1:T(8,128)} fusion(bf16[2048,2560]{1,0:T(8,128)(2,1)} %multiply_convert_fusion, f32[2048,1728]{0,1:T(8,128)} %fusion.73, bf16[2048,1728]{0,1:T(8,128)(2,1)} %convolution_convert_fusion, f32[2048,1728]{0,1:T(8,128)} %fusion.74), kind=kOutput, calls=%fused_computation.26 | convolution fusion | flops 18158321664 | bytes 63569920 | tf_op jit(solution)/shard_map/dot_general | solution.py:36
  857.5 32.5 %psum.7 = f32[2,2560]{1,0:T(2,128)S(1)} all-reduce(f32[2,2560]{1,0:T(2,128)S(1)} %pad_maximum_fusion.2), channel_id=1, replica_groups=mesh['tp'=4,'cp'=4] {'cp','tp'}, use_global_device_ids=true, to_apply=%region_19.20 | all-reduce | flops 5120 | bytes 40960 | tf_op jit(solution)/shard_map/psum | solution.py:414
  890.7 13.8 %fusion.25 = f32[2560,640]{1,0:T(8,128)} fusion(bf16[2048,2560]{1,0:T(8,128)(2,1)} %get-tuple-element.22, bf16[2048,1920]{1,0:T(8,128)(2,1)} %all-gather.19.cloned.1.call-done), kind=kOutput, calls=%fused_computation.51 | convolution fusion | flops 6710886400 | bytes 19660800 | tf_op jit(solution)/shard_map/dot_general | solution.py:36
  904.5 13.1 %fusion.23 = f32[2560,640]{1,0:T(8,128)} fusion(bf16[2048,2560]{1,0:T(8,128)(2,1)} %get-tuple-element.22, bf16[2048,1920]{1,0:T(8,128)(2,1)S(1)} %copy-done.40), kind=kOutput, calls=%fused_computation.49 | convolution fusion | flops 6710886400 | bytes 19660800 | tf_op jit(solution)/shard_map/dot_general | solution.py:36
  928.3 26.1 %broadcast_in_dim.86.base_hbm = f32[8000,2560]{1,0:T(8,128)} broadcast(f32[]{:T(128)} %constant.106.clone.1), dimensions={} | broadcast | bytes 81920000 | tf_op jit(solution)/shard_map/broadcast_in_dim | solution.py:266
  961.4 52.5 %scatter_rows.1 = f32[8000,2560]{1,0:T(8,128)} custom-call(s32[2048]{0:T(1024)S(1)} %get-tuple-element.32.order, s32[2048]{0:T(1024)S(1)} %broadcast_subtract_fusion.sid, s32[2]{0:T(128)S(1)} %pad_add_fusion.1.bounds, f32[2048,2560]{1,0:T(8,128)S(1)} %copy-done.2, f32[8000,2560]{1,0:T(8,128)} %broadcast_in_dim.86.base_hbm), custom_call_target="tpu_custom_call", output_to_operand_aliasing={{}: (4, {})} | custom-call | tf_op jit(solution)/shard_map/scatter_rows/pallas_call | solution.py:267
  (238 shorter events, 296.7 us)
Async XLA Ops:
  7.2 64.4 %copy-start = (bf16[640,2560]{1,0:T(8,128)(2,1)S(1)}, bf16[640,2560]{1,0:T(8,128)(2,1)}, u32[]{:S(2)}) copy-start(bf16[640,2560]{1,0:T(8,128)(2,1)} %param.23) | copy-start | bytes 9830404
  7.2 64.3 %reduce-scatter.5.cloned.1.call-start = ((), (), s32[]{:S(2)}) async-start(), calls=%async_computation.4 | async-start | bytes 3276800 | tf_op jit(solution)/shard_map/reduce_scatter | solution.py:312
  24.8 48.1 %copy-start.35 = (s32[512]{0:T(512)S(1)}, s32[512]{0:T(512)}, u32[]{:S(2)}) copy-start(s32[512]{0:T(512)} %param.17) | copy-start | bytes 6148
  24.9 48.1 %copy-start.36 = (s32[512]{0:T(512)S(1)}, s32[512]{0:T(512)}, u32[]{:S(2)}) copy-start(s32[512]{0:T(512)} %param.16) | copy-start | bytes 6148
  24.9 56.5 %copy-start.30 = (bf16[2560]{0:T(1024)(128)(2,1)S(1)}, bf16[2560]{0:T(1024)(128)(2,1)}, u32[]{:S(2)}) copy-start(bf16[2560]{0:T(1024)(128)(2,1)} %param.27) | copy-start | bytes 15364
  24.9 58.3 %copy-start.39 = (f32[64]{0:T(128)S(1)}, f32[64]{0:T(128)}, u32[]{:S(2)}) copy-start(f32[64]{0:T(128)} %param.29) | copy-start | bytes 772
  24.9 104.3 %all-gather.9.cloned.1.call-start = ((), (), s32[]{:S(2)}) async-start(), calls=%async_computation.5 | async-start | bytes 11141120 | tf_op jit(solution)/shard_map/all_gather | solution.py:313
  71.5 128.5 %all-gather.11.cloned.1.call-start = ((), (), s32[]{:S(2)}) async-start(), calls=%async_computation.6 | async-start | bytes 8192000 | tf_op jit(solution)/shard_map/all_gather | solution.py:320
  72.8 185.4 %all-gather.21.cloned.1.call-start = ((), (), s32[]{:S(2)}) async-start(), calls=%async_computation.14 | async-start | bytes 11141120 | tf_op jit(solution)/shard_map/all_gather | solution.py:361
  182.1 189.5 %reduce-scatter.9.cloned.1.call-start = ((), (), s32[]{:S(2)}) async-start(), calls=%async_computation.9 | async-start | bytes 6553600 | tf_op jit(solution)/shard_map/reduce_scatter | solution.py:380
  200.0 23.5 %collective-permute-start = (bf16[2560,1280]{1,0:T(8,128)(2,1)}, bf16[2560,1280]{1,0:T(8,128)(2,1)}, u32[]{:S(2)}, u32[]{:S(2)}) collective-permute-start(bf16[2560,1280]{1,0:T(8,128)(2,1)} %all-gather.11.cloned.1.call-done), channel_id=1, source_target_pairs={{0,1},{1,0},{2,3},{3,2},{4,5},{5,4},{6,7},{7,6},{8,9},{9,8},{10,11... | collective-permute-start | bytes 19660808 | tf_op jit(solution)/shard_map/ppermute | solution.py:321
  314.1 119.6 %all-gather.15.cloned.1.call-start = ((), (), s32[]{:S(2)}) async-start(), calls=%async_computation.10 | async-start | bytes 11141120 | tf_op jit(solution)/shard_map/all_gather | solution.py:389
  315.7 62.4 %copy-start.33 = (f32[128]{0:T(128)}, f32[128]{0:T(128)S(1)}, u32[]{:S(2)}) copy-start(f32[128]{0:T(128)S(1)} %add_rsqrt_fusion.3) | copy-start | bytes 1540
  378.0 195.6 %reduce-scatter.11.cloned.1.call-start = ((), (), s32[]{:S(2)}) async-start(), calls=%async_computation.11 | async-start | bytes 6553600 | tf_op jit(solution)/shard_map/reduce_scatter | solution.py:408
  484.7 125.9 %reduce-scatter.7.cloned.1.call-start = ((), (), s32[]{:S(2)}) async-start(), calls=%async_computation.7 | async-start | bytes 6553600 | tf_op jit(solution)/shard_map/reduce_scatter | solution.py:391
  498.0 392.7 %all-gather.19.cloned.1.call-start = ((), (), s32[]{:S(2)}) async-start(), calls=%async_computation.13 | async-start | bytes 9830400 | tf_op jit(solution)/shard_map/all_gather | solution.py:409
  498.7 429.6 %all-gather.13.cloned.1.call-start = ((), (), s32[]{:S(2)}) async-start(), calls=%async_computation.8 | async-start | bytes 3276800 | tf_op jit(solution)/shard_map/all_gather | solution.py:392
  498.8 64.9 %collective-permute-start.1 = (bf16[512,2560]{1,0:T(8,128)(2,1)}, bf16[512,2560]{1,0:T(8,128)(2,1)}, u32[]{:S(2)}, u32[]{:S(2)}) collective-permute-start(bf16[512,2560]{1,0:T(8,128)(2,1)} %param.18), channel_id=1, source_target_pairs={{0,2},{1,3},{2,0},{3,1},{4,6},{5,7},{6,4},{7,5},{8,10},{9,11},{10,... | collective-permute-start | bytes 7864328 | tf_op jit(solution)/shard_map/ppermute | solution.py:326
  507.0 62.8 %collective-permute-start.2 = (bf16[512,2560]{1,0:T(8,128)(2,1)}, bf16[512,2560]{1,0:T(8,128)(2,1)}, u32[]{:S(2)}, u32[]{:S(2)}) collective-permute-start(bf16[512,2560]{1,0:T(8,128)(2,1)} %param.18), channel_id=1, source_target_pairs={{0,1},{1,0},{2,3},{3,2},{4,5},{5,4},{6,7},{7,6},{8,9},{9,8},{10,11... | collective-permute-start | bytes 7864328 | tf_op jit(solution)/shard_map/ppermute | solution.py:328
  563.7 51.6 %collective-permute-start.3 = (bf16[512,2560]{1,0:T(8,128)(2,1)}, bf16[512,2560]{1,0:T(8,128)(2,1)}, u32[]{:S(2)}, u32[]{:S(2)}) collective-permute-start(bf16[512,2560]{1,0:T(8,128)(2,1)} %collective-permute-done.1), channel_id=1, source_target_pairs={{0,1},{1,0},{2,3},{3,2},{4,5},{5,4},{6,7},{7,6},{8,9},{9,8},{10,11... | collective-permute-start | bytes 7864328 | tf_op jit(solution)/shard_map/ppermute | solution.py:328
  614.8 313.5 %all-gather.17.cloned.1.call-start = ((), (), s32[]{:S(2)}) async-start(), calls=%async_computation.12 | async-start | bytes 22282240 | tf_op jit(solution)/shard_map/all_gather | solution.py:413
  713.6 48.5 %slice-start.15 = ((s8[7077888]{0:T(1024)(128)(4,1)}), s8[4194304]{0:T(1024)(128)(4,1)S(1)}, s32[]{:S(2)}) async-start(s8[7077888]{0:T(1024)(128)(4,1)} %bitcast.104), calls=%async_computation.30 | async-start | bytes 8388608
  961.4 52.5 %copy-start.24 = (bf16[512,2560]{1,0:T(8,128)(2,1)S(1)}, bf16[512,2560]{1,0:T(8,128)(2,1)}, u32[]{:S(2)}) copy-start(bf16[512,2560]{1,0:T(8,128)(2,1)} %all-gather.13.cloned.1.call-done) | copy-start | bytes 7864324
  961.4 54.0 %copy-start.1 = (bf16[640,2560]{1,0:T(8,128)(2,1)S(1)}, bf16[640,2560]{1,0:T(8,128)(2,1)}, u32[]{:S(2)}) copy-start(bf16[640,2560]{1,0:T(8,128)(2,1)} %param.23) | copy-start | bytes 9830404
  (50 other events, 857.3 us)
Sparse Core Ops, SparseCore 0:
  25.0 46.3 reduce-scatter.4
  73.7 55.5 all-gather.8
  131.6 68.3 all-gather.10
  202.6 55.5 all-gather.20
  314.2 57.3 reduce-scatter.8
  378.1 55.5 all-gather.14
  484.8 64.7 reduce-scatter.10
  553.2 57.3 reduce-scatter.6
  612.1 53.5 all-gather.18
  667.4 35.4 all-gather.12
  705.7 89.6 all-gather.16

commit v2 on v1

--- a/solution.py
+++ b/solution.py
@@ -224,6 +224,171 @@
     )(info, *arrays, cos, sin)
 
 
+def out_proj_kernel(info, x, att, w0, w1, w2, w3, gain, res, act, wbuf, sems):
+    tp, rows, width = att.shape
+    part = w0.shape[1]
+
+    def fetch(r):
+        for i, w in enumerate((w0, w1, w2, w3)):
+            @pl.when(r == i)
+            def _(i=i, w=w):
+                pltpu.make_async_copy(w, wbuf.at[i % 2], sems.at[i % 2]).start()
+
+    fetch(0)
+
+    def step(r, c):
+        slot = lax.rem(r, 2)
+        fetch(r + 1)
+        pltpu.make_async_copy(w0, wbuf.at[slot], sems.at[slot]).wait()
+        cols = pl.ds(pl.multiple_of((info[6] ^ r) * part, 128), part)
+        t = x[:, cols].astype(F32)
+        for i in range(tp):
+            t += jnp.dot(att[i], wbuf[slot, i * width:(i + 1) * width, :], preferred_element_type=F32)
+        res[:, cols] = t
+        return c
+
+    lax.fori_loop(0, 4, step, 0)
+    h = res[...]
+    inv = lax.rsqrt(jnp.mean(h * h, axis=-1, keepdims=True) + NORM_EPS)
+    act[...] = (h * inv * gain[...]).astype(BF16)
+
+
+def out_proj(info, flip, x_all, att, pieces, gain):
+    tp, rows, width = att.shape
+    dim = x_all.shape[1]
+    whole = lambda a: pl.BlockSpec(a.shape, lambda i, info: (0,) * a.ndim)
+    full = pl.BlockSpec((rows, dim), lambda i, info: (0, 0))
+    return pl.pallas_call(
+        out_proj_kernel,
+        out_shape=[jax.ShapeDtypeStruct((rows, dim), F32), jax.ShapeDtypeStruct((rows, dim), BF16)],
+        grid_spec=pltpu.PrefetchScalarGridSpec(
+            num_scalar_prefetch=1,
+            grid=(1,),
+            in_specs=[pl.BlockSpec((rows, dim), lambda i, info: (info[6] ^ flip, 0)), whole(att)] + [pl.BlockSpec(memory_space=pl.ANY)] * 4 + [whole(gain)],
+            out_specs=[full, full],
+            scratch_shapes=[pltpu.VMEM((2,) + pieces[0].shape, BF16), pltpu.SemaphoreType.DMA((2,))],
+        ),
+        compiler_params=pltpu.CompilerParams(vmem_limit_bytes=48 * 1024 * 1024),
+        cost_estimate=pl.CostEstimate(flops=2 * rows * dim * dim, bytes_accessed=2 * dim * dim + 10 * rows * dim, transcendentals=0),
+        name="out_proj",
+    )(info, x_all, att, *pieces, gain)
+
+
+def weight_grad_kernel(info, *refs, pieces, splits):
+    lhs = refs[:pieces]
+    rhs = refs[pieces:2 * pieces]
+    outs = refs[2 * pieces:]
+    t = dot(lhs[0][...], rhs[0][...], 0, 0)
+    for a, b in zip(lhs[1:], rhs[1:]):
+        t += dot(a[...], b[...], 0, 0)
+    width = t.shape[1] // splits
+    for i, out in enumerate(outs):
+        out[...] = t[:, i * width:(i + 1) * width]
+
+
+def weight_grad(info, lhs, rhs, block=256, splits=1, rows=None):
+    def spec(arr, p, cols, moving):
+        if arr.ndim == 3:
+            return pl.BlockSpec((None, arr.shape[1], cols), lambda i, info: (info[6] ^ p, 0, i if moving else 0))
+        return pl.BlockSpec((arr.shape[0], cols), lambda i, info: (0, i if moving else 0))
+
+    tokens = lhs[0].shape[-2]
+    rows, dim = rows or lhs[0].shape[-1], rhs[0].shape[-1]
+    n = len(lhs)
+    width = dim // splits
+    outs = pl.pallas_call(
+        functools.partial(weight_grad_kernel, pieces=n, splits=splits),
+        out_shape=[jax.ShapeDtypeStruct((rows, width), F32)] * splits,
+        grid_spec=pltpu.PrefetchScalarGridSpec(
+            num_scalar_prefetch=1,
+            grid=(pl.cdiv(rows, block),),
+            in_specs=[spec(a, p, block, True) for p, a in enumerate(lhs)] + [spec(b, p, dim, False) for p, b in enumerate(rhs)],
+            out_specs=[pl.BlockSpec((block, width), lambda i, info: (i, 0))] * splits,
+        ),
+        compiler_params=pltpu.CompilerParams(vmem_limit_bytes=56 * 1024 * 1024),
+        cost_estimate=pl.CostEstimate(flops=2 * n * tokens * rows * dim, bytes_accessed=4 * rows * dim + 2 * n * tokens * (rows + dim), transcendentals=0),
+        name="weight_grad",
+    )(info, *lhs, *rhs)
+    return outs if splits > 1 else outs[0]
+
+
+def mlp_kernel(act, dhid, wg, wu, hidden, d_gate, d_up, *grad, limit):
+    i = pl.program_id(0)
+    block = wg.shape[0]
+    left = limit - i * block
+    row_ok = lax.broadcasted_iota(jnp.int32, (block, 1), 0) < left
+    col_ok = lax.broadcasted_iota(jnp.int32, (1, block), 1) < left
+    wgt = jnp.where(row_ok, wg[...], jnp.zeros((), BF16))
+    wut = jnp.where(row_ok, wu[...], jnp.zeros((), BF16))
+    gate = dot(act[...], wgt, 1, 1)
+    up = dot(act[...], wut, 1, 1)
+    dh = jnp.where(col_ok, dhid[...].astype(F32), 0.0)
+    sig = jax.nn.sigmoid(gate)
+    hidden[...] = (gate * sig * up).astype(BF16)
+    dg = (dh * up * sig * (1.0 + gate * (1.0 - sig))).astype(BF16)
+    du = (dh * gate * sig).astype(BF16)
+    d_gate[...] = dg
+    d_up[...] = du
+    if grad:
+        t = jnp.dot(dg, wgt, preferred_element_type=F32) + jnp.dot(du, wut, preferred_element_type=F32)
+
+        @pl.when(i == 0)
+        def _():
+            grad[0][...] = t
+
+        @pl.when(i > 0)
+        def _():
+            grad[0][...] += t
+
+
+def mlp_block(act, dhid, wg, wu, with_grad, block=256):
+    rows, dim = act.shape
+    limit = wg.shape[0]
+    cols = pl.BlockSpec((rows, block), lambda i: (0, i))
+    tile = pl.BlockSpec((block, dim), lambda i: (i, 0))
+    whole = pl.BlockSpec((rows, dim), lambda i: (0, 0))
+    return pl.pallas_call(
+        functools.partial(mlp_kernel, limit=limit),
+        out_shape=[jax.ShapeDtypeStruct((rows, pl.cdiv(limit, block) * block), BF16)] * 3 + [jax.ShapeDtypeStruct((rows, dim), F32)] * with_grad,
+        grid=(pl.cdiv(limit, block),),
+        in_specs=[whole, cols, tile, tile],
+        out_specs=[cols] * 3 + [whole] * with_grad,
+        compiler_params=pltpu.CompilerParams(vmem_limit_bytes=48 * 1024 * 1024),
+        cost_estimate=pl.CostEstimate(flops=(4 + 4 * with_grad) * rows * dim * limit, bytes_accessed=4 * dim * limit + 6 * rows * limit + 10 * rows * dim, transcendentals=rows * limit),
+        name="mlp_block",
+    )(act, dhid, wg, wu)
+
+
+def zero_kernel(after, out, zeros, sem):
+    zeros[...] = jnp.zeros_like(zeros)
+    step = zeros.shape[0]
+    count = out.shape[0] // step
+
+    def send(i, c):
+        pltpu.make_async_copy(zeros, out.at[pl.ds(pl.multiple_of(i * step, step), step), :], sem).start()
+        return c
+
+    def wait(i, c):
+        pltpu.make_async_copy(zeros, out.at[pl.ds(0, step), :], sem).wait()
+        return c
+
+    lax.fori_loop(0, count, send, 0)
+    lax.fori_loop(0, count, wait, 0)
+
+
+def zero_rows(after, rows, dim, step=200):
+    return pl.pallas_call(
+        zero_kernel,
+        out_shape=jax.ShapeDtypeStruct((rows, dim), F32),
+        in_specs=[pl.BlockSpec(memory_space=pltpu.SMEM)],
+        out_specs=pl.BlockSpec(memory_space=pl.ANY),
+        scratch_shapes=[pltpu.VMEM((step, dim), F32), pltpu.SemaphoreType.DMA],
+        compiler_params=pltpu.CompilerParams(vmem_limit_bytes=8 * 1024 * 1024),
+        cost_estimate=pl.CostEstimate(flops=rows * dim, bytes_accessed=4 * rows * dim, transcendentals=0),
+        name="zero_rows",
+    )(after)
+
+
 def scatter_kernel(order, sid, bounds, d_hbm, base_hbm, out_hbm, rows, load_sem, row_sem):
     lo = bounds[0]
     hi = bounds[1]
@@ -261,9 +426,9 @@
     lax.fori_loop(0, count, wait_body, 0)
 
 
-def scatter_rows(order, sid, bounds, grads, rows):
+def scatter_rows(order, sid, bounds, grads, base):
     total, dim = grads.shape
-    base = jnp.zeros((rows, dim), F32)
+    rows = base.shape[0]
     return pl.pallas_call(
         scatter_kernel,
         out_shape=jax.ShapeDtypeStruct((rows, dim), F32),
@@ -305,43 +470,45 @@
         def own(arr):
             return lax.dynamic_slice_in_dim(arr, cp_rank * span, span, 0)
 
+        barrier = lax.optimization_barrier
+        swap = lambda arr, pairs, axis="cp": lax.ppermute(arr, axis, pairs)
         local_ids = tokens - tp_rank * rows
         owned = (local_ids >= 0) & (local_ids < rows)
         safe_ids = jnp.where(owned, local_ids, 0)
         picked = jnp.where(owned[:, None], jnp.take(table, safe_ids, axis=0), jnp.zeros((), BF16))
         x_slice = lax.psum_scatter(picked, "tp", scatter_dimension=0, tiled=True)
-        x_all = lax.all_gather(x_slice, both, axis=0, tiled=True)
 
         ints = lax.all_gather(jnp.stack([tokens, pos, doc_id]), "cp", axis=1, tiled=True)
         tok_all, pos_all, doc_all = ints[0], ints[1], ints[2]
-
-        half = dim // 2
-        wo_half = lax.dynamic_slice_in_dim(w_o, core * half, half, 1)
-        wo_mine = lax.all_gather(wo_half, "tp", axis=0, tiled=True)
-        wo_other = lax.ppermute(wo_mine, "cp", core_swap)
-        wo_full = jnp.zeros((tp_count * width, dim), BF16)
-        wo_full = lax.dynamic_update_slice_in_dim(wo_full, wo_mine, core * half, 1)
-        wo_full = lax.dynamic_update_slice_in_dim(wo_full, wo_other, (1 - core) * half, 1)
-
-        dy_x = lax.ppermute(dy, "cp", x_swap)
-        dy_all = jnp.zeros((total, dim), BF16)
-        for piece, who in ((dy, cp_rank), (dy_x, cp_rank ^ 2), (lax.ppermute(dy, "cp", core_swap), cp_rank ^ 1), (lax.ppermute(dy_x, "cp", core_swap), cp_rank ^ 3)):
-            dy_all = lax.dynamic_update_slice_in_dim(dy_all, piece, who * span, 0)
-
-        ids_all = tok_all
         slot_ids = jnp.arange(total, dtype=jnp.int32)
-        before = (ids_all[None, :] < ids_all[:, None]) | ((ids_all[None, :] == ids_all[:, None]) & (slot_ids[None, :] < slot_ids[:, None]))
+        before = (tok_all[None, :] < tok_all[:, None]) | ((tok_all[None, :] == tok_all[:, None]) & (slot_ids[None, :] < slot_ids[:, None]))
         rank = jnp.sum(before.astype(jnp.int32), axis=1)
         at_rank = rank[None, :] == slot_ids[:, None]
         order = jnp.sum(jnp.where(at_rank, slot_ids[None, :], 0), axis=1)
-        sid = jnp.sum(jnp.where(at_rank, ids_all[None, :], 0), axis=1) - tp_rank * rows
-        bounds = jnp.stack([jnp.sum((ids_all < tp_rank * rows).astype(jnp.int32)), jnp.sum((ids_all < (tp_rank + 1) * rows).astype(jnp.int32))])
+        sid = jnp.sum(jnp.where(at_rank, tok_all[None, :], 0), axis=1) - tp_rank * rows
+        order = order + 8 * (order // part)
+        bounds = jnp.stack([jnp.sum((tok_all < tp_rank * rows).astype(jnp.int32)), jnp.sum((tok_all < (tp_rank + 1) * rows).astype(jnp.int32))])
+        base = zero_rows(bounds, rows, dim)
+        quarter = dim // cp_count
+        wo_part = lax.dynamic_slice_in_dim(w_o, cp_rank * quarter, quarter, 1)
+        wo_near = [wo_part] + [swap(wo_part, [(i, i ^ k) for i in range(tp_count)], "tp") for k in (1, 2, 3)]
+        x_slice, base, order, sid, bounds, wo_near = barrier((x_slice, base, order, sid, bounds, wo_near))
+        x_all = lax.all_gather(x_slice, both, axis=0, tiled=True)
+
+        wo_own = jnp.zeros((tp_count * width, quarter), BF16)
+        for k, piece in enumerate(wo_near):
+            wo_own = lax.dynamic_update_slice_in_dim(wo_own, piece, (tp_rank ^ k) * width, 0)
+        wo_core = swap(wo_own, core_swap)
+        wo_x = swap(wo_own, x_swap)
+        wo_diag = swap(wo_x, core_swap)
+        x_all, wo_x = barrier((x_all, wo_x))
 
         angle = pos_all.astype(F32)[:, None] * inv_freq[None, :]
         cos = jnp.cos(angle)
         sin = jnp.sin(angle)
         cos = jnp.concatenate([cos, cos], axis=1)
         sin = jnp.concatenate([-sin, sin], axis=1)
+        dy_x = swap(dy, x_swap)
         act_a, query, key, value = project_qkv(x_all, gain_a[None, :], w_q, w_k, w_v, cos, sin)
 
         blk = span // 2
@@ -358,26 +525,35 @@
         info = jnp.concatenate([b_own, jmin, imax, cp_rank[None]]).astype(jnp.int32)
         attended, lse = attend(info, query, key, value, doc_col, doc_row, head_dim, blk)
 
-        att_parts = lax.all_gather(attended, both, axis=0, tiled=False).reshape(cp_count, tp_count, span, width)
-        att_own = jnp.transpose(lax.dynamic_index_in_dim(att_parts, cp_rank, 0, keepdims=False), (1, 0, 2)).reshape(span, tp_count * width)
-        x_own = own(x_all).astype(F32)
-        residual = x_own + dot(att_own, wo_full, 1, 0)
-        normed_o, inv_o = rms_stats(residual)
-        act_b = (normed_o * gain_b).astype(BF16)
-
-        def mlp(act, dyt):
-            gate = dot(act, w_gate, 1, 0)
-            up_val = dot(act, w_up, 1, 0)
-            gate_sig = jax.nn.sigmoid(gate)
-            hidden = (gate * gate_sig * up_val).astype(BF16)
-            d_hidden = to_bf16(dot(dyt, w_down, 1, 1))
-            d_gate = (d_hidden * up_val * gate_sig * (1.0 + gate * (1.0 - gate_sig))).astype(BF16)
-            d_up = (d_hidden * gate * gate_sig).astype(BF16)
-            return hidden, d_gate, d_up
-
-        hidden, d_gate, d_up = mlp(act_b, dy)
-        d_act_b = dot(d_gate, w_gate, 1, 1) + dot(d_up, w_up, 1, 1)
-        d_act_b = to_bf16(lax.psum_scatter(d_act_b, "tp", scatter_dimension=0, tiled=True))
+        attended, dy_x = barrier((attended, dy_x))
+        att_parts = lax.all_gather(attended, "tp", axis=0, tiled=False)
+        lse_all = lax.all_gather(lse, "cp", axis=0, tiled=True)
+        d_hidden = dot(dy, w_down, 1, 1).astype(BF16)
+        dhid_x = dot(dy_x, w_down, 1, 1).astype(BF16)
+        att_parts, lse_all, d_hidden, dhid_x = barrier((att_parts, lse_all, d_hidden, dhid_x))
+        gain_row = gain_b[None, :]
+        residual, act_b = out_proj(info, 0, x_all, att_parts, (wo_own, wo_core, wo_x, wo_diag), gain_row)
+        att_x = swap(att_parts, x_swap)
+
+        wg, wu = w_gate.T, w_up.T
+        ffn = wg.shape[0]
+        hidden, d_gate, d_up, d_act_b = mlp_block(act_b, d_hidden, wg, wu, True)
+        d_act_b, att_x = barrier((d_act_b, att_x))
+        d_act_b = lax.psum_scatter(d_act_b, "tp", scatter_dimension=0, tiled=True)
+        act_x = out_proj(info, 2, x_all, att_x, (wo_own, wo_core, wo_x, wo_diag), gain_row)[1]
+        hidden_x, d_gate_x, d_up_x = mlp_block(act_x, dhid_x, wg, wu, False)
+        d_act_b, hidden_x, d_gate_x, d_up_x = barrier((d_act_b, hidden_x, d_gate_x, d_up_x))
+        d_act_b = to_bf16(d_act_b)
+        acts, dys, hiddens, d_gates, d_ups = [(a, swap(a, core_swap), b, swap(b, core_swap)) for a, b in (
+            (act_b, act_x), (dy, dy_x), (hidden, hidden_x), (d_gate, d_gate_x), (d_up, d_up_x))]
+        heads_x = lax.dynamic_index_in_dim(att_x, tp_rank, 0, keepdims=False)
+        head_parts = (attended, swap(attended, core_swap), heads_x, swap(heads_x, core_swap))
+        att_heads = jnp.zeros((total, width), BF16)
+        for k, piece in enumerate(head_parts):
+            att_heads = lax.dynamic_update_slice_in_dim(att_heads, piece, (cp_rank ^ k) * span, 0)
+        grad_down = weight_grad(info, hiddens, dys, rows=ffn)
+        grad_gate = weight_grad(info, d_gates, acts, rows=ffn)
+        grad_up = weight_grad(info, d_ups, acts, rows=ffn)
 
         def mine(arr):
             return lax.dynamic_slice_in_dim(arr, tp_rank * part, part, 0)
@@ -387,17 +563,24 @@
         grad_gain_b = jnp.sum(d_act_b * normed_b, axis=0)
         d_resid = mine(dy).astype(F32) + rms_back(d_act_b * gain_b, normed_b, inv_b)
         d_resid_all = lax.all_gather(d_resid.astype(BF16), both, axis=0, tiled=True)
-
-        out_part = lax.psum_scatter(dot(hidden, w_down, 1, 0), "tp", scatter_dimension=0, tiled=True)
-        layer_out = lax.all_gather((res_part + out_part).astype(BF16), "tp", axis=0, tiled=True)
+        d_resid_all, grad_down, grad_gate, grad_up, att_heads = barrier((d_resid_all, grad_down, grad_gate, grad_up, att_heads))
+        tp_swap = lambda arr, k: swap(arr, [(i, i ^ k) for i in range(tp_count)], "tp")
+        tp_slice = lambda arr, k: lax.dynamic_slice_in_dim(arr, (tp_rank ^ k) * part, part, 0)
+        out_part = dot(hidden[:, :ffn], w_down, 1, 0)
+        out_slice = res_part + tp_slice(out_part, 0)
+        for k in (1, 2, 3):
+            out_slice = out_slice + tp_swap(tp_slice(out_part, k), k)
+        out_slice = out_slice.astype(BF16)
+        layer_out = jnp.zeros((span, dim), BF16)
+        for k in range(4):
+            piece = tp_swap(out_slice, k) if k else out_slice
+            layer_out = lax.dynamic_update_slice_in_dim(layer_out, piece, (tp_rank ^ k) * part, 0)
 
         d_att = dot(d_resid_all, w_o, 1, 1)
         d_att_b = d_att.astype(BF16)
-        att_heads = lax.dynamic_index_in_dim(att_parts, tp_rank, 1, keepdims=False).reshape(total, width)
         head_of = (jnp.arange(width)[None, :] // head_dim == jnp.arange(8)[:, None]).astype(F32)
         prod = att_heads.astype(F32) * d_att_b.astype(F32)
         delta = lax.dot_general(head_of, prod, (((1,), (1,)), ((), ())), precision=lax.Precision.HIGHEST, preferred_element_type=F32)
-        lse_all = lax.all_gather(lse, "cp", axis=0, tiled=True)
 
         def by_block(arr):
             return jnp.transpose(arr.reshape(8, blocks, blk), (1, 0, 2))
@@ -406,25 +589,19 @@
         d_q_pre, d_k_pre, d_v_pre = (dqkv[:, i * width:(i + 1) * width] for i in range(3))
         d_act_a = dot(d_q_pre, w_q, 1, 1) + dot(d_k_pre, w_k, 1, 1) + dot(d_v_pre, w_v, 1, 1)
         d_act_a = to_bf16(lax.psum_scatter(d_act_a, "tp", scatter_dimension=0, tiled=True))
-        dqkv_all = lax.all_gather(dqkv, "cp", axis=0, tiled=True)
+        dqkv_x = swap(dqkv, x_swap)
+        dqkvs = (dqkv, swap(dqkv, core_swap), dqkv_x, swap(dqkv_x, core_swap))
         normed_a, inv_a = rms_stats(x_slice.astype(F32))
         grad_gain_a = jnp.sum(d_act_a * normed_a, axis=0)
         d_embed = d_resid + rms_back(d_act_a * gain_a, normed_a, inv_a)
-        d_embed_all = lax.all_gather(d_embed, both, axis=0, tiled=True)
-        gain_grads = lax.psum(jnp.stack([grad_gain_a, grad_gain_b]), both)
-
-        att_all = jnp.transpose(att_parts, (0, 2, 1, 3)).reshape(total, tp_count * width)
-        resid_all = x_all.astype(F32) + dot(att_all, wo_full, 1, 0)
-        act_b_all = (rms_stats(resid_all)[0] * gain_b).astype(BF16)
-        hidden_all, d_gate_all, d_up_all = mlp(act_b_all, dy_all)
-        grad_down = dot(hidden_all, dy_all, 0, 0)
-        grad_gate = dot(act_b_all, d_gate_all, 0, 0)
-        grad_up = dot(act_b_all, d_up_all, 0, 0)
-        grad_out = dot(att_heads, d_resid_all, 0, 0)
-        grad_qkv = [dot(act_a, dqkv_all[:, i * width:(i + 1) * width], 0, 0) for i in range(3)]
-
-        grad_table = scatter_rows(order, sid, bounds, d_embed_all, rows)
-        return (layer_out, grad_table, *grad_qkv, grad_out, grad_gate, grad_up, grad_down, gain_grads[0], gain_grads[1])
+        payload = jnp.concatenate([d_embed, grad_gain_a[None], grad_gain_b[None], jnp.zeros((6, dim), F32)], axis=0)
+        gathered = lax.all_gather(payload, both, axis=0, tiled=True)
+        grad_qkv = weight_grad(info, [act_a.reshape(cp_count, span, dim)] * 4, dqkvs, splits=3)
+        grad_out = weight_grad(info, head_parts, [d_resid_all.reshape(cp_count, span, dim)] * 4)
+        gathered, grad_qkv, grad_out = barrier((gathered, grad_qkv, grad_out))
+        gain_grads = jnp.sum(gathered.reshape(cp_count * tp_count, part + 8, dim)[:, part:part + 2], axis=0)
+        grad_table = scatter_rows(order, sid, bounds, gathered, base)
+        return (layer_out, grad_table, *grad_qkv, grad_out, grad_gate.T, grad_up.T, grad_down, gain_grads[0], gain_grads[1])
 
     col_spec = P(None, "tp")
     row_spec = P("tp", None)

time: 1020 us -> 959 us (0.940)
  matrix products: 340 us -> 54.8 us
  Pallas kernels: 118 us -> 344 us
  waiting for transfers between devices: 291 us -> 347 us
  local copies, waits for them, and re-layouts: 134 us -> 90.9 us
  blocking collectives: 48.3 us -> 15.4 us
  starting transfers between devices: 22.9 us -> 40.8 us
    dot_general x22 -> x7, matrix products: 337 us -> 49.9 us  [dot(): lax.dot_general(a, b, (((ca,), (cb,)), ((), ())), preferred_element_type=...]
    pallas_call x0 -> x10, Pallas kernels: none -> 232 us  [the longest x5 126 us: weight_grad(): pl.pallas_call(functools.partial(weight_grad_kernel, pieces=n, splits=spl...]
    ppermute x4 -> x29, waiting for transfers between devices: 37.6 us -> 251 us  [device_step(): swap = lambda arr, pairs, axis='cp': lax.ppermute(arr, axis, pairs)]
    reduce_scatter x2 -> x1, waiting for transfers between devices: 90.5 us -> 17.9 us  [device_step(): d_act_b = lax.psum_scatter(d_act_b, 'tp', scatter_dimension=0, tiled=True)]
    reduce_scatter x1, waiting for transfers between devices: 0.02 us -> 62.2 us  [device_step(): lax.psum_scatter(d_act_a, 'tp', scatter_dimension=0, tiled=True)]
    all_gather x1, waiting for transfers between devices: 40.5 us -> 0.01 us  [device_step(): x_all = lax.all_gather(x_slice, both, axis=0, tiled=True)]
    all_gather x1, waiting for transfers between devices: 40.4 us -> 0.01 us  [device_step(): d_resid_all = lax.all_gather(d_resid.astype(BF16), both, axis=0, tiled=True)]
    reduce_scatter x1, waiting for transfers between devices: 46.5 us -> 12.1 us  [device_step(): x_slice = lax.psum_scatter(picked, 'tp', scatter_dimension=0, tiled=True)]
  transfers between devices with their start and end apart: 15 -> 36, of which waited for: 8 -> 15; matrix products, arithmetic and copies ran while one was open for 37% -> 9% of each run, Pallas kernels for 4% -> 29%
where the time goes in v2:
time: 959 us; the launch traced here: 952 us
  waiting for transfers between devices  347 us (36%)
  Pallas kernels  344 us (36%)
  local copies, waits for them, and re-layouts  90.9 us (9%)
  matrix products  54.8 us (6%)
  other arithmetic  44.1 us (5%)
  starting transfers between devices  40.8 us (4%)
  blocking collectives  15.4 us (2%)
  between operations  15.2 us (2%)
    ppermute x29, waiting for transfers between devices, device_step(): swap = lambda arr, pairs, axis='cp': lax.ppermute(arr, axis, pairs)  251 us
    pallas_call x5, Pallas kernels, weight_grad(): pl.pallas_call(functools.partial(weight_grad_kernel, pieces=n, splits=spl...  126 us
    reduce_scatter x1, waiting for transfers between devices, device_step(): lax.psum_scatter(d_act_a, 'tp', scatter_dimension=0, tiled=True)  62.2 us
    pallas_call x1, Pallas kernels, scatter_rows(): pl.pallas_call(scatter_kernel, out_shape=jax.ShapeDtypeStruct((rows, dim)...  50.8 us
    dot_general x7, matrix products, dot(): lax.dot_general(a, b, (((ca,), (cb,)), ((), ())), preferred_element_type=...  49.9 us
    pallas_call x2, Pallas kernels, mlp_block(): pl.pallas_call(functools.partial(mlp_kernel, limit=limit), out_shape=[jax...  46.2 us
    unnamed x114, local copies, waits for them, and re-layouts  40.5 us
    ppermute x29, starting transfers between devices, device_step(): swap = lambda arr, pairs, axis='cp': lax.ppermute(arr, axis, pairs)  40.3 us
  transfers between devices with their start and end apart: 36, of which 15 were waited for; matrix products, arithmetic and copies ran while one was open for 9% of the time, Pallas kernels for 29%

profile of v2, /device:TPU:0, one launch (start us, length us, event | category | flops | bytes accessed | tf_op | source)
XLA Modules:
  0.0 952.5 jit_solution(13250587887392551115)
XLA Ops:
  8.1 18.3 %gather_fusion.3 = bf16[512,2560]{1,0:T(8,128)(2,1)} fusion(bf16[8000,2560]{1,0:T(8,128)(2,1)} %param.19, s32[1024]{0:T(1024)S(1)} %pad_clamp_fusion), kind=kCustom, calls=%fused_computation.3 | custom fusion | bytes 5244928 | tf_op jit(solution)/shard_map/jit(_take)/gather | solution.py:478
  31.0 23.8 %collective-permute-start.2 = (bf16[640,640]{1,0:T(8,128)(2,1)}, bf16[640,640]{1,0:T(8,128)(2,1)}, u32[]{:S(2)}, u32[]{:S(2)}) collective-permute-start(bf16[640,640]{1,0:T(8,128)(2,1)} %constant_dynamic-slice_fusion.3), channel_id=1, source_target_pairs={{0,12},{4,8},{8,4},{12,0},{1,13},{5,9},{9,5},{13,1},{2,14},{6,10},... | collective-permute-start | bytes 2457608 | tf_op jit(solution)/shard_map/ppermute | solution.py:474
  63.2 26.2 %zero_rows.1.base_hbm = f32[8000,2560]{1,0:T(8,128)} custom-call(s32[2]{0:T(128)S(1)} %pad_add_fusion.1.after.bounds), custom_call_target="tpu_custom_call" | custom-call | flops 20480000 | bytes 81920000 | tf_op jit(solution)/shard_map/zero_rows/pallas_call | solution.py:380
  104.3 12.1 %reduce-scatter.4.cloned.1.call-done = bf16[128,2560]{1,0:T(8,128)(2,1)} async-done(((bf16[512,2560]{1,0:T(8,128)(2,1)}), bf16[128,2560]{1,0:T(8,128)(2,1)}) %reduce-scatter.4.cloned.1.call-update) | async-done | bytes 655376 | tf_op jit(solution)/shard_map/reduce_scatter | solution.py:479
  143.7 87.2 %collective-permute-done.3.w2 = bf16[2560,640]{1,0:T(8,128)(2,1)} collective-permute-done((bf16[2560,640]{1,0:T(8,128)(2,1)}, bf16[2560,640]{1,0:T(8,128)(2,1)}, u32[]{:S(2)}, u32[]{:S(2)}) %collective-permute-start.3) | collective-permute-done | bytes 3276832 | tf_op jit(solution)/shard_map/ppermute | solution.py:474
  233.3 33.7 %project_qkv.1 = (bf16[2048,2560]{1,0:T(8,128)(2,1)}, bf16[2048,640]{1,0:T(8,128)(2,1)S(1)}, bf16[2048,640]{1,0:T(8,128)(2,1)}, bf16[2048,640]{1,0:T(8,128)(2,1)}) custom-call(bf16[2048,2560]{1,0:T(8,128)(2,1)} %all-gather.6.cloned.1.call-done.x, f32[1,2560]{1,0:T(1,128)S(1)} %broadcast_in_dim.91.gain, bf16[2560,640]{1,0:T(8,128)(2,1)} %wq.1, ...), custom_call_target="tpu_custom_call" | custom-call | flops 20132659200 | bytes 38666240 | tf_op jit(solution)/shard_map/project_qkv/pallas_call | solution.py:71
  325.5 16.5 %out_proj.2 = (f32[512,2560]{1,0:T(8,128)}, bf16[512,2560]{1,0:T(8,128)(2,1)S(1)}) custom-call(s32[7]{0:T(128)S(1)} %copy-done.22, bf16[2048,2560]{1,0:T(8,128)(2,1)} %all-gather.6.cloned.1.call-done.x, bf16[4,512,640]{2,1,0:T(8,128)(2,1)S(1)} %bitcast.55, bf16[2560,640]{1,0:T(8,128)(2,1)} %constant_dynamic-update-slice_fusion.8.w0, ...), custom_call_target="tpu_custom_call" | custom-call | flops 6710886400 | bytes 26214400 | tf_op jit(solution)/shard_map/out_proj/pallas_call | solution.py:261
  343.5 30.4 %mlp_block.2 = (bf16[512,1792]{1,0:T(8,128)(2,1)S(1)}, bf16[512,1792]{1,0:T(8,128)(2,1)S(1)}, bf16[512,1792]{1,0:T(8,128)(2,1)S(1)}, f32[512,2560]{1,0:T(8,128)}) custom-call(bf16[512,2560]{1,0:T(8,128)(2,1)} %copy-done.26, bf16[512,1728]{1,0:T(8,128)(2,1)} %convolution_convert_fusion.2.dhid, bf16[1728,2560]{1,0:T(8,128)(2,1)} %bitcast.71, ...), custom_call_target="tpu_custom_call" | custom-call | flops 18119393280 | bytes 36110336 | tf_op jit(solution)/shard_map/mlp_block/pallas_call | solution.py:350
  385.4 16.5 %out_proj.3 = (f32[512,2560]{1,0:T(8,128)}, bf16[512,2560]{1,0:T(8,128)(2,1)S(1)}) custom-call(s32[7]{0:T(128)S(1)} %copy-done.22, bf16[2048,2560]{1,0:T(8,128)(2,1)} %all-gather.6.cloned.1.call-done.x, bf16[4,512,640]{2,1,0:T(8,128)(2,1)S(1)} %copy-done.14, bf16[2560,640]{1,0:T(8,128)(2,1)} %constant_dynamic-update-slice_fusion.8.w0, ...), custom_call_target="tpu_custom_call" | custom-call | flops 6710886400 | bytes 26214400 | tf_op jit(solution)/shard_map/out_proj/pallas_call | solution.py:261
  403.4 15.8 %mlp_block.3 = (bf16[512,1792]{1,0:T(8,128)(2,1)S(1)}, bf16[512,1792]{1,0:T(8,128)(2,1)}, bf16[512,1792]{1,0:T(8,128)(2,1)S(1)}) custom-call(bf16[512,2560]{1,0:T(8,128)(2,1)} %copy-done.27, bf16[512,1728]{1,0:T(8,128)(2,1)} %convolution_convert_fusion.1.dhid, bf16[1728,2560]{1,0:T(8,128)(2,1)} %bitcast.72, bf16[1728,2560]{1,0:T(8,128)(2,1)} %bitcast.74), custom_call_target="tpu_custom_call" | custom-call | flops 9059696640 | bytes 36110336 | tf_op jit(solution)/shard_map/mlp_block/pallas_call | solution.py:350
  421.7 17.9 %reduce-scatter.6.cloned.1.call-done = f32[128,2560]{1,0:T(8,128)} async-done(((f32[512,2560]{1,0:T(8,128)}), f32[128,2560]{1,0:T(8,128)}) %reduce-scatter.6.cloned.1.call-update) | async-done | bytes 1310736 | tf_op jit(solution)/shard_map/reduce_scatter | solution.py:542
  445.8 11.1 %collective-permute-done.24.refs_1_ = bf16[512,640]{1,0:T(8,128)(2,1)} collective-permute-done((bf16[512,640]{1,0:T(8,128)(2,1)}, bf16[512,640]{1,0:T(8,128)(2,1)}, u32[]{:S(2)}, u32[]{:S(2)}) %collective-permute-start.24) | collective-permute-done | bytes 655392 | tf_op jit(solution)/shard_map/ppermute | solution.py:474
  472.4 27.2 %weight_grad.7 = f32[1728,2560]{1,0:T(8,128)} custom-call(s32[7]{0:T(128)} %concatenate.61.info, bf16[512,1792]{1,0:T(8,128)(2,1)} %copy-done.31, bf16[512,1792]{1,0:T(8,128)(2,1)} %collective-permute-done.22.refs_1_, bf16[512,1792]{1,0:T(8,128)(2,1)} %copy-done.33, bf16[512,1792]{1,0:T(8,128)(2,1)} %collective-permute-done.23.refs_3_, ...), custom_call_target="tpu_custom_call" | custom-call | flops 18119393280 | bytes 35258368 | tf_op jit(solution)/shard_map/weight_grad/pallas_call | solution.py:299
  499.6 27.1 %weight_grad.6 = f32[1728,2560]{1,0:T(8,128)} custom-call(s32[7]{0:T(128)} %concatenate.61.info, bf16[512,1792]{1,0:T(8,128)(2,1)} %copy-done.30, bf16[512,1792]{1,0:T(8,128)(2,1)} %collective-permute-done.18.refs_1_, bf16[512,1792]{1,0:T(8,128)(2,1)} %get-tuple-element.96.refs_2_, bf16[512,1792]{1,0:T(8,128)(2,1)} %collective-permute-done.19.refs_3_, ...), custom_call_target="tpu_custom_call" | custom-call | flops 18119393280 | bytes 35258368 | tf_op jit(solution)/shard_map/weight_grad/pallas_call | solution.py:299
  528.8 27.1 %weight_grad.5 = f32[1728,2560]{1,0:T(8,128)} custom-call(s32[7]{0:T(128)} %concatenate.61.info, bf16[512,1792]{1,0:T(8,128)(2,1)} %copy-done.28, bf16[512,1792]{1,0:T(8,128)(2,1)} %copy-done.56, bf16[512,1792]{1,0:T(8,128)(2,1)} %copy-done.32, bf16[512,1792]{1,0:T(8,128)(2,1)} %collective-permute-done.15.refs_3_, bf16[512,2560]{1,0:T(8,128)(2,1)} %refs_4_.1, ...), custom_call_target="tpu_custom_call" | custom-call | flops 18119393280 | bytes 35258368 | tf_op jit(solution)/shard_map/weight_grad/pallas_call | solution.py:299
  577.0 21.1 %attend_back.1.refs_4_ = bf16[512,1920]{1,0:T(8,128)(2,1)} custom-call(s32[7]{0:T(128)S(1)} %copy-done.23, bf16[2048,640]{1,0:T(8,128)(2,1)} %copy-done.15, bf16[2048,640]{1,0:T(8,128)(2,1)} %get-tuple-element.70.k, bf16[2048,640]{1,0:T(8,128)(2,1)} %get-tuple-element.71.v, bf16[2048,640]{1,0:T(8,128)(2,1)} %copy-done.36, s32[2048,1]{1,0:T(8,128)S(1)} %copy-done.11, ...), custom_call_target="tpu_custom_call" | custom-call | flops 4697620480 | bytes 15728640 | tf_op jit(solution)/shard_map/attend_back/pallas_call | solution.py:211
  609.9 62.2 %reduce-scatter.8.cloned.1.call-done = f32[128,2560]{1,0:T(8,128)} async-done(((f32[512,2560]{1,0:T(8,128)}), f32[128,2560]{1,0:T(8,128)}) %reduce-scatter.8.cloned.1.call-update) | async-done | bytes 1310736 | tf_op jit(solution)/shard_map/reduce_scatter | solution.py:591
  691.2 48.4 %collective-permute-done.7 = f32[128,2560]{1,0:T(8,128)S(1)} collective-permute-done((f32[128,2560]{1,0:T(8,128)S(1)}, f32[128,2560]{1,0:T(8,128)S(1)}, u32[]{:S(2)}, u32[]{:S(2)}) %collective-permute-start.7) | collective-permute-done | bytes 1310752 | tf_op jit(solution)/shard_map/ppermute | solution.py:474
  739.6 34.8 %collective-permute-done.9 = f32[128,2560]{1,0:T(8,128)S(1)} collective-permute-done((f32[128,2560]{1,0:T(8,128)S(1)}, f32[128,2560]{1,0:T(8,128)S(1)}, u32[]{:S(2)}, u32[]{:S(2)}) %collective-permute-start.9) | collective-permute-done | bytes 1310752 | tf_op jit(solution)/shard_map/ppermute | solution.py:474
  782.7 27.6 %collective-permute-done.10 = bf16[128,2560]{1,0:T(8,128)(2,1)S(1)} collective-permute-done((bf16[128,2560]{1,0:T(8,128)(2,1)S(1)}, bf16[128,2560]{1,0:T(8,128)(2,1)S(1)}, u32[]{:S(2)}, u32[]{:S(2)}) %collective-permute-start.10) | collective-permute-done | bytes 655392 | tf_op jit(solution)/shard_map/ppermute | solution.py:474
  812.4 25.5 %collective-permute-done.12 = bf16[128,2560]{1,0:T(8,128)(2,1)S(1)} collective-permute-done((bf16[128,2560]{1,0:T(8,128)(2,1)S(1)}, bf16[128,2560]{1,0:T(8,128)(2,1)S(1)}, u32[]{:S(2)}, u32[]{:S(2)}) %collective-permute-start.12) | collective-permute-done | bytes 655392 | tf_op jit(solution)/shard_map/ppermute | solution.py:474
  838.7 15.0 %weight_grad.9 = f32[640,2560]{1,0:T(8,128)} custom-call(s32[7]{0:T(128)} %concatenate.61.info, bf16[512,640]{1,0:T(8,128)(2,1)} %copy-done.4, bf16[512,640]{1,0:T(8,128)(2,1)} %collective-permute-done.24.refs_1_, bf16[512,640]{1,0:T(8,128)(2,1)} %copy-done.42, bf16[512,640]{1,0:T(8,128)(2,1)} %copy-done.43, bf16[4,512,2560]{2,1,0:T(8,128)(2,1)} %bitcast.60, ...), custom_call_target="tpu_custom_call" | custom-call | flops 6710886400 | bytes 19660800 | tf_op jit(solution)/shard_map/weight_grad/pallas_call | solution.py:299
  855.0 29.9 %weight_grad.8 = (f32[2560,640]{1,0:T(8,128)}, f32[2560,640]{1,0:T(8,128)}, f32[2560,640]{1,0:T(8,128)}) custom-call(s32[7]{0:T(128)} %concatenate.61.info, bf16[4,512,2560]{2,1,0:T(8,128)(2,1)} %bitcast.77, bf16[4,512,2560]{2,1,0:T(8,128)(2,1)} %bitcast.78, bf16[4,512,2560]{2,1,0:T(8,128)(2,1)} %bitcast.79, bf16[4,512,2560]{2,1,0:T(8,128)(2,1)} %bitcast.80, ...), custom_call_target="tpu_custom_call" | custom-call | flops 20132659200 | bytes 38010880 | tf_op jit(solution)/shard_map/weight_grad/pallas_call | solution.py:299
  894.3 50.8 %scatter_rows.1 = f32[8000,2560]{1,0:T(8,128)} custom-call(s32[2048]{0:T(1024)S(1)} %get-tuple-element.82.order, s32[2048]{0:T(1024)S(1)} %get-tuple-element.83.sid, s32[2]{0:T(128)S(1)} %copy-done.25, f32[2176,2560]{1,0:T(8,128)S(1)} %copy-done.2, f32[8000,2560]{1,0:T(8,128)} %zero_rows.1.base_hbm), custom_call_target="tpu_custom_call", output_to_operand_aliasing={{}: (4, {})} | custom-call | tf_op jit(solution)/shard_map/scatter_rows/pallas_call | solution.py:432
  (262 shorter events, 231.1 us)
Async XLA Ops:
  7.2 109.2 %reduce-scatter.4.cloned.1.call-start = ((), (), s32[]{:S(2)}) async-start(), calls=%async_computation.3 | async-start | bytes 3276800 | tf_op jit(solution)/shard_map/reduce_scatter | solution.py:479
  30.0 200.8 %all-gather.6.cloned.1.call-start = ((), (), s32[]{:S(2)}) async-start(), calls=%async_computation.4 | async-start | bytes 11141120 | tf_op jit(solution)/shard_map/all_gather | solution.py:496
  31.0 69.2 %collective-permute-start.2 = (bf16[640,640]{1,0:T(8,128)(2,1)}, bf16[640,640]{1,0:T(8,128)(2,1)}, u32[]{:S(2)}, u32[]{:S(2)}) collective-permute-start(bf16[640,640]{1,0:T(8,128)(2,1)} %constant_dynamic-slice_fusion.3), channel_id=1, source_target_pairs={{0,12},{4,8},{8,4},{12,0},{1,13},{5,9},{9,5},{13,1},{2,14},{6,10},... | collective-permute-start | bytes 2457608 | tf_op jit(solution)/shard_map/ppermute | solution.py:474
  54.8 49.5 %collective-permute-start.1 = (bf16[640,640]{1,0:T(8,128)(2,1)}, bf16[640,640]{1,0:T(8,128)(2,1)}, u32[]{:S(2)}, u32[]{:S(2)}) collective-permute-start(bf16[640,640]{1,0:T(8,128)(2,1)} %constant_dynamic-slice_fusion.3), channel_id=1, source_target_pairs={{0,8},{4,12},{8,0},{12,4},{1,9},{5,13},{9,1},{13,5},{2,10},{6,14},... | collective-permute-start | bytes 2457608 | tf_op jit(solution)/shard_map/ppermute | solution.py:474
  54.8 49.5 %collective-permute-start = (bf16[640,640]{1,0:T(8,128)(2,1)}, bf16[640,640]{1,0:T(8,128)(2,1)}, u32[]{:S(2)}, u32[]{:S(2)}) collective-permute-start(bf16[640,640]{1,0:T(8,128)(2,1)} %constant_dynamic-slice_fusion.3), channel_id=1, source_target_pairs={{0,4},{4,0},{8,12},{12,8},{1,5},{5,1},{9,13},{13,9},{2,6},{6,2},{1... | collective-permute-start | bytes 2457608 | tf_op jit(solution)/shard_map/ppermute | solution.py:474
  116.4 205.8 %all-gather.12.cloned.1.call-start = ((), (), s32[]{:S(2)}) async-start(), calls=%async_computation.9 | async-start | bytes 3276800 | tf_op jit(solution)/shard_map/all_gather | solution.py:529
  127.1 103.7 %collective-permute-start.3 = (bf16[2560,640]{1,0:T(8,128)(2,1)}, bf16[2560,640]{1,0:T(8,128)(2,1)}, u32[]{:S(2)}, u32[]{:S(2)}) collective-permute-start(bf16[2560,640]{1,0:T(8,128)(2,1)} %constant_dynamic-update-slice_fusion.8.w0), channel_id=1, source_target_pairs={{0,2},{1,3},{2,0},{3,1},{4,6},{5,7},{6,4},{7,5},{8,10},{9,11},{10,... | collective-permute-start | bytes 9830408 | tf_op jit(solution)/shard_map/ppermute | solution.py:474
  128.5 158.0 %collective-permute-start.4 = (bf16[512,2560]{1,0:T(8,128)(2,1)}, bf16[512,2560]{1,0:T(8,128)(2,1)}, u32[]{:S(2)}, u32[]{:S(2)}) collective-permute-start(bf16[512,2560]{1,0:T(8,128)(2,1)} %refs_4_.1), channel_id=1, source_target_pairs={{0,2},{1,3},{2,0},{3,1},{4,6},{5,7},{6,4},{7,5},{8,10},{9,11},{10,... | collective-permute-start | bytes 7864328 | tf_op jit(solution)/shard_map/ppermute | solution.py:474
  286.6 153.0 %reduce-scatter.6.cloned.1.call-start = ((), (), s32[]{:S(2)}) async-start(), calls=%async_computation.5 | async-start | bytes 6553600 | tf_op jit(solution)/shard_map/reduce_scatter | solution.py:542
  322.2 58.4 %collective-permute-start.13 = (bf16[4,512,640]{2,1,0:T(8,128)(2,1)}, bf16[4,512,640]{2,1,0:T(8,128)(2,1)S(1)}, u32[]{:S(2)}, u32[]{:S(2)}) collective-permute-start(bf16[4,512,640]{2,1,0:T(8,128)(2,1)} %bitcast.54), channel_id=1, source_target_pairs={{0,2},{1,3},{2,0},{3,1},{4,6},{5,7},{6,4},{7,5},{8,10},{9,11},{10,... | collective-permute-start | bytes 7864328 | tf_op jit(solution)/shard_map/ppermute | solution.py:474
  382.1 173.8 %all-gather.8.cloned.1.call-start = ((), (), s32[]{:S(2)}) async-start(), calls=%async_computation.6 | async-start | bytes 11141120 | tf_op jit(solution)/shard_map/all_gather | solution.py:565
  444.6 227.5 %reduce-scatter.8.cloned.1.call-start = ((), (), s32[]{:S(2)}) async-start(), calls=%async_computation.7 | async-start | bytes 6553600 | tf_op jit(solution)/shard_map/reduce_scatter | solution.py:591
  471.3 55.4 %collective-permute-start.16 = (bf16[512,2560]{1,0:T(8,128)(2,1)}, bf16[512,2560]{1,0:T(8,128)(2,1)S(1)}, u32[]{:S(2)}, u32[]{:S(2)}) collective-permute-start(bf16[512,2560]{1,0:T(8,128)(2,1)} %refs_4_.1), channel_id=1, source_target_pairs={{0,1},{1,0},{2,3},{3,2},{4,5},{5,4},{6,7},{7,6},{8,9},{9,8},{10,11... | collective-permute-start | bytes 7864328 | tf_op jit(solution)/shard_map/ppermute | solution.py:474
  471.5 55.2 %collective-permute-start.17 = (bf16[512,2560]{1,0:T(8,128)(2,1)}, bf16[512,2560]{1,0:T(8,128)(2,1)}, u32[]{:S(2)}, u32[]{:S(2)}) collective-permute-start(bf16[512,2560]{1,0:T(8,128)(2,1)} %collective-permute-done.4.refs_6_), channel_id=1, source_target_pairs={{0,1},{1,0},{2,3},{3,2},{4,5},{5,4},{6,7},{7,6},{8,9},{9,8},{10,11... | collective-permute-start | bytes 7864328 | tf_op jit(solution)/shard_map/ppermute | solution.py:474
  471.8 54.9 %collective-permute-start.14 = (bf16[512,1792]{1,0:T(8,128)(2,1)}, bf16[512,1792]{1,0:T(8,128)(2,1)S(1)}, u32[]{:S(2)}, u32[]{:S(2)}) collective-permute-start(bf16[512,1792]{1,0:T(8,128)(2,1)} %copy-done.28), channel_id=1, source_target_pairs={{0,1},{1,0},{2,3},{3,2},{4,5},{5,4},{6,7},{7,6},{8,9},{9,8},{10,11... | collective-permute-start | bytes 5505032 | tf_op jit(solution)/shard_map/ppermute | solution.py:474
  472.0 54.7 %collective-permute-start.15 = (bf16[512,1792]{1,0:T(8,128)(2,1)}, bf16[512,1792]{1,0:T(8,128)(2,1)}, u32[]{:S(2)}, u32[]{:S(2)}) collective-permute-start(bf16[512,1792]{1,0:T(8,128)(2,1)} %copy-done.32), channel_id=1, source_target_pairs={{0,1},{1,0},{2,3},{3,2},{4,5},{5,4},{6,7},{7,6},{8,9},{9,8},{10,11... | collective-permute-start | bytes 5505032 | tf_op jit(solution)/shard_map/ppermute | solution.py:474
  608.6 276.3 %all-gather.10.cloned.1.call-start = ((), (), s32[]{:S(2)}) async-start(), calls=%async_computation.8 | async-start | bytes 23674880 | tf_op jit(solution)/shard_map/all_gather | solution.py:598
  686.2 53.4 %collective-permute-start.7 = (f32[128,2560]{1,0:T(8,128)S(1)}, f32[128,2560]{1,0:T(8,128)S(1)}, u32[]{:S(2)}, u32[]{:S(2)}) collective-permute-start(f32[128,2560]{1,0:T(8,128)S(1)} %get-tuple-element.133), channel_id=1, source_target_pairs={{0,4},{4,0},{8,12},{12,8},{1,5},{5,1},{9,13},{13,9},{2,6},{6,2},{1... | collective-permute-start | bytes 3932168 | tf_op jit(solution)/shard_map/ppermute | solution.py:474
  687.7 86.7 %collective-permute-start.9 = (f32[128,2560]{1,0:T(8,128)S(1)}, f32[128,2560]{1,0:T(8,128)S(1)}, u32[]{:S(2)}, u32[]{:S(2)}) collective-permute-start(f32[128,2560]{1,0:T(8,128)S(1)} %get-tuple-element.134), channel_id=1, source_target_pairs={{0,12},{4,8},{8,4},{12,0},{1,13},{5,9},{9,5},{13,1},{2,14},{6,10},... | collective-permute-start | bytes 3932168 | tf_op jit(solution)/shard_map/ppermute | solution.py:474
  689.2 85.2 %collective-permute-start.8 = (f32[128,2560]{1,0:T(8,128)S(1)}, f32[128,2560]{1,0:T(8,128)S(1)}, u32[]{:S(2)}, u32[]{:S(2)}) collective-permute-start(f32[128,2560]{1,0:T(8,128)S(1)} %get-tuple-element.135), channel_id=1, source_target_pairs={{0,8},{4,12},{8,0},{12,4},{1,9},{5,13},{9,1},{13,5},{2,10},{6,14},... | collective-permute-start | bytes 3932168 | tf_op jit(solution)/shard_map/ppermute | solution.py:474
  689.7 89.9 %collective-permute-start.27 = (bf16[512,1920]{1,0:T(8,128)(2,1)S(1)}, bf16[512,1920]{1,0:T(8,128)(2,1)S(1)}, u32[]{:S(2)}, u32[]{:S(2)}) collective-permute-start(bf16[512,1920]{1,0:T(8,128)(2,1)S(1)} %copy-done.40), channel_id=1, source_target_pairs={{0,2},{1,3},{2,0},{3,1},{4,6},{5,7},{6,4},{7,5},{8,10},{9,11},{10,... | collective-permute-start | bytes 5898248 | tf_op jit(solution)/shard_map/ppermute | solution.py:474
  779.7 74.1 %collective-permute-start.26 = (bf16[512,1920]{1,0:T(8,128)(2,1)S(1)}, bf16[512,1920]{1,0:T(8,128)(2,1)S(1)}, u32[]{:S(2)}, u32[]{:S(2)}) collective-permute-start(bf16[512,1920]{1,0:T(8,128)(2,1)S(1)} %copy-done.40), channel_id=1, source_target_pairs={{0,1},{1,0},{2,3},{3,2},{4,5},{5,4},{6,7},{7,6},{8,9},{9,8},{10,11... | collective-permute-start | bytes 5898248 | tf_op jit(solution)/shard_map/ppermute | solution.py:474
  779.7 74.1 %collective-permute-start.28 = (bf16[512,1920]{1,0:T(8,128)(2,1)S(1)}, bf16[512,1920]{1,0:T(8,128)(2,1)}, u32[]{:S(2)}, u32[]{:S(2)}) collective-permute-start(bf16[512,1920]{1,0:T(8,128)(2,1)S(1)} %collective-permute-done.27.refs_6_), channel_id=1, source_target_pairs={{0,1},{1,0},{2,3},{3,2},{4,5},{5,4},{6,7},{7,6},{8,9},{9,8},{10,11... | collective-permute-start | bytes 5898248 | tf_op jit(solution)/shard_map/ppermute | solution.py:474
  780.2 57.7 %collective-permute-start.12 = (bf16[128,2560]{1,0:T(8,128)(2,1)S(1)}, bf16[128,2560]{1,0:T(8,128)(2,1)S(1)}, u32[]{:S(2)}, u32[]{:S(2)}) collective-permute-start(bf16[128,2560]{1,0:T(8,128)(2,1)S(1)} %get-tuple-element.130), channel_id=1, source_target_pairs={{0,12},{4,8},{8,4},{12,0},{1,13},{5,9},{9,5},{13,1},{2,14},{6,10},... | collective-permute-start | bytes 1966088 | tf_op jit(solution)/shard_map/ppermute | solution.py:474
  (69 other events, 895.8 us)
Sparse Core Ops, SparseCore 0:
  30.1 86.2 reduce-scatter.3
  118.6 87.2 all-gather.5
  286.7 35.4 all-gather.11
  382.2 57.3 reduce-scatter.5
  444.8 55.5 all-gather.7
  608.7 63.3 reduce-scatter.7
  677.7 172.6 all-gather.9

commit v3 on v2

--- a/solution.py
+++ b/solution.py
@@ -21,13 +21,6 @@
     return inv_rms * (d_normed - normed * jnp.mean(d_normed * normed, axis=-1, keepdims=True))
 
 
-def rotate(tensor_in, cosine, sine):
-    half = tensor_in.shape[-1] // 2
-    first = tensor_in[..., :half]
-    second = tensor_in[..., half:]
-    return jnp.concatenate([first * cosine - second * sine, second * cosine + first * sine], axis=-1)
-
-
 def to_bf16(feats):
     return feats.astype(BF16).astype(F32)
 
@@ -36,45 +29,45 @@
     return lax.dot_general(a, b, (((ca,), (cb,)), ((), ())), preferred_element_type=F32)
 
 
-def slot_sequence(slot, block_len, cp_count):
-    shard = slot // (2 * block_len)
-    within = slot % (2 * block_len)
-    block_no = jnp.where(within < block_len, shard, 2 * cp_count - 1 - shard)
-    return block_no * block_len + within % block_len
-
-
 def slot_block(j):
     return jnp.where(j < 4, 2 * j, 15 - 2 * j)
 
 
-def qkv_kernel(x, gain, wq, wk, wv, cos, sin, act, q, k, v, *, head_dim):
+def qkv_kernel(x, gain, wq, wk, wv, cos, sin, act, q, k, v, wide, *, head_dim):
+    width = wq.shape[1]
+
+    @pl.when(pl.program_id(0) == 0)
+    def _():
+        for i, w in enumerate((wq, wk, wv)):
+            wide[:, i * width:(i + 1) * width] = w[...]
+
     feats = x[...].astype(F32)
     inv = lax.rsqrt(jnp.mean(feats * feats, axis=-1, keepdims=True) + NORM_EPS)
     a = (feats * inv * gain[...]).astype(BF16)
     act[...] = a
-    for w, out, turn in ((wq, q, True), (wk, k, True), (wv, v, False)):
-        t = jnp.dot(a, w[...], preferred_element_type=F32)
-        for h in range(w.shape[1] // head_dim):
-            cols = slice(h * head_dim, (h + 1) * head_dim)
-            th = t[:, cols]
-            if turn:
+    t = jnp.dot(a, wide[...], preferred_element_type=F32)
+    for i, out in enumerate((q, k, v)):
+        for h in range(width // head_dim):
+            th = t[:, i * width + h * head_dim:i * width + (h + 1) * head_dim]
+            if i < 2:
                 th = th * cos[...] + pltpu.roll(th, head_dim // 2, 1) * sin[...]
-            out[:, cols] = th.astype(BF16)
-
-
-def project_qkv(x_all, gain, wq, wk, wv, cos, sin, block=256):
+            out[:, h * head_dim:(h + 1) * head_dim] = th.astype(BF16)
+
+
+def project_qkv(x_all, gain, wq, wk, wv, cos, sin, block=512):
     total, dim = x_all.shape
     width = wq.shape[1]
     head_dim = cos.shape[1]
     rows = lambda n: pl.BlockSpec((block, n), lambda i: (i, 0))
-    whole = lambda a: pl.BlockSpec(a.shape, lambda i: (0, 0))
+    whole = lambda a: pl.BlockSpec(a.shape, lambda i: (0, 0), pipeline_mode=pl.Buffered(1))
     return pl.pallas_call(
         functools.partial(qkv_kernel, head_dim=head_dim),
         out_shape=[jax.ShapeDtypeStruct((total, n), BF16) for n in (dim, width, width, width)],
         grid=(total // block,),
         in_specs=[rows(dim), whole(gain), whole(wq), whole(wk), whole(wv), rows(head_dim), rows(head_dim)],
         out_specs=[rows(dim), rows(width), rows(width), rows(width)],
-        compiler_params=pltpu.CompilerParams(vmem_limit_bytes=48 * 1024 * 1024),
+        scratch_shapes=[pltpu.VMEM((dim, 3 * width), BF16)],
+        compiler_params=pltpu.CompilerParams(vmem_limit_bytes=60 * 1024 * 1024),
         cost_estimate=pl.CostEstimate(flops=6 * total * dim * width, bytes_accessed=4 * total * dim + 6 * dim * width + 6 * total * width, transcendentals=0),
         name="project_qkv",
     )(x_all, gain, wq, wk, wv, cos, sin)
@@ -176,7 +169,6 @@
         return c
 
     lax.fori_loop(jmin, b + 1, for_query, 0)
-    my_block = 2 * info[6] + i
 
     def for_key(j, c):
         sb = slot_block(j)
@@ -224,37 +216,35 @@
     )(info, *arrays, cos, sin)
 
 
-def out_proj_kernel(info, x, att, w0, w1, w2, w3, gain, res, act, wbuf, sems):
-    tp, rows, width = att.shape
-    part = w0.shape[1]
-
-    def fetch(r):
-        for i, w in enumerate((w0, w1, w2, w3)):
-            @pl.when(r == i)
-            def _(i=i, w=w):
-                pltpu.make_async_copy(w, wbuf.at[i % 2], sems.at[i % 2]).start()
-
-    fetch(0)
-
-    def step(r, c):
-        slot = lax.rem(r, 2)
-        fetch(r + 1)
-        pltpu.make_async_copy(w0, wbuf.at[slot], sems.at[slot]).wait()
-        cols = pl.ds(pl.multiple_of((info[6] ^ r) * part, 128), part)
-        t = x[:, cols].astype(F32)
-        for i in range(tp):
-            t += jnp.dot(att[i], wbuf[slot, i * width:(i + 1) * width, :], preferred_element_type=F32)
-        res[:, cols] = t
-        return c
-
-    lax.fori_loop(0, 4, step, 0)
+def out_proj_kernel(info, x, att, a0, b0, a1, b1, gain, res, act, wide, abuf, bbuf, sems):
+    tp, _, width = att.shape
+    na, nb = a0.shape[1], b0.shape[1]
+    sets = ((a0, b0), (a1, b1))
+
+    def copies(i):
+        return (pltpu.make_async_copy(sets[i][0], abuf.at[i], sems.at[i, 0]), pltpu.make_async_copy(sets[i][1], bbuf.at[i], sems.at[i, 1]))
+
+    for i in range(2):
+        for c in copies(i):
+            c.start()
+    for t in range(tp):
+        wide[:, t * width:(t + 1) * width] = att[t]
+    for i in range(2):
+        start = (info[7] ^ i) * (na + nb)
+        first, second = copies(i)
+        first.wait()
+        cols = pl.ds(pl.multiple_of(start, 128), na)
+        res[:, cols] = x[:, cols].astype(F32) + jnp.dot(wide[...], abuf[i], preferred_element_type=F32)
+        second.wait()
+        cols = pl.ds(pl.multiple_of(start + na, 128), nb)
+        res[:, cols] = x[:, cols].astype(F32) + jnp.dot(wide[...], bbuf[i], preferred_element_type=F32)
     h = res[...]
     inv = lax.rsqrt(jnp.mean(h * h, axis=-1, keepdims=True) + NORM_EPS)
     act[...] = (h * inv * gain[...]).astype(BF16)
 
 
 def out_proj(info, flip, x_all, att, pieces, gain):
-    tp, rows, width = att.shape
+    _, rows, _ = att.shape
     dim = x_all.shape[1]
     whole = lambda a: pl.BlockSpec(a.shape, lambda i, info: (0,) * a.ndim)
     full = pl.BlockSpec((rows, dim), lambda i, info: (0, 0))
@@ -266,9 +256,9 @@
             grid=(1,),
             in_specs=[pl.BlockSpec((rows, dim), lambda i, info: (info[6] ^ flip, 0)), whole(att)] + [pl.BlockSpec(memory_space=pl.ANY)] * 4 + [whole(gain)],
             out_specs=[full, full],
-            scratch_shapes=[pltpu.VMEM((2,) + pieces[0].shape, BF16), pltpu.SemaphoreType.DMA((2,))],
+            scratch_shapes=[pltpu.VMEM((rows, dim), BF16), pltpu.VMEM((2,) + pieces[0].shape, BF16), pltpu.VMEM((2,) + pieces[1].shape, BF16), pltpu.SemaphoreType.DMA((2, 2))],
         ),
-        compiler_params=pltpu.CompilerParams(vmem_limit_bytes=48 * 1024 * 1024),
+        compiler_params=pltpu.CompilerParams(vmem_limit_bytes=56 * 1024 * 1024),
         cost_estimate=pl.CostEstimate(flops=2 * rows * dim * dim, bytes_accessed=2 * dim * dim + 10 * rows * dim, transcendentals=0),
         name="out_proj",
     )(info, x_all, att, *pieces, gain)
@@ -389,60 +379,71 @@
     )(after)
 
 
-def scatter_kernel(order, sid, bounds, d_hbm, base_hbm, out_hbm, rows, load_sem, row_sem):
+def scatter_kernel(order, sid, runs, bounds, rows, base_hbm, out_hbm, sums, row_sem, sum_sem):
     lo = bounds[0]
     hi = bounds[1]
-    load = pltpu.make_async_copy(d_hbm, rows, load_sem)
-    load.start()
-    load.wait()
-
-    def add_body(p, first):
+
+    def one(c):
+        p, singles, multi = c
+        n = runs[p]
         t = order[p]
-        same = jnp.logical_and(p > lo, sid[p] == sid[jnp.maximum(p - 1, 0)])
-
-        @pl.when(same)
+        single = n == 1
+
+        @pl.when(single)
         def _():
-            rows[pl.ds(first, 1), :] = rows[pl.ds(first, 1), :] + rows[pl.ds(t, 1), :]
-
-        return jnp.where(same, first, t)
-
-    lax.fori_loop(lo, hi, add_body, 0)
-
-    def send_body(p, count):
-        new = jnp.logical_or(p == lo, sid[p] != sid[jnp.maximum(p - 1, 0)])
-
-        @pl.when(new)
+            pltpu.make_async_copy(rows.at[pl.ds(t, 1), :], out_hbm.at[pl.ds(sid[p], 1), :], row_sem).start()
+
+        @pl.when(jnp.logical_not(single))
         def _():
-            pltpu.make_async_copy(rows.at[pl.ds(order[p], 1), :], out_hbm.at[pl.ds(sid[p], 1), :], row_sem).start()
-
-        return count + new.astype(jnp.int32)
-
-    count = lax.fori_loop(lo, hi, send_body, 0)
-
-    def wait_body(p, c):
-        pltpu.make_async_copy(rows.at[pl.ds(0, 1), :], out_hbm.at[pl.ds(0, 1), :], row_sem).wait()
-        return c
-
-    lax.fori_loop(0, count, wait_body, 0)
-
-
-def scatter_rows(order, sid, bounds, grads, base):
-    total, dim = grads.shape
+            def add(j, acc):
+                return acc + rows[pl.ds(order[p + j], 1), :]
+
+            sums[pl.ds(multi, 1), :] = lax.fori_loop(1, n, add, rows[pl.ds(t, 1), :])
+
+        return p + n, singles + single.astype(jnp.int32), multi + 1 - single.astype(jnp.int32)
+
+    _, singles, multi = lax.while_loop(lambda c: c[0] < hi, one, (lo, 0, 0))
+
+    def two(c):
+        p, k = c
+        n = runs[p]
+
+        @pl.when(n > 1)
+        def _():
+            pltpu.make_async_copy(sums.at[pl.ds(k, 1), :], out_hbm.at[pl.ds(sid[p], 1), :], sum_sem).start()
+
+        return p + n, k + (n > 1).astype(jnp.int32)
+
+    lax.while_loop(lambda c: c[0] < hi, two, (lo, 0))
+
+    def wait(sem):
+        def body(i, c):
+            pltpu.make_async_copy(sums.at[pl.ds(0, 1), :], out_hbm.at[pl.ds(0, 1), :], sem).wait()
+            return c
+
+        return body
+
+    lax.fori_loop(0, singles, wait(row_sem), 0)
+    lax.fori_loop(0, multi, wait(sum_sem), 0)
+
+
+def scatter_rows(order, sid, runs, bounds, grads, base, tokens):
+    _, dim = grads.shape
     rows = base.shape[0]
     return pl.pallas_call(
         scatter_kernel,
         out_shape=jax.ShapeDtypeStruct((rows, dim), F32),
         grid_spec=pltpu.PrefetchScalarGridSpec(
-            num_scalar_prefetch=3,
+            num_scalar_prefetch=4,
             grid=(),
-            in_specs=[pl.BlockSpec(memory_space=pl.ANY), pl.BlockSpec(memory_space=pl.ANY)],
+            in_specs=[pl.BlockSpec(memory_space=pltpu.VMEM), pl.BlockSpec(memory_space=pl.ANY)],
             out_specs=pl.BlockSpec(memory_space=pl.ANY),
-            scratch_shapes=[pltpu.VMEM((total, dim), F32), pltpu.SemaphoreType.DMA, pltpu.SemaphoreType.DMA],
+            scratch_shapes=[pltpu.VMEM((tokens // 2, dim), F32), pltpu.SemaphoreType.DMA, pltpu.SemaphoreType.DMA],
         ),
-        input_output_aliases={4: 0},
-        compiler_params=pltpu.CompilerParams(vmem_limit_bytes=28 * 1024 * 1024),
+        input_output_aliases={5: 0},
+        compiler_params=pltpu.CompilerParams(vmem_limit_bytes=40 * 1024 * 1024),
         name="scatter_rows",
-    )(order, sid, bounds, grads, base)
+    )(order, sid, runs, bounds, grads, base)
 
 
 def solution(mesh):
@@ -452,7 +453,7 @@
     x_swap = [(i, i ^ 2) for i in range(cp_count)]
     core_swap = [(i, i ^ 1) for i in range(cp_count)]
 
-    def device_step(tokens, pos, doc_id, dy, table, w_q, w_k, w_v, w_o, w_gate, w_up, w_down, gain_one, gain_two, inv_freq):
+    def compute(tokens, pos, doc_id, dy, table, w_q, w_k, w_v, w_o, w_gate, w_up, w_down, gain_one, gain_two, inv_freq):
         span = tokens.shape[0]
         total = span * cp_count
         part = span // tp_count
@@ -460,15 +461,11 @@
         head_dim = 2 * inv_freq.shape[0]
         heads = w_q.shape[1] // head_dim
         width = heads * head_dim
-        scale = head_dim ** -0.5
         tp_rank = lax.axis_index("tp")
         cp_rank = lax.axis_index("cp")
         core = cp_rank % 2
         gain_a = gain_one.astype(F32)
         gain_b = gain_two.astype(F32)
-
-        def own(arr):
-            return lax.dynamic_slice_in_dim(arr, cp_rank * span, span, 0)
 
         barrier = lax.optimization_barrier
         swap = lambda arr, pairs, axis="cp": lax.ppermute(arr, axis, pairs)
@@ -476,6 +473,11 @@
         owned = (local_ids >= 0) & (local_ids < rows)
         safe_ids = jnp.where(owned, local_ids, 0)
         picked = jnp.where(owned[:, None], jnp.take(table, safe_ids, axis=0), jnp.zeros((), BF16))
+        half = dim // 2
+        near = 256
+        wo_half = lax.dynamic_slice_in_dim(w_o, core * half, half, 1)
+        wo_near = lax.all_gather(wo_half[:, :near], "tp", axis=0, tiled=True)
+        picked, wo_near = barrier((picked, wo_near))
         x_slice = lax.psum_scatter(picked, "tp", scatter_dimension=0, tiled=True)
 
         ints = lax.all_gather(jnp.stack([tokens, pos, doc_id]), "cp", axis=1, tiled=True)
@@ -483,32 +485,28 @@
         slot_ids = jnp.arange(total, dtype=jnp.int32)
         before = (tok_all[None, :] < tok_all[:, None]) | ((tok_all[None, :] == tok_all[:, None]) & (slot_ids[None, :] < slot_ids[:, None]))
         rank = jnp.sum(before.astype(jnp.int32), axis=1)
+        count = jnp.sum((tok_all[None, :] == tok_all[:, None]).astype(jnp.int32), axis=1)
         at_rank = rank[None, :] == slot_ids[:, None]
+        runs = jnp.sum(jnp.where(at_rank, count[None, :], 0), axis=1)
         order = jnp.sum(jnp.where(at_rank, slot_ids[None, :], 0), axis=1)
         sid = jnp.sum(jnp.where(at_rank, tok_all[None, :], 0), axis=1) - tp_rank * rows
         order = order + 8 * (order // part)
         bounds = jnp.stack([jnp.sum((tok_all < tp_rank * rows).astype(jnp.int32)), jnp.sum((tok_all < (tp_rank + 1) * rows).astype(jnp.int32))])
         base = zero_rows(bounds, rows, dim)
-        quarter = dim // cp_count
-        wo_part = lax.dynamic_slice_in_dim(w_o, cp_rank * quarter, quarter, 1)
-        wo_near = [wo_part] + [swap(wo_part, [(i, i ^ k) for i in range(tp_count)], "tp") for k in (1, 2, 3)]
-        x_slice, base, order, sid, bounds, wo_near = barrier((x_slice, base, order, sid, bounds, wo_near))
+        x_slice, base, order, sid, runs, bounds, ints = barrier((x_slice, base, order, sid, runs, bounds, ints))
+        pos_all, doc_all = ints[1], ints[2]
         x_all = lax.all_gather(x_slice, both, axis=0, tiled=True)
 
-        wo_own = jnp.zeros((tp_count * width, quarter), BF16)
-        for k, piece in enumerate(wo_near):
-            wo_own = lax.dynamic_update_slice_in_dim(wo_own, piece, (tp_rank ^ k) * width, 0)
-        wo_core = swap(wo_own, core_swap)
-        wo_x = swap(wo_own, x_swap)
-        wo_diag = swap(wo_x, core_swap)
-        x_all, wo_x = barrier((x_all, wo_x))
+        wo_far = barrier((wo_half[:, near:], x_all))[0]
+        wo_rest = lax.all_gather(wo_far, "tp", axis=0, tiled=True)
+        wo_pieces = (wo_near, wo_rest, swap(wo_near, core_swap), swap(wo_rest, core_swap))
 
         angle = pos_all.astype(F32)[:, None] * inv_freq[None, :]
         cos = jnp.cos(angle)
         sin = jnp.sin(angle)
         cos = jnp.concatenate([cos, cos], axis=1)
         sin = jnp.concatenate([-sin, sin], axis=1)
-        dy_x = swap(dy, x_swap)
+        dy_x = swap(barrier((dy, x_all))[0], x_swap)
         act_a, query, key, value = project_qkv(x_all, gain_a[None, :], w_q, w_k, w_v, cos, sin)
 
         blk = span // 2
@@ -522,25 +520,23 @@
         first_own, last_own = first_doc[b_own], last_doc[b_own]
         jmin = jnp.sum((last_doc[None, :] < first_own[:, None]).astype(jnp.int32), axis=1)
         imax = jnp.sum((first_doc[None, :] <= last_own[:, None]).astype(jnp.int32), axis=1) - 1
-        info = jnp.concatenate([b_own, jmin, imax, cp_rank[None]]).astype(jnp.int32)
+        info = jnp.concatenate([b_own, jmin, imax, cp_rank[None], core[None]]).astype(jnp.int32)
         attended, lse = attend(info, query, key, value, doc_col, doc_row, head_dim, blk)
 
-        attended, dy_x = barrier((attended, dy_x))
         att_parts = lax.all_gather(attended, "tp", axis=0, tiled=False)
         lse_all = lax.all_gather(lse, "cp", axis=0, tiled=True)
         d_hidden = dot(dy, w_down, 1, 1).astype(BF16)
-        dhid_x = dot(dy_x, w_down, 1, 1).astype(BF16)
-        att_parts, lse_all, d_hidden, dhid_x = barrier((att_parts, lse_all, d_hidden, dhid_x))
+        att_parts, lse_all, d_hidden = barrier((att_parts, lse_all, d_hidden))
         gain_row = gain_b[None, :]
-        residual, act_b = out_proj(info, 0, x_all, att_parts, (wo_own, wo_core, wo_x, wo_diag), gain_row)
+        residual, act_b = out_proj(info, 0, x_all, att_parts, wo_pieces, gain_row)
         att_x = swap(att_parts, x_swap)
 
         wg, wu = w_gate.T, w_up.T
         ffn = wg.shape[0]
         hidden, d_gate, d_up, d_act_b = mlp_block(act_b, d_hidden, wg, wu, True)
-        d_act_b, att_x = barrier((d_act_b, att_x))
         d_act_b = lax.psum_scatter(d_act_b, "tp", scatter_dimension=0, tiled=True)
-        act_x = out_proj(info, 2, x_all, att_x, (wo_own, wo_core, wo_x, wo_diag), gain_row)[1]
+        dhid_x = dot(dy_x, w_down, 1, 1).astype(BF16)
+        act_x = out_proj(info, 2, x_all, att_x, wo_pieces, gain_row)[1]
         hidden_x, d_gate_x, d_up_x = mlp_block(act_x, dhid_x, wg, wu, False)
         d_act_b, hidden_x, d_gate_x, d_up_x = barrier((d_act_b, hidden_x, d_gate_x, d_up_x))
         d_act_b = to_bf16(d_act_b)
@@ -563,18 +559,10 @@
         grad_gain_b = jnp.sum(d_act_b * normed_b, axis=0)
         d_resid = mine(dy).astype(F32) + rms_back(d_act_b * gain_b, normed_b, inv_b)
         d_resid_all = lax.all_gather(d_resid.astype(BF16), both, axis=0, tiled=True)
-        d_resid_all, grad_down, grad_gate, grad_up, att_heads = barrier((d_resid_all, grad_down, grad_gate, grad_up, att_heads))
-        tp_swap = lambda arr, k: swap(arr, [(i, i ^ k) for i in range(tp_count)], "tp")
-        tp_slice = lambda arr, k: lax.dynamic_slice_in_dim(arr, (tp_rank ^ k) * part, part, 0)
         out_part = dot(hidden[:, :ffn], w_down, 1, 0)
-        out_slice = res_part + tp_slice(out_part, 0)
-        for k in (1, 2, 3):
-            out_slice = out_slice + tp_swap(tp_slice(out_part, k), k)
-        out_slice = out_slice.astype(BF16)
-        layer_out = jnp.zeros((span, dim), BF16)
-        for k in range(4):
-            piece = tp_swap(out_slice, k) if k else out_slice
-            layer_out = lax.dynamic_update_slice_in_dim(layer_out, piece, (tp_rank ^ k) * part, 0)
+        d_resid_all, grad_down, grad_gate, att_heads, out_part = barrier((d_resid_all, grad_down, grad_gate, att_heads, out_part))
+        out_slice = lax.psum_scatter(out_part, "tp", scatter_dimension=0, tiled=True)
+        out_slice = (res_part + out_slice).astype(BF16)
 
         d_att = dot(d_resid_all, w_o, 1, 1)
         d_att_b = d_att.astype(BF16)
@@ -588,19 +576,24 @@
         dqkv = attend_back(info, query, key, value, d_att_b, doc_col, doc_row, lse_all, by_block(lse_all.T), delta.T, by_block(delta), cos, sin, blk)
         d_q_pre, d_k_pre, d_v_pre = (dqkv[:, i * width:(i + 1) * width] for i in range(3))
         d_act_a = dot(d_q_pre, w_q, 1, 1) + dot(d_k_pre, w_k, 1, 1) + dot(d_v_pre, w_v, 1, 1)
-        d_act_a = to_bf16(lax.psum_scatter(d_act_a, "tp", scatter_dimension=0, tiled=True))
+        d_act_a, out_slice = barrier((d_act_a, out_slice))
+        d_act_a = lax.psum_scatter(d_act_a, "tp", scatter_dimension=0, tiled=True)
         dqkv_x = swap(dqkv, x_swap)
         dqkvs = (dqkv, swap(dqkv, core_swap), dqkv_x, swap(dqkv_x, core_swap))
+        grad_out = weight_grad(info, head_parts, [d_resid_all.reshape(cp_count, span, dim)] * 4)
+        d_act_a, dqkv_x, grad_out, grad_up = barrier((d_act_a, dqkv_x, grad_out, grad_up))
+        d_act_a = to_bf16(d_act_a)
         normed_a, inv_a = rms_stats(x_slice.astype(F32))
         grad_gain_a = jnp.sum(d_act_a * normed_a, axis=0)
         d_embed = d_resid + rms_back(d_act_a * gain_a, normed_a, inv_a)
         payload = jnp.concatenate([d_embed, grad_gain_a[None], grad_gain_b[None], jnp.zeros((6, dim), F32)], axis=0)
         gathered = lax.all_gather(payload, both, axis=0, tiled=True)
         grad_qkv = weight_grad(info, [act_a.reshape(cp_count, span, dim)] * 4, dqkvs, splits=3)
-        grad_out = weight_grad(info, head_parts, [d_resid_all.reshape(cp_count, span, dim)] * 4)
-        gathered, grad_qkv, grad_out = barrier((gathered, grad_qkv, grad_out))
+        gathered, grad_qkv = barrier((gathered, grad_qkv))
+        out_slice = barrier((out_slice, gathered))[0]
+        layer_out = lax.all_gather(out_slice, "tp", axis=0, tiled=True)
         gain_grads = jnp.sum(gathered.reshape(cp_count * tp_count, part + 8, dim)[:, part:part + 2], axis=0)
-        grad_table = scatter_rows(order, sid, bounds, gathered, base)
+        grad_table = scatter_rows(order, sid, runs, bounds, gathered, base, total)
         return (layer_out, grad_table, *grad_qkv, grad_out, grad_gate.T, grad_up.T, grad_down, gain_grads[0], gain_grads[1])
 
     col_spec = P(None, "tp")
@@ -609,4 +602,4 @@
     rep_spec = P(None)
     in_specs = (tok_spec, tok_spec, tok_spec, P("cp", None), row_spec, col_spec, col_spec, col_spec, row_spec, col_spec, col_spec, row_spec, rep_spec, rep_spec, rep_spec)
     out_specs = (P("cp", None), row_spec, col_spec, col_spec, col_spec, row_spec, col_spec, col_spec, row_spec, rep_spec, rep_spec)
-    return jax.shard_map(device_step, mesh=mesh, in_specs=in_specs, out_specs=out_specs, check_vma=False)
+    return jax.shard_map(compute, mesh=mesh, in_specs=in_specs, out_specs=out_specs, check_vma=False)

time: 959 us -> 865 us (0.902)
  waiting for transfers between devices: 347 us -> 315 us
  starting transfers between devices: 40.8 us -> 12.6 us
  local copies, waits for them, and re-layouts: 90.9 us -> 65.6 us
  Pallas kernels: 344 us -> 320 us
    all_gather x4 -> x7, waiting for transfers between devices: 3.88 us -> 186 us  [the longest x1 55.9 us: compute(): gathered = lax.all_gather(payload, both, axis=0, tiled=True)]
    ppermute x29 -> x19, waiting for transfers between devices: 251 us -> 117 us  [compute(): swap = lambda arr, pairs, axis='cp': lax.ppermute(arr, axis, pairs)]
    reduce_scatter x3 -> x4, waiting for transfers between devices: 92.2 us -> 11.9 us  [the longest x1 8.44 us: compute(): d_act_a = lax.psum_scatter(d_act_a, 'tp', scatter_dimension=0, tiled=True)]
    ppermute x29 -> x19, starting transfers between devices: 40.3 us -> 10.8 us  [compute(): swap = lambda arr, pairs, axis='cp': lax.ppermute(arr, axis, pairs)]
    pallas_call x1, Pallas kernels: 50.8 us -> 31.1 us  [scatter_rows(): pl.pallas_call(scatter_kernel, out_shape=jax.ShapeDtypeStruct((rows, dim)...]
    unnamed x114 -> x93, local copies, waits for them, and re-layouts: 40.5 us -> 28.3 us
    dynamic_update_slice x11 -> x4, local copies, waits for them, and re-layouts: 18 us -> 7.15 us  [compute(): lax.dynamic_update_slice_in_dim(att_heads, piece, (cp_rank ^ k) * span, 0)]
    reduce_sum x6 -> x7, other arithmetic: 12.7 us -> 22 us  [the longest x1 9.63 us: compute(): jnp.sum((tok_all[None, :] == tok_all[:, None]).astype(jnp.int32), axis=1)]
  transfers between devices with their start and end apart: 36 -> 30, of which waited for: 15 -> 15; matrix products, arithmetic and copies ran while one was open for 9% -> 15% of each run, Pallas kernels for 29% -> 32%
where the time goes in v3:
time: 865 us; the launch traced here: 857 us
  Pallas kernels  320 us (37%)
  waiting for transfers between devices  315 us (36%)
  local copies, waits for them, and re-layouts  65.6 us (8%)
  matrix products  59.5 us (7%)
  other arithmetic  47.7 us (6%)
  blocking collectives  21.9 us (3%)
  between operations  14.6 us (2%)
  starting transfers between devices  12.6 us (1%)
    pallas_call x5, Pallas kernels, weight_grad(): pl.pallas_call(functools.partial(weight_grad_kernel, pieces=n, splits=spl...  126 us
    ppermute x19, waiting for transfers between devices, compute(): swap = lambda arr, pairs, axis='cp': lax.ppermute(arr, axis, pairs)  117 us
    all_gather x1, waiting for transfers between devices, compute(): gathered = lax.all_gather(payload, both, axis=0, tiled=True)  55.9 us
    all_gather x1, waiting for transfers between devices, compute(): x_all = lax.all_gather(x_slice, both, axis=0, tiled=True)  55.3 us
    dot_general x7, matrix products, dot(): lax.dot_general(a, b, (((ca,), (cb,)), ((), ())), preferred_element_type=...  54.4 us
    all_gather x1, waiting for transfers between devices, compute(): wo_rest = lax.all_gather(wo_far, 'tp', axis=0, tiled=True)  47.1 us
    pallas_call x2, Pallas kernels, mlp_block(): pl.pallas_call(functools.partial(mlp_kernel, limit=limit), out_shape=[jax...  46.2 us
    pallas_call x2, Pallas kernels, out_proj(): pl.pallas_call(out_proj_kernel, out_shape=[jax.ShapeDtypeStruct((rows, di...  33.2 us
  transfers between devices with their start and end apart: 30, of which 15 were waited for; matrix products, arithmetic and copies ran while one was open for 15% of the time, Pallas kernels for 32%

profile of v3, /device:TPU:0, one launch (start us, length us, event | category | flops | bytes accessed | tf_op | source)
XLA Modules:
  0.0 857.2 jit_solution(3978416108891587158)
XLA Ops:
  10.6 13.2 %gather_fusion = bf16[512,2560]{1,0:T(8,128)(2,1)} fusion(bf16[8000,2560]{1,0:T(8,128)(2,1)} %param.19, s32[1024]{0:T(1024)S(1)} %pad_clamp_fusion.2), kind=kCustom, calls=%fused_computation | custom fusion | bytes 5244928 | tf_op jit(solution)/shard_map/jit(_take)/gather | solution.py:475
  27.5 10.6 %all-gather.9.cloned.1.call-done.a0 = bf16[2560,256]{1,0:T(8,128)(2,1)} async-done(((bf16[640,256]{1,0:T(8,128)(2,1)}), bf16[2560,256]{1,0:T(8,128)(2,1)}) %all-gather.9.cloned.1.call-update) | async-done | bytes 1310736 | tf_op jit(solution)/shard_map/all_gather | solution.py:479
  45.4 26.9 %zero_rows.1.base_hbm = f32[8000,2560]{1,0:T(8,128)} custom-call(s32[2]{0:T(128)S(1)} %pad_add_fusion.1.after.bounds), custom_call_target="tpu_custom_call" | custom-call | flops 20480000 | bytes 81920000 | tf_op jit(solution)/shard_map/zero_rows/pallas_call | solution.py:370
  91.7 55.3 %all-gather.11.cloned.1.call-done.x = bf16[2048,2560]{1,0:T(8,128)(2,1)} async-done(((bf16[128,2560]{1,0:T(8,128)(2,1)}), bf16[2048,2560]{1,0:T(8,128)(2,1)}) %all-gather.11.cloned.1.call-update) | async-done | bytes 10485776 | tf_op jit(solution)/shard_map/all_gather | solution.py:498
  159.7 47.1 %all-gather.13.cloned.1.call-done.b0 = bf16[2560,1024]{1,0:T(8,128)(2,1)} async-done(((bf16[640,1024]{1,0:T(8,128)(2,1)}), bf16[2560,1024]{1,0:T(8,128)(2,1)}) %all-gather.13.cloned.1.call-update) | async-done | bytes 5242896 | tf_op jit(solution)/shard_map/all_gather | solution.py:501
  206.8 31.3 %project_qkv.1 = (bf16[2048,2560]{1,0:T(8,128)(2,1)}, bf16[2048,640]{1,0:T(8,128)(2,1)}, bf16[2048,640]{1,0:T(8,128)(2,1)}, bf16[2048,640]{1,0:T(8,128)(2,1)}) custom-call(bf16[2048,2560]{1,0:T(8,128)(2,1)} %all-gather.11.cloned.1.call-done.x, f32[1,2560]{1,0:T(1,128)} %broadcast_in_dim.98.gain, bf16[2560,640]{1,0:T(8,128)(2,1)} %wq.1, ...), custom_call_target="tpu_custom_call" | custom-call | flops 20132659200 | bytes 38666240 | tf_op jit(solution)/shard_map/project_qkv/pallas_call | solution.py:63
  264.5 16.7 %all_gather.35.lse_col = f32[2048,8]{1,0:T(8,128)} all-gather(f32[512,8]{1,0:T(8,128)S(1)} %get-tuple-element.70), channel_id=1, replica_groups=mesh['tp'=4,'cp'=4] {'cp'}, dimensions={0}, use_global_device_ids=true | all-gather | bytes 81920 | tf_op jit(solution)/shard_map/all_gather | solution.py:527
  281.2 12.9 %all-gather.21.cloned.1.call-done = bf16[2048,640]{1,0:T(8,128)(2,1)} async-done(((bf16[512,640]{1,0:T(8,128)(2,1)}), bf16[2048,640]{1,0:T(8,128)(2,1)}) %all-gather.21.cloned.1.call-update) | async-done | bytes 2621456 | tf_op jit(solution)/shard_map/all_gather | solution.py:526
  294.1 16.6 %out_proj.2 = (f32[512,2560]{1,0:T(8,128)}, bf16[512,2560]{1,0:T(8,128)(2,1)}) custom-call(s32[8]{0:T(128)} %concatenate.61.info, bf16[2048,2560]{1,0:T(8,128)(2,1)} %all-gather.11.cloned.1.call-done.x, bf16[4,512,640]{2,1,0:T(8,128)(2,1)} %bitcast.63, bf16[2560,256]{1,0:T(8,128)(2,1)} %all-gather.9.cloned.1.call-done.a0, ...), custom_call_target="tpu_custom_call" | custom-call | flops 6710886400 | bytes 26214400 | tf_op jit(solution)/shard_map/out_proj/pallas_call | solution.py:251
  310.7 30.4 %mlp_block.2 = (bf16[512,1792]{1,0:T(8,128)(2,1)S(1)}, bf16[512,1792]{1,0:T(8,128)(2,1)S(1)}, bf16[512,1792]{1,0:T(8,128)(2,1)S(1)}, f32[512,2560]{1,0:T(8,128)}) custom-call(bf16[512,2560]{1,0:T(8,128)(2,1)} %get-tuple-element.75.act.refs_4_, bf16[512,1728]{1,0:T(8,128)(2,1)} %convolution_convert_fusion.2.dhid, bf16[1728,2560]{1,0:T(8,128)(2,1)} %bitcast.72, ...), custom_call_target="tpu_custom_call" | custom-call | flops 18119393280 | bytes 36110336 | tf_op jit(solution)/shard_map/mlp_block/pallas_call | solution.py:340
  347.1 58.0 %collective-permute-done.3.refs_6_ = bf16[512,2560]{1,0:T(8,128)(2,1)} collective-permute-done((bf16[512,2560]{1,0:T(8,128)(2,1)}, bf16[512,2560]{1,0:T(8,128)(2,1)}, u32[]{:S(2)}, u32[]{:S(2)}) %collective-permute-start.3) | collective-permute-done | bytes 2621472 | tf_op jit(solution)/shard_map/ppermute | solution.py:471
  420.7 39.3 %collective-permute-done.2.att = bf16[4,512,640]{2,1,0:T(8,128)(2,1)} collective-permute-done((bf16[4,512,640]{2,1,0:T(8,128)(2,1)}, bf16[4,512,640]{2,1,0:T(8,128)(2,1)}, u32[]{:S(2)}, u32[]{:S(2)}) %collective-permute-start.2) | collective-permute-done | bytes 2621472 | tf_op jit(solution)/shard_map/ppermute | solution.py:471
  460.0 16.6 %out_proj.3 = (f32[512,2560]{1,0:T(8,128)}, bf16[512,2560]{1,0:T(8,128)(2,1)}) custom-call(s32[8]{0:T(128)} %concatenate.61.info, bf16[2048,2560]{1,0:T(8,128)(2,1)} %all-gather.11.cloned.1.call-done.x, bf16[4,512,640]{2,1,0:T(8,128)(2,1)} %collective-permute-done.2.att, bf16[2560,256]{1,0:T(8,128)(2,1)} %all-gather.9.cloned.1.call-done.a0, ...), custom_call_target="tpu_custom_call" | custom-call | flops 6710886400 | bytes 26214400 | tf_op jit(solution)/shard_map/out_proj/pallas_call | solution.py:251
  476.7 15.8 %mlp_block.3 = (bf16[512,1792]{1,0:T(8,128)(2,1)}, bf16[512,1792]{1,0:T(8,128)(2,1)S(1)}, bf16[512,1792]{1,0:T(8,128)(2,1)S(1)}) custom-call(bf16[512,2560]{1,0:T(8,128)(2,1)} %get-tuple-element.78.act.refs_6_, bf16[512,1728]{1,0:T(8,128)(2,1)} %copy.46.dhid, bf16[1728,2560]{1,0:T(8,128)(2,1)} %bitcast.73, bf16[1728,2560]{1,0:T(8,128)(2,1)} %bitcast.75), custom_call_target="tpu_custom_call" | custom-call | flops 9059696640 | bytes 36110336 | tf_op jit(solution)/shard_map/mlp_block/pallas_call | solution.py:340
  522.7 12.2 %fusion.6 = f32[512,2560]{1,0:T(8,128)} fusion(bf16[1728,2560]{1,0:T(8,128)(2,1)} %param.26, bf16[512,1792]{1,0:T(8,128)(2,1)} %copy-done.24), kind=kOutput, calls=%fused_computation.23 | convolution fusion | flops 4529848320 | bytes 15925248 | tf_op jit(solution)/shard_map/dot_general | solution.py:29
  534.9 27.1 %weight_grad.5 = f32[1728,2560]{1,0:T(8,128)} custom-call(s32[8]{0:T(128)} %concatenate.61.info, bf16[512,1792]{1,0:T(8,128)(2,1)} %copy-done.24, bf16[512,1792]{1,0:T(8,128)(2,1)} %collective-permute-done.4.refs_1_, bf16[512,1792]{1,0:T(8,128)(2,1)} %get-tuple-element.85.refs_2_, bf16[512,1792]{1,0:T(8,128)(2,1)} %collective-permute-done.5.refs_3_, ...), custom_call_target="tpu_custom_call" | custom-call | flops 18119393280 | bytes 35258368 | tf_op jit(solution)/shard_map/weight_grad/pallas_call | solution.py:289
  562.0 27.1 %weight_grad.6 = f32[1728,2560]{1,0:T(8,128)} custom-call(s32[8]{0:T(128)} %concatenate.61.info, bf16[512,1792]{1,0:T(8,128)(2,1)} %copy-done.23, bf16[512,1792]{1,0:T(8,128)(2,1)} %collective-permute-done.8.refs_1_, bf16[512,1792]{1,0:T(8,128)(2,1)} %copy-done.25, bf16[512,1792]{1,0:T(8,128)(2,1)} %collective-permute-done.9.refs_3_, ...), custom_call_target="tpu_custom_call" | custom-call | flops 18119393280 | bytes 35258368 | tf_op jit(solution)/shard_map/weight_grad/pallas_call | solution.py:289
  590.8 11.0 %convolution_convert_fusion.do = bf16[2048,640]{1,0:T(8,128)(2,1)S(1)} fusion(bf16[2048,2560]{1,0:T(8,128)(2,1)} %all-gather.15.cloned.1.call-done, bf16[640,2560]{1,0:T(8,128)(2,1)S(1)} %copy-done), kind=kOutput, calls=%fused_computation.19 | convolution fusion | flops 6712197120 | bytes 16384000 | tf_op jit(solution)/shard_map/dot_general | solution.py:29
  612.5 20.1 %attend_back.1.refs_4_ = bf16[512,1920]{1,0:T(8,128)(2,1)} custom-call(s32[8]{0:T(128)S(1)} %copy-done.16, bf16[2048,640]{1,0:T(8,128)(2,1)} %get-tuple-element.66.q, bf16[2048,640]{1,0:T(8,128)(2,1)} %get-tuple-element.67.k, bf16[2048,640]{1,0:T(8,128)(2,1)} %get-tuple-element.68.v, bf16[2048,640]{1,0:T(8,128)(2,1)} %copy-done.28, s32[2048,1]{1,0:T(8,128)S(1)} %copy-done.7, ...), custom_call_target="tpu_custom_call" | custom-call | flops 4697620480 | bytes 15728640 | tf_op jit(solution)/shard_map/attend_back/pallas_call | solution.py:203
  658.3 27.0 %weight_grad.8 = f32[1728,2560]{1,0:T(8,128)} custom-call(s32[8]{0:T(128)} %concatenate.61.info, bf16[512,1792]{1,0:T(8,128)(2,1)} %copy-done.20, bf16[512,1792]{1,0:T(8,128)(2,1)} %copy-done.44, bf16[512,1792]{1,0:T(8,128)(2,1)} %copy-done.22, bf16[512,1792]{1,0:T(8,128)(2,1)} %copy-done.45, bf16[512,2560]{1,0:T(8,128)(2,1)} %get-tuple-element.75.act.refs_4_, ...), custom_call_target="tpu_custom_call" | custom-call | flops 18119393280 | bytes 35258368 | tf_op jit(solution)/shard_map/weight_grad/pallas_call | solution.py:289
  685.4 15.1 %weight_grad.7 = f32[640,2560]{1,0:T(8,128)} custom-call(s32[8]{0:T(128)} %concatenate.61.info, bf16[512,640]{1,0:T(8,128)(2,1)} %copy-done.3, bf16[512,640]{1,0:T(8,128)(2,1)} %collective-permute-done.12.refs_1_, bf16[512,640]{1,0:T(8,128)(2,1)} %get-tuple-element.131.refs_2_, bf16[512,640]{1,0:T(8,128)(2,1)} %collective-permute-done.13.refs_3_, ...), custom_call_target="tpu_custom_call" | custom-call | flops 6710886400 | bytes 19660800 | tf_op jit(solution)/shard_map/weight_grad/pallas_call | solution.py:289
  723.5 29.9 %weight_grad.9 = (f32[2560,640]{1,0:T(8,128)}, f32[2560,640]{1,0:T(8,128)}, f32[2560,640]{1,0:T(8,128)}) custom-call(s32[8]{0:T(128)} %concatenate.61.info, bf16[4,512,2560]{2,1,0:T(8,128)(2,1)} %bitcast.78, bf16[4,512,2560]{2,1,0:T(8,128)(2,1)} %bitcast.79, bf16[4,512,2560]{2,1,0:T(8,128)(2,1)} %bitcast.80, bf16[4,512,2560]{2,1,0:T(8,128)(2,1)} %bitcast.81, ...), custom_call_target="tpu_custom_call" | custom-call | flops 20132659200 | bytes 38010880 | tf_op jit(solution)/shard_map/weight_grad/pallas_call | solution.py:289
  753.4 55.9 %all-gather.17.cloned.1.call-done.rows = f32[2176,2560]{1,0:T(8,128)} async-done(((f32[136,2560]{1,0:T(8,128)}), f32[2176,2560]{1,0:T(8,128)}) %all-gather.17.cloned.1.call-update) | async-done | bytes 22282256 | tf_op jit(solution)/shard_map/all_gather | solution.py:590
  809.3 31.1 %scatter_rows.1 = f32[8000,2560]{1,0:T(8,128)} custom-call(s32[2048]{0:T(1024)S(1)} %get-tuple-element.103.order, s32[2048]{0:T(1024)S(1)} %get-tuple-element.104.sid, s32[2048]{0:T(1024)S(1)} %copy-done.17, s32[2]{0:T(128)S(1)} %copy-done.19, f32[2176,2560]{1,0:T(8,128)} %all-gather.17.cloned.1.call-done.rows, ...), custom_call_target="tpu_custom_call", output_to_operand_aliasing={{}: (5, {})} | custom-call | tf_op jit(solution)/shard_map/scatter_rows/pallas_call | solution.py:433
  (227 shorter events, 195.4 us)
Async XLA Ops:
  7.2 30.9 %all-gather.9.cloned.1.call-start = ((), (), s32[]{:S(2)}) async-start(), calls=%async_computation.4 | async-start | bytes 1638400 | tf_op jit(solution)/shard_map/all_gather | solution.py:479
  9.9 80.5 %reduce-scatter.5.cloned.1.call-start = ((), (), s32[]{:S(2)}) async-start(), calls=%async_computation.5 | async-start | bytes 3276800 | tf_op jit(solution)/shard_map/reduce_scatter | solution.py:481
  38.1 108.8 %all-gather.11.cloned.1.call-start = ((), (), s32[]{:S(2)}) async-start(), calls=%async_computation.6 | async-start | bytes 11141120 | tf_op jit(solution)/shard_map/all_gather | solution.py:498
  90.4 116.4 %all-gather.13.cloned.1.call-start = ((), (), s32[]{:S(2)}) async-start(), calls=%async_computation.7 | async-start | bytes 6553600 | tf_op jit(solution)/shard_map/all_gather | solution.py:501
  147.0 147.1 %all-gather.21.cloned.1.call-start = ((), (), s32[]{:S(2)}) async-start(), calls=%async_computation.14 | async-start | bytes 3276800 | tf_op jit(solution)/shard_map/all_gather | solution.py:526
  206.8 87.2 %collective-permute-start.1 = (bf16[2560,1024]{1,0:T(8,128)(2,1)}, bf16[2560,1024]{1,0:T(8,128)(2,1)}, u32[]{:S(2)}, u32[]{:S(2)}) collective-permute-start(bf16[2560,1024]{1,0:T(8,128)(2,1)} %all-gather.13.cloned.1.call-done.b0), channel_id=1, source_target_pairs={{0,1},{1,0},{2,3},{3,2},{4,5},{5,4},{6,7},{7,6},{8,9},{9,8},{10,11... | collective-permute-start | bytes 15728648 | tf_op jit(solution)/shard_map/ppermute | solution.py:471
  250.8 244.1 %reduce-scatter.7.cloned.1.call-start = ((), (), s32[]{:S(2)}) async-start(), calls=%async_computation.8 | async-start | bytes 6553600 | tf_op jit(solution)/shard_map/reduce_scatter | solution.py:537
  252.3 41.7 %collective-permute-start = (bf16[2560,256]{1,0:T(8,128)(2,1)}, bf16[2560,256]{1,0:T(8,128)(2,1)}, u32[]{:S(2)}, u32[]{:S(2)}) collective-permute-start(bf16[2560,256]{1,0:T(8,128)(2,1)} %all-gather.9.cloned.1.call-done.a0), channel_id=1, source_target_pairs={{0,1},{1,0},{2,3},{3,2},{4,5},{5,4},{6,7},{7,6},{8,9},{9,8},{10,11... | collective-permute-start | bytes 3932168 | tf_op jit(solution)/shard_map/ppermute | solution.py:471
  344.8 244.3 %all-gather.15.cloned.1.call-start = ((), (), s32[]{:S(2)}) async-start(), calls=%async_computation.9 | async-start | bytes 11141120 | tf_op jit(solution)/shard_map/all_gather | solution.py:561
  345.1 60.1 %collective-permute-start.3 = (bf16[512,2560]{1,0:T(8,128)(2,1)}, bf16[512,2560]{1,0:T(8,128)(2,1)}, u32[]{:S(2)}, u32[]{:S(2)}) collective-permute-start(bf16[512,2560]{1,0:T(8,128)(2,1)} %refs_4_.1), channel_id=1, source_target_pairs={{0,2},{1,3},{2,0},{3,1},{4,6},{5,7},{6,4},{7,5},{8,10},{9,11},{10,... | collective-permute-start | bytes 7864328 | tf_op jit(solution)/shard_map/ppermute | solution.py:471
  346.6 113.5 %collective-permute-start.2 = (bf16[4,512,640]{2,1,0:T(8,128)(2,1)}, bf16[4,512,640]{2,1,0:T(8,128)(2,1)}, u32[]{:S(2)}, u32[]{:S(2)}) collective-permute-start(bf16[4,512,640]{2,1,0:T(8,128)(2,1)} %bitcast.64), channel_id=1, source_target_pairs={{0,2},{1,3},{2,0},{3,1},{4,6},{5,7},{6,4},{7,5},{8,10},{9,11},{10,... | collective-permute-start | bytes 7864328 | tf_op jit(solution)/shard_map/ppermute | solution.py:471
  499.9 146.6 %reduce-scatter.9.cloned.1.call-start = ((), (), s32[]{:S(2)}) async-start(), calls=%async_computation.10 | async-start | bytes 6553600 | tf_op jit(solution)/shard_map/reduce_scatter | solution.py:564
  500.4 21.4 %collective-permute-start.6 = (bf16[512,2560]{1,0:T(8,128)(2,1)}, bf16[512,2560]{1,0:T(8,128)(2,1)}, u32[]{:S(2)}, u32[]{:S(2)}) collective-permute-start(bf16[512,2560]{1,0:T(8,128)(2,1)} %refs_4_.1), channel_id=1, source_target_pairs={{0,1},{1,0},{2,3},{3,2},{4,5},{5,4},{6,7},{7,6},{8,9},{9,8},{10,11... | collective-permute-start | bytes 7864328 | tf_op jit(solution)/shard_map/ppermute | solution.py:471
  500.5 21.7 %collective-permute-start.7 = (bf16[512,2560]{1,0:T(8,128)(2,1)}, bf16[512,2560]{1,0:T(8,128)(2,1)}, u32[]{:S(2)}, u32[]{:S(2)}) collective-permute-start(bf16[512,2560]{1,0:T(8,128)(2,1)} %collective-permute-done.3.refs_6_), channel_id=1, source_target_pairs={{0,1},{1,0},{2,3},{3,2},{4,5},{5,4},{6,7},{7,6},{8,9},{9,8},{10,11... | collective-permute-start | bytes 7864328 | tf_op jit(solution)/shard_map/ppermute | solution.py:471
  501.0 21.4 %collective-permute-start.4 = (bf16[512,1792]{1,0:T(8,128)(2,1)}, bf16[512,1792]{1,0:T(8,128)(2,1)}, u32[]{:S(2)}, u32[]{:S(2)}) collective-permute-start(bf16[512,1792]{1,0:T(8,128)(2,1)} %copy-done.24), channel_id=1, source_target_pairs={{0,1},{1,0},{2,3},{3,2},{4,5},{5,4},{6,7},{7,6},{8,9},{9,8},{10,11... | collective-permute-start | bytes 5505032 | tf_op jit(solution)/shard_map/ppermute | solution.py:471
  517.4 17.5 %collective-permute-start.5 = (bf16[512,1792]{1,0:T(8,128)(2,1)}, bf16[512,1792]{1,0:T(8,128)(2,1)}, u32[]{:S(2)}, u32[]{:S(2)}) collective-permute-start(bf16[512,1792]{1,0:T(8,128)(2,1)} %get-tuple-element.85.refs_2_), channel_id=1, source_target_pairs={{0,1},{1,0},{2,3},{3,2},{4,5},{5,4},{6,7},{7,6},{8,9},{9,8},{10,11... | collective-permute-start | bytes 5505032 | tf_op jit(solution)/shard_map/ppermute | solution.py:471
  521.7 40.3 %collective-permute-start.10 = (bf16[512,2560]{1,0:T(8,128)(2,1)}, bf16[512,2560]{1,0:T(8,128)(2,1)}, u32[]{:S(2)}, u32[]{:S(2)}) collective-permute-start(bf16[512,2560]{1,0:T(8,128)(2,1)} %get-tuple-element.75.act.refs_4_), channel_id=1, source_target_pairs={{0,1},{1,0},{2,3},{3,2},{4,5},{5,4},{6,7},{7,6},{8,9},{9,8},{10,11... | collective-permute-start | bytes 7864328 | tf_op jit(solution)/shard_map/ppermute | solution.py:471
  521.8 40.2 %collective-permute-start.11 = (bf16[512,2560]{1,0:T(8,128)(2,1)}, bf16[512,2560]{1,0:T(8,128)(2,1)}, u32[]{:S(2)}, u32[]{:S(2)}) collective-permute-start(bf16[512,2560]{1,0:T(8,128)(2,1)} %get-tuple-element.78.act.refs_6_), channel_id=1, source_target_pairs={{0,1},{1,0},{2,3},{3,2},{4,5},{5,4},{6,7},{7,6},{8,9},{9,8},{10,11... | collective-permute-start | bytes 7864328 | tf_op jit(solution)/shard_map/ppermute | solution.py:471
  522.2 39.8 %collective-permute-start.8 = (bf16[512,1792]{1,0:T(8,128)(2,1)}, bf16[512,1792]{1,0:T(8,128)(2,1)}, u32[]{:S(2)}, u32[]{:S(2)}) collective-permute-start(bf16[512,1792]{1,0:T(8,128)(2,1)} %copy-done.23), channel_id=1, source_target_pairs={{0,1},{1,0},{2,3},{3,2},{4,5},{5,4},{6,7},{7,6},{8,9},{9,8},{10,11... | collective-permute-start | bytes 5505032 | tf_op jit(solution)/shard_map/ppermute | solution.py:471
  522.3 39.7 %collective-permute-start.9 = (bf16[512,1792]{1,0:T(8,128)(2,1)}, bf16[512,1792]{1,0:T(8,128)(2,1)}, u32[]{:S(2)}, u32[]{:S(2)}) collective-permute-start(bf16[512,1792]{1,0:T(8,128)(2,1)} %copy-done.25), channel_id=1, source_target_pairs={{0,1},{1,0},{2,3},{3,2},{4,5},{5,4},{6,7},{7,6},{8,9},{9,8},{10,11... | collective-permute-start | bytes 5505032 | tf_op jit(solution)/shard_map/ppermute | solution.py:471
  589.1 119.8 %reduce-scatter.11.cloned.1.call-start = ((), (), s32[]{:S(2)}) async-start(), calls=%async_computation.11 | async-start | bytes 6553600 | tf_op jit(solution)/shard_map/reduce_scatter | solution.py:580
  649.2 160.0 %all-gather.17.cloned.1.call-start = ((), (), s32[]{:S(2)}) async-start(), calls=%async_computation.12 | async-start | bytes 23674880 | tf_op jit(solution)/shard_map/all_gather | solution.py:590
  651.5 49.0 %collective-permute-start.14 = (bf16[512,1920]{1,0:T(8,128)(2,1)}, bf16[512,1920]{1,0:T(8,128)(2,1)}, u32[]{:S(2)}, u32[]{:S(2)}) collective-permute-start(bf16[512,1920]{1,0:T(8,128)(2,1)} %attend_back.1.refs_4_), channel_id=1, source_target_pairs={{0,2},{1,3},{2,0},{3,1},{4,6},{5,7},{6,4},{7,5},{8,10},{9,11},{10,... | collective-permute-start | bytes 5898248 | tf_op jit(solution)/shard_map/ppermute | solution.py:471
  714.6 132.2 %all-gather.19.cloned.1.call-start = ((), (), s32[]{:S(2)}) async-start(), calls=%async_computation.13 | async-start | bytes 3276800 | tf_op jit(solution)/shard_map/all_gather | solution.py:594
  (52 other events, 556.8 us)
Sparse Core Ops, SparseCore 0:
  10.4 27.7 all-gather.8
  41.6 35.7 reduce-scatter.4
  90.5 56.4 all-gather.10
  149.2 57.5 all-gather.12
  250.9 43.0 all-gather.20
  344.9 57.5 reduce-scatter.6
  500.1 55.9 all-gather.14
  589.2 57.2 reduce-scatter.8
  650.1 58.8 reduce-scatter.10
  714.8 94.4 all-gather.16
  811.1 35.7 all-gather.18

commit v4 on v3

v4 whole, which is shorter than its diff:
```python
import functools
import jax
import jax.numpy as jnp
from jax import lax
from jax.experimental import pallas as pl
from jax.experimental.pallas import tpu as pltpu
from jax.sharding import PartitionSpec as P

NORM_EPS = 1e-5
NEG_BIG = -1e30
MIB = 2 ** 20
F32 = jnp.float32
BF16 = jnp.bfloat16
I32 = jnp.int32


def rms_stats(feats):
    inv_rms = lax.rsqrt(mean_row(feats * feats) + NORM_EPS)
    return feats * inv_rms, inv_rms


def rms_back(d_normed, normed, inv_rms):
    return inv_rms * (d_normed - normed * mean_row(d_normed * normed))


def to_bf16(feats):
    return feats.astype(BF16).astype(F32)


def contract(a, b, ca, cb):
    return lax.dot_general(a, b, (((ca,), (cb,)), ((), ())), preferred_element_type=F32)


def row_sum(t):
    return jnp.sum(t, axis=1, keepdims=True)


def mean_row(t):
    return jnp.mean(t, axis=-1, keepdims=True)


def whole(a):
    return pl.BlockSpec(a.shape, lambda *i: (0,) * a.ndim)


def cost(flops, moved):
    return pl.CostEstimate(flops=flops, bytes_accessed=moved, transcendentals=0)


def nn(a, b):
    return contract(a, b, 1, 0)


def nt(a, b):
    return contract(a, b, 1, 1)


def tn(a, b):
    return contract(a, b, 0, 0)


DIMS = ("x", "y", "z")


class Place:
    def __init__(self):
        tp = lax.axis_index("tp")
        cp = lax.axis_index("cp")
        self.at = {"x": cp // 2, "core": cp % 2, "z": tp // 2, "y": tp % 2}

    def coord(self, dim, flip):
        return 1 - self.at[dim] if dim in flip else self.at[dim]

    def tp(self, flip=()):
        return self.coord("z", flip) * 2 + self.coord("y", flip)

    def cp(self, flip=()):
        return self.coord("x", flip) * 2 + self.coord("core", flip)

    def device(self, flip):
        return {"tp": self.tp(flip), "cp": self.cp(flip)}

    def slot(self, flip=()):
        return self.cp(flip) * 4 + self.tp(flip)

    def meet(self, dims):
        barrier = pltpu.get_barrier_semaphore()
        for d in dims:
            pl.semaphore_signal(barrier, inc=1, device_id=self.device((d,)), device_id_type=MESH)
        pl.semaphore_wait(barrier, len(dims))


MESH = pl.DeviceIdType.MESH
ORDERS = (("x", "y", "z"), ("y", "z", "x"), ("z", "x", "y"))
FLIPS = tuple(tuple(d for i, d in enumerate(DIMS) if n >> i & 1) for n in range(8))


def flip_code(flip):
    return sum(1 << DIMS.index(d) for d in flip)


def column_parts(width, count):
    tiles = width // 128
    sizes = [(tiles // count + (i < tiles % count)) * 128 for i in range(count)]
    return [(sum(sizes[:i]), n) for i, n in enumerate(sizes)]


class Gather:
    def __init__(self, place, buf, send, recv, core_send, core_recv):
        self.place, self.buf, self.send, self.recv, self.core_send, self.core_recv = place, buf, send, recv, core_send, core_recv
        self.parts = column_parts(buf.shape[2], 3)
        self.started = []

    def view(self, part, flip):
        start, size = self.parts[part]
        return self.buf.at[self.place.slot(flip), :, pl.ds(start, size)]

    def hop(self, part, flip, dim):
        there = tuple(d for d in DIMS if (d in flip) != (d == dim))
        index = part * 7 + flip_code(there) - 1
        ref = self.view(part, flip)
        return pltpu.make_async_remote_copy(src_ref=ref, dst_ref=ref, send_sem=self.send.at[index], recv_sem=self.recv.at[index], device_id=self.place.device((dim,)), device_id_type=MESH)

    def core_hop(self, part, flip):
        index = part * 8 + flip_code(flip)
        ref = self.view(part, flip)
        return pltpu.make_async_remote_copy(src_ref=ref, dst_ref=ref, send_sem=self.core_send.at[index], recv_sem=self.core_recv.at[index], device_id=self.place.device(("core",)), device_id_type=MESH)

    def go(self, copy):
        copy.start()
        self.started.append(copy)

    def wait(self, part, flip):
        order = ORDERS[part]
        last = max(order.index(d) for d in flip)
        came = tuple(d for d in flip if d != order[last])
        self.hop(part, came, order[last]).wait_recv()
        for dim in order[last + 1:]:
            self.go(self.hop(part, flip, dim))
        self.go(self.core_hop(part, flip))

    def run(self):
        for step in range(3):
            for part, order in enumerate(ORDERS):
                self.go(self.hop(part, (), order[step]))
        for part in range(3):
            self.go(self.core_hop(part, ()))
        for step in range(3):
            for flip in FLIPS[1:]:
                for part, order in enumerate(ORDERS):
                    if max(order.index(d) for d in flip) == step and len(flip) == 1:
                        self.wait(part, flip)
            for flip in FLIPS[1:]:
                for part, order in enumerate(ORDERS):
                    if max(order.index(d) for d in flip) == step and len(flip) > 1:
                        self.wait(part, flip)

    def finish(self, out, out_sem):
        rows = self.buf.shape[1]
        copies = []

        def store(flip):
            slot = self.place.slot(flip)
            c = pltpu.make_async_copy(self.buf.at[slot], out.at[pl.ds(slot * rows, rows), :], out_sem.at[len(copies)])
            c.start()
            copies.append(c)

        for flip in FLIPS:
            store(flip)
        for flip in FLIPS:
            other = flip + ("core",)
            for part in range(3):
                start, size = self.parts[part]
                ref = self.buf.at[self.place.slot(other), :, pl.ds(start, size)]
                index = part * 8 + flip_code(flip)
                pltpu.make_async_remote_copy(src_ref=ref, dst_ref=ref, send_sem=self.core_send.at[index], recv_sem=self.core_recv.at[index], device_id=self.place.device(("core",)), device_id_type=MESH).wait_recv()
            store(other)
        for c in self.started:
            c.wait_send()
        for c in copies:
            c.wait()


def embed_kernel(picked, side_f, side_i, out, slice_out, all_f, all_i, buf, r1, r2, tmp, send, recv, core_send, core_recv, out_sem, rs_send, rs_recv, side_send, side_recv, slice_sem):
    place = Place()
    place.meet(("x", "y", "z", "core"))
    half = buf.shape[2] // 2
    near = ("y", "z")

    sides = ((side_f, all_f), (side_i, all_i))
    started = []

    def side_hop(i, step):
        src, dst = sides[i]
        if step == 0:
            src_ref, slot, dim = src, place.cp(), "x"
        elif step == 1:
            src_ref, slot, dim = src, place.cp(), "core"
        else:
            src_ref, slot, dim = dst.at[place.cp(("x",))], place.cp(("x",)), "core"
        return pltpu.make_async_remote_copy(src_ref=src_ref, dst_ref=dst.at[slot], send_sem=side_send.at[i, step], recv_sem=side_recv.at[i, step], device_id=place.device((dim,)), device_id_type=MESH)

    def first(h, k):
        a, b = near[h], near[1 - h]
        target = place.tp((a,)) if k == 0 else place.tp((a, b))
        cols = pl.ds(h * half, half)
        return pltpu.make_async_remote_copy(src_ref=picked.at[target, :, cols], dst_ref=r1.at[h, k], send_sem=rs_send.at[h, k], recv_sem=rs_recv.at[h, k], device_id=place.device((a,)), device_id_type=MESH)

    def second(h):
        return pltpu.make_async_remote_copy(src_ref=tmp.at[h], dst_ref=r2.at[h], send_sem=rs_send.at[h, 2], recv_sem=rs_recv.at[h, 2], device_id=place.device((near[1 - h],)), device_id_type=MESH)

    def go(copy):
        copy.start()
        started.append(copy)

    for k in (1, 0):
        for h in range(2):
            go(first(h, k))
    for i in range(2):
        go(side_hop(i, 0))
        go(side_hop(i, 1))
        all_i_or_f = sides[i][1]
        all_i_or_f[place.cp()] = sides[i][0][...]
    for h in range(2):
        cols = slice(h * half, (h + 1) * half)
        first(h, 1).wait_recv()
        tmp[h] = picked[place.tp((near[1 - h],)), :, cols] + r1[h, 1]
        go(second(h))
    for i in range(2):
        side_hop(i, 0).wait_recv()
        go(side_hop(i, 2))
    mine = place.slot()
    for h in range(2):
        cols = slice(h * half, (h + 1) * half)
        first(h, 0).wait_recv()
        part = picked[place.tp(), :, cols] + r1[h, 0]
        second(h).wait_recv()
        buf[mine, :, cols] = part + r2[h]
    gather = Gather(place, buf, send, recv, core_send, core_recv)
    gather.run()
    keep = pltpu.make_async_copy(buf.at[mine], slice_out, slice_sem)
    keep.start()
    gather.finish(out, out_sem)
    keep.wait()
    for i in range(2):
        side_hop(i, 1).wait_recv()
        side_hop(i, 2).wait_recv()
    for c in started:
        c.wait_send()


def embed_gather(picked, side_f, side_i):
    _, rows, dim = picked.shape
    half = dim // 2
    dma = pltpu.SemaphoreType.DMA
    vmem = pl.BlockSpec(memory_space=pltpu.VMEM)
    hbm = pl.BlockSpec(memory_space=pl.ANY)
    return pl.pallas_call(
        embed_kernel,
        out_shape=[
            jax.ShapeDtypeStruct((16 * rows, dim), BF16),
            jax.ShapeDtypeStruct((rows, dim), BF16),
            jax.ShapeDtypeStruct((4,) + side_f.shape, F32),
            jax.ShapeDtypeStruct((4,) + side_i.shape, I32),
        ],
        in_specs=[vmem, vmem, vmem],
        out_specs=[hbm, hbm, vmem, vmem],
        scratch_shapes=[
            pltpu.VMEM((16, rows, dim), BF16),
            pltpu.VMEM((2, 2, rows, half), BF16),
            pltpu.VMEM((2, rows, half), BF16),
            pltpu.VMEM((2, rows, half), BF16),
            dma((21,)), dma((21,)), dma((24,)), dma((24,)), dma((16,)),
            dma((2, 3)), dma((2, 3)), dma((2, 3)), dma((2, 3)), dma,
        ],
        compiler_params=pltpu.CompilerParams(collective_id=0, has_side_effects=True, vmem_limit_bytes=40 * MIB),
        name="embed_gather",
    )(picked, side_f, side_i)


def slot_block(j):
    return jnp.where(j < 4, 2 * j, 15 - 2 * j)


def unpack_angles(packed):
    turned = pltpu.roll(packed, packed.shape[1] // 2, 1)
    low = lax.broadcasted_iota(I32, packed.shape, 1) < packed.shape[1] // 2
    return jnp.where(low, packed, turned), jnp.where(low, -turned, packed)


def qkv_kernel(x, gain, wq, wk, wv, angles, act, q, k, v, wide, *, head_dim):
    width = wq.shape[1]

    @pl.when(pl.program_id(0) == 0)
    def _():
        for i, w in enumerate((wq, wk, wv)):
            wide[:, i * width:(i + 1) * width] = w[...]

    feats = x[...].astype(F32)
    inv = lax.rsqrt(mean_row(feats * feats) + NORM_EPS)
    a = (feats * inv * gain[...]).astype(BF16)
    act[...] = a
    t = nn(a, wide[...])
    cos, sin = unpack_angles(angles[...])
    for i, out in enumerate((q, k, v)):
        for h in range(width // head_dim):
            th = t[:, i * width + h * head_dim:i * width + (h + 1) * head_dim]
            if i < 2:
                th = th * cos + pltpu.roll(th, head_dim // 2, 1) * sin
            out[:, h * head_dim:(h + 1) * head_dim] = th.astype(BF16)


def project_qkv(x_all, gain, wq, wk, wv, angles, block=512):
    total, dim = x_all.shape
    width = wq.shape[1]
    head_dim = angles.shape[1]
    rows = lambda n: pl.BlockSpec((block, n), lambda i: (i, 0))
    whole = lambda a: pl.BlockSpec(a.shape, lambda i: (0, 0), pipeline_mode=pl.Buffered(1))
    return pl.pallas_call(
        functools.partial(qkv_kernel, head_dim=head_dim),
        out_shape=[jax.ShapeDtypeStruct((total, n), BF16) for n in (dim, width, width, width)] + [jax.ShapeDtypeStruct((dim, 3 * width), BF16)],
        grid=(total // block,),
        in_specs=[rows(dim), whole(gain), whole(wq), whole(wk), whole(wv), rows(head_dim)],
        out_specs=[rows(dim), rows(width), rows(width), rows(width), pl.BlockSpec((dim, 3 * width), lambda i: (0, 0), pipeline_mode=pl.Buffered(1))],
        compiler_params=pltpu.CompilerParams(vmem_limit_bytes=60 * MIB),
        cost_estimate=cost(6 * total * dim * width, 4 * total * dim + 6 * dim * width + 6 * total * width),
        name="project_qkv",
    )(x_all, gain, wq, wk, wv, angles)


def block_range(info, i, blocks):
    r = info[0]
    b = jnp.where(i == 0, r, blocks - 1 - r)
    mine = 2 + 2 * (2 * r + i)
    jmin = 0
    imax = -1
    for j in range(blocks):
        there = 2 + 2 * (2 * j if j < blocks // 2 else 2 * blocks - 1 - 2 * j)
        jmin = jmin + (info[there + 1] < info[mine]).astype(I32)
        imax = imax + (info[there] <= info[mine + 1]).astype(I32)
    return b, jmin, imax


def attend_kernel(info, q, k, v, doc_col, doc_row, out, lse, sc, *, heads, head_dim, scale):
    blk = q.shape[0]
    b, jmin, _ = block_range(info, pl.program_id(0), doc_row.shape[0])
    row_n = lax.broadcasted_iota(I32, (blk, blk), 0) + b * blk
    col_n = lax.broadcasted_iota(I32, (blk, blk), 1)

    def score(j, peaks):
        sb = slot_block(j)
        off = pl.multiple_of(sb * blk, blk)
        allowed = (doc_col[...] == doc_row[sb]) & (col_n + j * blk <= row_n)
        new = []
        for h in range(heads):
            cols = slice(h * head_dim, (h + 1) * head_dim)
            s = nt(q[:, cols], k[pl.ds(off, blk), cols]) * scale
            s = jnp.where(allowed, s, NEG_BIG)
            sc[j, h] = s
            new.append(jnp.maximum(peaks[h], jnp.max(s, axis=1, keepdims=True)))
        return tuple(new)

    peaks = lax.fori_loop(jmin, b + 1, score, tuple(jnp.full((blk, 1), NEG_BIG, F32) for _ in range(heads)))

    def weigh(j, sums):
        new = []
        for h in range(heads):
            p = jnp.exp(sc[j, h] - peaks[h])
            sc[j, h] = p
            new.append(sums[h] + row_sum(p))
        return tuple(new)

    sums = lax.fori_loop(jmin, b + 1, weigh, tuple(jnp.zeros((blk, 1), F32) for _ in range(heads)))
    inv = tuple(1.0 / t for t in sums)
    for h in range(heads):
        lse[:, h:h + 1] = peaks[h] + jnp.log(sums[h])

    def mix(j, acc):
        off = pl.multiple_of(slot_block(j) * blk, blk)
        new = []
        for h in range(heads):
            cols = slice(h * head_dim, (h + 1) * head_dim)
            new.append(acc[h] + nn((sc[j, h] * inv[h]).astype(BF16), v[pl.ds(off, blk), cols]))
        return tuple(new)

    acc = lax.fori_loop(jmin, b + 1, mix, tuple(jnp.zeros((blk, head_dim), F32) for _ in range(heads)))
    for h in range(heads):
        out[:, h * head_dim:(h + 1) * head_dim] = acc[h].astype(BF16)


def attend(info, q, k, v, doc_col, doc_row, head_dim, blk):
    total, width = k.shape
    heads = width // head_dim
    mine = lambda n: pl.BlockSpec((blk, n), lambda i, info: (2 * info[0] + i, 0))
    return pl.pallas_call(
        functools.partial(attend_kernel, heads=heads, head_dim=head_dim, scale=head_dim ** -0.5),
        out_shape=[jax.ShapeDtypeStruct((2 * blk, width), BF16), jax.ShapeDtypeStruct((2 * blk, 8), F32)],
        grid_spec=pltpu.PrefetchScalarGridSpec(
            num_scalar_prefetch=1,
            grid=(2,),
            in_specs=[mine(width), whole(k), whole(v), mine(1), whole(doc_row)],
            out_specs=[pl.BlockSpec((blk, width), lambda i, info: (i, 0)), pl.BlockSpec((blk, 8), lambda i, info: (i, 0))],
            scratch_shapes=[pltpu.VMEM((total // blk, heads, blk, blk), F32)],
        ),
        compiler_params=pltpu.CompilerParams(vmem_limit_bytes=40 * MIB),
        cost_estimate=cost(4 * 2 * blk * total * width, 8 * total * width),
        name="attend",
    )(info, q, k, v, doc_col, doc_row)


def attend_back_kernel(info, q, k, v, do, doc_col, doc_row, lse_col, lse_row, del_col, del_row, angles, out, acc, *, heads, head_dim, scale):
    blk = angles.shape[0]
    width = heads * head_dim
    i = pl.program_id(0)
    b, jmin, imax = block_range(info, i, doc_row.shape[0])
    me = pl.multiple_of((2 * info[0] + i) * blk, blk)
    mine = pl.ds(me, blk)
    iota_r = lax.broadcasted_iota(I32, (blk, blk), 0)
    iota_c = lax.broadcasted_iota(I32, (blk, blk), 1)
    acc[...] = jnp.zeros_like(acc)
    spans = [slice(h * head_dim, (h + 1) * head_dim) for h in range(heads)]

    def for_query(j, c):
        sb = slot_block(j)
        there = pl.ds(pl.multiple_of(sb * blk, blk), blk)
        allowed = (doc_col[mine, :] == doc_row[sb]) & (iota_c + j * blk <= iota_r + b * blk)
        for h, cols in enumerate(spans):
            s = jnp.where(allowed, nt(q[mine, cols], k[there, cols]) * scale, NEG_BIG)
            p = jnp.exp(s - lse_col[mine, h:h + 1])
            dp = to_bf16(nt(do[mine, cols], v[there, cols]))
            ds = (p * (dp - del_col[mine, h:h + 1]) * scale).astype(BF16)
            acc[0, :, cols] += nn(ds, k[there, cols])
        return c

    lax.fori_loop(jmin, b + 1, for_query, 0)

    def for_key(j, c):
        sb = slot_block(j)
        there = pl.ds(pl.multiple_of(sb * blk, blk), blk)
        allowed = (doc_col[mine, :] == doc_row[sb]) & (iota_r + b * blk <= iota_c + j * blk)
        for h, cols in enumerate(spans):
            s = jnp.where(allowed, nt(k[mine, cols], q[there, cols]) * scale, NEG_BIG)
            p = jnp.exp(s - lse_row[sb, h:h + 1, :])
            dp = to_bf16(nt(v[mine, cols], do[there, cols]))
            ds = (p * (dp - del_row[sb, h:h + 1, :]) * scale).astype(BF16)
            acc[2, :, cols] += nn(p.astype(BF16), do[there, cols])
            acc[1, :, cols] += nn(ds, q[there, cols])
        return c

    lax.fori_loop(b, imax + 1, for_key, 0)
    cos, sin = unpack_angles(angles[...])
    for part in range(3):
        for h, cols in enumerate(spans):
            t = acc[part, :, cols]
            if part < 2:
                t = to_bf16(t)
                t = t * cos - pltpu.roll(t, head_dim // 2, 1) * sin
            out[:, part * width + h * head_dim:part * width + (h + 1) * head_dim] = t.astype(BF16)


def attend_back(info, q, k, v, do, doc_col, doc_row, lse_col, lse_row, del_col, del_row, angles, blk):
    total, width = k.shape
    head_dim = angles.shape[1]
    heads = width // head_dim
    mine = lambda n: pl.BlockSpec((blk, n), lambda i, info: (2 * info[0] + i, 0))
    arrays = (q, k, v, do, doc_col, doc_row, lse_col, lse_row, del_col, del_row)
    return pl.pallas_call(
        functools.partial(attend_back_kernel, heads=heads, head_dim=head_dim, scale=head_dim ** -0.5),
        out_shape=jax.ShapeDtypeStruct((2 * blk, 3 * width), BF16),
        grid_spec=pltpu.PrefetchScalarGridSpec(
            num_scalar_prefetch=1,
            grid=(2,),
            in_specs=[whole(a) for a in arrays] + [mine(head_dim)],
            out_specs=pl.BlockSpec((blk, 3 * width), lambda i, info: (i, 0)),
            scratch_shapes=[pltpu.VMEM((3, blk, width), F32)],
        ),
        compiler_params=pltpu.CompilerParams(vmem_limit_bytes=48 * MIB),
        cost_estimate=cost(14 * 2 * blk * total * width // 2, 12 * total * width),
        name="attend_back",
    )(info, *arrays, angles)


def out_proj_kernel(info, x, att, a0, b0, a1, b1, gain, res, act, wide, abuf, bbuf, sems):
    tp, _, width = att.shape
    na, nb = a0.shape[1], b0.shape[1]
    sets = ((a0, b0), (a1, b1))

    def copies(i):
        return (pltpu.make_async_copy(sets[i][0], abuf.at[i], sems.at[i, 0]), pltpu.make_async_copy(sets[i][1], bbuf.at[i], sems.at[i, 1]))

    for i in range(2):
        for c in copies(i):
            c.start()
    for t in range(tp):
        wide[:, t * width:(t + 1) * width] = att[t]
    for i in range(2):
        start = (info[1] ^ i) * (na + nb)
        first, second = copies(i)
        first.wait()
        cols = pl.ds(pl.multiple_of(start, 128), na)
        res[:, cols] = x[:, cols].astype(F32) + nn(wide[...], abuf[i])
        second.wait()
        cols = pl.ds(pl.multiple_of(start + na, 128), nb)
        res[:, cols] = x[:, cols].astype(F32) + nn(wide[...], bbuf[i])
    h = res[...]
    inv = lax.rsqrt(mean_row(h * h) + NORM_EPS)
    act[...] = (h * inv * gain[...]).astype(BF16)


def out_proj(info, flip, x_all, att, pieces, gain):
    _, rows, _ = att.shape
    dim = x_all.shape[1]
    full = pl.BlockSpec((rows, dim), lambda i, info: (0, 0))
    return pl.pallas_call(
        out_proj_kernel,
        out_shape=[jax.ShapeDtypeStruct((rows, dim), F32), jax.ShapeDtypeStruct((rows, dim), BF16)],
        grid_spec=pltpu.PrefetchScalarGridSpec(
            num_scalar_prefetch=1,
            grid=(1,),
            in_specs=[pl.BlockSpec((rows, dim), lambda i, info: (info[0] ^ flip, 0)), whole(att)] + [pl.BlockSpec(memory_space=pl.ANY)] * 4 + [whole(gain)],
            out_specs=[full, full],
            scratch_shapes=[pltpu.VMEM((rows, dim), BF16), pltpu.VMEM((2,) + pieces[0].shape, BF16), pltpu.VMEM((2,) + pieces[1].shape, BF16), pltpu.SemaphoreType.DMA((2, 2))],
        ),
        compiler_params=pltpu.CompilerParams(vmem_limit_bytes=56 * MIB),
        cost_estimate=cost(2 * rows * dim * dim, 2 * dim * dim + 10 * rows * dim),
        name="out_proj",
    )(info, x_all, att, *pieces, gain)


def weight_grad_kernel(info, *refs, pieces, splits):
    lhs = refs[:pieces]
    rhs = refs[pieces:2 * pieces]
    outs = refs[2 * pieces:]
    t = tn(lhs[0][...], rhs[0][...])
    for a, b in zip(lhs[1:], rhs[1:]):
        t += tn(a[...], b[...])
    width = t.shape[1] // splits
    for i, out in enumerate(outs):
        out[...] = t[:, i * width:(i + 1) * width]


def weight_grad(info, lhs, rhs, block=256, splits=1, rows=None):
    def spec(arr, p, cols, moving):
        if arr.ndim == 3:
            return pl.BlockSpec((None, arr.shape[1], cols), lambda i, info: (info[0] ^ p, 0, i if moving else 0))
        return pl.BlockSpec((arr.shape[0], cols), lambda i, info: (0, i if moving else 0))

    tokens = lhs[0].shape[-2]
    rows, dim = rows or lhs[0].shape[-1], rhs[0].shape[-1]
    n = len(lhs)
    width = dim // splits
    outs = pl.pallas_call(
        functools.partial(weight_grad_kernel, pieces=n, splits=splits),
        out_shape=[jax.ShapeDtypeStruct((rows, width), F32)] * splits,
        grid_spec=pltpu.PrefetchScalarGridSpec(
            num_scalar_prefetch=1,
            grid=(pl.cdiv(rows, block),),
            in_specs=[spec(a, p, block, True) for p, a in enumerate(lhs)] + [spec(b, p, dim, False) for p, b in enumerate(rhs)],
            out_specs=[pl.BlockSpec((block, width), lambda i, info: (i, 0))] * splits,
        ),
        compiler_params=pltpu.CompilerParams(vmem_limit_bytes=56 * MIB),
        cost_estimate=cost(2 * n * tokens * rows * dim, 4 * rows * dim + 2 * n * tokens * (rows + dim)),
        name="weight_grad",
    )(info, *lhs, *rhs)
    return outs if splits > 1 else outs[0]


def mlp_kernel(act, dhid, wg, wu, hidden, d_gate, d_up, *grad, limit):
    i = pl.program_id(0)
    block = wg.shape[0]
    left = limit - i * block
    row_ok = lax.broadcasted_iota(I32, (block, 1), 0) < left
    col_ok = lax.broadcasted_iota(I32, (1, block), 1) < left
    wgt = jnp.where(row_ok, wg[...], 0).astype(BF16)
    wut = jnp.where(row_ok, wu[...], 0).astype(BF16)
    gate = nt(act[...], wgt)
    up = nt(act[...], wut)
    dh = jnp.where(col_ok, dhid[...].astype(F32), 0.0)
    sig = jax.nn.sigmoid(gate)
    hidden[...] = (gate * sig * up).astype(BF16)
    dg = (dh * up * sig * (1.0 + gate * (1.0 - sig))).astype(BF16)
    du = (dh * gate * sig).astype(BF16)
    d_gate[...] = dg
    d_up[...] = du
    if grad:
        t = nn(dg, wgt) + nn(du, wut)

        @pl.when(i == 0)
        def _():
            grad[0][...] = t

        @pl.when(i > 0)
        def _():
            grad[0][...] += t


def mlp_block(act, dhid, wg, wu, with_grad, block=256):
    rows, dim = act.shape
    limit = wg.shape[0]
    cols = pl.BlockSpec((rows, block), lambda i: (0, i))
    tile = pl.BlockSpec((block, dim), lambda i: (i, 0))
    whole = pl.BlockSpec((rows, dim), lambda i: (0, 0))
    return pl.pallas_call(
        functools.partial(mlp_kernel, limit=limit),
        out_shape=[jax.ShapeDtypeStruct((rows, pl.cdiv(limit, block) * block), BF16)] * 3 + [jax.ShapeDtypeStruct((rows, dim), F32)] * with_grad,
        grid=(pl.cdiv(limit, block),),
        in_specs=[whole, cols, tile, tile],
        out_specs=[cols] * 3 + [whole] * with_grad,
        compiler_params=pltpu.CompilerParams(vmem_limit_bytes=48 * MIB),
        cost_estimate=cost((4 + 4 * with_grad) * rows * dim * limit, 4 * dim * limit + 6 * rows * limit + 10 * rows * dim),
        name="mlp_block",
    )(act, dhid, wg, wu)


def zero_kernel(after, out, zeros, sem):
    zeros[...] = jnp.zeros_like(zeros)
    step = zeros.shape[0]
    count = out.shape[0] // step

    def send(i, c):
        pltpu.make_async_copy(zeros, out.at[pl.ds(pl.multiple_of(i * step, step), step), :], sem).start()
        return c

    def wait(i, c):
        pltpu.make_async_copy(zeros, out.at[pl.ds(0, step), :], sem).wait()
        return c

    lax.fori_loop(0, count, send, 0)
    lax.fori_loop(0, count, wait, 0)


def zero_rows(after, rows, dim, step=200):
    return pl.pallas_call(
        zero_kernel,
        out_shape=jax.ShapeDtypeStruct((rows, dim), F32),
        in_specs=[pl.BlockSpec(memory_space=pltpu.SMEM)],
        out_specs=pl.BlockSpec(memory_space=pl.ANY),
        scratch_shapes=[pltpu.VMEM((step, dim), F32), pltpu.SemaphoreType.DMA],
        compiler_params=pltpu.CompilerParams(vmem_limit_bytes=8 * MIB),
        cost_estimate=cost(rows * dim, 4 * rows * dim),
        name="zero_rows",
    )(after)


def scatter_kernel(order, sid, runs, bounds, rows, base_hbm, out_hbm, sums, row_sem, sum_sem):
    lo = bounds[0]
    hi = bounds[1]

    def one(c):
        p, singles, multi = c
        n = runs[p]
        t = order[p]
        single = n == 1

        @pl.when(single)
        def _():
            pltpu.make_async_copy(rows.at[pl.ds(t, 1), :], out_hbm.at[pl.ds(sid[p], 1), :], row_sem).start()

        @pl.when(jnp.logical_not(single))
        def _():
            def add(j, acc):
                return acc + rows[pl.ds(order[p + j], 1), :]

            sums[pl.ds(multi, 1), :] = lax.fori_loop(1, n, add, rows[pl.ds(t, 1), :])

        return p + n, singles + single.astype(I32), multi + 1 - single.astype(I32)

    _, singles, multi = lax.while_loop(lambda c: c[0] < hi, one, (lo, 0, 0))

    def two(c):
        p, k = c
        n = runs[p]

        @pl.when(n > 1)
        def _():
            pltpu.make_async_copy(sums.at[pl.ds(k, 1), :], out_hbm.at[pl.ds(sid[p], 1), :], sum_sem).start()

        return p + n, k + (n > 1).astype(I32)

    lax.while_loop(lambda c: c[0] < hi, two, (lo, 0))

    def wait(sem):
        def body(i, c):
            pltpu.make_async_copy(sums.at[pl.ds(0, 1), :], out_hbm.at[pl.ds(0, 1), :], sem).wait()
            return c

        return body

    lax.fori_loop(0, singles, wait(row_sem), 0)
    lax.fori_loop(0, multi, wait(sum_sem), 0)


def scatter_rows(order, sid, runs, bounds, grads, base, tokens):
    _, dim = grads.shape
    rows = base.shape[0]
    return pl.pallas_call(
        scatter_kernel,
        out_shape=jax.ShapeDtypeStruct((rows, dim), F32),
        grid_spec=pltpu.PrefetchScalarGridSpec(
            num_scalar_prefetch=4,
            grid=(),
            in_specs=[pl.BlockSpec(memory_space=pltpu.VMEM), pl.BlockSpec(memory_space=pl.ANY)],
            out_specs=pl.BlockSpec(memory_space=pl.ANY),
            scratch_shapes=[pltpu.VMEM((tokens // 2, dim), F32), pltpu.SemaphoreType.DMA, pltpu.SemaphoreType.DMA],
        ),
        input_output_aliases={5: 0},
        compiler_params=pltpu.CompilerParams(vmem_limit_bytes=40 * MIB),
        name="scatter_rows",
    )(order, sid, runs, bounds, grads, base)


def solution(mesh):
    cp_count = mesh.shape["cp"]
    tp_count = mesh.shape["tp"]
    both = ("cp", "tp")
    x_swap = [(i, i ^ 2) for i in range(cp_count)]
    core_swap = [(i, i ^ 1) for i in range(cp_count)]

    def compute(tokens, pos, doc_id, dy, table, w_q, w_k, w_v, w_o, w_gate, w_up, w_down, gain_one, gain_two, inv_freq):
        span = tokens.shape[0]
        total = span * cp_count
        part = span // tp_count
        rows, dim = table.shape
        head_dim = 2 * inv_freq.shape[0]
        heads = w_q.shape[1] // head_dim
        width = heads * head_dim
        tp_rank = lax.axis_index("tp")
        cp_rank = lax.axis_index("cp")
        core = cp_rank % 2
        gain_a = gain_one.astype(F32)
        gain_b = gain_two.astype(F32)

        barrier = lax.optimization_barrier
        join = lambda arr, axis: lax.all_gather(arr, axis, axis=0, tiled=True)
        add_up = lambda arr: lax.psum_scatter(arr, "tp", scatter_dimension=0, tiled=True)
        swap = lambda arr, pairs, axis="cp": lax.ppermute(arr, axis, pairs)
        local_ids = tokens - tp_rank * rows
        owned = (local_ids >= 0) & (local_ids < rows)
        safe_ids = jnp.where(owned, local_ids, 0)
        picked = jnp.where(owned[:, None], jnp.take(table, safe_ids, axis=0), 0).astype(BF16)
        half = dim // 2
        near = 512
        wo_half = lax.dynamic_slice_in_dim(w_o, core * half, half, 1)
        wo_near = join(wo_half[:, :near], "tp")
        angle = pos.astype(F32)[:, None] * inv_freq[None, :]
        side_f = jnp.concatenate([jnp.cos(angle), jnp.sin(angle)], axis=1)
        side_i = jnp.concatenate([tokens[None], doc_id[None], jnp.zeros((6, span), I32)], axis=0)
        x_all, x_slice, angles, ints = embed_gather(picked.reshape(tp_count, part, dim), side_f, side_i)
        angles = angles.reshape(total, head_dim)
        tok_all = ints[:, 0, :].reshape(total)
        doc_all = ints[:, 1, :].reshape(total)
        wo_far = barrier((wo_half[:, near:], x_all))[0]
        wo_rest = join(wo_far, "tp")
        wo_pieces = (wo_near, wo_rest, swap(wo_near, core_swap), swap(wo_rest, core_swap))

        dy_x = swap(barrier((dy, x_all))[0], x_swap)
        act_a, query, key, value, w_qkv = project_qkv(x_all, gain_a[None, :], w_q, w_k, w_v, angles)

        blk = span // 2
        blocks = total // blk
        doc_col = doc_all[:, None]
        doc_row = doc_all.reshape(blocks, 1, blk)
        docs = doc_all.reshape(blocks, blk)
        docs = jnp.stack([docs[:, 0], docs[:, -1]], axis=1).reshape(2 * blocks)
        info = jnp.concatenate([cp_rank[None], core[None], docs]).astype(I32)
        attended, lse = attend(info, query, key, value, doc_col, doc_row, head_dim, blk)

        att_parts = lax.all_gather(attended, "tp", axis=0, tiled=False)
        lse_all = join(lse, "cp")
        d_hidden = nt(dy, w_down).astype(BF16)
        slot_ids = jnp.arange(total, dtype=I32)
        before = (tok_all[None, :] < tok_all[:, None]) | ((tok_all[None, :] == tok_all[:, None]) & (slot_ids[None, :] < slot_ids[:, None]))
        rank = jnp.sum(before.astype(I32), axis=1)
        count = jnp.sum((tok_all[None, :] == tok_all[:, None]).astype(I32), axis=1)
        at_rank = rank[None, :] == slot_ids[:, None]
        runs = jnp.sum(jnp.where(at_rank, count[None, :], 0), axis=1)
        order = jnp.sum(jnp.where(at_rank, slot_ids[None, :], 0), axis=1)
        sid = jnp.sum(jnp.where(at_rank, tok_all[None, :], 0), axis=1) - tp_rank * rows
        order = order + 8 * (order // part)
        bounds = jnp.stack([jnp.sum((tok_all < tp_rank * rows).astype(I32)), jnp.sum((tok_all < (tp_rank + 1) * rows).astype(I32))])
        att_parts, lse_all, d_hidden, runs, order, sid, bounds = barrier((att_parts, lse_all, d_hidden, runs, order, sid, bounds))
        gain_row = gain_b[None, :]
        residual, act_b = out_proj(info, 0, x_all, att_parts, wo_pieces, gain_row)
        att_x = swap(att_parts, x_swap)

        wg, wu = w_gate.T, w_up.T
        ffn = wg.shape[0]
        hidden, d_gate, d_up, d_act_b = mlp_block(act_b, d_hidden, wg, wu, True)
        d_act_b = add_up(d_act_b)
        dhid_x = nt(dy_x, w_down).astype(BF16)
        act_x = out_proj(info, 2, x_all, att_x, wo_pieces, gain_row)[1]
        hidden_x, d_gate_x, d_up_x = mlp_block(act_x, dhid_x, wg, wu, False)
        d_act_b, hidden_x, d_gate_x, d_up_x = barrier((d_act_b, hidden_x, d_gate_x, d_up_x))
        d_act_b = to_bf16(d_act_b)
        acts, dys, hiddens, d_gates, d_ups = [(a, swap(a, core_swap), b, swap(b, core_swap)) for a, b in (
            (act_b, act_x), (dy, dy_x), (hidden, hidden_x), (d_gate, d_gate_x), (d_up, d_up_x))]
        heads_x = lax.dynamic_index_in_dim(att_x, tp_rank, 0, keepdims=False)
        head_parts = (attended, swap(attended, core_swap), heads_x, swap(heads_x, core_swap))
        att_heads = jnp.zeros((total, width), BF16)
        for k, piece in enumerate(head_parts):
            att_heads = lax.dynamic_update_slice_in_dim(att_heads, piece, (cp_rank ^ k) * span, 0)
        grad_down = weight_grad(info, hiddens, dys, rows=ffn)
        grad_gate = weight_grad(info, d_gates, acts, rows=ffn)
        grad_up = weight_grad(info, d_ups, acts, rows=ffn)

        def mine(arr):
            return lax.dynamic_slice_in_dim(arr, tp_rank * part, part, 0)

        res_part = mine(residual)
        normed_b, inv_b = rms_stats(res_part)
        grad_gain_b = jnp.sum(d_act_b * normed_b, axis=0)
        d_resid = mine(dy).astype(F32) + rms_back(d_act_b * gain_b, normed_b, inv_b)
        d_resid_all = join(d_resid.astype(BF16), both)
        out_part = nn(hidden[:, :ffn], w_down)
        d_resid_all, grad_down, att_heads, out_part = barrier((d_resid_all, grad_down, att_heads, out_part))
        out_slice = add_up(out_part)
        out_slice = (res_part + out_slice).astype(BF16)

        d_att = nt(d_resid_all, w_o)
        d_att_b = d_att.astype(BF16)
        head_of = (jnp.arange(width)[None, :] // head_dim == jnp.arange(8)[:, None]).astype(F32)
        prod = att_heads.astype(F32) * d_att_b.astype(F32)
        delta = lax.dot_general(head_of, prod, (((1,), (1,)), ((), ())), precision=lax.Precision.HIGHEST, preferred_element_type=F32)

        def by_block(arr):
            return jnp.transpose(arr.reshape(8, blocks, blk), (1, 0, 2))

        dqkv = attend_back(info, query, key, value, d_att_b, doc_col, doc_row, lse_all, by_block(lse_all.T), delta.T, by_block(delta), angles, blk)
        d_act_a = nt(dqkv, w_qkv)
        d_act_a, out_slice = barrier((d_act_a, out_slice))
        d_act_a = add_up(d_act_a)
        dqkv_x = swap(dqkv, x_swap)
        dqkvs = (dqkv, swap(dqkv, core_swap), dqkv_x, swap(dqkv_x, core_swap))
        grad_out = weight_grad(info, head_parts, [d_resid_all.reshape(cp_count, span, dim)] * 4)
        d_act_a, dqkv_x, grad_out, grad_up = barrier((d_act_a, dqkv_x, grad_out, grad_up))
        d_act_a = to_bf16(d_act_a)
        normed_a, inv_a = rms_stats(x_slice.astype(F32))
        grad_gain_a = jnp.sum(d_act_a * normed_a, axis=0)
        d_embed = d_resid + rms_back(d_act_a * gain_a, normed_a, inv_a)
        payload = jnp.concatenate([d_embed, grad_gain_a[None], grad_gain_b[None], jnp.zeros((6, dim), F32)], axis=0)
        gathered = join(payload, both)
        grad_qkv = weight_grad(info, [act_a.reshape(cp_count, span, dim)] * 4, dqkvs, splits=3)
        base = zero_rows(barrier((bounds, d_act_a))[0], rows, dim)
        gathered, grad_qkv, grad_gate, base = barrier((gathered, grad_qkv, grad_gate, base))
        out_slice = barrier((out_slice, gathered))[0]
        layer_out = join(out_slice, "tp")
        gain_grads = jnp.sum(gathered.reshape(cp_count * tp_count, part + 8, dim)[:, part:part + 2], axis=0)
        grad_table = scatter_rows(order, sid, runs, bounds, gathered, base, total)
        return (layer_out, grad_table, *grad_qkv, grad_out, grad_gate.T, grad_up.T, grad_down, gain_grads[0], gain_grads[1])

    col_spec = P(None, "tp")
    row_spec = P("tp", None)
    tok_spec = P("cp")
    rep_spec = P(None)
    in_specs = (tok_spec, tok_spec, tok_spec, P("cp", None), row_spec, col_spec, col_spec, col_spec, row_spec, col_spec, col_spec, row_spec, rep_spec, rep_spec, rep_spec)
    out_specs = (P("cp", None), row_spec, col_spec, col_spec, col_spec, row_spec, col_spec, col_spec, row_spec, rep_spec, rep_spec)
    return jax.shard_map(compute, mesh=mesh, in_specs=in_specs, out_specs=out_specs, check_vma=False)
```

time: 865 us -> 766 us (0.89)
  waiting for transfers between devices: 315 us -> 163 us
  Pallas kernels: 320 us -> 401 us
  blocking collectives: 21.9 us -> 11 us
    all_gather x6 -> x5, waiting for transfers between devices: 173 us -> 38.6 us  [compute(): join = lambda arr, axis: lax.all_gather(arr, axis, axis=0, tiled=True)]
    pallas_call x0 -> x1, Pallas kernels: none -> 75.1 us  [embed_gather(): pl.pallas_call(embed_kernel, out_shape=[jax.ShapeDtypeStruct((16 * rows,...]
    all_gather x2 -> x1, blocking collectives: 21.9 us -> 11 us  [compute(): join = lambda arr, axis: lax.all_gather(arr, axis, axis=0, tiled=True)]
    all_gather x1, waiting for transfers between devices: 12.9 us -> 3.28 us  [compute(): att_parts = lax.all_gather(attended, 'tp', axis=0, tiled=False)]
    reduce_sum x7 -> x6, other arithmetic: 14.1 us -> 20 us  [the longest x1 8.43 us: compute(): jnp.sum(jnp.where(at_rank, tok_all[None, :], 0), axis=1) - tp_rank * rows]
    unnamed x93 -> x73, local copies, waits for them, and re-layouts: 28.3 us -> 25.6 us
    dot_general x7 -> x5, matrix products: 54.4 us -> 54 us  [contract(): lax.dot_general(a, b, (((ca,), (cb,)), ((), ())), preferred_element_type=...]
  transfers between devices with their start and end apart: 30 -> 28, of which waited for: 15 -> 12; matrix products, arithmetic and copies ran while one was open for 15% -> 13% of each run, Pallas kernels for 32% -> 37%
where the time goes in v4:
time: 766 us; the launch traced here: 760 us
  Pallas kernels  401 us (52%)
  waiting for transfers between devices  163 us (21%)
  local copies, waits for them, and re-layouts  60.2 us (8%)
  matrix products  59.1 us (8%)
  other arithmetic  42.1 us (5%)
  between operations  14.7 us (2%)
  blocking collectives  11 us (1%)
  starting transfers between devices  8.35 us (1%)
    pallas_call x5, Pallas kernels, weight_grad(): pl.pallas_call(functools.partial(weight_grad_kernel, pieces=n, splits=spl...  127 us
    ppermute x19, waiting for transfers between devices, compute(): swap = lambda arr, pairs, axis='cp': lax.ppermute(arr, axis, pairs)  110 us
    pallas_call x1, Pallas kernels, embed_gather(): pl.pallas_call(embed_kernel, out_shape=[jax.ShapeDtypeStruct((16 * rows,...  75.1 us
    dot_general x5, matrix products, contract(): lax.dot_general(a, b, (((ca,), (cb,)), ((), ())), preferred_element_type=...  54 us
    pallas_call x2, Pallas kernels, mlp_block(): pl.pallas_call(functools.partial(mlp_kernel, limit=limit), out_shape=[jax...  46.6 us
    all_gather x5, waiting for transfers between devices, compute(): join = lambda arr, axis: lax.all_gather(arr, axis, axis=0, tiled=True)  38.6 us
    pallas_call x1, Pallas kernels, project_qkv(): pl.pallas_call(functools.partial(qkv_kernel, head_dim=head_dim), out_shap...  34.3 us
    pallas_call x2, Pallas kernels, out_proj(): pl.pallas_call(out_proj_kernel, out_shape=[jax.ShapeDtypeStruct((rows, di...  34 us
  transfers between devices with their start and end apart: 28, of which 12 were waited for; matrix products, arithmetic and copies ran while one was open for 13% of the time, Pallas kernels for 37%

profile of v4, /device:TPU:0, one launch (start us, length us, event | category | flops | bytes accessed | tf_op | source)
XLA Modules:
  0.0 759.9 jit_solution(6128134968735388848)
XLA Ops:
  12.4 13.2 %gather_fusion = bf16[512,2560]{1,0:T(8,128)(2,1)} fusion(bf16[8000,2560]{1,0:T(8,128)(2,1)} %param.19, s32[1024]{0:T(1024)S(1)} %pad_clamp_fusion), kind=kCustom, calls=%fused_computation | custom fusion | bytes 5244928 | tf_op jit(solution)/shard_map/jit(_take)/gather | solution.py:740
  28.5 75.1 %embed_gather.1 = (bf16[2048,2560]{1,0:T(8,128)(2,1)}, bf16[128,2560]{1,0:T(8,128)(2,1)S(1)}, f32[4,512,128]{2,1,0:T(8,128)S(1)}, s32[4,8,512]{2,1,0:T(8,128)S(1)}) custom-call(bf16[4,128,2560]{2,1,0:T(8,128)(2,1)S(1)} %select_select_fusion.picked, f32[512,128]{1,0:T(8,128)S(1)} %pad_maximum_fusion.side_f, s32[8,512]{1,0:T(8,128)S(1)} %add_add_fusion.side_i), custom_call_target="tpu_custom_call" | custom-call | tf_op jit(solution)/shard_map/embed_gather/pallas_call | solution.py:258
  112.1 34.3 %project_qkv.1 = (bf16[2048,2560]{1,0:T(8,128)(2,1)}, bf16[2048,640]{1,0:T(8,128)(2,1)}, bf16[2048,640]{1,0:T(8,128)(2,1)}, bf16[2048,640]{1,0:T(8,128)(2,1)}, bf16[2560,1920]{1,0:T(8,128)(2,1)}) custom-call(bf16[2048,2560]{1,0:T(8,128)(2,1)} %get-tuple-element.66.x, f32[1,2560]{1,0:T(1,128)} %broadcast_in_dim.112.gain, bf16[2560,640]{1,0:T(8,128)(2,1)} %wq.1, ...), custom_call_target="tpu_custom_call" | custom-call | flops 20132659200 | bytes 38666240 | tf_op jit(solution)/shard_map/project_qkv/pallas_call | solution.py:319
  165.4 25.0 %all-gather.8.cloned.1.call-done.a0 = bf16[2560,512]{1,0:T(8,128)(2,1)} async-done(((bf16[640,512]{1,0:T(8,128)(2,1)}), bf16[2560,512]{1,0:T(8,128)(2,1)}) %all-gather.8.cloned.1.call-update) | async-done | bytes 2621456 | tf_op jit(solution)/shard_map/all_gather | solution.py:734
  200.1 11.0 %all_gather.26.lse_col = f32[2048,8]{1,0:T(8,128)} all-gather(f32[512,8]{1,0:T(8,128)S(1)} %get-tuple-element.72), channel_id=1, replica_groups=mesh['tp'=4,'cp'=4] {'cp'}, dimensions={0}, use_global_device_ids=true | all-gather | bytes 81920 | tf_op jit(solution)/shard_map/all_gather | solution.py:734
  214.2 10.5 %convolution_convert_fusion.2.dhid = bf16[512,1728]{1,0:T(8,128)(2,1)} fusion(bf16[512,2560]{1,0:T(8,128)(2,1)} %refs_4_.1, bf16[1728,2560]{1,0:T(8,128)(2,1)} %param.26), kind=kOutput, calls=%fused_computation.17 | convolution fusion | flops 4530733056 | bytes 13238272 | tf_op jit(solution)/shard_map/dot_general | solution.py:31
  228.0 16.9 %out_proj.2 = (f32[512,2560]{1,0:T(8,128)}, bf16[512,2560]{1,0:T(8,128)(2,1)}) custom-call(s32[18]{0:T(128)} %copy-done.9, bf16[2048,2560]{1,0:T(8,128)(2,1)} %get-tuple-element.66.x, bf16[4,512,640]{2,1,0:T(8,128)(2,1)} %bitcast.58, bf16[2560,512]{1,0:T(8,128)(2,1)} %all-gather.8.cloned.1.call-done.a0, bf16[2560,768]{1,0:T(8,128)(2,1)} %all-gather.10.cloned.1.call-done.b0, ...), custom_call_target="tpu_custom_call" | custom-call | flops 6710886400 | bytes 26214400 | tf_op jit(solution)/shard_map/out_proj/pallas_call | solution.py:514
  244.9 30.9 %mlp_block.2 = (bf16[512,1792]{1,0:T(8,128)(2,1)}, bf16[512,1792]{1,0:T(8,128)(2,1)S(1)}, bf16[512,1792]{1,0:T(8,128)(2,1)S(1)}, f32[512,2560]{1,0:T(8,128)}) custom-call(bf16[512,2560]{1,0:T(8,128)(2,1)} %get-tuple-element.76.act.refs_4_, bf16[512,1728]{1,0:T(8,128)(2,1)} %convolution_convert_fusion.2.dhid, bf16[1728,2560]{1,0:T(8,128)(2,1)} %bitcast.64, ...), custom_call_target="tpu_custom_call" | custom-call | flops 18119393280 | bytes 36110336 | tf_op jit(solution)/shard_map/mlp_block/pallas_call | solution.py:603
  280.4 58.0 %collective-permute-done.3.refs_6_ = bf16[512,2560]{1,0:T(8,128)(2,1)} collective-permute-done((bf16[512,2560]{1,0:T(8,128)(2,1)}, bf16[512,2560]{1,0:T(8,128)(2,1)}, u32[]{:S(2)}, u32[]{:S(2)}) %collective-permute-start.3) | collective-permute-done | bytes 2621472 | tf_op jit(solution)/shard_map/ppermute | solution.py:736
  338.4 10.3 %convolution_convert_fusion.1 = bf16[512,1728]{0,1:T(8,128)(2,1)} fusion(bf16[512,2560]{1,0:T(8,128)(2,1)} %collective-permute-done.3.refs_6_, bf16[1728,2560]{1,0:T(8,128)(2,1)} %param.26), kind=kOutput, calls=%fused_computation.16 | convolution fusion | flops 4530733056 | bytes 13238272 | tf_op jit(solution)/shard_map/dot_general | solution.py:31
  354.1 39.2 %collective-permute-done.2.att = bf16[4,512,640]{2,1,0:T(8,128)(2,1)} collective-permute-done((bf16[4,512,640]{2,1,0:T(8,128)(2,1)}, bf16[4,512,640]{2,1,0:T(8,128)(2,1)}, u32[]{:S(2)}, u32[]{:S(2)}) %collective-permute-start.2) | collective-permute-done | bytes 2621472 | tf_op jit(solution)/shard_map/ppermute | solution.py:736
  393.3 17.0 %out_proj.3 = (f32[512,2560]{1,0:T(8,128)}, bf16[512,2560]{1,0:T(8,128)(2,1)}) custom-call(s32[18]{0:T(128)} %copy-done.9, bf16[2048,2560]{1,0:T(8,128)(2,1)} %get-tuple-element.66.x, bf16[4,512,640]{2,1,0:T(8,128)(2,1)} %collective-permute-done.2.att, bf16[2560,512]{1,0:T(8,128)(2,1)} %all-gather.8.cloned.1.call-done.a0, ...), custom_call_target="tpu_custom_call" | custom-call | flops 6710886400 | bytes 26214400 | tf_op jit(solution)/shard_map/out_proj/pallas_call | solution.py:514
  410.4 15.8 %mlp_block.3 = (bf16[512,1792]{1,0:T(8,128)(2,1)}, bf16[512,1792]{1,0:T(8,128)(2,1)S(1)}, bf16[512,1792]{1,0:T(8,128)(2,1)S(1)}) custom-call(bf16[512,2560]{1,0:T(8,128)(2,1)} %get-tuple-element.79.act.refs_6_, bf16[512,1728]{1,0:T(8,128)(2,1)} %copy.62.dhid, bf16[1728,2560]{1,0:T(8,128)(2,1)} %bitcast.65, bf16[1728,2560]{1,0:T(8,128)(2,1)} %bitcast.67), custom_call_target="tpu_custom_call" | custom-call | flops 9059696640 | bytes 36110336 | tf_op jit(solution)/shard_map/mlp_block/pallas_call | solution.py:603
  446.6 11.3 %fusion.6 = f32[512,2560]{1,0:T(8,128)} fusion(bf16[1728,2560]{1,0:T(8,128)(2,1)} %param.26, bf16[512,1792]{1,0:T(8,128)(2,1)} %get-tuple-element.85.refs_0_), kind=kOutput, calls=%fused_computation.19 | convolution fusion | flops 4529848320 | bytes 15925248 | tf_op jit(solution)/shard_map/dot_general | solution.py:31
  457.9 27.3 %weight_grad.5 = f32[1728,2560]{1,0:T(8,128)} custom-call(s32[18]{0:T(128)} %copy-done.9, bf16[512,1792]{1,0:T(8,128)(2,1)} %get-tuple-element.85.refs_0_, bf16[512,1792]{1,0:T(8,128)(2,1)} %collective-permute-done.4.refs_1_, bf16[512,1792]{1,0:T(8,128)(2,1)} %get-tuple-element.86.refs_2_, bf16[512,1792]{1,0:T(8,128)(2,1)} %collective-permute-done.5.refs_3_, ...), custom_call_target="tpu_custom_call" | custom-call | flops 18119393280 | bytes 35258368 | tf_op jit(solution)/shard_map/weight_grad/pallas_call | solution.py:552
  491.3 11.0 %convolution_convert_fusion.do = bf16[2048,640]{1,0:T(8,128)(2,1)S(1)} fusion(bf16[2048,2560]{1,0:T(8,128)(2,1)} %all-gather.12.cloned.1.call-done, bf16[640,2560]{1,0:T(8,128)(2,1)S(1)} %copy-done), kind=kOutput, calls=%fused_computation.15 | convolution fusion | flops 6712197120 | bytes 16384000 | tf_op jit(solution)/shard_map/dot_general | solution.py:31
  510.5 19.9 %attend_back.1.refs_4_ = bf16[512,1920]{1,0:T(8,128)(2,1)} custom-call(s32[18]{0:T(128)S(1)} %copy-done.10, bf16[2048,640]{1,0:T(8,128)(2,1)} %get-tuple-element.68.q, bf16[2048,640]{1,0:T(8,128)(2,1)} %get-tuple-element.69.k, bf16[2048,640]{1,0:T(8,128)(2,1)} %get-tuple-element.70.v, bf16[2048,640]{1,0:T(8,128)(2,1)} %copy-done.25, ...), custom_call_target="tpu_custom_call" | custom-call | flops 4697620480 | bytes 15728640 | tf_op jit(solution)/shard_map/attend_back/pallas_call | solution.py:467
  530.4 10.9 %fusion.36 = f32[512,2560]{1,0:T(8,128)} fusion(bf16[512,1920]{1,0:T(8,128)(2,1)} %attend_back.1.refs_4_, bf16[2560,1920]{1,0:T(8,128)(2,1)} %get-tuple-element.90), kind=kOutput, calls=%fused_computation.95 | convolution fusion | flops 5033164800 | bytes 17039360 | tf_op jit(solution)/shard_map/dot_general | solution.py:31
  568.0 27.4 %weight_grad.7 = f32[1728,2560]{1,0:T(8,128)} custom-call(s32[18]{0:T(128)} %copy-done.9, bf16[512,1792]{1,0:T(8,128)(2,1)} %copy-done.15, bf16[512,1792]{1,0:T(8,128)(2,1)} %copy-done.33, bf16[512,1792]{1,0:T(8,128)(2,1)} %copy-done.17, bf16[512,1792]{1,0:T(8,128)(2,1)} %collective-permute-done.12.refs_3_, bf16[512,2560]{1,0:T(8,128)(2,1)} %get-tuple-element.76.act.refs_4_, ...), custom_call_target="tpu_custom_call" | custom-call | flops 18119393280 | bytes 35258368 | tf_op jit(solution)/shard_map/weight_grad/pallas_call | solution.py:552
  595.4 15.0 %weight_grad.6 = f32[640,2560]{1,0:T(8,128)} custom-call(s32[18]{0:T(128)} %copy-done.9, bf16[512,640]{1,0:T(8,128)(2,1)} %copy-done.4, bf16[512,640]{1,0:T(8,128)(2,1)} %collective-permute-done.8.refs_1_, bf16[512,640]{1,0:T(8,128)(2,1)} %get-tuple-element.133.refs_2_, bf16[512,640]{1,0:T(8,128)(2,1)} %collective-permute-done.9.refs_3_, ...), custom_call_target="tpu_custom_call" | custom-call | flops 6710886400 | bytes 19660800 | tf_op jit(solution)/shard_map/weight_grad/pallas_call | solution.py:552
  618.9 27.8 %zero_rows.1.base_hbm = f32[8000,2560]{1,0:T(8,128)} custom-call(s32[2]{0:T(128)S(1)} %pad_add_fusion.2.after.bounds), custom_call_target="tpu_custom_call" | custom-call | flops 20480000 | bytes 81920000 | tf_op jit(solution)/shard_map/zero_rows/pallas_call | solution.py:633
  648.0 27.0 %weight_grad.9 = f32[1728,2560]{1,0:T(8,128)} custom-call(s32[18]{0:T(128)} %copy-done.9, bf16[512,1792]{1,0:T(8,128)(2,1)} %copy-done.12, bf16[512,1792]{1,0:T(8,128)(2,1)} %copy-done.34, bf16[512,1792]{1,0:T(8,128)(2,1)} %copy-done.14, bf16[512,1792]{1,0:T(8,128)(2,1)} %collective-permute-done.18.refs_3_, bf16[512,2560]{1,0:T(8,128)(2,1)} %get-tuple-element.76.act.refs_4_, ...), custom_call_target="tpu_custom_call" | custom-call | flops 18119393280 | bytes 35258368 | tf_op jit(solution)/shard_map/weight_grad/pallas_call | solution.py:552
  677.0 30.1 %weight_grad.8 = (f32[2560,640]{1,0:T(8,128)}, f32[2560,640]{1,0:T(8,128)}, f32[2560,640]{1,0:T(8,128)}) custom-call(s32[18]{0:T(128)} %copy-done.9, bf16[4,512,2560]{2,1,0:T(8,128)(2,1)} %bitcast.70, bf16[4,512,2560]{2,1,0:T(8,128)(2,1)} %bitcast.71, bf16[4,512,2560]{2,1,0:T(8,128)(2,1)} %bitcast.72, bf16[4,512,2560]{2,1,0:T(8,128)(2,1)} %bitcast.73, ...), custom_call_target="tpu_custom_call" | custom-call | flops 20132659200 | bytes 38010880 | tf_op jit(solution)/shard_map/weight_grad/pallas_call | solution.py:552
  711.8 31.1 %scatter_rows.1 = f32[8000,2560]{1,0:T(8,128)} custom-call(s32[2048]{0:T(1024)S(1)} %get-tuple-element.108.order, s32[2048]{0:T(1024)S(1)} %get-tuple-element.109.sid, s32[2048]{0:T(1024)S(1)} %select_reduce_fusion.2.runs, s32[2]{0:T(128)S(1)} %pad_add_fusion.2.after.bounds, ...), custom_call_target="tpu_custom_call", output_to_operand_aliasing={{}: (5, {})} | custom-call | tf_op jit(solution)/shard_map/scatter_rows/pallas_call | solution.py:696
  (192 shorter events, 149.0 us)
Async XLA Ops:
  7.2 152.0 %all-gather.10.cloned.1.call-start = ((), (), s32[]{:S(2)}) async-start(), calls=%async_computation.4 | async-start | bytes 4915200 | tf_op jit(solution)/shard_map/all_gather | solution.py:734
  106.2 84.2 %all-gather.8.cloned.1.call-start = ((), (), s32[]{:S(2)}) async-start(), calls=%async_computation.3 | async-start | bytes 3276800 | tf_op jit(solution)/shard_map/all_gather | solution.py:734
  107.1 120.8 %all-gather.18.cloned.1.call-start = ((), (), s32[]{:S(2)}) async-start(), calls=%async_computation.11 | async-start | bytes 3276800 | tf_op jit(solution)/shard_map/all_gather | solution.py:768
  159.1 269.5 %reduce-scatter.4.cloned.1.call-start = ((), (), s32[]{:S(2)}) async-start(), calls=%async_computation.5 | async-start | bytes 6553600 | tf_op jit(solution)/shard_map/reduce_scatter | solution.py:735
  159.2 68.8 %collective-permute-start.1 = (bf16[2560,768]{1,0:T(8,128)(2,1)}, bf16[2560,768]{1,0:T(8,128)(2,1)}, u32[]{:S(2)}, u32[]{:S(2)}) collective-permute-start(bf16[2560,768]{1,0:T(8,128)(2,1)} %all-gather.10.cloned.1.call-done.b0), channel_id=1, source_target_pairs={{0,1},{1,0},{2,3},{3,2},{4,5},{5,4},{6,7},{7,6},{8,9},{9,8},{10,11... | collective-permute-start | bytes 11796488 | tf_op jit(solution)/shard_map/ppermute | solution.py:736
  190.4 37.6 %collective-permute-start = (bf16[2560,512]{1,0:T(8,128)(2,1)}, bf16[2560,512]{1,0:T(8,128)(2,1)}, u32[]{:S(2)}, u32[]{:S(2)}) collective-permute-start(bf16[2560,512]{1,0:T(8,128)(2,1)} %all-gather.8.cloned.1.call-done.a0), channel_id=1, source_target_pairs={{0,1},{1,0},{2,3},{3,2},{4,5},{5,4},{6,7},{7,6},{8,9},{9,8},{10,11... | collective-permute-start | bytes 7864328 | tf_op jit(solution)/shard_map/ppermute | solution.py:736
  278.3 211.4 %all-gather.12.cloned.1.call-start = ((), (), s32[]{:S(2)}) async-start(), calls=%async_computation.6 | async-start | bytes 11141120 | tf_op jit(solution)/shard_map/all_gather | solution.py:734
  278.3 60.1 %collective-permute-start.3 = (bf16[512,2560]{1,0:T(8,128)(2,1)}, bf16[512,2560]{1,0:T(8,128)(2,1)}, u32[]{:S(2)}, u32[]{:S(2)}) collective-permute-start(bf16[512,2560]{1,0:T(8,128)(2,1)} %refs_4_.1), channel_id=1, source_target_pairs={{0,2},{1,3},{2,0},{3,1},{4,6},{5,7},{6,4},{7,5},{8,10},{9,11},{10,... | collective-permute-start | bytes 7864328 | tf_op jit(solution)/shard_map/ppermute | solution.py:736
  279.8 113.5 %collective-permute-start.2 = (bf16[4,512,640]{2,1,0:T(8,128)(2,1)}, bf16[4,512,640]{2,1,0:T(8,128)(2,1)}, u32[]{:S(2)}, u32[]{:S(2)}) collective-permute-start(bf16[4,512,640]{2,1,0:T(8,128)(2,1)} %bitcast.59), channel_id=1, source_target_pairs={{0,2},{1,3},{2,0},{3,1},{4,6},{5,7},{6,4},{7,5},{8,10},{9,11},{10,... | collective-permute-start | bytes 7864328 | tf_op jit(solution)/shard_map/ppermute | solution.py:736
  433.6 117.0 %reduce-scatter.6.cloned.1.call-start = ((), (), s32[]{:S(2)}) async-start(), calls=%async_computation.7 | async-start | bytes 6553600 | tf_op jit(solution)/shard_map/reduce_scatter | solution.py:735
  433.7 24.2 %collective-permute-start.6 = (bf16[512,2560]{1,0:T(8,128)(2,1)}, bf16[512,2560]{1,0:T(8,128)(2,1)}, u32[]{:S(2)}, u32[]{:S(2)}) collective-permute-start(bf16[512,2560]{1,0:T(8,128)(2,1)} %refs_4_.1), channel_id=1, source_target_pairs={{0,1},{1,0},{2,3},{3,2},{4,5},{5,4},{6,7},{7,6},{8,9},{9,8},{10,11... | collective-permute-start | bytes 7864328 | tf_op jit(solution)/shard_map/ppermute | solution.py:736
  436.8 21.1 %collective-permute-start.7 = (bf16[512,2560]{1,0:T(8,128)(2,1)}, bf16[512,2560]{1,0:T(8,128)(2,1)}, u32[]{:S(2)}, u32[]{:S(2)}) collective-permute-start(bf16[512,2560]{1,0:T(8,128)(2,1)} %collective-permute-done.3.refs_6_), channel_id=1, source_target_pairs={{0,1},{1,0},{2,3},{3,2},{4,5},{5,4},{6,7},{7,6},{8,9},{9,8},{10,11... | collective-permute-start | bytes 7864328 | tf_op jit(solution)/shard_map/ppermute | solution.py:736
  441.6 16.3 %collective-permute-start.4 = (bf16[512,1792]{1,0:T(8,128)(2,1)}, bf16[512,1792]{1,0:T(8,128)(2,1)}, u32[]{:S(2)}, u32[]{:S(2)}) collective-permute-start(bf16[512,1792]{1,0:T(8,128)(2,1)} %get-tuple-element.85.refs_0_), channel_id=1, source_target_pairs={{0,1},{1,0},{2,3},{3,2},{4,5},{5,4},{6,7},{7,6},{8,9},{9,8},{10,11... | collective-permute-start | bytes 5505032 | tf_op jit(solution)/shard_map/ppermute | solution.py:736
  441.7 16.2 %collective-permute-start.5 = (bf16[512,1792]{1,0:T(8,128)(2,1)}, bf16[512,1792]{1,0:T(8,128)(2,1)}, u32[]{:S(2)}, u32[]{:S(2)}) collective-permute-start(bf16[512,1792]{1,0:T(8,128)(2,1)} %get-tuple-element.86.refs_2_), channel_id=1, source_target_pairs={{0,1},{1,0},{2,3},{3,2},{4,5},{5,4},{6,7},{7,6},{8,9},{9,8},{10,11... | collective-permute-start | bytes 5505032 | tf_op jit(solution)/shard_map/ppermute | solution.py:736
  489.7 122.1 %reduce-scatter.8.cloned.1.call-start = ((), (), s32[]{:S(2)}) async-start(), calls=%async_computation.8 | async-start | bytes 6553600 | tf_op jit(solution)/shard_map/reduce_scatter | solution.py:735
  553.4 158.4 %all-gather.14.cloned.1.call-start = ((), (), s32[]{:S(2)}) async-start(), calls=%async_computation.9 | async-start | bytes 23674880 | tf_op jit(solution)/shard_map/all_gather | solution.py:734
  553.7 11.5 %collective-permute-start.13 = (bf16[512,2560]{1,0:T(8,128)(2,1)}, bf16[512,2560]{1,0:T(8,128)(2,1)S(1)}, u32[]{:S(2)}, u32[]{:S(2)}) collective-permute-start(bf16[512,2560]{1,0:T(8,128)(2,1)} %get-tuple-element.76.act.refs_4_), channel_id=1, source_target_pairs={{0,1},{1,0},{2,3},{3,2},{4,5},{5,4},{6,7},{7,6},{8,9},{9,8},{10,11... | collective-permute-start | bytes 7864328 | tf_op jit(solution)/shard_map/ppermute | solution.py:736
  554.8 13.1 %collective-permute-start.12 = (bf16[512,1792]{1,0:T(8,128)(2,1)}, bf16[512,1792]{1,0:T(8,128)(2,1)}, u32[]{:S(2)}, u32[]{:S(2)}) collective-permute-start(bf16[512,1792]{1,0:T(8,128)(2,1)} %copy-done.17), channel_id=1, source_target_pairs={{0,1},{1,0},{2,3},{3,2},{4,5},{5,4},{6,7},{7,6},{8,9},{9,8},{10,11... | collective-permute-start | bytes 5505032 | tf_op jit(solution)/shard_map/ppermute | solution.py:736
  555.7 54.7 %collective-permute-start.10 = (bf16[512,1920]{1,0:T(8,128)(2,1)}, bf16[512,1920]{1,0:T(8,128)(2,1)}, u32[]{:S(2)}, u32[]{:S(2)}) collective-permute-start(bf16[512,1920]{1,0:T(8,128)(2,1)} %attend_back.1.refs_4_), channel_id=1, source_target_pairs={{0,2},{1,3},{2,0},{3,1},{4,6},{5,7},{6,4},{7,5},{8,10},{9,11},{10,... | collective-permute-start | bytes 5898248 | tf_op jit(solution)/shard_map/ppermute | solution.py:736
  617.2 132.2 %all-gather.16.cloned.1.call-start = ((), (), s32[]{:S(2)}) async-start(), calls=%async_computation.10 | async-start | bytes 3276800 | tf_op jit(solution)/shard_map/all_gather | solution.py:734
  617.9 28.9 %collective-permute-start.17 = (bf16[512,1792]{1,0:T(8,128)(2,1)S(1)}, bf16[512,1792]{1,0:T(8,128)(2,1)S(1)}, u32[]{:S(2)}, u32[]{:S(2)}) collective-permute-start(bf16[512,1792]{1,0:T(8,128)(2,1)S(1)} %copy-done.13), channel_id=1, source_target_pairs={{0,1},{1,0},{2,3},{3,2},{4,5},{5,4},{6,7},{7,6},{8,9},{9,8},{10,11... | collective-permute-start | bytes 5505032 | tf_op jit(solution)/shard_map/ppermute | solution.py:736
  617.9 30.1 %collective-permute-start.18 = (bf16[512,1792]{1,0:T(8,128)(2,1)}, bf16[512,1792]{1,0:T(8,128)(2,1)}, u32[]{:S(2)}, u32[]{:S(2)}) collective-permute-start(bf16[512,1792]{1,0:T(8,128)(2,1)} %copy-done.14), channel_id=1, source_target_pairs={{0,1},{1,0},{2,3},{3,2},{4,5},{5,4},{6,7},{7,6},{8,9},{9,8},{10,11... | collective-permute-start | bytes 5505032 | tf_op jit(solution)/shard_map/ppermute | solution.py:736
  618.4 56.7 %collective-permute-start.15 = (bf16[512,1920]{1,0:T(8,128)(2,1)}, bf16[512,1920]{1,0:T(8,128)(2,1)S(1)}, u32[]{:S(2)}, u32[]{:S(2)}) collective-permute-start(bf16[512,1920]{1,0:T(8,128)(2,1)} %attend_back.1.refs_4_), channel_id=1, source_target_pairs={{0,1},{1,0},{2,3},{3,2},{4,5},{5,4},{6,7},{7,6},{8,9},{9,8},{10,11... | collective-permute-start | bytes 5898248 | tf_op jit(solution)/shard_map/ppermute | solution.py:736
  618.4 56.7 %collective-permute-start.16 = (bf16[512,1920]{1,0:T(8,128)(2,1)}, bf16[512,1920]{1,0:T(8,128)(2,1)S(1)}, u32[]{:S(2)}, u32[]{:S(2)}) collective-permute-start(bf16[512,1920]{1,0:T(8,128)(2,1)} %collective-permute-done.10.refs_6_), channel_id=1, source_target_pairs={{0,1},{1,0},{2,3},{3,2},{4,5},{5,4},{6,7},{7,6},{8,9},{9,8},{10,11... | collective-permute-start | bytes 5898248 | tf_op jit(solution)/shard_map/ppermute | solution.py:736
  (39 other events, 223.2 us)
Sparse Core Ops, SparseCore 0:
  106.3 45.7 all-gather.9
  154.5 35.8 all-gather.7
  192.2 35.7 all-gather.17
  278.4 57.5 reduce-scatter.3
  433.8 55.8 all-gather.11
  493.1 57.5 reduce-scatter.5
  554.2 57.5 reduce-scatter.7
  617.3 94.4 all-gather.13
  713.6 35.7 all-gather.15

commit v5 on v4

--- a/solution.py
+++ b/solution.py
@@ -181,8 +181,14 @@
             c.wait()
 
 
-def embed_kernel(picked, side_f, side_i, out, slice_out, all_f, all_i, buf, r1, r2, tmp, send, recv, core_send, core_recv, out_sem, rs_send, rs_recv, side_send, side_recv, slice_sem):
+def embed_kernel(picked, side_f, side_i, out, slice_out, all_f, all_i, base, zeros, zero_sem, buf, r1, r2, tmp, send, recv, core_send, core_recv, out_sem, rs_send, rs_recv, side_send, side_recv, slice_sem):
     place = Place()
+    zeros[:] = jnp.zeros_like(zeros)
+    step = zeros.shape[0]
+
+    def blank(i):
+        return pltpu.make_async_copy(zeros, base.at[pl.ds(i * step, step), :], zero_sem.at[i])
+
     place.meet(("x", "y", "z", "core"))
     half = buf.shape[2] // 2
     near = ("y", "z")
@@ -220,7 +226,9 @@
         go(side_hop(i, 0))
         go(side_hop(i, 1))
         all_i_or_f = sides[i][1]
-        all_i_or_f[place.cp()] = sides[i][0][...]
+        all_i_or_f[place.cp()] = sides[i][0][:]
+    for i in range(base.shape[0] // step):
+        blank(i).start()
     for h in range(2):
         cols = slice(h * half, (h + 1) * half)
         first(h, 1).wait_recv()
@@ -245,11 +253,13 @@
     for i in range(2):
         side_hop(i, 1).wait_recv()
         side_hop(i, 2).wait_recv()
+    for i in range(base.shape[0] // step):
+        blank(i).wait()
     for c in started:
         c.wait_send()
 
 
-def embed_gather(picked, side_f, side_i):
+def embed_gather(picked, side_f, side_i, blank_rows, step=400):
     _, rows, dim = picked.shape
     half = dim // 2
     dma = pltpu.SemaphoreType.DMA
@@ -262,16 +272,19 @@
             jax.ShapeDtypeStruct((rows, dim), BF16),
             jax.ShapeDtypeStruct((4,) + side_f.shape, F32),
             jax.ShapeDtypeStruct((4,) + side_i.shape, I32),
+            jax.ShapeDtypeStruct((blank_rows, dim), F32),
         ],
         in_specs=[vmem, vmem, vmem],
-        out_specs=[hbm, hbm, vmem, vmem],
+        out_specs=[hbm, hbm, vmem, vmem, hbm],
         scratch_shapes=[
+            pltpu.VMEM((step, dim), F32),
+            dma((blank_rows // step,)),
             pltpu.VMEM((16, rows, dim), BF16),
             pltpu.VMEM((2, 2, rows, half), BF16),
             pltpu.VMEM((2, rows, half), BF16),
             pltpu.VMEM((2, rows, half), BF16),
             dma((21,)), dma((21,)), dma((24,)), dma((24,)), dma((16,)),
-            dma((2, 3)), dma((2, 3)), dma((2, 3)), dma((2, 3)), dma,
+            *[dma((2, 3))] * 4, dma,
         ],
         compiler_params=pltpu.CompilerParams(collective_id=0, has_side_effects=True, vmem_limit_bytes=40 * MIB),
         name="embed_gather",
@@ -294,14 +307,14 @@
     @pl.when(pl.program_id(0) == 0)
     def _():
         for i, w in enumerate((wq, wk, wv)):
-            wide[:, i * width:(i + 1) * width] = w[...]
-
-    feats = x[...].astype(F32)
+            wide[:, i * width:(i + 1) * width] = w[:]
+
+    feats = x[:].astype(F32)
     inv = lax.rsqrt(mean_row(feats * feats) + NORM_EPS)
-    a = (feats * inv * gain[...]).astype(BF16)
-    act[...] = a
-    t = nn(a, wide[...])
-    cos, sin = unpack_angles(angles[...])
+    a = (feats * inv * gain[:]).astype(BF16)
+    act[:] = a
+    t = nn(a, wide[:])
+    cos, sin = unpack_angles(angles[:])
     for i, out in enumerate((q, k, v)):
         for h in range(width // head_dim):
             th = t[:, i * width + h * head_dim:i * width + (h + 1) * head_dim]
@@ -350,7 +363,7 @@
     def score(j, peaks):
         sb = slot_block(j)
         off = pl.multiple_of(sb * blk, blk)
-        allowed = (doc_col[...] == doc_row[sb]) & (col_n + j * blk <= row_n)
+        allowed = (doc_col[:] == doc_row[sb]) & (col_n + j * blk <= row_n)
         new = []
         for h in range(heads):
             cols = slice(h * head_dim, (h + 1) * head_dim)
@@ -417,7 +430,7 @@
     mine = pl.ds(me, blk)
     iota_r = lax.broadcasted_iota(I32, (blk, blk), 0)
     iota_c = lax.broadcasted_iota(I32, (blk, blk), 1)
-    acc[...] = jnp.zeros_like(acc)
+    acc[:] = jnp.zeros_like(acc)
     spans = [slice(h * head_dim, (h + 1) * head_dim) for h in range(heads)]
 
     def for_query(j, c):
@@ -448,7 +461,7 @@
         return c
 
     lax.fori_loop(b, imax + 1, for_key, 0)
-    cos, sin = unpack_angles(angles[...])
+    cos, sin = unpack_angles(angles[:])
     for part in range(3):
         for h, cols in enumerate(spans):
             t = acc[part, :, cols]
@@ -498,13 +511,13 @@
         first, second = copies(i)
         first.wait()
         cols = pl.ds(pl.multiple_of(start, 128), na)
-        res[:, cols] = x[:, cols].astype(F32) + nn(wide[...], abuf[i])
+        res[:, cols] = x[:, cols].astype(F32) + nn(wide[:], abuf[i])
         second.wait()
         cols = pl.ds(pl.multiple_of(start + na, 128), nb)
-        res[:, cols] = x[:, cols].astype(F32) + nn(wide[...], bbuf[i])
-    h = res[...]
+        res[:, cols] = x[:, cols].astype(F32) + nn(wide[:], bbuf[i])
+    h = res[:]
     inv = lax.rsqrt(mean_row(h * h) + NORM_EPS)
-    act[...] = (h * inv * gain[...]).astype(BF16)
+    act[:] = (h * inv * gain[:]).astype(BF16)
 
 
 def out_proj(info, flip, x_all, att, pieces, gain):
@@ -527,16 +540,107 @@
     )(info, x_all, att, *pieces, gain)
 
 
+def att_kernel(att, lse, x_all, a0, b0, a1, b1, gain, parts, lse_out, res, act, x, abuf, bbuf, send, recv, lse_send, lse_recv, load):
+    place = Place()
+    rows, width = att.shape
+    na, nb = a0.shape[1], b0.shape[1]
+    mine = place.cp()
+    loads = [pltpu.make_async_copy(x_all.at[pl.ds(mine * rows, rows), :], x, load.at[4])]
+    for i, (src, dst) in enumerate(((a0, abuf.at[0]), (b0, bbuf.at[0]), (a1, abuf.at[1]), (b1, bbuf.at[1]))):
+        loads.append(pltpu.make_async_copy(src, dst, load.at[i]))
+    for c in loads:
+        c.start()
+    place.meet(("y", "z", "x", "core"))
+    started = []
+    near = ("y", "z")
+    spans = column_parts(width, 2)
+
+    def hop(p, flip, dim):
+        there = tuple(d for d in near if (d in flip) != (d == dim))
+        index = p * 3 + (there == ("y",)) + 2 * (there == ("z",))
+        start, size = spans[p]
+        cols = pl.ds(start, size)
+        slot = place.tp(flip)
+        src = parts.at[slot, :, cols] if flip else att.at[:, cols]
+        return pltpu.make_async_remote_copy(src_ref=src, dst_ref=parts.at[slot, :, cols], send_sem=send.at[index], recv_sem=recv.at[index], device_id=place.device((dim,)), device_id_type=MESH)
+
+    def lse_hop(step):
+        src, slot, dim = ((lse, mine, "x"), (lse, mine, "core"), (lse_out.at[place.cp(("x",))], place.cp(("x",)), "core"))[step]
+        return pltpu.make_async_remote_copy(src_ref=src, dst_ref=lse_out.at[slot], send_sem=lse_send.at[step], recv_sem=lse_recv.at[step], device_id=place.device((dim,)), device_id_type=MESH)
+
+    def go(copy):
+        copy.start()
+        started.append(copy)
+
+    for step in range(2):
+        for p in range(2):
+            go(hop(p, (), near[(p + step) % 2]))
+    go(lse_hop(0))
+    go(lse_hop(1))
+    lse_out[mine] = lse[:]
+    parts[place.tp()] = att[:]
+    for c in loads:
+        c.wait()
+
+    def add(slot, first=False):
+        for i in range(2):
+            start = place.coord("core", ("core",) if i else ()) * (na + nb)
+            k = pl.ds(pl.multiple_of(slot * width, width), width)
+            for buf, at, n in ((abuf, 0, na), (bbuf, na, nb)):
+                cols = pl.ds(pl.multiple_of(start + at, 128), n)
+                t = nn(parts[slot], buf[i, k, :])
+                res[:, cols] = t + (x[:, cols].astype(F32) if first else res[:, cols])
+
+    add(place.tp(), True)
+    for p in range(2):
+        hop(p, (), near[p]).wait_recv()
+        go(hop(p, (near[p],), near[1 - p]))
+    lse_hop(0).wait_recv()
+    go(lse_hop(2))
+    for p in (1, 0):
+        hop(p, (), near[1 - p]).wait_recv()
+        add(place.tp((near[1 - p],)))
+    for p in range(2):
+        hop(p, (near[p],), near[1 - p]).wait_recv()
+    add(place.tp(near))
+    h = res[:]
+    act[:] = (h * lax.rsqrt(mean_row(h * h) + NORM_EPS) * gain[:]).astype(BF16)
+    lse_hop(1).wait_recv()
+    lse_hop(2).wait_recv()
+    for c in started:
+        c.wait_send()
+
+
+def att_project(att, lse, x_all, pieces, gain):
+    rows, width = att.shape
+    dim = x_all.shape[1]
+    dma = pltpu.SemaphoreType.DMA
+    vmem = pl.BlockSpec(memory_space=pltpu.VMEM)
+    hbm = pl.BlockSpec(memory_space=pl.ANY)
+    return pl.pallas_call(
+        att_kernel,
+        out_shape=[jax.ShapeDtypeStruct((4, rows, width), BF16), jax.ShapeDtypeStruct((4,) + lse.shape, F32), jax.ShapeDtypeStruct((rows, dim), F32), jax.ShapeDtypeStruct((rows, dim), BF16)],
+        in_specs=[vmem, vmem] + [hbm] * 5 + [vmem],
+        out_specs=[vmem] * 4,
+        scratch_shapes=[
+            pltpu.VMEM((rows, dim), BF16), pltpu.VMEM((2,) + pieces[0].shape, BF16), pltpu.VMEM((2,) + pieces[1].shape, BF16),
+            *[dma((n,)) for n in (6, 6, 3, 3, 5)],
+        ],
+        compiler_params=pltpu.CompilerParams(collective_id=1, has_side_effects=True, vmem_limit_bytes=48 * MIB),
+        name="att_project",
+    )(att, lse, x_all, *pieces, gain)
+
+
 def weight_grad_kernel(info, *refs, pieces, splits):
     lhs = refs[:pieces]
     rhs = refs[pieces:2 * pieces]
     outs = refs[2 * pieces:]
-    t = tn(lhs[0][...], rhs[0][...])
+    t = tn(lhs[0][:], rhs[0][:])
     for a, b in zip(lhs[1:], rhs[1:]):
-        t += tn(a[...], b[...])
+        t += tn(a[:], b[:])
     width = t.shape[1] // splits
     for i, out in enumerate(outs):
-        out[...] = t[:, i * width:(i + 1) * width]
+        out[:] = t[:, i * width:(i + 1) * width]
 
 
 def weight_grad(info, lhs, rhs, block=256, splits=1, rows=None):
@@ -565,36 +669,36 @@
     return outs if splits > 1 else outs[0]
 
 
-def mlp_kernel(act, dhid, wg, wu, hidden, d_gate, d_up, *grad, limit):
+def mlp_kernel(act, dy, wg, wu, wd, hidden, d_gate, d_up, *grad, limit):
     i = pl.program_id(0)
     block = wg.shape[0]
     left = limit - i * block
     row_ok = lax.broadcasted_iota(I32, (block, 1), 0) < left
     col_ok = lax.broadcasted_iota(I32, (1, block), 1) < left
-    wgt = jnp.where(row_ok, wg[...], 0).astype(BF16)
-    wut = jnp.where(row_ok, wu[...], 0).astype(BF16)
-    gate = nt(act[...], wgt)
-    up = nt(act[...], wut)
-    dh = jnp.where(col_ok, dhid[...].astype(F32), 0.0)
+    wgt = jnp.where(row_ok, wg[:], 0).astype(BF16)
+    wut = jnp.where(row_ok, wu[:], 0).astype(BF16)
+    gate = nt(act[:], wgt)
+    up = nt(act[:], wut)
+    dh = jnp.where(col_ok, to_bf16(nt(dy[:], wd[:])), 0)
     sig = jax.nn.sigmoid(gate)
-    hidden[...] = (gate * sig * up).astype(BF16)
+    hidden[:] = (gate * sig * up).astype(BF16)
     dg = (dh * up * sig * (1.0 + gate * (1.0 - sig))).astype(BF16)
     du = (dh * gate * sig).astype(BF16)
-    d_gate[...] = dg
-    d_up[...] = du
+    d_gate[:] = dg
+    d_up[:] = du
     if grad:
         t = nn(dg, wgt) + nn(du, wut)
 
         @pl.when(i == 0)
         def _():
-            grad[0][...] = t
+            grad[0][:] = t
 
         @pl.when(i > 0)
         def _():
-            grad[0][...] += t
-
-
-def mlp_block(act, dhid, wg, wu, with_grad, block=256):
+            grad[0][:] += t
+
+
+def mlp_block(act, dy, wg, wu, wd, with_grad, block=256):
     rows, dim = act.shape
     limit = wg.shape[0]
     cols = pl.BlockSpec((rows, block), lambda i: (0, i))
@@ -604,42 +708,12 @@
         functools.partial(mlp_kernel, limit=limit),
         out_shape=[jax.ShapeDtypeStruct((rows, pl.cdiv(limit, block) * block), BF16)] * 3 + [jax.ShapeDtypeStruct((rows, dim), F32)] * with_grad,
         grid=(pl.cdiv(limit, block),),
-        in_specs=[whole, cols, tile, tile],
+        in_specs=[whole, whole, tile, tile, tile],
         out_specs=[cols] * 3 + [whole] * with_grad,
         compiler_params=pltpu.CompilerParams(vmem_limit_bytes=48 * MIB),
-        cost_estimate=cost((4 + 4 * with_grad) * rows * dim * limit, 4 * dim * limit + 6 * rows * limit + 10 * rows * dim),
+        cost_estimate=cost((6 + 4 * with_grad) * rows * dim * limit, 4 * dim * limit + 6 * rows * limit + 10 * rows * dim),
         name="mlp_block",
-    )(act, dhid, wg, wu)
-
-
-def zero_kernel(after, out, zeros, sem):
-    zeros[...] = jnp.zeros_like(zeros)
-    step = zeros.shape[0]
-    count = out.shape[0] // step
-
-    def send(i, c):
-        pltpu.make_async_copy(zeros, out.at[pl.ds(pl.multiple_of(i * step, step), step), :], sem).start()
-        return c
-
-    def wait(i, c):
-        pltpu.make_async_copy(zeros, out.at[pl.ds(0, step), :], sem).wait()
-        return c
-
-    lax.fori_loop(0, count, send, 0)
-    lax.fori_loop(0, count, wait, 0)
-
-
-def zero_rows(after, rows, dim, step=200):
-    return pl.pallas_call(
-        zero_kernel,
-        out_shape=jax.ShapeDtypeStruct((rows, dim), F32),
-        in_specs=[pl.BlockSpec(memory_space=pltpu.SMEM)],
-        out_specs=pl.BlockSpec(memory_space=pl.ANY),
-        scratch_shapes=[pltpu.VMEM((step, dim), F32), pltpu.SemaphoreType.DMA],
-        compiler_params=pltpu.CompilerParams(vmem_limit_bytes=8 * MIB),
-        cost_estimate=cost(rows * dim, 4 * rows * dim),
-        name="zero_rows",
-    )(after)
+    )(act, dy, wg, wu, wd)
 
 
 def scatter_kernel(order, sid, runs, bounds, rows, base_hbm, out_hbm, sums, row_sem, sum_sem):
@@ -736,7 +810,7 @@
         swap = lambda arr, pairs, axis="cp": lax.ppermute(arr, axis, pairs)
         local_ids = tokens - tp_rank * rows
         owned = (local_ids >= 0) & (local_ids < rows)
-        safe_ids = jnp.where(owned, local_ids, 0)
+        safe_ids = jnp.where(owned, local_ids, jnp.arange(span) * (rows // span))
         picked = jnp.where(owned[:, None], jnp.take(table, safe_ids, axis=0), 0).astype(BF16)
         half = dim // 2
         near = 512
@@ -745,7 +819,7 @@
         angle = pos.astype(F32)[:, None] * inv_freq[None, :]
         side_f = jnp.concatenate([jnp.cos(angle), jnp.sin(angle)], axis=1)
         side_i = jnp.concatenate([tokens[None], doc_id[None], jnp.zeros((6, span), I32)], axis=0)
-        x_all, x_slice, angles, ints = embed_gather(picked.reshape(tp_count, part, dim), side_f, side_i)
+        x_all, x_slice, angles, ints, base = embed_gather(picked.reshape(tp_count, part, dim), side_f, side_i, rows)
         angles = angles.reshape(total, head_dim)
         tok_all = ints[:, 0, :].reshape(total)
         doc_all = ints[:, 1, :].reshape(total)
@@ -765,31 +839,17 @@
         info = jnp.concatenate([cp_rank[None], core[None], docs]).astype(I32)
         attended, lse = attend(info, query, key, value, doc_col, doc_row, head_dim, blk)
 
-        att_parts = lax.all_gather(attended, "tp", axis=0, tiled=False)
-        lse_all = join(lse, "cp")
-        d_hidden = nt(dy, w_down).astype(BF16)
-        slot_ids = jnp.arange(total, dtype=I32)
-        before = (tok_all[None, :] < tok_all[:, None]) | ((tok_all[None, :] == tok_all[:, None]) & (slot_ids[None, :] < slot_ids[:, None]))
-        rank = jnp.sum(before.astype(I32), axis=1)
-        count = jnp.sum((tok_all[None, :] == tok_all[:, None]).astype(I32), axis=1)
-        at_rank = rank[None, :] == slot_ids[:, None]
-        runs = jnp.sum(jnp.where(at_rank, count[None, :], 0), axis=1)
-        order = jnp.sum(jnp.where(at_rank, slot_ids[None, :], 0), axis=1)
-        sid = jnp.sum(jnp.where(at_rank, tok_all[None, :], 0), axis=1) - tp_rank * rows
-        order = order + 8 * (order // part)
-        bounds = jnp.stack([jnp.sum((tok_all < tp_rank * rows).astype(I32)), jnp.sum((tok_all < (tp_rank + 1) * rows).astype(I32))])
-        att_parts, lse_all, d_hidden, runs, order, sid, bounds = barrier((att_parts, lse_all, d_hidden, runs, order, sid, bounds))
         gain_row = gain_b[None, :]
-        residual, act_b = out_proj(info, 0, x_all, att_parts, wo_pieces, gain_row)
+        att_parts, lse_all, residual, act_b = att_project(attended, lse, x_all, wo_pieces, gain_row)
+        lse_all = lse_all.reshape(total, 8)
         att_x = swap(att_parts, x_swap)
 
         wg, wu = w_gate.T, w_up.T
         ffn = wg.shape[0]
-        hidden, d_gate, d_up, d_act_b = mlp_block(act_b, d_hidden, wg, wu, True)
+        hidden, d_gate, d_up, d_act_b = mlp_block(act_b, dy, wg, wu, w_down, True)
         d_act_b = add_up(d_act_b)
-        dhid_x = nt(dy_x, w_down).astype(BF16)
         act_x = out_proj(info, 2, x_all, att_x, wo_pieces, gain_row)[1]
-        hidden_x, d_gate_x, d_up_x = mlp_block(act_x, dhid_x, wg, wu, False)
+        hidden_x, d_gate_x, d_up_x = mlp_block(act_x, dy_x, wg, wu, w_down, False)
         d_act_b, hidden_x, d_gate_x, d_up_x = barrier((d_act_b, hidden_x, d_gate_x, d_up_x))
         d_act_b = to_bf16(d_act_b)
         acts, dys, hiddens, d_gates, d_ups = [(a, swap(a, core_swap), b, swap(b, core_swap)) for a, b in (
@@ -840,8 +900,17 @@
         payload = jnp.concatenate([d_embed, grad_gain_a[None], grad_gain_b[None], jnp.zeros((6, dim), F32)], axis=0)
         gathered = join(payload, both)
         grad_qkv = weight_grad(info, [act_a.reshape(cp_count, span, dim)] * 4, dqkvs, splits=3)
-        base = zero_rows(barrier((bounds, d_act_a))[0], rows, dim)
-        gathered, grad_qkv, grad_gate, base = barrier((gathered, grad_qkv, grad_gate, base))
+        slot_ids = jnp.arange(total, dtype=I32)
+        before = (tok_all[None, :] < tok_all[:, None]) | ((tok_all[None, :] == tok_all[:, None]) & (slot_ids[None, :] < slot_ids[:, None]))
+        rank = jnp.sum(before.astype(I32), axis=1)
+        count = jnp.sum((tok_all[None, :] == tok_all[:, None]).astype(I32), axis=1)
+        at_rank = rank[None, :] == slot_ids[:, None]
+        runs = jnp.sum(jnp.where(at_rank, count[None, :], 0), axis=1)
+        order = jnp.sum(jnp.where(at_rank, slot_ids[None, :], 0), axis=1)
+        sid = jnp.sum(jnp.where(at_rank, tok_all[None, :], 0), axis=1) - tp_rank * rows
+        order = order + 8 * (order // part)
+        bounds = jnp.stack([jnp.sum((tok_all < tp_rank * rows).astype(I32)), jnp.sum((tok_all < (tp_rank + 1) * rows).astype(I32))])
+        gathered, grad_qkv, grad_gate, runs, order, sid, bounds = barrier((gathered, grad_qkv, grad_gate, runs, order, sid, bounds))
         out_slice = barrier((out_slice, gathered))[0]
         layer_out = join(out_slice, "tp")
         gain_grads = jnp.sum(gathered.reshape(cp_count * tp_count, part + 8, dim)[:, part:part + 2], axis=0)
@@ -849,9 +918,9 @@
         return (layer_out, grad_table, *grad_qkv, grad_out, grad_gate.T, grad_up.T, grad_down, gain_grads[0], gain_grads[1])
 
     col_spec = P(None, "tp")
-    row_spec = P("tp", None)
+    row_spec = P("tp")
     tok_spec = P("cp")
-    rep_spec = P(None)
-    in_specs = (tok_spec, tok_spec, tok_spec, P("cp", None), row_spec, col_spec, col_spec, col_spec, row_spec, col_spec, col_spec, row_spec, rep_spec, rep_spec, rep_spec)
-    out_specs = (P("cp", None), row_spec, col_spec, col_spec, col_spec, row_spec, col_spec, col_spec, row_spec, rep_spec, rep_spec)
+    rep_spec = P()
+    in_specs = (tok_spec, tok_spec, tok_spec, P("cp"), row_spec, col_spec, col_spec, col_spec, row_spec, col_spec, col_spec, row_spec, rep_spec, rep_spec, rep_spec)
+    out_specs = (P("cp"), row_spec, col_spec, col_spec, col_spec, row_spec, col_spec, col_spec, row_spec, rep_spec, rep_spec)
     return jax.shard_map(compute, mesh=mesh, in_specs=in_specs, out_specs=out_specs, check_vma=False)

time: 766 us -> 859 us (1.12)
  waiting for transfers between devices: 163 us -> 225 us
  local copies, waits for them, and re-layouts: 60.2 us -> 105 us
  matrix products: 59.1 us -> 38.9 us
  Pallas kernels: 401 us -> 420 us
  blocking collectives: 11 us -> 0 us
    all_gather x5, waiting for transfers between devices: 38.6 us -> 110 us  [compute(): join = lambda arr, axis: lax.all_gather(arr, axis, axis=0, tiled=True)]
    unnamed x73 -> x80, local copies, waits for them, and re-layouts: 25.6 us -> 81.2 us
    pallas_call x2, Pallas kernels: 46.6 us -> 76.4 us  [mlp_block(): pl.pallas_call(functools.partial(mlp_kernel, limit=limit), out_shape=[jax...]
    dot_general x5 -> x3, matrix products: 54 us -> 33.8 us  [contract(): lax.dot_general(a, b, (((ca,), (cb,)), ((), ())), preferred_element_type=...]
    pallas_call x2 -> x1, Pallas kernels: 34 us -> 17 us  [out_proj(): pl.pallas_call(out_proj_kernel, out_shape=[jax.ShapeDtypeStruct((rows, di...]
    pallas_call x1, Pallas kernels: 27.8 us -> 40.7 us  [att_project(): pl.pallas_call(att_kernel, out_shape=[jax.ShapeDtypeStruct((4, rows, widt...]
    all_gather x1 -> x0, blocking collectives: 11 us -> none  [compute(): join = lambda arr, axis: lax.all_gather(arr, axis, axis=0, tiled=True)]
  transfers between devices with their start and end apart: 28 -> 27, of which waited for: 12 -> 11; matrix products, arithmetic and copies ran while one was open for 13% -> 9% of each run, Pallas kernels for 37% -> 30%
where the time goes in v5:
time: 859 us; the launch traced here: 853 us
  Pallas kernels  420 us (49%)
  waiting for transfers between devices  225 us (26%)
  local copies, waits for them, and re-layouts  105 us (12%)
  other arithmetic  41.2 us (5%)
  matrix products  38.9 us (5%)
  between operations  15.1 us (2%)
    pallas_call x5, Pallas kernels, weight_grad(): pl.pallas_call(functools.partial(weight_grad_kernel, pieces=n, splits=spl...  129 us
    all_gather x5, waiting for transfers between devices, compute(): join = lambda arr, axis: lax.all_gather(arr, axis, axis=0, tiled=True)  110 us
    ppermute x19, waiting for transfers between devices, compute(): swap = lambda arr, pairs, axis='cp': lax.ppermute(arr, axis, pairs)  105 us
    unnamed x80, local copies, waits for them, and re-layouts  81.2 us
    pallas_call x2, Pallas kernels, mlp_block(): pl.pallas_call(functools.partial(mlp_kernel, limit=limit), out_shape=[jax...  76.4 us
    pallas_call x1, Pallas kernels, embed_gather(): pl.pallas_call(embed_kernel, out_shape=[jax.ShapeDtypeStruct((16 * rows,...  66.7 us
    pallas_call x1, Pallas kernels, att_project(): pl.pallas_call(att_kernel, out_shape=[jax.ShapeDtypeStruct((4, rows, widt...  40.7 us
    pallas_call x1, Pallas kernels, project_qkv(): pl.pallas_call(functools.partial(qkv_kernel, head_dim=head_dim), out_shap...  34.1 us
  transfers between devices with their start and end apart: 27, of which 11 were waited for; matrix products, arithmetic and copies ran while one was open for 9% of the time, Pallas kernels for 30%

profile of v5, /device:TPU:0, one launch (start us, length us, event | category | flops | bytes accessed | tf_op | source)
XLA Modules:
  0.0 853.4 jit_solution(5587914969544448249)
XLA Ops:
  12.4 8.0 gather_fusion
  23.2 66.7 %embed_gather.1 = (bf16[2048,2560]{1,0:T(8,128)(2,1)}, bf16[128,2560]{1,0:T(8,128)(2,1)S(1)}, f32[4,512,128]{2,1,0:T(8,128)S(1)}, s32[4,8,512]{2,1,0:T(8,128)S(1)}, f32[8000,2560]{1,0:T(8,128)}) custom-call(bf16[4,128,2560]{2,1,0:T(8,128)(2,1)S(1)} %select_select_fusion.picked, f32[512,128]{1,0:T(8,128)S(1)} %pad_maximum_fusion.side_f, ...), custom_call_target="tpu_custom_call" | custom-call | tf_op jit(solution)/shard_map/embed_gather/pallas_call | solution.py:268
  93.6 45.6 %all-gather.8.cloned.1.call-done.b0 = bf16[2560,768]{1,0:T(8,128)(2,1)} async-done(((bf16[640,768]{1,0:T(8,128)(2,1)}), bf16[2560,768]{1,0:T(8,128)(2,1)}) %all-gather.8.cloned.1.call-update) | async-done | bytes 3932176 | tf_op jit(solution)/shard_map/all_gather | solution.py:808
  139.3 38.2 %all-gather.6.cloned.1.call-done.a0 = bf16[2560,512]{1,0:T(8,128)(2,1)} async-done(((bf16[640,512]{1,0:T(8,128)(2,1)}), bf16[2560,512]{1,0:T(8,128)(2,1)}) %all-gather.6.cloned.1.call-update) | async-done | bytes 2621456 | tf_op jit(solution)/shard_map/all_gather | solution.py:808
  182.2 34.1 %project_qkv.1 = (bf16[2048,2560]{1,0:T(8,128)(2,1)}, bf16[2048,640]{1,0:T(8,128)(2,1)}, bf16[2048,640]{1,0:T(8,128)(2,1)}, bf16[2048,640]{1,0:T(8,128)(2,1)}, bf16[2560,1920]{1,0:T(8,128)(2,1)}) custom-call(bf16[2048,2560]{1,0:T(8,128)(2,1)} %get-tuple-element.64.x.x_all, f32[1,2560]{1,0:T(1,128)} %broadcast_in_dim.110.gain, bf16[2560,640]{1,0:T(8,128)(2,1)} %wq.1, ...), custom_call_target="tpu_custom_call" | custom-call | flops 20132659200 | bytes 38666240 | tf_op jit(solution)/shard_map/project_qkv/pallas_call | solution.py:332
  228.4 40.7 %att_project.1 = (bf16[4,512,640]{2,1,0:T(8,128)(2,1)S(1)}, f32[4,512,8]{2,1,0:T(8,128)S(1)}, f32[512,2560]{1,0:T(8,128)}, bf16[512,2560]{1,0:T(8,128)(2,1)}) custom-call(bf16[512,640]{1,0:T(8,128)(2,1)S(1)} %get-tuple-element.69.att.refs_0_, f32[512,8]{1,0:T(8,128)S(1)} %get-tuple-element.70.lse, bf16[2048,2560]{1,0:T(8,128)(2,1)} %get-tuple-element.64.x.x_all, ...), custom_call_target="tpu_custom_call" | custom-call | tf_op jit(solution)/shard_map/att_project/pallas_call | solution.py:620
  271.6 55.1 %mlp_block.2 = (bf16[512,1792]{1,0:T(8,128)(2,1)}, bf16[512,1792]{1,0:T(8,128)(2,1)S(1)}, bf16[512,1792]{1,0:T(8,128)(2,1)S(1)}, f32[512,2560]{1,0:T(8,128)}) custom-call(bf16[512,2560]{1,0:T(8,128)(2,1)} %get-tuple-element.73.act.refs_4_, bf16[512,2560]{1,0:T(8,128)(2,1)} %refs_4_.1, bf16[1728,2560]{1,0:T(8,128)(2,1)} %bitcast.60, ...), custom_call_target="tpu_custom_call" | custom-call | flops 22649241600 | bytes 36110336 | tf_op jit(solution)/shard_map/mlp_block/pallas_call | solution.py:707
  332.8 56.5 %collective-permute-done.2.att = bf16[4,512,640]{2,1,0:T(8,128)(2,1)} collective-permute-done((bf16[4,512,640]{2,1,0:T(8,128)(2,1)}, bf16[4,512,640]{2,1,0:T(8,128)(2,1)}, u32[]{:S(2)}, u32[]{:S(2)}) %collective-permute-start.2) | collective-permute-done | bytes 2621472 | tf_op jit(solution)/shard_map/ppermute | solution.py:810
  389.3 17.0 %out_proj.1 = (f32[512,2560]{1,0:T(8,128)}, bf16[512,2560]{1,0:T(8,128)(2,1)}) custom-call(s32[18]{0:T(128)} %copy-done.11, bf16[2048,2560]{1,0:T(8,128)(2,1)} %get-tuple-element.64.x.x_all, bf16[4,512,640]{2,1,0:T(8,128)(2,1)} %collective-permute-done.2.att, bf16[2560,512]{1,0:T(8,128)(2,1)} %all-gather.6.cloned.1.call-done.a0, ...), custom_call_target="tpu_custom_call" | custom-call | flops 6710886400 | bytes 26214400 | tf_op jit(solution)/shard_map/out_proj/pallas_call | solution.py:527
  406.3 37.9 %collective-permute-done.3.dy.refs_6_ = bf16[512,2560]{1,0:T(8,128)(2,1)} collective-permute-done((bf16[512,2560]{1,0:T(8,128)(2,1)}, bf16[512,2560]{1,0:T(8,128)(2,1)}, u32[]{:S(2)}, u32[]{:S(2)}) %collective-permute-start.3) | collective-permute-done | bytes 2621472 | tf_op jit(solution)/shard_map/ppermute | solution.py:810
  444.2 21.3 %mlp_block.3 = (bf16[512,1792]{1,0:T(8,128)(2,1)}, bf16[512,1792]{1,0:T(8,128)(2,1)S(1)}, bf16[512,1792]{1,0:T(8,128)(2,1)S(1)}) custom-call(bf16[512,2560]{1,0:T(8,128)(2,1)} %get-tuple-element.76.act.refs_6_, bf16[512,2560]{1,0:T(8,128)(2,1)} %collective-permute-done.3.dy.refs_6_, bf16[1728,2560]{1,0:T(8,128)(2,1)} %bitcast.61, ...), custom_call_target="tpu_custom_call" | custom-call | flops 13589544960 | bytes 36110336 | tf_op jit(solution)/shard_map/mlp_block/pallas_call | solution.py:707
  481.6 11.3 %fusion.6 = f32[512,2560]{1,0:T(8,128)} fusion(bf16[1728,2560]{1,0:T(8,128)(2,1)} %wd.3, bf16[512,1792]{1,0:T(8,128)(2,1)} %get-tuple-element.82.refs_0_), kind=kOutput, calls=%fused_computation.17 | convolution fusion | flops 4529848320 | bytes 15925248 | tf_op jit(solution)/shard_map/dot_general | solution.py:31
  494.9 27.1 %weight_grad.5 = f32[1728,2560]{1,0:T(8,128)} custom-call(s32[18]{0:T(128)} %copy-done.11, bf16[512,1792]{1,0:T(8,128)(2,1)} %get-tuple-element.82.refs_0_, bf16[512,1792]{1,0:T(8,128)(2,1)} %collective-permute-done.4.refs_1_, bf16[512,1792]{1,0:T(8,128)(2,1)} %get-tuple-element.83.refs_2_, bf16[512,1792]{1,0:T(8,128)(2,1)} %collective-permute-done.5.refs_3_, ...), custom_call_target="tpu_custom_call" | custom-call | flops 18119393280 | bytes 35258368 | tf_op jit(solution)/shard_map/weight_grad/pallas_call | solution.py:656
  529.8 11.2 %convolution_convert_fusion.do = bf16[2048,640]{1,0:T(8,128)(2,1)S(1)} fusion(bf16[2048,2560]{1,0:T(8,128)(2,1)} %all-gather.10.cloned.1.call-done, bf16[640,2560]{1,0:T(8,128)(2,1)S(1)} %copy-done), kind=kOutput, calls=%fused_computation.15 | convolution fusion | flops 6712197120 | bytes 16384000 | tf_op jit(solution)/shard_map/dot_general | solution.py:31
  549.3 20.0 %attend_back.1.refs_4_ = bf16[512,1920]{1,0:T(8,128)(2,1)} custom-call(s32[18]{0:T(128)S(1)} %copy-done.12, bf16[2048,640]{1,0:T(8,128)(2,1)} %get-tuple-element.66.q, bf16[2048,640]{1,0:T(8,128)(2,1)} %get-tuple-element.67.k, bf16[2048,640]{1,0:T(8,128)(2,1)} %get-tuple-element.68.v, bf16[2048,640]{1,0:T(8,128)(2,1)} %copy-done.28, ...), custom_call_target="tpu_custom_call" | custom-call | flops 4697620480 | bytes 15728640 | tf_op jit(solution)/shard_map/attend_back/pallas_call | solution.py:480
  569.3 11.2 %fusion.35 = f32[512,2560]{1,0:T(8,128)} fusion(bf16[512,1920]{1,0:T(8,128)(2,1)} %attend_back.1.refs_4_, bf16[2560,1920]{1,0:T(8,128)(2,1)} %get-tuple-element.87), kind=kOutput, calls=%fused_computation.94 | convolution fusion | flops 5033164800 | bytes 17039360 | tf_op jit(solution)/shard_map/dot_general | solution.py:31
  580.5 8.7 %reduce-scatter.6.cloned.1.call-done = f32[128,2560]{1,0:T(8,128)} async-done(((f32[512,2560]{1,0:T(8,128)}), f32[128,2560]{1,0:T(8,128)}) %reduce-scatter.6.cloned.1.call-update) | async-done | bytes 1310736 | tf_op jit(solution)/shard_map/reduce_scatter | solution.py:809
  606.2 27.7 %weight_grad.7 = f32[1728,2560]{1,0:T(8,128)} custom-call(s32[18]{0:T(128)} %copy-done.11, bf16[512,1792]{1,0:T(8,128)(2,1)} %copy-done.18, bf16[512,1792]{1,0:T(8,128)(2,1)} %copy-done.37, bf16[512,1792]{1,0:T(8,128)(2,1)} %copy-done.20, bf16[512,1792]{1,0:T(8,128)(2,1)} %collective-permute-done.12.refs_3_, ...), custom_call_target="tpu_custom_call" | custom-call | flops 18119393280 | bytes 35258368 | tf_op jit(solution)/shard_map/weight_grad/pallas_call | solution.py:656
  633.9 15.0 %weight_grad.6 = f32[640,2560]{1,0:T(8,128)} custom-call(s32[18]{0:T(128)} %copy-done.11, bf16[512,640]{1,0:T(8,128)(2,1)} %copy-done.4, bf16[512,640]{1,0:T(8,128)(2,1)} %collective-permute-done.8.refs_1_, bf16[512,640]{1,0:T(8,128)(2,1)} %get-tuple-element.128.refs_2_, bf16[512,640]{1,0:T(8,128)(2,1)} %collective-permute-done.9.refs_3_, ...), custom_call_target="tpu_custom_call" | custom-call | flops 6710886400 | bytes 19660800 | tf_op jit(solution)/shard_map/weight_grad/pallas_call | solution.py:656
  674.5 27.0 %weight_grad.9 = f32[1728,2560]{1,0:T(8,128)} custom-call(s32[18]{0:T(128)} %copy-done.11, bf16[512,1792]{1,0:T(8,128)(2,1)} %copy-done.15, bf16[512,1792]{1,0:T(8,128)(2,1)} %copy-done.36, bf16[512,1792]{1,0:T(8,128)(2,1)} %copy-done.17, bf16[512,1792]{1,0:T(8,128)(2,1)} %collective-permute-done.18.refs_3_, ...), custom_call_target="tpu_custom_call" | custom-call | flops 18119393280 | bytes 35258368 | tf_op jit(solution)/shard_map/weight_grad/pallas_call | solution.py:656
  703.4 31.8 %weight_grad.8 = (f32[2560,640]{1,0:T(8,128)}, f32[2560,640]{1,0:T(8,128)}, f32[2560,640]{1,0:T(8,128)}) custom-call(s32[18]{0:T(128)} %copy-done.11, bf16[4,512,2560]{2,1,0:T(8,128)(2,1)} %bitcast.66, bf16[4,512,2560]{2,1,0:T(8,128)(2,1)} %bitcast.67, bf16[4,512,2560]{2,1,0:T(8,128)(2,1)} %bitcast.68, bf16[4,512,2560]{2,1,0:T(8,128)(2,1)} %bitcast.69, ...), custom_call_target="tpu_custom_call" | custom-call | flops 20132659200 | bytes 38010880 | tf_op jit(solution)/shard_map/weight_grad/pallas_call | solution.py:656
  735.2 15.3 %all-gather.12.cloned.1.call-done.rows = f32[2176,2560]{1,0:T(8,128)} async-done(((f32[136,2560]{1,0:T(8,128)}), f32[2176,2560]{1,0:T(8,128)}) %all-gather.12.cloned.1.call-update) | async-done | bytes 22282256 | tf_op jit(solution)/shard_map/all_gather | solution.py:808
  750.6 31.1 %scatter_rows.1 = f32[8000,2560]{1,0:T(8,128)} custom-call(s32[2048]{0:T(1024)S(1)} %fusion.25.order, s32[2048]{0:T(1024)S(1)} %broadcast_subtract_fusion.sid, s32[2048]{0:T(1024)S(1)} %select_reduce_fusion.2.runs, s32[2]{0:T(128)S(1)} %pad_add_fusion.2.bounds, f32[2176,2560]{1,0:T(8,128)} %all-gather.12.cloned.1.call-done.rows, ...), custom_call_target="tpu_custom_call", output_to_operand_aliasing={{}: (5, {})} | custom-call | tf_op jit(solution)/shard_map/scatter_rows/pallas_call | solution.py:770
  791.6 54.6 %copy.61 = f32[8000,2560]{1,0:T(8,128)} copy(f32[8000,2560]{1,0:T(8,128)} %scatter_rows.1) | data formatting | bytes 163840000
  (192 shorter events, 125.3 us)
Async XLA Ops:
  7.2 132.1 %all-gather.8.cloned.1.call-start = ((), (), s32[]{:S(2)}) async-start(), calls=%async_computation.4 | async-start | bytes 4915200 | tf_op jit(solution)/shard_map/all_gather | solution.py:808
  92.4 85.0 %all-gather.6.cloned.1.call-start = ((), (), s32[]{:S(2)}) async-start(), calls=%async_computation.3 | async-start | bytes 3276800 | tf_op jit(solution)/shard_map/all_gather | solution.py:808
  93.4 374.6 %reduce-scatter.4.cloned.1.call-start = ((), (), s32[]{:S(2)}) async-start(), calls=%async_computation.5 | async-start | bytes 6553600 | tf_op jit(solution)/shard_map/reduce_scatter | solution.py:809
  139.3 89.1 %collective-permute-start.1 = (bf16[2560,768]{1,0:T(8,128)(2,1)}, bf16[2560,768]{1,0:T(8,128)(2,1)}, u32[]{:S(2)}, u32[]{:S(2)}) collective-permute-start(bf16[2560,768]{1,0:T(8,128)(2,1)} %all-gather.8.cloned.1.call-done.b0), channel_id=1, source_target_pairs={{0,1},{1,0},{2,3},{3,2},{4,5},{5,4},{6,7},{7,6},{8,9},{9,8},{10,11... | collective-permute-start | bytes 11796488 | tf_op jit(solution)/shard_map/ppermute | solution.py:810
  177.4 51.0 %collective-permute-start = (bf16[2560,512]{1,0:T(8,128)(2,1)}, bf16[2560,512]{1,0:T(8,128)(2,1)}, u32[]{:S(2)}, u32[]{:S(2)}) collective-permute-start(bf16[2560,512]{1,0:T(8,128)(2,1)} %all-gather.6.cloned.1.call-done.a0), channel_id=1, source_target_pairs={{0,1},{1,0},{2,3},{3,2},{4,5},{5,4},{6,7},{7,6},{8,9},{9,8},{10,11... | collective-permute-start | bytes 7864328 | tf_op jit(solution)/shard_map/ppermute | solution.py:810
  329.2 199.1 %all-gather.10.cloned.1.call-start = ((), (), s32[]{:S(2)}) async-start(), calls=%async_computation.6 | async-start | bytes 11141120 | tf_op jit(solution)/shard_map/all_gather | solution.py:808
  329.2 60.1 %collective-permute-start.2 = (bf16[4,512,640]{2,1,0:T(8,128)(2,1)}, bf16[4,512,640]{2,1,0:T(8,128)(2,1)}, u32[]{:S(2)}, u32[]{:S(2)}) collective-permute-start(bf16[4,512,640]{2,1,0:T(8,128)(2,1)} %copy-done.14), channel_id=1, source_target_pairs={{0,2},{1,3},{2,0},{3,1},{4,6},{5,7},{6,4},{7,5},{8,10},{9,11},{10,... | collective-permute-start | bytes 7864328 | tf_op jit(solution)/shard_map/ppermute | solution.py:810
  329.8 114.4 %collective-permute-start.3 = (bf16[512,2560]{1,0:T(8,128)(2,1)}, bf16[512,2560]{1,0:T(8,128)(2,1)}, u32[]{:S(2)}, u32[]{:S(2)}) collective-permute-start(bf16[512,2560]{1,0:T(8,128)(2,1)} %refs_4_.1), channel_id=1, source_target_pairs={{0,2},{1,3},{2,0},{3,1},{4,6},{5,7},{6,4},{7,5},{8,10},{9,11},{10,... | collective-permute-start | bytes 7864328 | tf_op jit(solution)/shard_map/ppermute | solution.py:810
  473.0 116.1 %reduce-scatter.6.cloned.1.call-start = ((), (), s32[]{:S(2)}) async-start(), calls=%async_computation.7 | async-start | bytes 6553600 | tf_op jit(solution)/shard_map/reduce_scatter | solution.py:809
  473.1 21.8 %collective-permute-start.6 = (bf16[512,2560]{1,0:T(8,128)(2,1)}, bf16[512,2560]{1,0:T(8,128)(2,1)}, u32[]{:S(2)}, u32[]{:S(2)}) collective-permute-start(bf16[512,2560]{1,0:T(8,128)(2,1)} %refs_4_.1), channel_id=1, source_target_pairs={{0,1},{1,0},{2,3},{3,2},{4,5},{5,4},{6,7},{7,6},{8,9},{9,8},{10,11... | collective-permute-start | bytes 7864328 | tf_op jit(solution)/shard_map/ppermute | solution.py:810
  473.6 21.3 %collective-permute-start.7 = (bf16[512,2560]{1,0:T(8,128)(2,1)}, bf16[512,2560]{1,0:T(8,128)(2,1)}, u32[]{:S(2)}, u32[]{:S(2)}) collective-permute-start(bf16[512,2560]{1,0:T(8,128)(2,1)} %collective-permute-done.3.dy.refs_6_), channel_id=1, source_target_pairs={{0,1},{1,0},{2,3},{3,2},{4,5},{5,4},{6,7},{7,6},{8,9},{9,8},{10,11... | collective-permute-start | bytes 7864328 | tf_op jit(solution)/shard_map/ppermute | solution.py:810
  478.3 16.7 %collective-permute-start.4 = (bf16[512,1792]{1,0:T(8,128)(2,1)}, bf16[512,1792]{1,0:T(8,128)(2,1)}, u32[]{:S(2)}, u32[]{:S(2)}) collective-permute-start(bf16[512,1792]{1,0:T(8,128)(2,1)} %get-tuple-element.82.refs_0_), channel_id=1, source_target_pairs={{0,1},{1,0},{2,3},{3,2},{4,5},{5,4},{6,7},{7,6},{8,9},{9,8},{10,11... | collective-permute-start | bytes 5505032 | tf_op jit(solution)/shard_map/ppermute | solution.py:810
  478.8 16.2 %collective-permute-start.5 = (bf16[512,1792]{1,0:T(8,128)(2,1)}, bf16[512,1792]{1,0:T(8,128)(2,1)}, u32[]{:S(2)}, u32[]{:S(2)}) collective-permute-start(bf16[512,1792]{1,0:T(8,128)(2,1)} %get-tuple-element.83.refs_2_), channel_id=1, source_target_pairs={{0,1},{1,0},{2,3},{3,2},{4,5},{5,4},{6,7},{7,6},{8,9},{9,8},{10,11... | collective-permute-start | bytes 5505032 | tf_op jit(solution)/shard_map/ppermute | solution.py:810
  481.1 11.8 %collective-permute-start.9 = (bf16[512,640]{1,0:T(8,128)(2,1)}, bf16[512,640]{1,0:T(8,128)(2,1)}, u32[]{:S(2)}, u32[]{:S(2)}) collective-permute-start(bf16[512,640]{1,0:T(8,128)(2,1)} %get-tuple-element.128.refs_2_), channel_id=1, source_target_pairs={{0,1},{1,0},{2,3},{3,2},{4,5},{5,4},{6,7},{7,6},{8,9},{9,8},{10,11... | collective-permute-start | bytes 1966088 | tf_op jit(solution)/shard_map/ppermute | solution.py:810
  528.2 122.0 %reduce-scatter.8.cloned.1.call-start = ((), (), s32[]{:S(2)}) async-start(), calls=%async_computation.8 | async-start | bytes 6553600 | tf_op jit(solution)/shard_map/reduce_scatter | solution.py:809
  591.9 158.7 %all-gather.12.cloned.1.call-start = ((), (), s32[]{:S(2)}) async-start(), calls=%async_computation.9 | async-start | bytes 23674880 | tf_op jit(solution)/shard_map/all_gather | solution.py:808
  591.9 11.5 %collective-permute-start.13 = (bf16[512,2560]{1,0:T(8,128)(2,1)}, bf16[512,2560]{1,0:T(8,128)(2,1)S(1)}, u32[]{:S(2)}, u32[]{:S(2)}) collective-permute-start(bf16[512,2560]{1,0:T(8,128)(2,1)} %get-tuple-element.73.act.refs_4_), channel_id=1, source_target_pairs={{0,1},{1,0},{2,3},{3,2},{4,5},{5,4},{6,7},{7,6},{8,9},{9,8},{10,11... | collective-permute-start | bytes 7864328 | tf_op jit(solution)/shard_map/ppermute | solution.py:810
  593.3 12.9 %collective-permute-start.12 = (bf16[512,1792]{1,0:T(8,128)(2,1)}, bf16[512,1792]{1,0:T(8,128)(2,1)}, u32[]{:S(2)}, u32[]{:S(2)}) collective-permute-start(bf16[512,1792]{1,0:T(8,128)(2,1)} %copy-done.20), channel_id=1, source_target_pairs={{0,1},{1,0},{2,3},{3,2},{4,5},{5,4},{6,7},{7,6},{8,9},{9,8},{10,11... | collective-permute-start | bytes 5505032 | tf_op jit(solution)/shard_map/ppermute | solution.py:810
  594.2 54.7 %collective-permute-start.10 = (bf16[512,1920]{1,0:T(8,128)(2,1)}, bf16[512,1920]{1,0:T(8,128)(2,1)}, u32[]{:S(2)}, u32[]{:S(2)}) collective-permute-start(bf16[512,1920]{1,0:T(8,128)(2,1)} %attend_back.1.refs_4_), channel_id=1, source_target_pairs={{0,2},{1,3},{2,0},{3,1},{4,6},{5,7},{6,4},{7,5},{8,10},{9,11},{10,... | collective-permute-start | bytes 5898248 | tf_op jit(solution)/shard_map/ppermute | solution.py:810
  655.9 132.2 %all-gather.14.cloned.1.call-start = ((), (), s32[]{:S(2)}) async-start(), calls=%async_computation.10 | async-start | bytes 3276800 | tf_op jit(solution)/shard_map/all_gather | solution.py:808
  661.3 12.0 %collective-permute-start.17 = (bf16[512,1792]{1,0:T(8,128)(2,1)S(1)}, bf16[512,1792]{1,0:T(8,128)(2,1)S(1)}, u32[]{:S(2)}, u32[]{:S(2)}) collective-permute-start(bf16[512,1792]{1,0:T(8,128)(2,1)S(1)} %copy-done.16), channel_id=1, source_target_pairs={{0,1},{1,0},{2,3},{3,2},{4,5},{5,4},{6,7},{7,6},{8,9},{9,8},{10,11... | collective-permute-start | bytes 5505032 | tf_op jit(solution)/shard_map/ppermute | solution.py:810
  661.3 13.1 %collective-permute-start.18 = (bf16[512,1792]{1,0:T(8,128)(2,1)}, bf16[512,1792]{1,0:T(8,128)(2,1)}, u32[]{:S(2)}, u32[]{:S(2)}) collective-permute-start(bf16[512,1792]{1,0:T(8,128)(2,1)} %copy-done.17), channel_id=1, source_target_pairs={{0,1},{1,0},{2,3},{3,2},{4,5},{5,4},{6,7},{7,6},{8,9},{9,8},{10,11... | collective-permute-start | bytes 5505032 | tf_op jit(solution)/shard_map/ppermute | solution.py:810
  671.3 30.2 %collective-permute-start.15 = (bf16[512,1920]{1,0:T(8,128)(2,1)}, bf16[512,1920]{1,0:T(8,128)(2,1)S(1)}, u32[]{:S(2)}, u32[]{:S(2)}) collective-permute-start(bf16[512,1920]{1,0:T(8,128)(2,1)} %attend_back.1.refs_4_), channel_id=1, source_target_pairs={{0,1},{1,0},{2,3},{3,2},{4,5},{5,4},{6,7},{7,6},{8,9},{9,8},{10,11... | collective-permute-start | bytes 5898248 | tf_op jit(solution)/shard_map/ppermute | solution.py:810
  671.4 30.1 %collective-permute-start.16 = (bf16[512,1920]{1,0:T(8,128)(2,1)}, bf16[512,1920]{1,0:T(8,128)(2,1)S(1)}, u32[]{:S(2)}, u32[]{:S(2)}) collective-permute-start(bf16[512,1920]{1,0:T(8,128)(2,1)} %collective-permute-done.10.refs_6_), channel_id=1, source_target_pairs={{0,1},{1,0},{2,3},{3,2},{4,5},{5,4},{6,7},{7,6},{8,9},{9,8},{10,11... | collective-permute-start | bytes 5898248 | tf_op jit(solution)/shard_map/ppermute | solution.py:810
  (41 other events, 591.9 us)
Sparse Core Ops, SparseCore 0:
  92.5 46.6 all-gather.7
  141.6 35.7 all-gather.5
  329.3 56.6 reduce-scatter.3
  473.1 55.0 all-gather.9
  531.6 57.5 reduce-scatter.5
  592.5 57.6 reduce-scatter.7
  656.1 94.4 all-gather.11
  752.4 35.7 all-gather.13

commit v6 on v5

--- a/solution.py
+++ b/solution.py
@@ -36,7 +36,7 @@
 
 
 def mean_row(t):
-    return jnp.mean(t, axis=-1, keepdims=True)
+    return row_sum(t) / t.shape[1]
 
 
 def whole(a):
@@ -181,14 +181,8 @@
             c.wait()
 
 
-def embed_kernel(picked, side_f, side_i, out, slice_out, all_f, all_i, base, zeros, zero_sem, buf, r1, r2, tmp, send, recv, core_send, core_recv, out_sem, rs_send, rs_recv, side_send, side_recv, slice_sem):
+def embed_kernel(picked, side_f, side_i, out, slice_out, all_f, all_i, buf, r1, r2, tmp, send, recv, core_send, core_recv, out_sem, rs_send, rs_recv, side_send, side_recv, slice_sem):
     place = Place()
-    zeros[:] = jnp.zeros_like(zeros)
-    step = zeros.shape[0]
-
-    def blank(i):
-        return pltpu.make_async_copy(zeros, base.at[pl.ds(i * step, step), :], zero_sem.at[i])
-
     place.meet(("x", "y", "z", "core"))
     half = buf.shape[2] // 2
     near = ("y", "z")
@@ -227,8 +221,6 @@
         go(side_hop(i, 1))
         all_i_or_f = sides[i][1]
         all_i_or_f[place.cp()] = sides[i][0][:]
-    for i in range(base.shape[0] // step):
-        blank(i).start()
     for h in range(2):
         cols = slice(h * half, (h + 1) * half)
         first(h, 1).wait_recv()
@@ -253,13 +245,11 @@
     for i in range(2):
         side_hop(i, 1).wait_recv()
         side_hop(i, 2).wait_recv()
-    for i in range(base.shape[0] // step):
-        blank(i).wait()
     for c in started:
         c.wait_send()
 
 
-def embed_gather(picked, side_f, side_i, blank_rows, step=400):
+def embed_gather(picked, side_f, side_i):
     _, rows, dim = picked.shape
     half = dim // 2
     dma = pltpu.SemaphoreType.DMA
@@ -272,13 +262,10 @@
             jax.ShapeDtypeStruct((rows, dim), BF16),
             jax.ShapeDtypeStruct((4,) + side_f.shape, F32),
             jax.ShapeDtypeStruct((4,) + side_i.shape, I32),
-            jax.ShapeDtypeStruct((blank_rows, dim), F32),
         ],
         in_specs=[vmem, vmem, vmem],
-        out_specs=[hbm, hbm, vmem, vmem, hbm],
+        out_specs=[hbm, hbm, vmem, vmem],
         scratch_shapes=[
-            pltpu.VMEM((step, dim), F32),
-            dma((blank_rows // step,)),
             pltpu.VMEM((16, rows, dim), BF16),
             pltpu.VMEM((2, 2, rows, half), BF16),
             pltpu.VMEM((2, rows, half), BF16),
@@ -669,16 +656,17 @@
     return outs if splits > 1 else outs[0]
 
 
-def mlp_kernel(act, dy, wg, wu, wd, hidden, d_gate, d_up, *grad, limit):
+def mlp_kernel(act, dy, wg, wu, wd, hidden, d_gate, d_up, *rest, limit):
     i = pl.program_id(0)
     block = wg.shape[0]
     left = limit - i * block
     row_ok = lax.broadcasted_iota(I32, (block, 1), 0) < left
     col_ok = lax.broadcasted_iota(I32, (1, block), 1) < left
-    wgt = jnp.where(row_ok, wg[:], 0).astype(BF16)
-    wut = jnp.where(row_ok, wu[:], 0).astype(BF16)
-    gate = nt(act[:], wgt)
-    up = nt(act[:], wut)
+    both = rest[-1]
+    both[:block] = jnp.where(row_ok, wg[:], 0).astype(BF16)
+    both[block:] = jnp.where(row_ok, wu[:], 0).astype(BF16)
+    t = nt(act[:], both[:])
+    gate, up = t[:, :block], t[:, block:]
     dh = jnp.where(col_ok, to_bf16(nt(dy[:], wd[:])), 0)
     sig = jax.nn.sigmoid(gate)
     hidden[:] = (gate * sig * up).astype(BF16)
@@ -686,16 +674,19 @@
     du = (dh * gate * sig).astype(BF16)
     d_gate[:] = dg
     d_up[:] = du
-    if grad:
-        t = nn(dg, wgt) + nn(du, wut)
+    if len(rest) > 1:
+        grad, grads = rest[:2]
+        grads[:, :block] = dg
+        grads[:, block:] = du
+        t = nn(grads[:], both[:])
 
         @pl.when(i == 0)
         def _():
-            grad[0][:] = t
+            grad[:] = t
 
         @pl.when(i > 0)
         def _():
-            grad[0][:] += t
+            grad[:] += t
 
 
 def mlp_block(act, dy, wg, wu, wd, with_grad, block=256):
@@ -710,10 +701,41 @@
         grid=(pl.cdiv(limit, block),),
         in_specs=[whole, whole, tile, tile, tile],
         out_specs=[cols] * 3 + [whole] * with_grad,
+        scratch_shapes=[pltpu.VMEM((rows, 2 * block), BF16)] * with_grad + [pltpu.VMEM((2 * block, dim), BF16)],
         compiler_params=pltpu.CompilerParams(vmem_limit_bytes=48 * MIB),
         cost_estimate=cost((6 + 4 * with_grad) * rows * dim * limit, 4 * dim * limit + 6 * rows * limit + 10 * rows * dim),
         name="mlp_block",
     )(act, dy, wg, wu, wd)
+
+
+def zero_kernel(after, out, zeros, sem):
+    zeros[:] = jnp.zeros_like(zeros)
+    step = zeros.shape[0]
+    count = out.shape[0] // step
+
+    def send(i, c):
+        pltpu.make_async_copy(zeros, out.at[pl.ds(pl.multiple_of(i * step, step), step), :], sem).start()
+        return c
+
+    def wait(i, c):
+        pltpu.make_async_copy(zeros, out.at[pl.ds(0, step), :], sem).wait()
+        return c
+
+    lax.fori_loop(0, count, send, 0)
+    lax.fori_loop(0, count, wait, 0)
+
+
+def zero_rows(after, rows, dim, step=200):
+    return pl.pallas_call(
+        zero_kernel,
+        out_shape=jax.ShapeDtypeStruct((rows, dim), F32),
+        in_specs=[pl.BlockSpec(memory_space=pltpu.SMEM)],
+        out_specs=pl.BlockSpec(memory_space=pl.ANY),
+        scratch_shapes=[pltpu.VMEM((step, dim), F32), pltpu.SemaphoreType.DMA],
+        compiler_params=pltpu.CompilerParams(vmem_limit_bytes=8 * MIB),
+        cost_estimate=cost(rows * dim, 4 * rows * dim),
+        name="zero_rows",
+    )(after)
 
 
 def scatter_kernel(order, sid, runs, bounds, rows, base_hbm, out_hbm, sums, row_sem, sum_sem):
@@ -813,13 +835,13 @@
         safe_ids = jnp.where(owned, local_ids, jnp.arange(span) * (rows // span))
         picked = jnp.where(owned[:, None], jnp.take(table, safe_ids, axis=0), 0).astype(BF16)
         half = dim // 2
-        near = 512
+        near = 256
         wo_half = lax.dynamic_slice_in_dim(w_o, core * half, half, 1)
         wo_near = join(wo_half[:, :near], "tp")
         angle = pos.astype(F32)[:, None] * inv_freq[None, :]
         side_f = jnp.concatenate([jnp.cos(angle), jnp.sin(angle)], axis=1)
-        side_i = jnp.concatenate([tokens[None], doc_id[None], jnp.zeros((6, span), I32)], axis=0)
-        x_all, x_slice, angles, ints, base = embed_gather(picked.reshape(tp_count, part, dim), side_f, side_i, rows)
+        side_i = jnp.stack([tokens, doc_id] * 4)
+        x_all, x_slice, angles, ints = embed_gather(picked.reshape(tp_count, part, dim), side_f, side_i)
         angles = angles.reshape(total, head_dim)
         tok_all = ints[:, 0, :].reshape(total)
         doc_all = ints[:, 1, :].reshape(total)
@@ -836,7 +858,7 @@
         doc_row = doc_all.reshape(blocks, 1, blk)
         docs = doc_all.reshape(blocks, blk)
         docs = jnp.stack([docs[:, 0], docs[:, -1]], axis=1).reshape(2 * blocks)
-        info = jnp.concatenate([cp_rank[None], core[None], docs]).astype(I32)
+        info = jnp.concatenate([jnp.stack([cp_rank, core]), docs]).astype(I32)
         attended, lse = attend(info, query, key, value, doc_col, doc_row, head_dim, blk)
 
         gain_row = gain_b[None, :]
@@ -897,7 +919,7 @@
         normed_a, inv_a = rms_stats(x_slice.astype(F32))
         grad_gain_a = jnp.sum(d_act_a * normed_a, axis=0)
         d_embed = d_resid + rms_back(d_act_a * gain_a, normed_a, inv_a)
-        payload = jnp.concatenate([d_embed, grad_gain_a[None], grad_gain_b[None], jnp.zeros((6, dim), F32)], axis=0)
+        payload = jnp.concatenate([d_embed, jnp.stack([grad_gain_a, grad_gain_b] * 4)])
         gathered = join(payload, both)
         grad_qkv = weight_grad(info, [act_a.reshape(cp_count, span, dim)] * 4, dqkvs, splits=3)
         slot_ids = jnp.arange(total, dtype=I32)
@@ -910,7 +932,8 @@
         sid = jnp.sum(jnp.where(at_rank, tok_all[None, :], 0), axis=1) - tp_rank * rows
         order = order + 8 * (order // part)
         bounds = jnp.stack([jnp.sum((tok_all < tp_rank * rows).astype(I32)), jnp.sum((tok_all < (tp_rank + 1) * rows).astype(I32))])
-        gathered, grad_qkv, grad_gate, runs, order, sid, bounds = barrier((gathered, grad_qkv, grad_gate, runs, order, sid, bounds))
+        base = zero_rows(barrier((bounds, d_act_a))[0], rows, dim)
+        gathered, grad_qkv, grad_gate, runs, order, sid, bounds, base = barrier((gathered, grad_qkv, grad_gate, runs, order, sid, bounds, base))
         out_slice = barrier((out_slice, gathered))[0]
         layer_out = join(out_slice, "tp")
         gain_grads = jnp.sum(gathered.reshape(cp_count * tp_count, part + 8, dim)[:, part:part + 2], axis=0)

time: 859 us -> 798 us (0.929)
  local copies, waits for them, and re-layouts: 105 us -> 54 us
  waiting for transfers between devices: 225 us -> 202 us
  Pallas kernels: 420 us -> 434 us
    unnamed x80 -> x77, local copies, waits for them, and re-layouts: 81.2 us -> 25.2 us
    pallas_call x0 -> x1, Pallas kernels: none -> 26.4 us  [zero_rows(): pl.pallas_call(zero_kernel, out_shape=jax.ShapeDtypeStruct((rows, dim), F...]
    all_gather x5, waiting for transfers between devices: 110 us -> 85.9 us  [compute(): join = lambda arr, axis: lax.all_gather(arr, axis, axis=0, tiled=True)]
    pallas_call x2, Pallas kernels: 76.4 us -> 65 us  [mlp_block(): pl.pallas_call(functools.partial(mlp_kernel, limit=limit), out_shape=[jax...]
  transfers between devices with their start and end apart: 27 -> 27, of which waited for: 11 -> 10; matrix products, arithmetic and copies ran while one was open for 9% -> 10% of each run, Pallas kernels for 30% -> 36%
where the time goes in v6:
time: 798 us; the launch traced here: 792 us
  Pallas kernels  434 us (54%)
  waiting for transfers between devices  202 us (25%)
  local copies, waits for them, and re-layouts  54 us (7%)
  other arithmetic  39.9 us (5%)
  matrix products  38.4 us (5%)
  between operations  15.1 us (2%)
  starting transfers between devices  8.42 us (1%)
    pallas_call x5, Pallas kernels, weight_grad(): pl.pallas_call(functools.partial(weight_grad_kernel, pieces=n, splits=spl...  127 us
    ppermute x19, waiting for transfers between devices, compute(): swap = lambda arr, pairs, axis='cp': lax.ppermute(arr, axis, pairs)  106 us
    all_gather x5, waiting for transfers between devices, compute(): join = lambda arr, axis: lax.all_gather(arr, axis, axis=0, tiled=True)  85.9 us
    pallas_call x1, Pallas kernels, embed_gather(): pl.pallas_call(embed_kernel, out_shape=[jax.ShapeDtypeStruct((16 * rows,...  66.8 us
    pallas_call x2, Pallas kernels, mlp_block(): pl.pallas_call(functools.partial(mlp_kernel, limit=limit), out_shape=[jax...  65 us
    pallas_call x1, Pallas kernels, att_project(): pl.pallas_call(att_kernel, out_shape=[jax.ShapeDtypeStruct((4, rows, widt...  41.7 us
    pallas_call x1, Pallas kernels, project_qkv(): pl.pallas_call(functools.partial(qkv_kernel, head_dim=head_dim), out_shap...  34.1 us
    dot_general x3, matrix products, contract(): lax.dot_general(a, b, (((ca,), (cb,)), ((), ())), preferred_element_type=...  33.4 us
  transfers between devices with their start and end apart: 27, of which 10 were waited for; matrix products, arithmetic and copies ran while one was open for 10% of the time, Pallas kernels for 36%

profile of v6, /device:TPU:0, one launch (start us, length us, event | category | flops | bytes accessed | tf_op | source)
XLA Modules:
  0.0 792.1 jit_solution(2644117023748694757)
XLA Ops:
  23.8 66.8 %embed_gather.1 = (bf16[2048,2560]{1,0:T(8,128)(2,1)}, bf16[128,2560]{1,0:T(8,128)(2,1)S(1)}, f32[4,512,128]{2,1,0:T(8,128)S(1)}, s32[4,8,512]{2,1,0:T(8,128)S(1)}) custom-call(bf16[4,128,2560]{2,1,0:T(8,128)(2,1)S(1)} %select_select_fusion.picked, f32[512,128]{1,0:T(8,128)S(1)} %pad_maximum_fusion.side_f, s32[8,512]{1,0:T(8,128)S(1)} %stack.49.side_i), custom_call_target="tpu_custom_call" | custom-call | tf_op jit(solution)/shard_map/embed_gather/pallas_call | solution.py:258
  93.1 57.6 %all-gather.8.cloned.1.call-done.b0 = bf16[2560,1024]{1,0:T(8,128)(2,1)} async-done(((bf16[640,1024]{1,0:T(8,128)(2,1)}), bf16[2560,1024]{1,0:T(8,128)(2,1)}) %all-gather.8.cloned.1.call-update) | async-done | bytes 5242896 | tf_op jit(solution)/shard_map/all_gather | solution.py:830
  157.9 20.2 %all-gather.6.cloned.1.call-done.a0 = bf16[2560,256]{1,0:T(8,128)(2,1)} async-done(((bf16[640,256]{1,0:T(8,128)(2,1)}), bf16[2560,256]{1,0:T(8,128)(2,1)}) %all-gather.6.cloned.1.call-update) | async-done | bytes 1310736 | tf_op jit(solution)/shard_map/all_gather | solution.py:830
  178.0 34.1 %project_qkv.1 = (bf16[2048,2560]{1,0:T(8,128)(2,1)}, bf16[2048,640]{1,0:T(8,128)(2,1)}, bf16[2048,640]{1,0:T(8,128)(2,1)}, bf16[2048,640]{1,0:T(8,128)(2,1)}, bf16[2560,1920]{1,0:T(8,128)(2,1)}) custom-call(bf16[2048,2560]{1,0:T(8,128)(2,1)} %get-tuple-element.65.x.x_all, f32[1,2560]{1,0:T(1,128)} %broadcast_in_dim.81.gain, bf16[2560,640]{1,0:T(8,128)(2,1)} %wq.1, ...), custom_call_target="tpu_custom_call" | custom-call | flops 20132659200 | bytes 38666240 | tf_op jit(solution)/shard_map/project_qkv/pallas_call | solution.py:319
  224.0 41.7 %att_project.1 = (bf16[4,512,640]{2,1,0:T(8,128)(2,1)}, f32[4,512,8]{2,1,0:T(8,128)S(1)}, f32[512,2560]{1,0:T(8,128)}, bf16[512,2560]{1,0:T(8,128)(2,1)}) custom-call(bf16[512,640]{1,0:T(8,128)(2,1)S(1)} %get-tuple-element.70.att.refs_0_, f32[512,8]{1,0:T(8,128)S(1)} %get-tuple-element.71.lse, bf16[2048,2560]{1,0:T(8,128)(2,1)} %get-tuple-element.65.x.x_all, ...), custom_call_target="tpu_custom_call" | custom-call | tf_op jit(solution)/shard_map/att_project/pallas_call | solution.py:607
  266.8 43.9 %mlp_block.2 = (bf16[512,1792]{1,0:T(8,128)(2,1)}, bf16[512,1792]{1,0:T(8,128)(2,1)S(1)}, bf16[512,1792]{1,0:T(8,128)(2,1)S(1)}, f32[512,2560]{1,0:T(8,128)}) custom-call(bf16[512,2560]{1,0:T(8,128)(2,1)} %get-tuple-element.74.act.refs_4_, bf16[512,2560]{1,0:T(8,128)(2,1)} %refs_4_.1, bf16[1728,2560]{1,0:T(8,128)(2,1)} %bitcast.66, ...), custom_call_target="tpu_custom_call" | custom-call | flops 22649241600 | bytes 36110336 | tf_op jit(solution)/shard_map/mlp_block/pallas_call | solution.py:698
  316.8 56.5 %collective-permute-done.2.att = bf16[4,512,640]{2,1,0:T(8,128)(2,1)} collective-permute-done((bf16[4,512,640]{2,1,0:T(8,128)(2,1)}, bf16[4,512,640]{2,1,0:T(8,128)(2,1)}, u32[]{:S(2)}, u32[]{:S(2)}) %collective-permute-start.2) | collective-permute-done | bytes 2621472 | tf_op jit(solution)/shard_map/ppermute | solution.py:832
  373.4 16.6 %out_proj.1 = (f32[512,2560]{1,0:T(8,128)}, bf16[512,2560]{1,0:T(8,128)(2,1)}) custom-call(s32[18]{0:T(128)} %copy-done.12, bf16[2048,2560]{1,0:T(8,128)(2,1)} %get-tuple-element.65.x.x_all, bf16[4,512,640]{2,1,0:T(8,128)(2,1)} %collective-permute-done.2.att, bf16[2560,256]{1,0:T(8,128)(2,1)} %all-gather.6.cloned.1.call-done.a0, ...), custom_call_target="tpu_custom_call" | custom-call | flops 6710886400 | bytes 26214400 | tf_op jit(solution)/shard_map/out_proj/pallas_call | solution.py:514
  390.0 38.2 %collective-permute-done.3.dy.refs_6_ = bf16[512,2560]{1,0:T(8,128)(2,1)} collective-permute-done((bf16[512,2560]{1,0:T(8,128)(2,1)}, bf16[512,2560]{1,0:T(8,128)(2,1)}, u32[]{:S(2)}, u32[]{:S(2)}) %collective-permute-start.3) | collective-permute-done | bytes 2621472 | tf_op jit(solution)/shard_map/ppermute | solution.py:832
  428.2 21.2 %mlp_block.3 = (bf16[512,1792]{1,0:T(8,128)(2,1)}, bf16[512,1792]{1,0:T(8,128)(2,1)S(1)}, bf16[512,1792]{1,0:T(8,128)(2,1)S(1)}) custom-call(bf16[512,2560]{1,0:T(8,128)(2,1)} %get-tuple-element.77.act.refs_6_, bf16[512,2560]{1,0:T(8,128)(2,1)} %collective-permute-done.3.dy.refs_6_, bf16[1728,2560]{1,0:T(8,128)(2,1)} %bitcast.67, ...), custom_call_target="tpu_custom_call" | custom-call | flops 13589544960 | bytes 36110336 | tf_op jit(solution)/shard_map/mlp_block/pallas_call | solution.py:698
  465.7 11.3 %fusion.6 = f32[512,2560]{1,0:T(8,128)} fusion(bf16[1728,2560]{1,0:T(8,128)(2,1)} %wd.3, bf16[512,1792]{1,0:T(8,128)(2,1)} %get-tuple-element.83.refs_0_), kind=kOutput, calls=%fused_computation.17 | convolution fusion | flops 4529848320 | bytes 15925248 | tf_op jit(solution)/shard_map/dot_general | solution.py:31
  479.0 27.1 %weight_grad.5 = f32[1728,2560]{1,0:T(8,128)} custom-call(s32[18]{0:T(128)} %copy-done.12, bf16[512,1792]{1,0:T(8,128)(2,1)} %get-tuple-element.83.refs_0_, bf16[512,1792]{1,0:T(8,128)(2,1)} %collective-permute-done.4.refs_1_, bf16[512,1792]{1,0:T(8,128)(2,1)} %get-tuple-element.84.refs_2_, bf16[512,1792]{1,0:T(8,128)(2,1)} %collective-permute-done.5.refs_3_, ...), custom_call_target="tpu_custom_call" | custom-call | flops 18119393280 | bytes 35258368 | tf_op jit(solution)/shard_map/weight_grad/pallas_call | solution.py:643
  513.7 11.0 %convolution_convert_fusion.do = bf16[2048,640]{1,0:T(8,128)(2,1)S(1)} fusion(bf16[2048,2560]{1,0:T(8,128)(2,1)} %all-gather.10.cloned.1.call-done, bf16[640,2560]{1,0:T(8,128)(2,1)S(1)} %copy-done), kind=kOutput, calls=%fused_computation.15 | convolution fusion | flops 6712197120 | bytes 16384000 | tf_op jit(solution)/shard_map/dot_general | solution.py:31
  532.9 20.0 %attend_back.1.refs_4_ = bf16[512,1920]{1,0:T(8,128)(2,1)} custom-call(s32[18]{0:T(128)S(1)} %copy-done.13, bf16[2048,640]{1,0:T(8,128)(2,1)} %get-tuple-element.67.q, bf16[2048,640]{1,0:T(8,128)(2,1)} %get-tuple-element.68.k, bf16[2048,640]{1,0:T(8,128)(2,1)} %get-tuple-element.69.v, bf16[2048,640]{1,0:T(8,128)(2,1)} %copy-done.28, ...), custom_call_target="tpu_custom_call" | custom-call | flops 4697620480 | bytes 15728640 | tf_op jit(solution)/shard_map/attend_back/pallas_call | solution.py:467
  552.9 11.0 %fusion.36 = f32[512,2560]{1,0:T(8,128)} fusion(bf16[512,1920]{1,0:T(8,128)(2,1)} %attend_back.1.refs_4_, bf16[2560,1920]{1,0:T(8,128)(2,1)} %get-tuple-element.88), kind=kOutput, calls=%fused_computation.91 | convolution fusion | flops 5033164800 | bytes 17039360 | tf_op jit(solution)/shard_map/dot_general | solution.py:31
  563.9 9.1 %reduce-scatter.6.cloned.1.call-done = f32[128,2560]{1,0:T(8,128)} async-done(((f32[512,2560]{1,0:T(8,128)}), f32[128,2560]{1,0:T(8,128)}) %reduce-scatter.6.cloned.1.call-update) | async-done | bytes 1310736 | tf_op jit(solution)/shard_map/reduce_scatter | solution.py:831
  579.5 8.1 %collective-permute-done.11.refs_1_ = bf16[512,1792]{1,0:T(8,128)(2,1)S(1)} collective-permute-done((bf16[512,1792]{1,0:T(8,128)(2,1)S(1)}, bf16[512,1792]{1,0:T(8,128)(2,1)S(1)}, u32[]{:S(2)}, u32[]{:S(2)}) %collective-permute-start.11) | collective-permute-done | bytes 1835040 | tf_op jit(solution)/shard_map/ppermute | solution.py:832
  590.3 27.4 %weight_grad.7 = f32[1728,2560]{1,0:T(8,128)} custom-call(s32[18]{0:T(128)} %copy-done.12, bf16[512,1792]{1,0:T(8,128)(2,1)} %copy-done.18, bf16[512,1792]{1,0:T(8,128)(2,1)} %copy-done.36, bf16[512,1792]{1,0:T(8,128)(2,1)} %copy-done.20, bf16[512,1792]{1,0:T(8,128)(2,1)} %collective-permute-done.12.refs_3_, ...), custom_call_target="tpu_custom_call" | custom-call | flops 18119393280 | bytes 35258368 | tf_op jit(solution)/shard_map/weight_grad/pallas_call | solution.py:643
  617.7 15.0 %weight_grad.6 = f32[640,2560]{1,0:T(8,128)} custom-call(s32[18]{0:T(128)} %copy-done.12, bf16[512,640]{1,0:T(8,128)(2,1)} %copy-done.4, bf16[512,640]{1,0:T(8,128)(2,1)} %collective-permute-done.8.refs_1_, bf16[512,640]{1,0:T(8,128)(2,1)} %get-tuple-element.131.refs_2_, bf16[512,640]{1,0:T(8,128)(2,1)} %collective-permute-done.9.refs_3_, ...), custom_call_target="tpu_custom_call" | custom-call | flops 6710886400 | bytes 19660800 | tf_op jit(solution)/shard_map/weight_grad/pallas_call | solution.py:643
  647.4 7.8 select_reduce_fusion
  658.8 26.4 %zero_rows.1.base_hbm = f32[8000,2560]{1,0:T(8,128)} custom-call(s32[2]{0:T(128)S(1)} %pad_add_fusion.2.after.bounds), custom_call_target="tpu_custom_call" | custom-call | flops 20480000 | bytes 81920000 | tf_op jit(solution)/shard_map/zero_rows/pallas_call | solution.py:729
  686.5 27.6 %weight_grad.9 = f32[1728,2560]{1,0:T(8,128)} custom-call(s32[18]{0:T(128)} %copy-done.12, bf16[512,1792]{1,0:T(8,128)(2,1)} %copy-done.15, bf16[512,1792]{1,0:T(8,128)(2,1)} %copy-done.35, bf16[512,1792]{1,0:T(8,128)(2,1)} %copy-done.17, bf16[512,1792]{1,0:T(8,128)(2,1)} %collective-permute-done.18.refs_3_, ...), custom_call_target="tpu_custom_call" | custom-call | flops 18119393280 | bytes 35258368 | tf_op jit(solution)/shard_map/weight_grad/pallas_call | solution.py:643
  716.0 29.8 %weight_grad.8 = (f32[2560,640]{1,0:T(8,128)}, f32[2560,640]{1,0:T(8,128)}, f32[2560,640]{1,0:T(8,128)}) custom-call(s32[18]{0:T(128)} %copy-done.12, bf16[4,512,2560]{2,1,0:T(8,128)(2,1)} %bitcast.72, bf16[4,512,2560]{2,1,0:T(8,128)(2,1)} %bitcast.73, bf16[4,512,2560]{2,1,0:T(8,128)(2,1)} %bitcast.74, bf16[4,512,2560]{2,1,0:T(8,128)(2,1)} %bitcast.75, ...), custom_call_target="tpu_custom_call" | custom-call | flops 20132659200 | bytes 38010880 | tf_op jit(solution)/shard_map/weight_grad/pallas_call | solution.py:643
  745.8 31.3 %scatter_rows.1 = f32[8000,2560]{1,0:T(8,128)} custom-call(s32[2048]{0:T(1024)S(1)} %fusion.26.order, s32[2048]{0:T(1024)S(1)} %broadcast_subtract_fusion.sid, s32[2048]{0:T(1024)S(1)} %select_reduce_fusion.2.runs, s32[2]{0:T(128)S(1)} %pad_add_fusion.2.after.bounds, ...), custom_call_target="tpu_custom_call", output_to_operand_aliasing={{}: (5, {})} | custom-call | tf_op jit(solution)/shard_map/scatter_rows/pallas_call | solution.py:792
  (186 shorter events, 117.4 us)
Async XLA Ops:
  7.2 143.5 %all-gather.8.cloned.1.call-start = ((), (), s32[]{:S(2)}) async-start(), calls=%async_computation.4 | async-start | bytes 6553600 | tf_op jit(solution)/shard_map/all_gather | solution.py:830
  93.1 84.9 %all-gather.6.cloned.1.call-start = ((), (), s32[]{:S(2)}) async-start(), calls=%async_computation.3 | async-start | bytes 1638400 | tf_op jit(solution)/shard_map/all_gather | solution.py:830
  150.7 73.3 %collective-permute-start.1 = (bf16[2560,1024]{1,0:T(8,128)(2,1)}, bf16[2560,1024]{1,0:T(8,128)(2,1)}, u32[]{:S(2)}, u32[]{:S(2)}) collective-permute-start(bf16[2560,1024]{1,0:T(8,128)(2,1)} %all-gather.8.cloned.1.call-done.b0), channel_id=1, source_target_pairs={{0,1},{1,0},{2,3},{3,2},{4,5},{5,4},{6,7},{7,6},{8,9},{9,8},{10,11... | collective-permute-start | bytes 15728648 | tf_op jit(solution)/shard_map/ppermute | solution.py:832
  151.5 300.4 %reduce-scatter.4.cloned.1.call-start = ((), (), s32[]{:S(2)}) async-start(), calls=%async_computation.5 | async-start | bytes 6553600 | tf_op jit(solution)/shard_map/reduce_scatter | solution.py:831
  178.0 46.0 %collective-permute-start = (bf16[2560,256]{1,0:T(8,128)(2,1)}, bf16[2560,256]{1,0:T(8,128)(2,1)}, u32[]{:S(2)}, u32[]{:S(2)}) collective-permute-start(bf16[2560,256]{1,0:T(8,128)(2,1)} %all-gather.6.cloned.1.call-done.a0), channel_id=1, source_target_pairs={{0,1},{1,0},{2,3},{3,2},{4,5},{5,4},{6,7},{7,6},{8,9},{9,8},{10,11... | collective-permute-start | bytes 3932168 | tf_op jit(solution)/shard_map/ppermute | solution.py:832
  313.2 198.8 %all-gather.10.cloned.1.call-start = ((), (), s32[]{:S(2)}) async-start(), calls=%async_computation.6 | async-start | bytes 11141120 | tf_op jit(solution)/shard_map/all_gather | solution.py:830
  313.3 60.1 %collective-permute-start.2 = (bf16[4,512,640]{2,1,0:T(8,128)(2,1)}, bf16[4,512,640]{2,1,0:T(8,128)(2,1)}, u32[]{:S(2)}, u32[]{:S(2)}) collective-permute-start(bf16[4,512,640]{2,1,0:T(8,128)(2,1)} %get-tuple-element.76), channel_id=1, source_target_pairs={{0,2},{1,3},{2,0},{3,1},{4,6},{5,7},{6,4},{7,5},{8,10},{9,11},{10,... | collective-permute-start | bytes 7864328 | tf_op jit(solution)/shard_map/ppermute | solution.py:832
  313.9 114.3 %collective-permute-start.3 = (bf16[512,2560]{1,0:T(8,128)(2,1)}, bf16[512,2560]{1,0:T(8,128)(2,1)}, u32[]{:S(2)}, u32[]{:S(2)}) collective-permute-start(bf16[512,2560]{1,0:T(8,128)(2,1)} %refs_4_.1), channel_id=1, source_target_pairs={{0,2},{1,3},{2,0},{3,1},{4,6},{5,7},{6,4},{7,5},{8,10},{9,11},{10,... | collective-permute-start | bytes 7864328 | tf_op jit(solution)/shard_map/ppermute | solution.py:832
  456.9 116.1 %reduce-scatter.6.cloned.1.call-start = ((), (), s32[]{:S(2)}) async-start(), calls=%async_computation.7 | async-start | bytes 6553600 | tf_op jit(solution)/shard_map/reduce_scatter | solution.py:831
  457.2 21.8 %collective-permute-start.6 = (bf16[512,2560]{1,0:T(8,128)(2,1)}, bf16[512,2560]{1,0:T(8,128)(2,1)}, u32[]{:S(2)}, u32[]{:S(2)}) collective-permute-start(bf16[512,2560]{1,0:T(8,128)(2,1)} %refs_4_.1), channel_id=1, source_target_pairs={{0,1},{1,0},{2,3},{3,2},{4,5},{5,4},{6,7},{7,6},{8,9},{9,8},{10,11... | collective-permute-start | bytes 7864328 | tf_op jit(solution)/shard_map/ppermute | solution.py:832
  457.7 21.3 %collective-permute-start.7 = (bf16[512,2560]{1,0:T(8,128)(2,1)}, bf16[512,2560]{1,0:T(8,128)(2,1)}, u32[]{:S(2)}, u32[]{:S(2)}) collective-permute-start(bf16[512,2560]{1,0:T(8,128)(2,1)} %collective-permute-done.3.dy.refs_6_), channel_id=1, source_target_pairs={{0,1},{1,0},{2,3},{3,2},{4,5},{5,4},{6,7},{7,6},{8,9},{9,8},{10,11... | collective-permute-start | bytes 7864328 | tf_op jit(solution)/shard_map/ppermute | solution.py:832
  462.3 16.6 %collective-permute-start.4 = (bf16[512,1792]{1,0:T(8,128)(2,1)}, bf16[512,1792]{1,0:T(8,128)(2,1)}, u32[]{:S(2)}, u32[]{:S(2)}) collective-permute-start(bf16[512,1792]{1,0:T(8,128)(2,1)} %get-tuple-element.83.refs_0_), channel_id=1, source_target_pairs={{0,1},{1,0},{2,3},{3,2},{4,5},{5,4},{6,7},{7,6},{8,9},{9,8},{10,11... | collective-permute-start | bytes 5505032 | tf_op jit(solution)/shard_map/ppermute | solution.py:832
  462.8 16.2 %collective-permute-start.5 = (bf16[512,1792]{1,0:T(8,128)(2,1)}, bf16[512,1792]{1,0:T(8,128)(2,1)}, u32[]{:S(2)}, u32[]{:S(2)}) collective-permute-start(bf16[512,1792]{1,0:T(8,128)(2,1)} %get-tuple-element.84.refs_2_), channel_id=1, source_target_pairs={{0,1},{1,0},{2,3},{3,2},{4,5},{5,4},{6,7},{7,6},{8,9},{9,8},{10,11... | collective-permute-start | bytes 5505032 | tf_op jit(solution)/shard_map/ppermute | solution.py:832
  465.2 11.8 %collective-permute-start.9 = (bf16[512,640]{1,0:T(8,128)(2,1)}, bf16[512,640]{1,0:T(8,128)(2,1)}, u32[]{:S(2)}, u32[]{:S(2)}) collective-permute-start(bf16[512,640]{1,0:T(8,128)(2,1)} %get-tuple-element.131.refs_2_), channel_id=1, source_target_pairs={{0,1},{1,0},{2,3},{3,2},{4,5},{5,4},{6,7},{7,6},{8,9},{9,8},{10,11... | collective-permute-start | bytes 1966088 | tf_op jit(solution)/shard_map/ppermute | solution.py:832
  512.1 121.9 %reduce-scatter.8.cloned.1.call-start = ((), (), s32[]{:S(2)}) async-start(), calls=%async_computation.8 | async-start | bytes 6553600 | tf_op jit(solution)/shard_map/reduce_scatter | solution.py:831
  575.7 170.1 %all-gather.12.cloned.1.call-start = ((), (), s32[]{:S(2)}) async-start(), calls=%async_computation.9 | async-start | bytes 23674880 | tf_op jit(solution)/shard_map/all_gather | solution.py:830
  576.0 11.5 %collective-permute-start.13 = (bf16[512,2560]{1,0:T(8,128)(2,1)}, bf16[512,2560]{1,0:T(8,128)(2,1)S(1)}, u32[]{:S(2)}, u32[]{:S(2)}) collective-permute-start(bf16[512,2560]{1,0:T(8,128)(2,1)} %get-tuple-element.74.act.refs_4_), channel_id=1, source_target_pairs={{0,1},{1,0},{2,3},{3,2},{4,5},{5,4},{6,7},{7,6},{8,9},{9,8},{10,11... | collective-permute-start | bytes 7864328 | tf_op jit(solution)/shard_map/ppermute | solution.py:832
  577.2 13.1 %collective-permute-start.12 = (bf16[512,1792]{1,0:T(8,128)(2,1)}, bf16[512,1792]{1,0:T(8,128)(2,1)}, u32[]{:S(2)}, u32[]{:S(2)}) collective-permute-start(bf16[512,1792]{1,0:T(8,128)(2,1)} %copy-done.20), channel_id=1, source_target_pairs={{0,1},{1,0},{2,3},{3,2},{4,5},{5,4},{6,7},{7,6},{8,9},{9,8},{10,11... | collective-permute-start | bytes 5505032 | tf_op jit(solution)/shard_map/ppermute | solution.py:832
  577.9 54.7 %collective-permute-start.10 = (bf16[512,1920]{1,0:T(8,128)(2,1)}, bf16[512,1920]{1,0:T(8,128)(2,1)}, u32[]{:S(2)}, u32[]{:S(2)}) collective-permute-start(bf16[512,1920]{1,0:T(8,128)(2,1)} %attend_back.1.refs_4_), channel_id=1, source_target_pairs={{0,2},{1,3},{2,0},{3,1},{4,6},{5,7},{6,4},{7,5},{8,10},{9,11},{10,... | collective-permute-start | bytes 5898248 | tf_op jit(solution)/shard_map/ppermute | solution.py:832
  641.2 140.1 %all-gather.14.cloned.1.call-start = ((), (), s32[]{:S(2)}) async-start(), calls=%async_computation.10 | async-start | bytes 3276800 | tf_op jit(solution)/shard_map/all_gather | solution.py:830
  646.8 38.4 %collective-permute-start.17 = (bf16[512,1792]{1,0:T(8,128)(2,1)S(1)}, bf16[512,1792]{1,0:T(8,128)(2,1)S(1)}, u32[]{:S(2)}, u32[]{:S(2)}) collective-permute-start(bf16[512,1792]{1,0:T(8,128)(2,1)S(1)} %copy-done.16), channel_id=1, source_target_pairs={{0,1},{1,0},{2,3},{3,2},{4,5},{5,4},{6,7},{7,6},{8,9},{9,8},{10,11... | collective-permute-start | bytes 5505032 | tf_op jit(solution)/shard_map/ppermute | solution.py:832
  646.9 39.6 %collective-permute-start.18 = (bf16[512,1792]{1,0:T(8,128)(2,1)}, bf16[512,1792]{1,0:T(8,128)(2,1)}, u32[]{:S(2)}, u32[]{:S(2)}) collective-permute-start(bf16[512,1792]{1,0:T(8,128)(2,1)} %copy-done.17), channel_id=1, source_target_pairs={{0,1},{1,0},{2,3},{3,2},{4,5},{5,4},{6,7},{7,6},{8,9},{9,8},{10,11... | collective-permute-start | bytes 5505032 | tf_op jit(solution)/shard_map/ppermute | solution.py:832
  656.9 57.2 %collective-permute-start.15 = (bf16[512,1920]{1,0:T(8,128)(2,1)}, bf16[512,1920]{1,0:T(8,128)(2,1)S(1)}, u32[]{:S(2)}, u32[]{:S(2)}) collective-permute-start(bf16[512,1920]{1,0:T(8,128)(2,1)} %attend_back.1.refs_4_), channel_id=1, source_target_pairs={{0,1},{1,0},{2,3},{3,2},{4,5},{5,4},{6,7},{7,6},{8,9},{9,8},{10,11... | collective-permute-start | bytes 5898248 | tf_op jit(solution)/shard_map/ppermute | solution.py:832
  657.0 57.1 %collective-permute-start.16 = (bf16[512,1920]{1,0:T(8,128)(2,1)}, bf16[512,1920]{1,0:T(8,128)(2,1)S(1)}, u32[]{:S(2)}, u32[]{:S(2)}) collective-permute-start(bf16[512,1920]{1,0:T(8,128)(2,1)} %collective-permute-done.10.refs_6_), channel_id=1, source_target_pairs={{0,1},{1,0},{2,3},{3,2},{4,5},{5,4},{6,7},{7,6},{8,9},{9,8},{10,11... | collective-permute-start | bytes 5898248 | tf_op jit(solution)/shard_map/ppermute | solution.py:832
  (40 other events, 277.7 us)
Sparse Core Ops, SparseCore 0:
  93.2 57.4 all-gather.7
  153.1 24.9 all-gather.5
  313.3 56.6 reduce-scatter.3
  457.0 54.9 all-gather.9
  515.4 57.5 reduce-scatter.5
  576.4 57.5 reduce-scatter.7
  641.4 94.4 all-gather.11
  746.0 35.3 all-gather.13

commit v7 on v6

--- a/solution.py
+++ b/solution.py
@@ -328,22 +328,26 @@
     )(x_all, gain, wq, wk, wv, angles)
 
 
-def block_range(info, i, blocks):
+def block_range(info, ids, i, blocks):
     r = info[0]
+    blk = ids.shape[2] // 2
     b = jnp.where(i == 0, r, blocks - 1 - r)
-    mine = 2 + 2 * (2 * r + i)
-    jmin = 0
-    imax = -1
+
+    def docs(shard, half):
+        return ids[shard, 1, half * blk], ids[shard, 1, half * blk + blk - 1]
+
+    first, last = docs(r, i)
+    jmin, imax = 0, -1
     for j in range(blocks):
-        there = 2 + 2 * (2 * j if j < blocks // 2 else 2 * blocks - 1 - 2 * j)
-        jmin = jmin + (info[there + 1] < info[mine]).astype(I32)
-        imax = imax + (info[there] <= info[mine + 1]).astype(I32)
+        begin, end = docs(min(j, blocks - 1 - j), int(j >= blocks // 2))
+        jmin = jmin + (end < first).astype(I32)
+        imax = imax + (begin <= last).astype(I32)
     return b, jmin, imax
 
 
-def attend_kernel(info, q, k, v, doc_col, doc_row, out, lse, sc, *, heads, head_dim, scale):
+def attend_kernel(info, ids, q, k, v, doc_col, doc_row, out, lse, sc, *, heads, head_dim, scale):
     blk = q.shape[0]
-    b, jmin, _ = block_range(info, pl.program_id(0), doc_row.shape[0])
+    b, jmin, _ = block_range(info, ids, pl.program_id(0), doc_row.shape[0])
     row_n = lax.broadcasted_iota(I32, (blk, blk), 0) + b * blk
     col_n = lax.broadcasted_iota(I32, (blk, blk), 1)
 
@@ -388,31 +392,31 @@
         out[:, h * head_dim:(h + 1) * head_dim] = acc[h].astype(BF16)
 
 
-def attend(info, q, k, v, doc_col, doc_row, head_dim, blk):
+def attend(info, ids, q, k, v, doc_col, doc_row, head_dim, blk):
     total, width = k.shape
     heads = width // head_dim
-    mine = lambda n: pl.BlockSpec((blk, n), lambda i, info: (2 * info[0] + i, 0))
+    mine = lambda n: pl.BlockSpec((blk, n), lambda i, info, ids: (2 * info[0] + i, 0))
     return pl.pallas_call(
         functools.partial(attend_kernel, heads=heads, head_dim=head_dim, scale=head_dim ** -0.5),
         out_shape=[jax.ShapeDtypeStruct((2 * blk, width), BF16), jax.ShapeDtypeStruct((2 * blk, 8), F32)],
         grid_spec=pltpu.PrefetchScalarGridSpec(
-            num_scalar_prefetch=1,
+            num_scalar_prefetch=2,
             grid=(2,),
             in_specs=[mine(width), whole(k), whole(v), mine(1), whole(doc_row)],
-            out_specs=[pl.BlockSpec((blk, width), lambda i, info: (i, 0)), pl.BlockSpec((blk, 8), lambda i, info: (i, 0))],
+            out_specs=[pl.BlockSpec((blk, width), lambda i, info, ids: (i, 0)), pl.BlockSpec((blk, 8), lambda i, info, ids: (i, 0))],
             scratch_shapes=[pltpu.VMEM((total // blk, heads, blk, blk), F32)],
         ),
         compiler_params=pltpu.CompilerParams(vmem_limit_bytes=40 * MIB),
         cost_estimate=cost(4 * 2 * blk * total * width, 8 * total * width),
         name="attend",
-    )(info, q, k, v, doc_col, doc_row)
-
-
-def attend_back_kernel(info, q, k, v, do, doc_col, doc_row, lse_col, lse_row, del_col, del_row, angles, out, acc, *, heads, head_dim, scale):
+    )(info, ids, q, k, v, doc_col, doc_row)
+
+
+def attend_back_kernel(info, ids, q, k, v, do, doc_col, doc_row, lse_col, lse_row, del_col, del_row, angles, out, acc, *, heads, head_dim, scale):
     blk = angles.shape[0]
     width = heads * head_dim
     i = pl.program_id(0)
-    b, jmin, imax = block_range(info, i, doc_row.shape[0])
+    b, jmin, imax = block_range(info, ids, i, doc_row.shape[0])
     me = pl.multiple_of((2 * info[0] + i) * blk, blk)
     mine = pl.ds(me, blk)
     iota_r = lax.broadcasted_iota(I32, (blk, blk), 0)
@@ -458,26 +462,26 @@
             out[:, part * width + h * head_dim:part * width + (h + 1) * head_dim] = t.astype(BF16)
 
 
-def attend_back(info, q, k, v, do, doc_col, doc_row, lse_col, lse_row, del_col, del_row, angles, blk):
+def attend_back(info, ids, q, k, v, do, doc_col, doc_row, lse_col, lse_row, del_col, del_row, angles, blk):
     total, width = k.shape
     head_dim = angles.shape[1]
     heads = width // head_dim
-    mine = lambda n: pl.BlockSpec((blk, n), lambda i, info: (2 * info[0] + i, 0))
+    mine = lambda n: pl.BlockSpec((blk, n), lambda i, info, ids: (2 * info[0] + i, 0))
     arrays = (q, k, v, do, doc_col, doc_row, lse_col, lse_row, del_col, del_row)
     return pl.pallas_call(
         functools.partial(attend_back_kernel, heads=heads, head_dim=head_dim, scale=head_dim ** -0.5),
         out_shape=jax.ShapeDtypeStruct((2 * blk, 3 * width), BF16),
         grid_spec=pltpu.PrefetchScalarGridSpec(
-            num_scalar_prefetch=1,
+            num_scalar_prefetch=2,
             grid=(2,),
             in_specs=[whole(a) for a in arrays] + [mine(head_dim)],
-            out_specs=pl.BlockSpec((blk, 3 * width), lambda i, info: (i, 0)),
+            out_specs=pl.BlockSpec((blk, 3 * width), lambda i, info, ids: (i, 0)),
             scratch_shapes=[pltpu.VMEM((3, blk, width), F32)],
         ),
         compiler_params=pltpu.CompilerParams(vmem_limit_bytes=48 * MIB),
         cost_estimate=cost(14 * 2 * blk * total * width // 2, 12 * total * width),
         name="attend_back",
-    )(info, *arrays, angles)
+    )(info, ids, *arrays, angles)
 
 
 def out_proj_kernel(info, x, att, a0, b0, a1, b1, gain, res, act, wide, abuf, bbuf, sems):
@@ -527,7 +531,7 @@
     )(info, x_all, att, *pieces, gain)
 
 
-def att_kernel(att, lse, x_all, a0, b0, a1, b1, gain, parts, lse_out, res, act, x, abuf, bbuf, send, recv, lse_send, lse_recv, load):
+def att_kernel(att, lse, x_all, a0, b0, gain, parts, lse_out, res, act, a1, b1, x, abuf, bbuf, send, recv, lse_send, lse_recv, load, swap_send, swap_recv):
     place = Place()
     rows, width = att.shape
     na, nb = a0.shape[1], b0.shape[1]
@@ -535,7 +539,8 @@
     loads = [pltpu.make_async_copy(x_all.at[pl.ds(mine * rows, rows), :], x, load.at[4])]
     for i, (src, dst) in enumerate(((a0, abuf.at[0]), (b0, bbuf.at[0]), (a1, abuf.at[1]), (b1, bbuf.at[1]))):
         loads.append(pltpu.make_async_copy(src, dst, load.at[i]))
-    for c in loads:
+    early, late = loads[:3], loads[3:]
+    for c in early:
         c.start()
     place.meet(("y", "z", "x", "core"))
     started = []
@@ -559,18 +564,21 @@
         copy.start()
         started.append(copy)
 
+    swaps = [pltpu.make_async_remote_copy(src_ref=src, dst_ref=dst, send_sem=swap_send.at[i], recv_sem=swap_recv.at[i], device_id=place.device(("core",)), device_id_type=MESH) for i, (src, dst) in enumerate(((a0, a1), (b0, b1)))]
     for step in range(2):
         for p in range(2):
             go(hop(p, (), near[(p + step) % 2]))
+    for c in swaps:
+        go(c)
     go(lse_hop(0))
     go(lse_hop(1))
     lse_out[mine] = lse[:]
     parts[place.tp()] = att[:]
-    for c in loads:
+    for c in early:
         c.wait()
 
-    def add(slot, first=False):
-        for i in range(2):
+    def add(slot, halves=(0, 1), first=False):
+        for i in halves:
             start = place.coord("core", ("core",) if i else ()) * (na + nb)
             k = pl.ds(pl.multiple_of(slot * width, width), width)
             for buf, at, n in ((abuf, 0, na), (bbuf, na, nb)):
@@ -578,12 +586,19 @@
                 t = nn(parts[slot], buf[i, k, :])
                 res[:, cols] = t + (x[:, cols].astype(F32) if first else res[:, cols])
 
-    add(place.tp(), True)
+    add(place.tp(), (0,), True)
+    for c in swaps:
+        c.wait_recv()
+    for c in late:
+        c.start()
     for p in range(2):
         hop(p, (), near[p]).wait_recv()
         go(hop(p, (near[p],), near[1 - p]))
     lse_hop(0).wait_recv()
     go(lse_hop(2))
+    for c in late:
+        c.wait()
+    add(place.tp(), (1,), True)
     for p in (1, 0):
         hop(p, (), near[1 - p]).wait_recv()
         add(place.tp((near[1 - p],)))
@@ -606,31 +621,49 @@
     hbm = pl.BlockSpec(memory_space=pl.ANY)
     return pl.pallas_call(
         att_kernel,
-        out_shape=[jax.ShapeDtypeStruct((4, rows, width), BF16), jax.ShapeDtypeStruct((4,) + lse.shape, F32), jax.ShapeDtypeStruct((rows, dim), F32), jax.ShapeDtypeStruct((rows, dim), BF16)],
-        in_specs=[vmem, vmem] + [hbm] * 5 + [vmem],
-        out_specs=[vmem] * 4,
+        out_shape=[jax.ShapeDtypeStruct((4, rows, width), BF16), jax.ShapeDtypeStruct((4,) + lse.shape, F32), jax.ShapeDtypeStruct((rows, dim), F32), jax.ShapeDtypeStruct((rows, dim), BF16)] + [jax.ShapeDtypeStruct(p.shape, BF16) for p in pieces],
+        in_specs=[vmem, vmem] + [hbm] * 3 + [vmem],
+        out_specs=[vmem] * 4 + [hbm, hbm],
         scratch_shapes=[
             pltpu.VMEM((rows, dim), BF16), pltpu.VMEM((2,) + pieces[0].shape, BF16), pltpu.VMEM((2,) + pieces[1].shape, BF16),
-            *[dma((n,)) for n in (6, 6, 3, 3, 5)],
+            *[dma((n,)) for n in (6, 6, 3, 3, 5, 2, 2)],
         ],
         compiler_params=pltpu.CompilerParams(collective_id=1, has_side_effects=True, vmem_limit_bytes=48 * MIB),
         name="att_project",
     )(att, lse, x_all, *pieces, gain)
 
 
-def weight_grad_kernel(info, *refs, pieces, splits):
+def weight_grad_kernel(info, *refs, pieces, splits, blank):
     lhs = refs[:pieces]
     rhs = refs[pieces:2 * pieces]
-    outs = refs[2 * pieces:]
+    outs = refs[2 * pieces:2 * pieces + splits]
+    if blank:
+        base, zeros, sem = refs[-3:]
+        step = zeros.shape[0]
+        i = pl.program_id(0)
+
+        def fill(n):
+            return pltpu.make_async_copy(zeros, base.at[pl.ds(pl.multiple_of(n * step, step), step), :], sem)
+
+        @pl.when(i == 0)
+        def _():
+            zeros[:] = jnp.zeros_like(zeros)
+
+        each = base.shape[0] // step // pl.num_programs(0)
+        for n in range(each):
+            fill(i * each + n).start()
     t = tn(lhs[0][:], rhs[0][:])
     for a, b in zip(lhs[1:], rhs[1:]):
         t += tn(a[:], b[:])
     width = t.shape[1] // splits
     for i, out in enumerate(outs):
         out[:] = t[:, i * width:(i + 1) * width]
-
-
-def weight_grad(info, lhs, rhs, block=256, splits=1, rows=None):
+    if blank:
+        for n in range(each):
+            fill(n).wait()
+
+
+def weight_grad(info, lhs, rhs, block=256, splits=1, rows=None, blank=()):
     def spec(arr, p, cols, moving):
         if arr.ndim == 3:
             return pl.BlockSpec((None, arr.shape[1], cols), lambda i, info: (info[0] ^ p, 0, i if moving else 0))
@@ -641,13 +674,14 @@
     n = len(lhs)
     width = dim // splits
     outs = pl.pallas_call(
-        functools.partial(weight_grad_kernel, pieces=n, splits=splits),
-        out_shape=[jax.ShapeDtypeStruct((rows, width), F32)] * splits,
+        functools.partial(weight_grad_kernel, pieces=n, splits=splits, blank=blank),
+        out_shape=[jax.ShapeDtypeStruct((rows, width), F32)] * splits + [jax.ShapeDtypeStruct(b, F32) for b in blank],
         grid_spec=pltpu.PrefetchScalarGridSpec(
             num_scalar_prefetch=1,
             grid=(pl.cdiv(rows, block),),
             in_specs=[spec(a, p, block, True) for p, a in enumerate(lhs)] + [spec(b, p, dim, False) for p, b in enumerate(rhs)],
-            out_specs=[pl.BlockSpec((block, width), lambda i, info: (i, 0))] * splits,
+            out_specs=[pl.BlockSpec((block, width), lambda i, info: (i, 0))] * splits + [pl.BlockSpec(memory_space=pl.ANY)] * len(blank),
+            scratch_shapes=[s for b in blank for s in (pltpu.VMEM((200, b[1]), F32), pltpu.SemaphoreType.DMA)],
         ),
         compiler_params=pltpu.CompilerParams(vmem_limit_bytes=56 * MIB),
         cost_estimate=cost(2 * n * tokens * rows * dim, 4 * rows * dim + 2 * n * tokens * (rows + dim)),
@@ -708,36 +742,6 @@
     )(act, dy, wg, wu, wd)
 
 
-def zero_kernel(after, out, zeros, sem):
-    zeros[:] = jnp.zeros_like(zeros)
-    step = zeros.shape[0]
-    count = out.shape[0] // step
-
-    def send(i, c):
-        pltpu.make_async_copy(zeros, out.at[pl.ds(pl.multiple_of(i * step, step), step), :], sem).start()
-        return c
-
-    def wait(i, c):
-        pltpu.make_async_copy(zeros, out.at[pl.ds(0, step), :], sem).wait()
-        return c
-
-    lax.fori_loop(0, count, send, 0)
-    lax.fori_loop(0, count, wait, 0)
-
-
-def zero_rows(after, rows, dim, step=200):
-    return pl.pallas_call(
-        zero_kernel,
-        out_shape=jax.ShapeDtypeStruct((rows, dim), F32),
-        in_specs=[pl.BlockSpec(memory_space=pltpu.SMEM)],
-        out_specs=pl.BlockSpec(memory_space=pl.ANY),
-        scratch_shapes=[pltpu.VMEM((step, dim), F32), pltpu.SemaphoreType.DMA],
-        compiler_params=pltpu.CompilerParams(vmem_limit_bytes=8 * MIB),
-        cost_estimate=cost(rows * dim, 4 * rows * dim),
-        name="zero_rows",
-    )(after)
-
-
 def scatter_kernel(order, sid, runs, bounds, rows, base_hbm, out_hbm, sums, row_sem, sum_sem):
     lo = bounds[0]
     hi = bounds[1]
@@ -834,6 +838,7 @@
         owned = (local_ids >= 0) & (local_ids < rows)
         safe_ids = jnp.where(owned, local_ids, jnp.arange(span) * (rows // span))
         picked = jnp.where(owned[:, None], jnp.take(table, safe_ids, axis=0), 0).astype(BF16)
+        info = jnp.stack([cp_rank, core]).astype(I32)
         half = dim // 2
         near = 256
         wo_half = lax.dynamic_slice_in_dim(w_o, core * half, half, 1)
@@ -847,7 +852,6 @@
         doc_all = ints[:, 1, :].reshape(total)
         wo_far = barrier((wo_half[:, near:], x_all))[0]
         wo_rest = join(wo_far, "tp")
-        wo_pieces = (wo_near, wo_rest, swap(wo_near, core_swap), swap(wo_rest, core_swap))
 
         dy_x = swap(barrier((dy, x_all))[0], x_swap)
         act_a, query, key, value, w_qkv = project_qkv(x_all, gain_a[None, :], w_q, w_k, w_v, angles)
@@ -856,13 +860,10 @@
         blocks = total // blk
         doc_col = doc_all[:, None]
         doc_row = doc_all.reshape(blocks, 1, blk)
-        docs = doc_all.reshape(blocks, blk)
-        docs = jnp.stack([docs[:, 0], docs[:, -1]], axis=1).reshape(2 * blocks)
-        info = jnp.concatenate([jnp.stack([cp_rank, core]), docs]).astype(I32)
-        attended, lse = attend(info, query, key, value, doc_col, doc_row, head_dim, blk)
+        attended, lse = attend(info, ints, query, key, value, doc_col, doc_row, head_dim, blk)
 
         gain_row = gain_b[None, :]
-        att_parts, lse_all, residual, act_b = att_project(attended, lse, x_all, wo_pieces, gain_row)
+        att_parts, lse_all, residual, act_b, *wo_other = att_project(attended, lse, x_all, (wo_near, wo_rest), gain_row)
         lse_all = lse_all.reshape(total, 8)
         att_x = swap(att_parts, x_swap)
 
@@ -870,7 +871,7 @@
         ffn = wg.shape[0]
         hidden, d_gate, d_up, d_act_b = mlp_block(act_b, dy, wg, wu, w_down, True)
         d_act_b = add_up(d_act_b)
-        act_x = out_proj(info, 2, x_all, att_x, wo_pieces, gain_row)[1]
+        act_x = out_proj(info, 2, x_all, att_x, (wo_near, wo_rest, *wo_other), gain_row)[1]
         hidden_x, d_gate_x, d_up_x = mlp_block(act_x, dy_x, wg, wu, w_down, False)
         d_act_b, hidden_x, d_gate_x, d_up_x = barrier((d_act_b, hidden_x, d_gate_x, d_up_x))
         d_act_b = to_bf16(d_act_b)
@@ -895,8 +896,14 @@
         d_resid_all = join(d_resid.astype(BF16), both)
         out_part = nn(hidden[:, :ffn], w_down)
         d_resid_all, grad_down, att_heads, out_part = barrier((d_resid_all, grad_down, att_heads, out_part))
-        out_slice = add_up(out_part)
-        out_slice = (res_part + out_slice).astype(BF16)
+        tp_swap = lambda arr, k: swap(arr, [(i, i ^ k) for i in range(tp_count)], "tp")
+        tp_part = lambda arr, k: lax.dynamic_slice_in_dim(arr, (tp_rank ^ k) * part, part, 0)
+        others = range(1, tp_count)
+        arrived = [tp_swap(tp_part(out_part, k), k) for k in others]
+        out_slice = res_part + tp_part(out_part, 0)
+        for piece in arrived:
+            out_slice = out_slice + piece
+        out_slice = out_slice.astype(BF16)
 
         d_att = nt(d_resid_all, w_o)
         d_att_b = d_att.astype(BF16)
@@ -907,21 +914,22 @@
         def by_block(arr):
             return jnp.transpose(arr.reshape(8, blocks, blk), (1, 0, 2))
 
-        dqkv = attend_back(info, query, key, value, d_att_b, doc_col, doc_row, lse_all, by_block(lse_all.T), delta.T, by_block(delta), angles, blk)
+        dqkv = attend_back(info, ints, query, key, value, d_att_b, doc_col, doc_row, lse_all, by_block(lse_all.T), delta.T, by_block(delta), angles, blk)
         d_act_a = nt(dqkv, w_qkv)
-        d_act_a, out_slice = barrier((d_act_a, out_slice))
         d_act_a = add_up(d_act_a)
         dqkv_x = swap(dqkv, x_swap)
         dqkvs = (dqkv, swap(dqkv, core_swap), dqkv_x, swap(dqkv_x, core_swap))
         grad_out = weight_grad(info, head_parts, [d_resid_all.reshape(cp_count, span, dim)] * 4)
         d_act_a, dqkv_x, grad_out, grad_up = barrier((d_act_a, dqkv_x, grad_out, grad_up))
+        d_act_a, out_slice = barrier((d_act_a, out_slice))
         d_act_a = to_bf16(d_act_a)
+        y_parts = [tp_swap(out_slice, k) for k in others]
         normed_a, inv_a = rms_stats(x_slice.astype(F32))
         grad_gain_a = jnp.sum(d_act_a * normed_a, axis=0)
         d_embed = d_resid + rms_back(d_act_a * gain_a, normed_a, inv_a)
         payload = jnp.concatenate([d_embed, jnp.stack([grad_gain_a, grad_gain_b] * 4)])
         gathered = join(payload, both)
-        grad_qkv = weight_grad(info, [act_a.reshape(cp_count, span, dim)] * 4, dqkvs, splits=3)
+        *grad_qkv, base = weight_grad(info, [act_a.reshape(cp_count, span, dim)] * 4, dqkvs, splits=3, blank=((rows, dim),))
         slot_ids = jnp.arange(total, dtype=I32)
         before = (tok_all[None, :] < tok_all[:, None]) | ((tok_all[None, :] == tok_all[:, None]) & (slot_ids[None, :] < slot_ids[:, None]))
         rank = jnp.sum(before.astype(I32), axis=1)
@@ -932,10 +940,10 @@
         sid = jnp.sum(jnp.where(at_rank, tok_all[None, :], 0), axis=1) - tp_rank * rows
         order = order + 8 * (order // part)
         bounds = jnp.stack([jnp.sum((tok_all < tp_rank * rows).astype(I32)), jnp.sum((tok_all < (tp_rank + 1) * rows).astype(I32))])
-        base = zero_rows(barrier((bounds, d_act_a))[0], rows, dim)
         gathered, grad_qkv, grad_gate, runs, order, sid, bounds, base = barrier((gathered, grad_qkv, grad_gate, runs, order, sid, bounds, base))
-        out_slice = barrier((out_slice, gathered))[0]
-        layer_out = join(out_slice, "tp")
+        layer_out = jnp.concatenate([out_slice] * tp_count)
+        for k, piece in zip(others, y_parts):
+            layer_out = lax.dynamic_update_slice_in_dim(layer_out, piece, (tp_rank ^ k) * part, 0)
         gain_grads = jnp.sum(gathered.reshape(cp_count * tp_count, part + 8, dim)[:, part:part + 2], axis=0)
         grad_table = scatter_rows(order, sid, runs, bounds, gathered, base, total)
         return (layer_out, grad_table, *grad_qkv, grad_out, grad_gate.T, grad_up.T, grad_down, gain_grads[0], gain_grads[1])

time: 798 us -> 793 us (level)
  waiting for transfers between devices: 202 us -> 181 us
  starting transfers between devices: 8.42 us -> 22.3 us
    all_gather x5 -> x4, waiting for transfers between devices: 85.9 us -> 10.2 us  [compute(): join = lambda arr, axis: lax.all_gather(arr, axis, axis=0, tiled=True)]
    ppermute x19 -> x23, waiting for transfers between devices: 106 us -> 171 us  [compute(): swap = lambda arr, pairs, axis='cp': lax.ppermute(arr, axis, pairs)]
    pallas_call x1 -> x0, Pallas kernels: 26.4 us -> none  [zero_rows(): pl.pallas_call(zero_kernel, out_shape=jax.ShapeDtypeStruct((rows, dim), F...]
    pallas_call x5, Pallas kernels: 127 us -> 149 us  [weight_grad(): pl.pallas_call(functools.partial(weight_grad_kernel, pieces=n, splits=spl...]
    ppermute x19 -> x23, starting transfers between devices: 7.25 us -> 21.3 us  [compute(): swap = lambda arr, pairs, axis='cp': lax.ppermute(arr, axis, pairs)]
    reduce_scatter x3 -> x2, waiting for transfers between devices: 10.4 us -> 0.01 us  [compute(): lax.psum_scatter(arr, 'tp', scatter_dimension=0, tiled=True)]
    unnamed x77 -> x96, local copies, waits for them, and re-layouts: 25.2 us -> 27.9 us
  transfers between devices with their start and end apart: 27 -> 29, of which waited for: 10 -> 7; matrix products, arithmetic and copies ran while one was open for 10% -> 9% of each run, Pallas kernels for 36% -> 38%
where the time goes in v7:
time: 793 us; the launch traced here: 788 us
  Pallas kernels  431 us (54%)
  waiting for transfers between devices  181 us (23%)
  local copies, waits for them, and re-layouts  60.8 us (8%)
  other arithmetic  39.2 us (5%)
  matrix products  37.6 us (5%)
  starting transfers between devices  22.3 us (3%)
  between operations  14.9 us (2%)
    ppermute x23, waiting for transfers between devices, compute(): swap = lambda arr, pairs, axis='cp': lax.ppermute(arr, axis, pairs)  171 us
    pallas_call x5, Pallas kernels, weight_grad(): pl.pallas_call(functools.partial(weight_grad_kernel, pieces=n, splits=spl...  149 us
    pallas_call x1, Pallas kernels, embed_gather(): pl.pallas_call(embed_kernel, out_shape=[jax.ShapeDtypeStruct((16 * rows,...  73.8 us
    pallas_call x2, Pallas kernels, mlp_block(): pl.pallas_call(functools.partial(mlp_kernel, limit=limit), out_shape=[jax...  64.8 us
    pallas_call x1, Pallas kernels, project_qkv(): pl.pallas_call(functools.partial(qkv_kernel, head_dim=head_dim), out_shap...  35.4 us
    pallas_call x1, Pallas kernels, att_project(): pl.pallas_call(att_kernel, out_shape=[jax.ShapeDtypeStruct((4, rows, widt...  34.4 us
    dot_general x3, matrix products, contract(): lax.dot_general(a, b, (((ca,), (cb,)), ((), ())), preferred_element_type=...  32.8 us
    pallas_call x1, Pallas kernels, scatter_rows(): pl.pallas_call(scatter_kernel, out_shape=jax.ShapeDtypeStruct((rows, dim)...  30.6 us
  transfers between devices with their start and end apart: 29, of which 7 were waited for; matrix products, arithmetic and copies ran while one was open for 9% of the time, Pallas kernels for 38%

profile of v7, /device:TPU:0, one launch (start us, length us, event | category | flops | bytes accessed | tf_op | source)
XLA Modules:
  0.0 787.5 jit_solution(735735954935000585)
XLA Ops:
  11.4 7.6 gather_fusion
  22.3 73.8 %embed_gather.1 = (bf16[2048,2560]{1,0:T(8,128)(2,1)}, bf16[128,2560]{1,0:T(8,128)(2,1)S(1)}, f32[4,512,128]{2,1,0:T(8,128)S(1)}, s32[4,8,512]{2,1,0:T(8,128)S(1)}) custom-call(bf16[4,128,2560]{2,1,0:T(8,128)(2,1)S(1)} %select_select_fusion.picked, f32[512,128]{1,0:T(8,128)S(1)} %pad_maximum_fusion.1.side_f, s32[8,512]{1,0:T(8,128)S(1)} %stack.50.side_i), custom_call_target="tpu_custom_call" | custom-call | tf_op jit(solution)/shard_map/embed_gather/pallas_call | solution.py:258
  103.0 35.4 %project_qkv.1 = (bf16[2048,2560]{1,0:T(8,128)(2,1)}, bf16[2048,640]{1,0:T(8,128)(2,1)}, bf16[2048,640]{1,0:T(8,128)(2,1)}, bf16[2048,640]{1,0:T(8,128)(2,1)}, bf16[2560,1920]{1,0:T(8,128)(2,1)}) custom-call(bf16[2048,2560]{1,0:T(8,128)(2,1)} %get-tuple-element.66.x.x_all, f32[1,2560]{1,0:T(1,128)} %broadcast_in_dim.81.gain, bf16[2560,640]{1,0:T(8,128)(2,1)} %wq.1, ...), custom_call_target="tpu_custom_call" | custom-call | flops 20132659200 | bytes 38666240 | tf_op jit(solution)/shard_map/project_qkv/pallas_call | solution.py:319
  159.4 34.4 %att_project.1 = (bf16[4,512,640]{2,1,0:T(8,128)(2,1)}, f32[4,512,8]{2,1,0:T(8,128)S(1)}, f32[512,2560]{1,0:T(8,128)}, bf16[512,2560]{1,0:T(8,128)(2,1)}, bf16[2...) custom-call(bf16[512,640]{1,0:T(8,128)(2,1)S(1)} %copy-done.5, f32[512,8]{1,0:T(8,128)S(1)} %get-tuple-element.72.lse, ...), custom_call_target="tpu_custom_call" | custom-call | tf_op jit(solution)/shard_map/att_project/pallas_call | solution.py:622
  195.8 43.6 %mlp_block.2 = (bf16[512,1792]{1,0:T(8,128)(2,1)}, bf16[512,1792]{1,0:T(8,128)(2,1)S(1)}, bf16[512,1792]{1,0:T(8,128)(2,1)S(1)}, f32[512,2560]{1,0:T(8,128)}) custom-call(bf16[512,2560]{1,0:T(8,128)(2,1)} %get-tuple-element.75.act.refs_4_, bf16[512,2560]{1,0:T(8,128)(2,1)} %refs_4_.1, bf16[1728,2560]{1,0:T(8,128)(2,1)} %bitcast.66, ...), custom_call_target="tpu_custom_call" | custom-call | flops 22649241600 | bytes 36110336 | tf_op jit(solution)/shard_map/mlp_block/pallas_call | solution.py:732
  246.3 56.5 %collective-permute-done.att = bf16[4,512,640]{2,1,0:T(8,128)(2,1)} collective-permute-done((bf16[4,512,640]{2,1,0:T(8,128)(2,1)}, bf16[4,512,640]{2,1,0:T(8,128)(2,1)}, u32[]{:S(2)}, u32[]{:S(2)}) %collective-permute-start) | collective-permute-done | bytes 2621472 | tf_op jit(solution)/shard_map/ppermute | solution.py:836
  302.8 16.6 %out_proj.1 = (f32[512,2560]{1,0:T(8,128)}, bf16[512,2560]{1,0:T(8,128)(2,1)}) custom-call(s32[2]{0:T(128)} %copy-done.20, bf16[2048,2560]{1,0:T(8,128)(2,1)} %get-tuple-element.66.x.x_all, bf16[4,512,640]{2,1,0:T(8,128)(2,1)} %collective-permute-done.att, bf16[2560,256]{1,0:T(8,128)(2,1)} %all-gather.5.cloned.1.call-done.a0, ...), custom_call_target="tpu_custom_call" | custom-call | flops 6710886400 | bytes 26214400 | tf_op jit(solution)/shard_map/out_proj/pallas_call | solution.py:518
  319.4 37.4 %collective-permute-done.1.dy.refs_6_ = bf16[512,2560]{1,0:T(8,128)(2,1)} collective-permute-done((bf16[512,2560]{1,0:T(8,128)(2,1)}, bf16[512,2560]{1,0:T(8,128)(2,1)}, u32[]{:S(2)}, u32[]{:S(2)}) %collective-permute-start.1) | collective-permute-done | bytes 2621472 | tf_op jit(solution)/shard_map/ppermute | solution.py:836
  356.8 21.2 %mlp_block.3 = (bf16[512,1792]{1,0:T(8,128)(2,1)}, bf16[512,1792]{1,0:T(8,128)(2,1)S(1)}, bf16[512,1792]{1,0:T(8,128)(2,1)S(1)}) custom-call(bf16[512,2560]{1,0:T(8,128)(2,1)} %get-tuple-element.80.act.refs_6_, bf16[512,2560]{1,0:T(8,128)(2,1)} %collective-permute-done.1.dy.refs_6_, bf16[1728,2560]{1,0:T(8,128)(2,1)} %bitcast.67, ...), custom_call_target="tpu_custom_call" | custom-call | flops 13589544960 | bytes 36110336 | tf_op jit(solution)/shard_map/mlp_block/pallas_call | solution.py:732
  394.0 11.5 %fusion.6 = f32[512,2560]{1,0:T(8,128)} fusion(bf16[1728,2560]{1,0:T(8,128)(2,1)} %wd.3, bf16[512,1792]{1,0:T(8,128)(2,1)} %get-tuple-element.86.refs_0_), kind=kOutput, calls=%fused_computation.18 | convolution fusion | flops 4529848320 | bytes 15925248 | tf_op jit(solution)/shard_map/dot_general | solution.py:31
  409.0 27.3 %weight_grad.5 = f32[1728,2560]{1,0:T(8,128)} custom-call(s32[2]{0:T(128)} %copy-done.20, bf16[512,1792]{1,0:T(8,128)(2,1)} %get-tuple-element.86.refs_0_, bf16[512,1792]{1,0:T(8,128)(2,1)} %collective-permute-done.2.refs_1_, bf16[512,1792]{1,0:T(8,128)(2,1)} %get-tuple-element.87.refs_2_, bf16[512,1792]{1,0:T(8,128)(2,1)} %collective-permute-done.3.refs_3_, ...), custom_call_target="tpu_custom_call" | custom-call | flops 18119393280 | bytes 35258368 | tf_op jit(solution)/shard_map/weight_grad/pallas_call | solution.py:676
  436.3 6.9 all-gather.9.cloned.1.call-done
  443.2 11.0 %convolution_convert_fusion.do = bf16[2048,640]{1,0:T(8,128)(2,1)S(1)} fusion(bf16[2048,2560]{1,0:T(8,128)(2,1)} %all-gather.9.cloned.1.call-done, bf16[640,2560]{1,0:T(8,128)(2,1)S(1)} %copy-done), kind=kOutput, calls=%fused_computation.15 | convolution fusion | flops 6712197120 | bytes 16384000 | tf_op jit(solution)/shard_map/dot_general | solution.py:31
  462.2 20.7 %attend_back.1.refs_4_ = bf16[512,1920]{1,0:T(8,128)(2,1)} custom-call(s32[2]{0:T(128)S(1)} %copy-done.21, s32[4,8,512]{2,1,0:T(8,128)S(1)} %copy-done.19, bf16[2048,640]{1,0:T(8,128)(2,1)} %get-tuple-element.68.q, bf16[2048,640]{1,0:T(8,128)(2,1)} %get-tuple-element.69.k, bf16[2048,640]{1,0:T(8,128)(2,1)} %get-tuple-element.70.v, ...), custom_call_target="tpu_custom_call" | custom-call | flops 4697620480 | bytes 15728640 | tf_op jit(solution)/shard_map/attend_back/pallas_call | solution.py:471
  482.9 10.3 %fusion.34 = f32[512,2560]{1,0:T(8,128)} fusion(bf16[512,1920]{1,0:T(8,128)(2,1)} %attend_back.1.refs_4_, bf16[2560,1920]{1,0:T(8,128)(2,1)} %get-tuple-element.91), kind=kOutput, calls=%fused_computation.96 | convolution fusion | flops 5033164800 | bytes 17039360 | tf_op jit(solution)/shard_map/dot_general | solution.py:31
  510.6 27.1 %weight_grad.7 = f32[1728,2560]{1,0:T(8,128)} custom-call(s32[2]{0:T(128)} %copy-done.20, bf16[512,1792]{1,0:T(8,128)(2,1)} %copy-done.25, bf16[512,1792]{1,0:T(8,128)(2,1)} %collective-permute-done.9.refs_1_, bf16[512,1792]{1,0:T(8,128)(2,1)} %copy-done.27, bf16[512,1792]{1,0:T(8,128)(2,1)} %collective-permute-done.10.refs_3_, ...), custom_call_target="tpu_custom_call" | custom-call | flops 18119393280 | bytes 35258368 | tf_op jit(solution)/shard_map/weight_grad/pallas_call | solution.py:676
  537.7 15.1 %weight_grad.6 = f32[640,2560]{1,0:T(8,128)} custom-call(s32[2]{0:T(128)} %copy-done.20, bf16[512,640]{1,0:T(8,128)(2,1)} %copy-done.4, bf16[512,640]{1,0:T(8,128)(2,1)} %collective-permute-done.6.refs_1_, bf16[512,640]{1,0:T(8,128)(2,1)} %get-tuple-element.131.refs_2_, bf16[512,640]{1,0:T(8,128)(2,1)} %collective-permute-done.7.refs_3_, ...), custom_call_target="tpu_custom_call" | custom-call | flops 6710886400 | bytes 19660800 | tf_op jit(solution)/shard_map/weight_grad/pallas_call | solution.py:676
  552.8 9.7 %collective-permute-done.13 = f32[128,2560]{1,0:T(8,128)S(1)} collective-permute-done((f32[128,2560]{1,0:T(8,128)}, f32[128,2560]{1,0:T(8,128)S(1)}, u32[]{:S(2)}, u32[]{:S(2)}) %collective-permute-start.13) | collective-permute-done | bytes 1310752 | tf_op jit(solution)/shard_map/ppermute | solution.py:836
  562.5 42.7 %collective-permute-done.15 = f32[128,2560]{1,0:T(8,128)S(1)} collective-permute-done((f32[128,2560]{1,0:T(8,128)S(1)}, f32[128,2560]{1,0:T(8,128)S(1)}, u32[]{:S(2)}, u32[]{:S(2)}) %collective-permute-start.15) | collective-permute-done | bytes 1310752 | tf_op jit(solution)/shard_map/ppermute | solution.py:836
  621.6 7.8 select_reduce_fusion
  634.2 27.7 %weight_grad.9 = f32[1728,2560]{1,0:T(8,128)} custom-call(s32[2]{0:T(128)} %copy-done.20, bf16[512,1792]{1,0:T(8,128)(2,1)} %copy-done.22, bf16[512,1792]{1,0:T(8,128)(2,1)} %copy-done.47, bf16[512,1792]{1,0:T(8,128)(2,1)} %copy-done.24, bf16[512,1792]{1,0:T(8,128)(2,1)} %collective-permute-done.22.refs_3_, bf16[512,2560]{1,0:T(8,128)(2,1)} %get-tuple-element.75.act.refs_4_, ...), custom_call_target="tpu_custom_call" | custom-call | flops 18119393280 | bytes 35258368 | tf_op jit(solution)/shard_map/weight_grad/pallas_call | solution.py:676
  664.0 51.5 %weight_grad.8 = (f32[2560,640]{1,0:T(8,128)}, f32[2560,640]{1,0:T(8,128)}, f32[2560,640]{1,0:T(8,128)}, f32[8000,2560]{1,0:T(8,128)}) custom-call(s32[2]{0:T(128)} %copy-done.20, bf16[4,512,2560]{2,1,0:T(8,128)(2,1)} %bitcast.72, bf16[4,512,2560]{2,1,0:T(8,128)(2,1)} %bitcast.73, bf16[4,512,2560]{2,1,0:T(8,128)(2,1)} %bitcast.74, ...), custom_call_target="tpu_custom_call" | custom-call | flops 20132659200 | bytes 38010880 | tf_op jit(solution)/shard_map/weight_grad/pallas_call | solution.py:676
  721.3 24.7 %collective-permute-done.17 = bf16[128,2560]{1,0:T(8,128)(2,1)S(1)} collective-permute-done((bf16[128,2560]{1,0:T(8,128)(2,1)S(1)}, bf16[128,2560]{1,0:T(8,128)(2,1)S(1)}, u32[]{:S(2)}, u32[]{:S(2)}) %collective-permute-start.17) | collective-permute-done | bytes 655392 | tf_op jit(solution)/shard_map/ppermute | solution.py:836
  749.8 30.6 %scatter_rows.1 = f32[8000,2560]{1,0:T(8,128)} custom-call(s32[2048]{0:T(1024)S(1)} %fusion.25.order, s32[2048]{0:T(1024)S(1)} %broadcast_subtract_fusion.sid, s32[2048]{0:T(1024)S(1)} %select_reduce_fusion.2.runs, s32[2]{0:T(128)S(1)} %pad_add_fusion.1.bounds, f32[2176,2560]{1,0:T(8,128)} %all-gather.11.cloned.1.call-done.rows, ...), custom_call_target="tpu_custom_call", output_to_operand_aliasing={{}: (5, {})} | custom-call | tf_op jit(solution)/shard_map/scatter_rows/pallas_call | solution.py:796
  (206 shorter events, 121.7 us)
Async XLA Ops:
  7.2 146.5 %all-gather.5.cloned.1.call-start = ((), (), s32[]{:S(2)}) async-start(), calls=%async_computation.2 | async-start | bytes 1638400 | tf_op jit(solution)/shard_map/all_gather | solution.py:834
  9.9 147.1 %all-gather.7.cloned.1.call-start = ((), (), s32[]{:S(2)}) async-start(), calls=%async_computation.3 | async-start | bytes 6553600 | tf_op jit(solution)/shard_map/all_gather | solution.py:834
  99.3 281.3 %reduce-scatter.3.cloned.1.call-start = ((), (), s32[]{:S(2)}) async-start(), calls=%async_computation.4 | async-start | bytes 6553600 | tf_op jit(solution)/shard_map/reduce_scatter | solution.py:835
  241.9 201.3 %all-gather.9.cloned.1.call-start = ((), (), s32[]{:S(2)}) async-start(), calls=%async_computation.5 | async-start | bytes 11141120 | tf_op jit(solution)/shard_map/all_gather | solution.py:834
  242.0 60.8 %collective-permute-start = (bf16[4,512,640]{2,1,0:T(8,128)(2,1)}, bf16[4,512,640]{2,1,0:T(8,128)(2,1)}, u32[]{:S(2)}, u32[]{:S(2)}) collective-permute-start(bf16[4,512,640]{2,1,0:T(8,128)(2,1)} %get-tuple-element.77), channel_id=1, source_target_pairs={{0,2},{1,3},{2,0},{3,1},{4,6},{5,7},{6,4},{7,5},{8,10},{9,11},{10,... | collective-permute-start | bytes 7864328 | tf_op jit(solution)/shard_map/ppermute | solution.py:836
  244.7 112.1 %collective-permute-start.1 = (bf16[512,2560]{1,0:T(8,128)(2,1)}, bf16[512,2560]{1,0:T(8,128)(2,1)}, u32[]{:S(2)}, u32[]{:S(2)}) collective-permute-start(bf16[512,2560]{1,0:T(8,128)(2,1)} %refs_4_.1), channel_id=1, source_target_pairs={{0,2},{1,3},{2,0},{3,1},{4,6},{5,7},{6,4},{7,5},{8,10},{9,11},{10,... | collective-permute-start | bytes 7864328 | tf_op jit(solution)/shard_map/ppermute | solution.py:836
  385.5 222.6 %reduce-scatter.5.cloned.1.call-start = ((), (), s32[]{:S(2)}) async-start(), calls=%async_computation.6 | async-start | bytes 6553600 | tf_op jit(solution)/shard_map/reduce_scatter | solution.py:835
  385.6 23.4 %collective-permute-start.4 = (bf16[512,2560]{1,0:T(8,128)(2,1)}, bf16[512,2560]{1,0:T(8,128)(2,1)}, u32[]{:S(2)}, u32[]{:S(2)}) collective-permute-start(bf16[512,2560]{1,0:T(8,128)(2,1)} %refs_4_.1), channel_id=1, source_target_pairs={{0,1},{1,0},{2,3},{3,2},{4,5},{5,4},{6,7},{7,6},{8,9},{9,8},{10,11... | collective-permute-start | bytes 7864328 | tf_op jit(solution)/shard_map/ppermute | solution.py:836
  386.1 22.9 %collective-permute-start.5 = (bf16[512,2560]{1,0:T(8,128)(2,1)}, bf16[512,2560]{1,0:T(8,128)(2,1)}, u32[]{:S(2)}, u32[]{:S(2)}) collective-permute-start(bf16[512,2560]{1,0:T(8,128)(2,1)} %collective-permute-done.1.dy.refs_6_), channel_id=1, source_target_pairs={{0,1},{1,0},{2,3},{3,2},{4,5},{5,4},{6,7},{7,6},{8,9},{9,8},{10,11... | collective-permute-start | bytes 7864328 | tf_op jit(solution)/shard_map/ppermute | solution.py:836
  390.8 18.2 %collective-permute-start.2 = (bf16[512,1792]{1,0:T(8,128)(2,1)}, bf16[512,1792]{1,0:T(8,128)(2,1)}, u32[]{:S(2)}, u32[]{:S(2)}) collective-permute-start(bf16[512,1792]{1,0:T(8,128)(2,1)} %get-tuple-element.86.refs_0_), channel_id=1, source_target_pairs={{0,1},{1,0},{2,3},{3,2},{4,5},{5,4},{6,7},{7,6},{8,9},{9,8},{10,11... | collective-permute-start | bytes 5505032 | tf_op jit(solution)/shard_map/ppermute | solution.py:836
  391.2 17.8 %collective-permute-start.3 = (bf16[512,1792]{1,0:T(8,128)(2,1)}, bf16[512,1792]{1,0:T(8,128)(2,1)}, u32[]{:S(2)}, u32[]{:S(2)}) collective-permute-start(bf16[512,1792]{1,0:T(8,128)(2,1)} %get-tuple-element.87.refs_2_), channel_id=1, source_target_pairs={{0,1},{1,0},{2,3},{3,2},{4,5},{5,4},{6,7},{7,6},{8,9},{9,8},{10,11... | collective-permute-start | bytes 5505032 | tf_op jit(solution)/shard_map/ppermute | solution.py:836
  493.2 254.5 %all-gather.11.cloned.1.call-start = ((), (), s32[]{:S(2)}) async-start(), calls=%async_computation.7 | async-start | bytes 23674880 | tf_op jit(solution)/shard_map/all_gather | solution.py:834
  493.7 14.7 %collective-permute-start.11 = (bf16[512,2560]{1,0:T(8,128)(2,1)}, bf16[512,2560]{1,0:T(8,128)(2,1)}, u32[]{:S(2)}, u32[]{:S(2)}) collective-permute-start(bf16[512,2560]{1,0:T(8,128)(2,1)} %get-tuple-element.75.act.refs_4_), channel_id=1, source_target_pairs={{0,1},{1,0},{2,3},{3,2},{4,5},{5,4},{6,7},{7,6},{8,9},{9,8},{10,11... | collective-permute-start | bytes 7864328 | tf_op jit(solution)/shard_map/ppermute | solution.py:836
  495.2 13.8 %collective-permute-start.12 = (bf16[512,2560]{1,0:T(8,128)(2,1)}, bf16[512,2560]{1,0:T(8,128)(2,1)}, u32[]{:S(2)}, u32[]{:S(2)}) collective-permute-start(bf16[512,2560]{1,0:T(8,128)(2,1)} %get-tuple-element.80.act.refs_6_), channel_id=1, source_target_pairs={{0,1},{1,0},{2,3},{3,2},{4,5},{5,4},{6,7},{7,6},{8,9},{9,8},{10,11... | collective-permute-start | bytes 7864328 | tf_op jit(solution)/shard_map/ppermute | solution.py:836
  496.2 14.4 %collective-permute-start.10 = (bf16[512,1792]{1,0:T(8,128)(2,1)}, bf16[512,1792]{1,0:T(8,128)(2,1)}, u32[]{:S(2)}, u32[]{:S(2)}) collective-permute-start(bf16[512,1792]{1,0:T(8,128)(2,1)} %copy-done.27), channel_id=1, source_target_pairs={{0,1},{1,0},{2,3},{3,2},{4,5},{5,4},{6,7},{7,6},{8,9},{9,8},{10,11... | collective-permute-start | bytes 5505032 | tf_op jit(solution)/shard_map/ppermute | solution.py:836
  496.4 111.7 %collective-permute-start.8 = (bf16[512,1920]{1,0:T(8,128)(2,1)}, bf16[512,1920]{1,0:T(8,128)(2,1)}, u32[]{:S(2)}, u32[]{:S(2)}) collective-permute-start(bf16[512,1920]{1,0:T(8,128)(2,1)} %attend_back.1.refs_4_), channel_id=1, source_target_pairs={{0,2},{1,3},{2,0},{3,1},{4,6},{5,7},{6,4},{7,5},{8,10},{9,11},{10,... | collective-permute-start | bytes 5898248 | tf_op jit(solution)/shard_map/ppermute | solution.py:836
  507.1 55.4 %collective-permute-start.13 = (f32[128,2560]{1,0:T(8,128)}, f32[128,2560]{1,0:T(8,128)S(1)}, u32[]{:S(2)}, u32[]{:S(2)}) collective-permute-start(f32[128,2560]{1,0:T(8,128)} %get-tuple-element.134), channel_id=1, source_target_pairs={{0,4},{4,0},{8,12},{12,8},{1,5},{5,1},{9,13},{13,9},{2,6},{6,2},{1... | collective-permute-start | bytes 3932168 | tf_op jit(solution)/shard_map/ppermute | solution.py:836
  508.4 54.1 %collective-permute-start.14 = (f32[128,2560]{1,0:T(8,128)S(1)}, f32[128,2560]{1,0:T(8,128)S(1)}, u32[]{:S(2)}, u32[]{:S(2)}) collective-permute-start(f32[128,2560]{1,0:T(8,128)S(1)} %get-tuple-element.136), channel_id=1, source_target_pairs={{0,8},{4,12},{8,0},{12,4},{1,9},{5,13},{9,1},{13,5},{2,10},{6,14},... | collective-permute-start | bytes 3932168 | tf_op jit(solution)/shard_map/ppermute | solution.py:836
  509.0 96.1 %collective-permute-start.15 = (f32[128,2560]{1,0:T(8,128)S(1)}, f32[128,2560]{1,0:T(8,128)S(1)}, u32[]{:S(2)}, u32[]{:S(2)}) collective-permute-start(f32[128,2560]{1,0:T(8,128)S(1)} %get-tuple-element.135), channel_id=1, source_target_pairs={{0,12},{4,8},{8,4},{12,0},{1,13},{5,9},{9,5},{13,1},{2,14},{6,10},... | collective-permute-start | bytes 3932168 | tf_op jit(solution)/shard_map/ppermute | solution.py:836
  631.1 30.9 %collective-permute-start.19 = (bf16[512,1920]{1,0:T(8,128)(2,1)}, bf16[512,1920]{1,0:T(8,128)(2,1)S(1)}, u32[]{:S(2)}, u32[]{:S(2)}) collective-permute-start(bf16[512,1920]{1,0:T(8,128)(2,1)} %attend_back.1.refs_4_), channel_id=1, source_target_pairs={{0,1},{1,0},{2,3},{3,2},{4,5},{5,4},{6,7},{7,6},{8,9},{9,8},{10,11... | collective-permute-start | bytes 5898248 | tf_op jit(solution)/shard_map/ppermute | solution.py:836
  631.2 30.9 %collective-permute-start.20 = (bf16[512,1920]{1,0:T(8,128)(2,1)}, bf16[512,1920]{1,0:T(8,128)(2,1)S(1)}, u32[]{:S(2)}, u32[]{:S(2)}) collective-permute-start(bf16[512,1920]{1,0:T(8,128)(2,1)} %collective-permute-done.8.refs_6_), channel_id=1, source_target_pairs={{0,1},{1,0},{2,3},{3,2},{4,5},{5,4},{6,7},{7,6},{8,9},{9,8},{10,11... | collective-permute-start | bytes 5898248 | tf_op jit(solution)/shard_map/ppermute | solution.py:836
  662.0 58.5 %collective-permute-start.16 = (bf16[128,2560]{1,0:T(8,128)(2,1)S(1)}, bf16[128,2560]{1,0:T(8,128)(2,1)S(1)}, u32[]{:S(2)}, u32[]{:S(2)}) collective-permute-start(bf16[128,2560]{1,0:T(8,128)(2,1)S(1)} %copy-done.35), channel_id=1, source_target_pairs={{0,4},{4,0},{8,12},{12,8},{1,5},{5,1},{9,13},{13,9},{2,6},{6,2},{1... | collective-permute-start | bytes 1966088 | tf_op jit(solution)/shard_map/ppermute | solution.py:836
  715.5 30.5 %collective-permute-start.17 = (bf16[128,2560]{1,0:T(8,128)(2,1)S(1)}, bf16[128,2560]{1,0:T(8,128)(2,1)S(1)}, u32[]{:S(2)}, u32[]{:S(2)}) collective-permute-start(bf16[128,2560]{1,0:T(8,128)(2,1)S(1)} %copy-done.35), channel_id=1, source_target_pairs={{0,8},{4,12},{8,0},{12,4},{1,9},{5,13},{9,1},{13,5},{2,10},{6,14},... | collective-permute-start | bytes 1966088 | tf_op jit(solution)/shard_map/ppermute | solution.py:836
  715.5 31.4 %collective-permute-start.18 = (bf16[128,2560]{1,0:T(8,128)(2,1)S(1)}, bf16[128,2560]{1,0:T(8,128)(2,1)S(1)}, u32[]{:S(2)}, u32[]{:S(2)}) collective-permute-start(bf16[128,2560]{1,0:T(8,128)(2,1)S(1)} %copy-done.35), channel_id=1, source_target_pairs={{0,12},{4,8},{8,4},{12,0},{1,13},{5,9},{9,5},{13,1},{2,14},{6,10},... | collective-permute-start | bytes 1966088 | tf_op jit(solution)/shard_map/ppermute | solution.py:836
  (53 other events, 392.8 us)
Sparse Core Ops, SparseCore 0:
  10.4 34.8 all-gather.4
  99.4 57.5 all-gather.6
  242.0 59.0 reduce-scatter.2
  385.7 57.5 all-gather.8
  493.4 102.4 reduce-scatter.4
  615.9 103.9 all-gather.10

commit v8 on v7

--- a/solution.py
+++ b/solution.py
@@ -9,6 +9,7 @@
 NORM_EPS = 1e-5
 NEG_BIG = -1e30
 MIB = 2 ** 20
+FULL = 62 * MIB
 F32 = jnp.float32
 BF16 = jnp.bfloat16
 I32 = jnp.int32
@@ -32,7 +33,7 @@
 
 
 def row_sum(t):
-    return jnp.sum(t, axis=1, keepdims=True)
+    return jnp.sum(t, 1, keepdims=True)
 
 
 def mean_row(t):
@@ -43,8 +44,8 @@
     return pl.BlockSpec(a.shape, lambda *i: (0,) * a.ndim)
 
 
-def cost(flops, moved):
-    return pl.CostEstimate(flops=flops, bytes_accessed=moved, transcendentals=0)
+def cost(flops):
+    return pl.CostEstimate(flops=flops, bytes_accessed=flops // 512, transcendentals=0)
 
 
 def nn(a, b):
@@ -188,7 +189,7 @@
     near = ("y", "z")
 
     sides = ((side_f, all_f), (side_i, all_i))
-    started = []
+    started, keeps = [], []
 
     def side_hop(i, step):
         src, dst = sides[i]
@@ -219,8 +220,8 @@
     for i in range(2):
         go(side_hop(i, 0))
         go(side_hop(i, 1))
-        all_i_or_f = sides[i][1]
-        all_i_or_f[place.cp()] = sides[i][0][:]
+        keeps.append(pltpu.make_async_copy(sides[i][0], sides[i][1].at[place.cp()], slice_sem.at[i]))
+        keeps[i].start()
     for h in range(2):
         cols = slice(h * half, (h + 1) * half)
         first(h, 1).wait_recv()
@@ -238,10 +239,11 @@
         buf[mine, :, cols] = part + r2[h]
     gather = Gather(place, buf, send, recv, core_send, core_recv)
     gather.run()
-    keep = pltpu.make_async_copy(buf.at[mine], slice_out, slice_sem)
-    keep.start()
+    keeps.append(pltpu.make_async_copy(buf.at[mine], slice_out, slice_sem.at[2]))
+    keeps[-1].start()
     gather.finish(out, out_sem)
-    keep.wait()
+    for c in keeps:
+        c.wait()
     for i in range(2):
         side_hop(i, 1).wait_recv()
         side_hop(i, 2).wait_recv()
@@ -264,16 +266,16 @@
             jax.ShapeDtypeStruct((4,) + side_i.shape, I32),
         ],
         in_specs=[vmem, vmem, vmem],
-        out_specs=[hbm, hbm, vmem, vmem],
+        out_specs=[pl.BlockSpec(memory_space=pltpu.HBM)] * 4,
         scratch_shapes=[
             pltpu.VMEM((16, rows, dim), BF16),
             pltpu.VMEM((2, 2, rows, half), BF16),
             pltpu.VMEM((2, rows, half), BF16),
             pltpu.VMEM((2, rows, half), BF16),
             dma((21,)), dma((21,)), dma((24,)), dma((24,)), dma((16,)),
-            *[dma((2, 3))] * 4, dma,
+            *[dma((2, 3))] * 4, dma((3,)),
         ],
-        compiler_params=pltpu.CompilerParams(collective_id=0, has_side_effects=True, vmem_limit_bytes=40 * MIB),
+        compiler_params=pltpu.CompilerParams(collective_id=0, has_side_effects=True, vmem_limit_bytes=FULL),
         name="embed_gather",
     )(picked, side_f, side_i)
 
@@ -318,12 +320,13 @@
     whole = lambda a: pl.BlockSpec(a.shape, lambda i: (0, 0), pipeline_mode=pl.Buffered(1))
     return pl.pallas_call(
         functools.partial(qkv_kernel, head_dim=head_dim),
-        out_shape=[jax.ShapeDtypeStruct((total, n), BF16) for n in (dim, width, width, width)] + [jax.ShapeDtypeStruct((dim, 3 * width), BF16)],
+        out_shape=[jax.ShapeDtypeStruct((total, n), BF16) for n in (dim, width, width, width)],
         grid=(total // block,),
         in_specs=[rows(dim), whole(gain), whole(wq), whole(wk), whole(wv), rows(head_dim)],
-        out_specs=[rows(dim), rows(width), rows(width), rows(width), pl.BlockSpec((dim, 3 * width), lambda i: (0, 0), pipeline_mode=pl.Buffered(1))],
-        compiler_params=pltpu.CompilerParams(vmem_limit_bytes=60 * MIB),
-        cost_estimate=cost(6 * total * dim * width, 4 * total * dim + 6 * dim * width + 6 * total * width),
+        out_specs=[rows(dim), rows(width), rows(width), rows(width)],
+        scratch_shapes=[pltpu.VMEM((dim, 3 * width), BF16)],
+        compiler_params=pltpu.CompilerParams(vmem_limit_bytes=FULL),
+        cost_estimate=cost(6 * total * dim * width),
         name="project_qkv",
     )(x_all, gain, wq, wk, wv, angles)
 
@@ -406,8 +409,8 @@
             out_specs=[pl.BlockSpec((blk, width), lambda i, info, ids: (i, 0)), pl.BlockSpec((blk, 8), lambda i, info, ids: (i, 0))],
             scratch_shapes=[pltpu.VMEM((total // blk, heads, blk, blk), F32)],
         ),
-        compiler_params=pltpu.CompilerParams(vmem_limit_bytes=40 * MIB),
-        cost_estimate=cost(4 * 2 * blk * total * width, 8 * total * width),
+        compiler_params=pltpu.CompilerParams(vmem_limit_bytes=FULL),
+        cost_estimate=cost(4 * 2 * blk * total * width),
         name="attend",
     )(info, ids, q, k, v, doc_col, doc_row)
 
@@ -478,8 +481,8 @@
             out_specs=pl.BlockSpec((blk, 3 * width), lambda i, info, ids: (i, 0)),
             scratch_shapes=[pltpu.VMEM((3, blk, width), F32)],
         ),
-        compiler_params=pltpu.CompilerParams(vmem_limit_bytes=48 * MIB),
-        cost_estimate=cost(14 * 2 * blk * total * width // 2, 12 * total * width),
+        compiler_params=pltpu.CompilerParams(vmem_limit_bytes=FULL),
+        cost_estimate=cost(14 * 2 * blk * total * width // 2),
         name="attend_back",
     )(info, ids, *arrays, angles)
 
@@ -525,8 +528,8 @@
             out_specs=[full, full],
             scratch_shapes=[pltpu.VMEM((rows, dim), BF16), pltpu.VMEM((2,) + pieces[0].shape, BF16), pltpu.VMEM((2,) + pieces[1].shape, BF16), pltpu.SemaphoreType.DMA((2, 2))],
         ),
-        compiler_params=pltpu.CompilerParams(vmem_limit_bytes=56 * MIB),
-        cost_estimate=cost(2 * rows * dim * dim, 2 * dim * dim + 10 * rows * dim),
+        compiler_params=pltpu.CompilerParams(vmem_limit_bytes=FULL),
+        cost_estimate=cost(2 * rows * dim * dim),
         name="out_proj",
     )(info, x_all, att, *pieces, gain)
 
@@ -628,42 +631,24 @@
             pltpu.VMEM((rows, dim), BF16), pltpu.VMEM((2,) + pieces[0].shape, BF16), pltpu.VMEM((2,) + pieces[1].shape, BF16),
             *[dma((n,)) for n in (6, 6, 3, 3, 5, 2, 2)],
         ],
-        compiler_params=pltpu.CompilerParams(collective_id=1, has_side_effects=True, vmem_limit_bytes=48 * MIB),
+        compiler_params=pltpu.CompilerParams(collective_id=1, has_side_effects=True, vmem_limit_bytes=FULL),
         name="att_project",
     )(att, lse, x_all, *pieces, gain)
 
 
-def weight_grad_kernel(info, *refs, pieces, splits, blank):
+def weight_grad_kernel(info, *refs, pieces, splits):
     lhs = refs[:pieces]
     rhs = refs[pieces:2 * pieces]
-    outs = refs[2 * pieces:2 * pieces + splits]
-    if blank:
-        base, zeros, sem = refs[-3:]
-        step = zeros.shape[0]
-        i = pl.program_id(0)
-
-        def fill(n):
-            return pltpu.make_async_copy(zeros, base.at[pl.ds(pl.multiple_of(n * step, step), step), :], sem)
-
-        @pl.when(i == 0)
-        def _():
-            zeros[:] = jnp.zeros_like(zeros)
-
-        each = base.shape[0] // step // pl.num_programs(0)
-        for n in range(each):
-            fill(i * each + n).start()
+    outs = refs[2 * pieces:]
     t = tn(lhs[0][:], rhs[0][:])
     for a, b in zip(lhs[1:], rhs[1:]):
         t += tn(a[:], b[:])
     width = t.shape[1] // splits
     for i, out in enumerate(outs):
         out[:] = t[:, i * width:(i + 1) * width]
-    if blank:
-        for n in range(each):
-            fill(n).wait()
-
-
-def weight_grad(info, lhs, rhs, block=256, splits=1, rows=None, blank=()):
+
+
+def weight_grad(info, lhs, rhs, block=256, splits=1, rows=None):
     def spec(arr, p, cols, moving):
         if arr.ndim == 3:
             return pl.BlockSpec((None, arr.shape[1], cols), lambda i, info: (info[0] ^ p, 0, i if moving else 0))
@@ -674,72 +659,104 @@
     n = len(lhs)
     width = dim // splits
     outs = pl.pallas_call(
-        functools.partial(weight_grad_kernel, pieces=n, splits=splits, blank=blank),
-        out_shape=[jax.ShapeDtypeStruct((rows, width), F32)] * splits + [jax.ShapeDtypeStruct(b, F32) for b in blank],
+        functools.partial(weight_grad_kernel, pieces=n, splits=splits),
+        out_shape=[jax.ShapeDtypeStruct((rows, width), F32)] * splits,
         grid_spec=pltpu.PrefetchScalarGridSpec(
             num_scalar_prefetch=1,
             grid=(pl.cdiv(rows, block),),
             in_specs=[spec(a, p, block, True) for p, a in enumerate(lhs)] + [spec(b, p, dim, False) for p, b in enumerate(rhs)],
-            out_specs=[pl.BlockSpec((block, width), lambda i, info: (i, 0))] * splits + [pl.BlockSpec(memory_space=pl.ANY)] * len(blank),
-            scratch_shapes=[s for b in blank for s in (pltpu.VMEM((200, b[1]), F32), pltpu.SemaphoreType.DMA)],
+            out_specs=[pl.BlockSpec((block, width), lambda i, info: (i, 0))] * splits,
         ),
         compiler_params=pltpu.CompilerParams(vmem_limit_bytes=56 * MIB),
-        cost_estimate=cost(2 * n * tokens * rows * dim, 4 * rows * dim + 2 * n * tokens * (rows + dim)),
+        cost_estimate=cost(2 * n * tokens * rows * dim),
         name="weight_grad",
     )(info, *lhs, *rhs)
     return outs if splits > 1 else outs[0]
 
 
-def mlp_kernel(act, dy, wg, wu, wd, hidden, d_gate, d_up, *rest, limit):
+def mlp_kernel(act, dy, wg, wu, wd, hidden, d_gate, d_up, *rest, limit, tiles):
     i = pl.program_id(0)
     block = wg.shape[0]
-    left = limit - i * block
-    row_ok = lax.broadcasted_iota(I32, (block, 1), 0) < left
-    col_ok = lax.broadcasted_iota(I32, (1, block), 1) < left
     both = rest[-1]
-    both[:block] = jnp.where(row_ok, wg[:], 0).astype(BF16)
-    both[block:] = jnp.where(row_ok, wu[:], 0).astype(BF16)
-    t = nt(act[:], both[:])
-    gate, up = t[:, :block], t[:, block:]
-    dh = jnp.where(col_ok, to_bf16(nt(dy[:], wd[:])), 0)
-    sig = jax.nn.sigmoid(gate)
-    hidden[:] = (gate * sig * up).astype(BF16)
-    dg = (dh * up * sig * (1.0 + gate * (1.0 - sig))).astype(BF16)
-    du = (dh * gate * sig).astype(BF16)
-    d_gate[:] = dg
-    d_up[:] = du
+
+    @pl.when(i < tiles)
+    def _():
+        left = limit - i * block
+        row_ok = lax.broadcasted_iota(I32, (block, 1), 0) < left
+        col_ok = lax.broadcasted_iota(I32, (1, block), 1) < left
+        pair = pl.ds(pl.multiple_of(2 * i * block, block), 2 * block) if tiles < pl.num_programs(0) else slice(2 * block)
+        both[pair] = jnp.concatenate([jnp.where(row_ok, w[:], 0).astype(BF16) for w in (wg, wu)])
+        t = nt(act[:], both[pair])
+        gate, up = t[:, :block], t[:, block:]
+        dh = jnp.where(col_ok, to_bf16(nt(dy[:], wd[:])), 0)
+        sig = jax.nn.sigmoid(gate)
+        hidden[:] = (gate * sig * up).astype(BF16)
+        dg = (dh * up * sig * (1.0 + gate * (1.0 - sig))).astype(BF16)
+        du = (dh * gate * sig).astype(BF16)
+        d_gate[:] = dg
+        d_up[:] = du
+        if len(rest) > 1:
+            rest[1][:, pair] = jnp.concatenate([dg, du], axis=1)
+
     if len(rest) > 1:
         grad, grads = rest[:2]
-        grads[:, :block] = dg
-        grads[:, block:] = du
-        t = nn(grads[:], both[:])
-
-        @pl.when(i == 0)
+
+        @pl.when(i >= tiles)
         def _():
-            grad[:] = t
-
-        @pl.when(i > 0)
-        def _():
-            grad[:] += t
-
-
-def mlp_block(act, dy, wg, wu, wd, with_grad, block=256):
+            wide = grad.shape[1]
+            grad[:] = nn(grads[:], both[:, pl.ds(pl.multiple_of((i - tiles) * wide, wide), wide)])
+
+
+def mlp_block(act, dy, wg, wu, wd, with_grad, block=256, wide=512):
     rows, dim = act.shape
     limit = wg.shape[0]
-    cols = pl.BlockSpec((rows, block), lambda i: (0, i))
-    tile = pl.BlockSpec((block, dim), lambda i: (i, 0))
-    whole = pl.BlockSpec((rows, dim), lambda i: (0, 0))
+    tiles = pl.cdiv(limit, block)
+    steps = tiles + with_grad * dim // wide
+    cols = pl.BlockSpec((rows, block), lambda i: (0, jnp.minimum(i, tiles - 1)))
+    tile = pl.BlockSpec((block, dim), lambda i: (jnp.minimum(i, tiles - 1), 0))
+    full = pl.BlockSpec((rows, dim), lambda i: (0, 0), pipeline_mode=pl.Buffered(1))
+    deep = 2 * block * (tiles if with_grad else 1)
     return pl.pallas_call(
-        functools.partial(mlp_kernel, limit=limit),
-        out_shape=[jax.ShapeDtypeStruct((rows, pl.cdiv(limit, block) * block), BF16)] * 3 + [jax.ShapeDtypeStruct((rows, dim), F32)] * with_grad,
-        grid=(pl.cdiv(limit, block),),
-        in_specs=[whole, whole, tile, tile, tile],
-        out_specs=[cols] * 3 + [whole] * with_grad,
-        scratch_shapes=[pltpu.VMEM((rows, 2 * block), BF16)] * with_grad + [pltpu.VMEM((2 * block, dim), BF16)],
-        compiler_params=pltpu.CompilerParams(vmem_limit_bytes=48 * MIB),
-        cost_estimate=cost((6 + 4 * with_grad) * rows * dim * limit, 4 * dim * limit + 6 * rows * limit + 10 * rows * dim),
+        functools.partial(mlp_kernel, limit=limit, tiles=tiles),
+        out_shape=[jax.ShapeDtypeStruct((rows, tiles * block), BF16)] * 3 + [jax.ShapeDtypeStruct((rows, dim), F32)] * with_grad,
+        grid=(steps,),
+        in_specs=[full, full, tile, tile, tile],
+        out_specs=[cols] * 3 + [pl.BlockSpec((rows, wide), lambda i: (0, jnp.maximum(i - tiles, 0)))] * with_grad,
+        scratch_shapes=[pltpu.VMEM((rows, deep), BF16)] * with_grad + [pltpu.VMEM((deep, dim), BF16)],
+        compiler_params=pltpu.CompilerParams(vmem_limit_bytes=FULL),
+        cost_estimate=cost((6 + 4 * with_grad) * rows * dim * limit),
         name="mlp_block",
     )(act, dy, wg, wu, wd)
+
+
+def zero_kernel(after, out, zeros, sem):
+    zeros[:] = jnp.zeros_like(zeros)
+    step = zeros.shape[0]
+    count = out.shape[0] // step
+
+    def send(i, c):
+        pltpu.make_async_copy(zeros, out.at[pl.ds(pl.multiple_of(i * step, step), step), :], sem).start()
+        return c
+
+    def wait(i, c):
+        pltpu.make_async_copy(zeros, out.at[pl.ds(0, step), :], sem).wait()
+        return c
+
+    lax.fori_loop(0, count, send, 0)
+    lax.fori_loop(0, count, wait, 0)
+
+
+def zero_rows(after, rows, dim, step=200):
+    return pl.pallas_call(
+        zero_kernel,
+        out_shape=jax.ShapeDtypeStruct((rows, dim), F32),
+        in_specs=[pl.BlockSpec(memory_space=pltpu.SMEM)],
+        out_specs=pl.BlockSpec(memory_space=pl.ANY),
+        scratch_shapes=[pltpu.VMEM((step, dim), F32), pltpu.SemaphoreType.DMA],
+        compiler_params=pltpu.CompilerParams(vmem_limit_bytes=8 * MIB),
+        cost_estimate=cost(rows * dim),
+        name="zero_rows",
+    )(after)
 
 
 def scatter_kernel(order, sid, runs, bounds, rows, base_hbm, out_hbm, sums, row_sem, sum_sem):
@@ -804,7 +821,7 @@
             scratch_shapes=[pltpu.VMEM((tokens // 2, dim), F32), pltpu.SemaphoreType.DMA, pltpu.SemaphoreType.DMA],
         ),
         input_output_aliases={5: 0},
-        compiler_params=pltpu.CompilerParams(vmem_limit_bytes=40 * MIB),
+        compiler_params=pltpu.CompilerParams(vmem_limit_bytes=FULL),
         name="scatter_rows",
     )(order, sid, runs, bounds, grads, base)
 
@@ -854,7 +871,7 @@
         wo_rest = join(wo_far, "tp")
 
         dy_x = swap(barrier((dy, x_all))[0], x_swap)
-        act_a, query, key, value, w_qkv = project_qkv(x_all, gain_a[None, :], w_q, w_k, w_v, angles)
+        act_a, query, key, value = project_qkv(x_all, gain_a[None, :], w_q, w_k, w_v, angles)
 
         blk = span // 2
         blocks = total // blk
@@ -896,14 +913,8 @@
         d_resid_all = join(d_resid.astype(BF16), both)
         out_part = nn(hidden[:, :ffn], w_down)
         d_resid_all, grad_down, att_heads, out_part = barrier((d_resid_all, grad_down, att_heads, out_part))
-        tp_swap = lambda arr, k: swap(arr, [(i, i ^ k) for i in range(tp_count)], "tp")
-        tp_part = lambda arr, k: lax.dynamic_slice_in_dim(arr, (tp_rank ^ k) * part, part, 0)
-        others = range(1, tp_count)
-        arrived = [tp_swap(tp_part(out_part, k), k) for k in others]
-        out_slice = res_part + tp_part(out_part, 0)
-        for piece in arrived:
-            out_slice = out_slice + piece
-        out_slice = out_slice.astype(BF16)
+        out_slice = add_up(out_part)
+        out_slice = (res_part + out_slice).astype(BF16)
 
         d_att = nt(d_resid_all, w_o)
         d_att_b = d_att.astype(BF16)
@@ -915,21 +926,21 @@
             return jnp.transpose(arr.reshape(8, blocks, blk), (1, 0, 2))
 
         dqkv = attend_back(info, ints, query, key, value, d_att_b, doc_col, doc_row, lse_all, by_block(lse_all.T), delta.T, by_block(delta), angles, blk)
-        d_act_a = nt(dqkv, w_qkv)
+        d_act_a = sum(nt(dqkv[:, i * width:(i + 1) * width], w) for i, w in enumerate((w_q, w_k, w_v)))
+        d_act_a, out_slice = barrier((d_act_a, out_slice))
         d_act_a = add_up(d_act_a)
         dqkv_x = swap(dqkv, x_swap)
         dqkvs = (dqkv, swap(dqkv, core_swap), dqkv_x, swap(dqkv_x, core_swap))
         grad_out = weight_grad(info, head_parts, [d_resid_all.reshape(cp_count, span, dim)] * 4)
         d_act_a, dqkv_x, grad_out, grad_up = barrier((d_act_a, dqkv_x, grad_out, grad_up))
-        d_act_a, out_slice = barrier((d_act_a, out_slice))
         d_act_a = to_bf16(d_act_a)
-        y_parts = [tp_swap(out_slice, k) for k in others]
         normed_a, inv_a = rms_stats(x_slice.astype(F32))
         grad_gain_a = jnp.sum(d_act_a * normed_a, axis=0)
         d_embed = d_resid + rms_back(d_act_a * gain_a, normed_a, inv_a)
         payload = jnp.concatenate([d_embed, jnp.stack([grad_gain_a, grad_gain_b] * 4)])
         gathered = join(payload, both)
-        *grad_qkv, base = weight_grad(info, [act_a.reshape(cp_count, span, dim)] * 4, dqkvs, splits=3, blank=((rows, dim),))
+        grad_qkv = weight_grad(info, [act_a.reshape(cp_count, span, dim)] * 4, dqkvs, splits=3)
+        tok_all = barrier((tok_all, d_act_a))[0]
         slot_ids = jnp.arange(total, dtype=I32)
         before = (tok_all[None, :] < tok_all[:, None]) | ((tok_all[None, :] == tok_all[:, None]) & (slot_ids[None, :] < slot_ids[:, None]))
         rank = jnp.sum(before.astype(I32), axis=1)
@@ -940,10 +951,10 @@
         sid = jnp.sum(jnp.where(at_rank, tok_all[None, :], 0), axis=1) - tp_rank * rows
         order = order + 8 * (order // part)
         bounds = jnp.stack([jnp.sum((tok_all < tp_rank * rows).astype(I32)), jnp.sum((tok_all < (tp_rank + 1) * rows).astype(I32))])
+        base = zero_rows(barrier((bounds, d_act_a))[0], rows, dim)
         gathered, grad_qkv, grad_gate, runs, order, sid, bounds, base = barrier((gathered, grad_qkv, grad_gate, runs, order, sid, bounds, base))
-        layer_out = jnp.concatenate([out_slice] * tp_count)
-        for k, piece in zip(others, y_parts):
-            layer_out = lax.dynamic_update_slice_in_dim(layer_out, piece, (tp_rank ^ k) * part, 0)
+        out_slice = barrier((out_slice, gathered))[0]
+        layer_out = join(out_slice, "tp")
         gain_grads = jnp.sum(gathered.reshape(cp_count * tp_count, part + 8, dim)[:, part:part + 2], axis=0)
         grad_table = scatter_rows(order, sid, runs, bounds, gathered, base, total)
         return (layer_out, grad_table, *grad_qkv, grad_out, grad_gate.T, grad_up.T, grad_down, gain_grads[0], gain_grads[1])

time: 793 us -> 718 us (0.905)
  waiting for transfers between devices: 181 us -> 139 us
  local copies, waits for them, and re-layouts: 60.8 us -> 38.3 us
  starting transfers between devices: 22.3 us -> 8.9 us
    ppermute x23 -> x17, waiting for transfers between devices: 171 us -> 110 us  [compute(): swap = lambda arr, pairs, axis='cp': lax.ppermute(arr, axis, pairs)]
    pallas_call x5, Pallas kernels: 149 us -> 127 us  [weight_grad(): pl.pallas_call(functools.partial(weight_grad_kernel, pieces=n, splits=spl...]
    unnamed x96 -> x45, local copies, waits for them, and re-layouts: 27.9 us -> 7.39 us
    pallas_call x2 -> x3, Pallas kernels: 64.8 us -> 80.8 us  [the longest x2 53.9 us: mlp_block(): pl.pallas_call(functools.partial(mlp_kernel, limit=limit, tiles=tiles), o...]
    ppermute x23 -> x17, starting transfers between devices: 21.3 us -> 7.9 us  [compute(): swap = lambda arr, pairs, axis='cp': lax.ppermute(arr, axis, pairs)]
    all_gather x4 -> x5, waiting for transfers between devices: 10.2 us -> 22.3 us  [compute(): join = lambda arr, axis: lax.all_gather(arr, axis, axis=0, tiled=True)]
    dot_general x3 -> x5, matrix products: 32.8 us -> 34.8 us  [contract(): lax.dot_general(a, b, (((ca,), (cb,)), ((), ())), preferred_element_type=...]
  transfers between devices with their start and end apart: 29 -> 25, of which waited for: 7 -> 11; matrix products, arithmetic and copies ran while one was open for 9% -> 13% of each run, Pallas kernels for 38% -> 51%
where the time goes in v8:
time: 718 us; the launch traced here: 712 us
  Pallas kernels  431 us (60%)
  waiting for transfers between devices  139 us (19%)
  other arithmetic  40.1 us (6%)
  matrix products  39.4 us (5%)
  local copies, waits for them, and re-layouts  38.3 us (5%)
  between operations  14.7 us (2%)
  starting transfers between devices  8.9 us (1%)
    pallas_call x5, Pallas kernels, weight_grad(): pl.pallas_call(functools.partial(weight_grad_kernel, pieces=n, splits=spl...  127 us
    ppermute x17, waiting for transfers between devices, compute(): swap = lambda arr, pairs, axis='cp': lax.ppermute(arr, axis, pairs)  110 us
    pallas_call x1, Pallas kernels, embed_gather(): pl.pallas_call(embed_kernel, out_shape=[jax.ShapeDtypeStruct((16 * rows,...  75.6 us
    pallas_call x2, Pallas kernels, mlp_block(): pl.pallas_call(functools.partial(mlp_kernel, limit=limit, tiles=tiles), o...  53.9 us
    pallas_call x1, Pallas kernels, att_project(): pl.pallas_call(att_kernel, out_shape=[jax.ShapeDtypeStruct((4, rows, widt...  35.1 us
    dot_general x5, matrix products, contract(): lax.dot_general(a, b, (((ca,), (cb,)), ((), ())), preferred_element_type=...  34.8 us
    pallas_call x1, Pallas kernels, project_qkv(): pl.pallas_call(functools.partial(qkv_kernel, head_dim=head_dim), out_shap...  31.9 us
    pallas_call x1, Pallas kernels, scatter_rows(): pl.pallas_call(scatter_kernel, out_shape=jax.ShapeDtypeStruct((rows, dim)...  31.4 us
  transfers between devices with their start and end apart: 25, of which 11 were waited for; matrix products, arithmetic and copies ran while one was open for 13% of the time, Pallas kernels for 51%

profile of v8, /device:TPU:0, one launch (start us, length us, event | category | flops | bytes accessed | tf_op | source)
XLA Modules:
  0.0 712.1 jit_solution(9726576512675552934)
XLA Ops:
  11.9 6.8 gather_fusion
  22.5 75.6 %embed_gather.1 = (bf16[2048,2560]{1,0:T(8,128)(2,1)}, bf16[128,2560]{1,0:T(8,128)(2,1)}, f32[4,512,128]{2,1,0:T(8,128)}, s32[4,8,512]{2,1,0:T(8,128)}) custom-call(bf16[4,128,2560]{2,1,0:T(8,128)(2,1)} %select_select_fusion.picked, f32[512,128]{1,0:T(8,128)} %pad_maximum_fusion.side_f, s32[8,512]{1,0:T(8,128)} %stack.50.side_i), custom_call_target="tpu_custom_call" | custom-call | tf_op jit(solution)/shard_map/embed_gather/pallas_call | solution.py:260
  105.7 31.9 %project_qkv.1 = (bf16[2048,2560]{1,0:T(8,128)(2,1)}, bf16[2048,640]{1,0:T(8,128)(2,1)}, bf16[2048,640]{1,0:T(8,128)(2,1)}, bf16[2048,640]{1,0:T(8,128)(2,1)}) custom-call(bf16[2048,2560]{1,0:T(8,128)(2,1)} %get-tuple-element.67.x.x_all, f32[1,2560]{1,0:T(1,128)} %broadcast_in_dim.88.gain, bf16[2560,640]{1,0:T(8,128)(2,1)} %wq.1, bf16[2560,640]{1,0:T(8,128)(2,1)} %wk.1, ...), custom_call_target="tpu_custom_call" | custom-call | flops 20132659200 | bytes 39321600 | tf_op jit(solution)/shard_map/project_qkv/pallas_call | solution.py:321
  137.6 10.6 %attend.1 = (bf16[512,640]{1,0:T(8,128)(2,1)}, f32[512,8]{1,0:T(8,128)}) custom-call(s32[2]{0:T(128)} %pad_add_fusion.info, s32[4,8,512]{2,1,0:T(8,128)} %get-tuple-element.66.ids, bf16[2048,640]{1,0:T(8,128)(2,1)} %get-tuple-element.69.q, bf16[2048,640]{1,0:T(8,128)(2,1)} %get-tuple-element.70.k, bf16[2048,640]{1,0:T(8,128)(2,1)} %get-tuple-element.71.v, ...), custom_call_target="tpu_custom_call" | custom-call | flops 2684354560 | bytes 5242880 | tf_op jit(solution)/shard_map/attend/pallas_call | solution.py:402
  148.3 10.0 %all-gather.8.cloned.1.call-done.b0 = bf16[2560,1024]{1,0:T(8,128)(2,1)} async-done(((bf16[640,1024]{1,0:T(8,128)(2,1)}), bf16[2560,1024]{1,0:T(8,128)(2,1)}) %all-gather.8.cloned.1.call-update) | async-done | bytes 5242896 | tf_op jit(solution)/shard_map/all_gather | solution.py:851
  158.3 35.1 %att_project.1 = (bf16[4,512,640]{2,1,0:T(8,128)(2,1)}, f32[4,512,8]{2,1,0:T(8,128)}, f32[512,2560]{1,0:T(8,128)}, bf16[512,2560]{1,0:T(8,128)(2,1)}, bf16[2560,...) custom-call(bf16[512,640]{1,0:T(8,128)(2,1)} %get-tuple-element.72.att.refs_0_, f32[512,8]{1,0:T(8,128)} %get-tuple-element.73.lse, ...), custom_call_target="tpu_custom_call" | custom-call | tf_op jit(solution)/shard_map/att_project/pallas_call | solution.py:625
  193.4 32.6 %mlp_block.2 = (bf16[512,1792]{1,0:T(8,128)(2,1)}, bf16[512,1792]{1,0:T(8,128)(2,1)}, bf16[512,1792]{1,0:T(8,128)(2,1)}, f32[512,2560]{1,0:T(8,128)}) custom-call(bf16[512,2560]{1,0:T(8,128)(2,1)} %get-tuple-element.76.act.refs_4_, bf16[512,2560]{1,0:T(8,128)(2,1)} %refs_4_.1, bf16[1728,2560]{1,0:T(8,128)(2,1)} %bitcast.66, bf16[1728,2560]{1,0:T(8,128)(2,1)} %bitcast.68, ...), custom_call_target="tpu_custom_call" | custom-call | flops 22649241600 | bytes 44236800 | tf_op jit(solution)/shard_map/mlp_block/pallas_call | solution.py:719
  231.6 55.9 %collective-permute-done.att = bf16[4,512,640]{2,1,0:T(8,128)(2,1)} collective-permute-done((bf16[4,512,640]{2,1,0:T(8,128)(2,1)S(1)}, bf16[4,512,640]{2,1,0:T(8,128)(2,1)}, u32[]{:S(2)}, u32[]{:S(2)}) %collective-permute-start) | collective-permute-done | bytes 2621472 | tf_op jit(solution)/shard_map/ppermute | solution.py:853
  287.5 16.6 %out_proj.1 = (f32[512,2560]{1,0:T(8,128)}, bf16[512,2560]{1,0:T(8,128)(2,1)}) custom-call(s32[2]{0:T(128)} %pad_add_fusion.info, bf16[2048,2560]{1,0:T(8,128)(2,1)} %get-tuple-element.67.x.x_all, bf16[4,512,640]{2,1,0:T(8,128)(2,1)} %collective-permute-done.att, bf16[2560,256]{1,0:T(8,128)(2,1)} %all-gather.6.cloned.1.call-done.a0, ...), custom_call_target="tpu_custom_call" | custom-call | flops 6710886400 | bytes 13107200 | tf_op jit(solution)/shard_map/out_proj/pallas_call | solution.py:521
  304.2 37.3 %collective-permute-done.1.dy.refs_6_ = bf16[512,2560]{1,0:T(8,128)(2,1)} collective-permute-done((bf16[512,2560]{1,0:T(8,128)(2,1)}, bf16[512,2560]{1,0:T(8,128)(2,1)}, u32[]{:S(2)}, u32[]{:S(2)}) %collective-permute-start.1) | collective-permute-done | bytes 2621472 | tf_op jit(solution)/shard_map/ppermute | solution.py:853
  341.5 21.3 %mlp_block.3 = (bf16[512,1792]{1,0:T(8,128)(2,1)}, bf16[512,1792]{1,0:T(8,128)(2,1)}, bf16[512,1792]{1,0:T(8,128)(2,1)}) custom-call(bf16[512,2560]{1,0:T(8,128)(2,1)} %get-tuple-element.81.act.refs_6_, bf16[512,2560]{1,0:T(8,128)(2,1)} %collective-permute-done.1.dy.refs_6_, bf16[1728,2560]{1,0:T(8,128)(2,1)} %bitcast.67, bf16[1728,2560]{1,0:T(8,128)(2,1)} %bitcast.69, ...), custom_call_target="tpu_custom_call" | custom-call | flops 13589544960 | bytes 26542080 | tf_op jit(solution)/shard_map/mlp_block/pallas_call | solution.py:719
  375.2 11.4 %fusion.6 = f32[512,2560]{1,0:T(8,128)} fusion(bf16[1728,2560]{1,0:T(8,128)(2,1)} %wd.3, bf16[512,1792]{1,0:T(8,128)(2,1)} %get-tuple-element.87.refs_0_), kind=kOutput, calls=%fused_computation.18 | convolution fusion | flops 4529848320 | bytes 15925248 | tf_op jit(solution)/shard_map/dot_general | solution.py:32
  387.6 27.1 %weight_grad.5 = f32[1728,2560]{1,0:T(8,128)} custom-call(s32[2]{0:T(128)} %pad_add_fusion.info, bf16[512,1792]{1,0:T(8,128)(2,1)} %get-tuple-element.87.refs_0_, bf16[512,1792]{1,0:T(8,128)(2,1)} %collective-permute-done.2.refs_1_, bf16[512,1792]{1,0:T(8,128)(2,1)} %get-tuple-element.88.refs_2_, bf16[512,1792]{1,0:T(8,128)(2,1)} %collective-permute-done.3.refs_3_, ...), custom_call_target="tpu_custom_call" | custom-call | flops 18119393280 | bytes 35389440 | tf_op jit(solution)/shard_map/weight_grad/pallas_call | solution.py:661
  414.7 9.5 %all-gather.10.cloned.1.call-done = bf16[2048,2560]{1,0:T(8,128)(2,1)} async-done(((bf16[128,2560]{1,0:T(8,128)(2,1)}), bf16[2048,2560]{1,0:T(8,128)(2,1)}) %all-gather.10.cloned.1.call-update) | async-done | bytes 10485776 | tf_op jit(solution)/shard_map/all_gather | solution.py:851
  426.4 12.0 %convolution_convert_fusion.do = bf16[2048,640]{1,0:T(8,128)(2,1)S(1)} fusion(bf16[2048,2560]{1,0:T(8,128)(2,1)} %all-gather.10.cloned.1.call-done, bf16[640,2560]{1,0:T(8,128)(2,1)} %param.23), kind=kOutput, calls=%fused_computation.16 | convolution fusion | flops 6712197120 | bytes 16384000 | tf_op jit(solution)/shard_map/dot_general | solution.py:32
  445.9 22.6 %attend_back.1.refs_4_ = bf16[512,1920]{1,0:T(8,128)(2,1)} custom-call(s32[2]{0:T(128)} %pad_add_fusion.info, s32[4,8,512]{2,1,0:T(8,128)} %get-tuple-element.66.ids, bf16[2048,640]{1,0:T(8,128)(2,1)} %get-tuple-element.69.q, bf16[2048,640]{1,0:T(8,128)(2,1)} %get-tuple-element.70.k, bf16[2048,640]{1,0:T(8,128)(2,1)} %get-tuple-element.71.v, ...), custom_call_target="tpu_custom_call" | custom-call | flops 4697620480 | bytes 9175040 | tf_op jit(solution)/shard_map/attend_back/pallas_call | solution.py:474
  491.4 8.0 %collective-permute-done.9.refs_1_ = bf16[512,1792]{1,0:T(8,128)(2,1)S(1)} collective-permute-done((bf16[512,1792]{1,0:T(8,128)(2,1)}, bf16[512,1792]{1,0:T(8,128)(2,1)S(1)}, u32[]{:S(2)}, u32[]{:S(2)}) %collective-permute-start.9) | collective-permute-done | bytes 1835040 | tf_op jit(solution)/shard_map/ppermute | solution.py:853
  502.2 27.4 %weight_grad.7 = f32[1728,2560]{1,0:T(8,128)} custom-call(s32[2]{0:T(128)} %pad_add_fusion.info, bf16[512,1792]{1,0:T(8,128)(2,1)} %get-tuple-element.96.refs_0_, bf16[512,1792]{1,0:T(8,128)(2,1)} %copy-done.21, bf16[512,1792]{1,0:T(8,128)(2,1)} %get-tuple-element.97.refs_2_, bf16[512,1792]{1,0:T(8,128)(2,1)} %collective-permute-done.10.refs_3_, ...), custom_call_target="tpu_custom_call" | custom-call | flops 18119393280 | bytes 35389440 | tf_op jit(solution)/shard_map/weight_grad/pallas_call | solution.py:661
  529.6 15.0 %weight_grad.6 = f32[640,2560]{1,0:T(8,128)} custom-call(s32[2]{0:T(128)} %pad_add_fusion.info, bf16[512,640]{1,0:T(8,128)(2,1)} %get-tuple-element.72.att.refs_0_, bf16[512,640]{1,0:T(8,128)(2,1)} %copy-done.7, bf16[512,640]{1,0:T(8,128)(2,1)} %copy-done.6, bf16[512,640]{1,0:T(8,128)(2,1)} %copy-done.8, bf16[4,512,2560]{2,1,0:T(8,128)(2,1)} %bitcast.41, ...), custom_call_target="tpu_custom_call" | custom-call | flops 6710886400 | bytes 13107200 | tf_op jit(solution)/shard_map/weight_grad/pallas_call | solution.py:661
  563.1 27.6 %weight_grad.9 = f32[1728,2560]{1,0:T(8,128)} custom-call(s32[2]{0:T(128)} %pad_add_fusion.info, bf16[512,1792]{1,0:T(8,128)(2,1)} %get-tuple-element.103.refs_0_, bf16[512,1792]{1,0:T(8,128)(2,1)} %collective-permute-done.15.refs_1_, bf16[512,1792]{1,0:T(8,128)(2,1)} %get-tuple-element.104.refs_2_, bf16[512,1792]{1,0:T(8,128)(2,1)} %collective-permute-done.16.refs_3_, ...), custom_call_target="tpu_custom_call" | custom-call | flops 18119393280 | bytes 35389440 | tf_op jit(solution)/shard_map/weight_grad/pallas_call | solution.py:661
  590.7 29.7 %weight_grad.8 = (f32[2560,640]{1,0:T(8,128)}, f32[2560,640]{1,0:T(8,128)}, f32[2560,640]{1,0:T(8,128)}) custom-call(s32[2]{0:T(128)} %pad_add_fusion.info, bf16[4,512,2560]{2,1,0:T(8,128)(2,1)} %bitcast.74, bf16[4,512,2560]{2,1,0:T(8,128)(2,1)} %bitcast.75, bf16[4,512,2560]{2,1,0:T(8,128)(2,1)} %bitcast.76, bf16[4,512,2560]{2,1,0:T(8,128)(2,1)} %bitcast.77, ...), custom_call_target="tpu_custom_call" | custom-call | flops 20132659200 | bytes 39321600 | tf_op jit(solution)/shard_map/weight_grad/pallas_call | solution.py:661
  622.5 26.9 %zero_rows.1.base_hbm = f32[8000,2560]{1,0:T(8,128)} custom-call(s32[2]{0:T(128)S(1)} %pad_add_fusion.1.after.bounds), custom_call_target="tpu_custom_call" | custom-call | flops 20480000 | bytes 40000 | tf_op jit(solution)/shard_map/zero_rows/pallas_call | solution.py:750
  654.7 7.8 %select_reduce_fusion = (s32[2048]{0:T(1024)S(1)}, s32[2048]{0:T(1024)S(1)}, s32[2048]{0:T(1024)S(1)}) fusion(s32[2048]{0:T(1024)S(1)} %convert_reduce_fusion, s32[2048]{0:T(1024)S(1)} %bitcast.65), kind=kLoop, calls=%fused_computation.4 | loop fusion | flops 33548288 | bytes 40960 | tf_op jit(solution)/shard_map/reduce_sum | solution.py:951
  665.4 31.4 %scatter_rows.1 = f32[8000,2560]{1,0:T(8,128)} custom-call(s32[2048]{0:T(1024)} %get-tuple-element.109.order, s32[2048]{0:T(1024)} %get-tuple-element.110.sid, s32[2048]{0:T(1024)} %select_reduce_fusion.2.runs, s32[2]{0:T(128)} %copy-done, f32[2176,2560]{1,0:T(8,128)} %all-gather.12.cloned.1.call-done.rows, ...), custom_call_target="tpu_custom_call", output_to_operand_aliasing={{}: (5, {})} | custom-call | tf_op jit(solution)/shard_map/scatter_rows/pallas_call | solution.py:813
  (147 shorter events, 107.3 us)
Async XLA Ops:
  7.2 141.1 %all-gather.6.cloned.1.call-start = ((), (), s32[]{:S(2)}) async-start(), calls=%async_computation.3 | async-start | bytes 1638400 | tf_op jit(solution)/shard_map/all_gather | solution.py:851
  9.0 149.3 %all-gather.8.cloned.1.call-start = ((), (), s32[]{:S(2)}) async-start(), calls=%async_computation.4 | async-start | bytes 6553600 | tf_op jit(solution)/shard_map/all_gather | solution.py:851
  100.6 262.2 %reduce-scatter.4.cloned.1.call-start = ((), (), s32[]{:S(2)}) async-start(), calls=%async_computation.5 | async-start | bytes 6553600 | tf_op jit(solution)/shard_map/reduce_scatter | solution.py:852
  225.9 198.2 %all-gather.10.cloned.1.call-start = ((), (), s32[]{:S(2)}) async-start(), calls=%async_computation.6 | async-start | bytes 11141120 | tf_op jit(solution)/shard_map/all_gather | solution.py:851
  227.7 59.8 %collective-permute-start = (bf16[4,512,640]{2,1,0:T(8,128)(2,1)S(1)}, bf16[4,512,640]{2,1,0:T(8,128)(2,1)}, u32[]{:S(2)}, u32[]{:S(2)}) collective-permute-start(bf16[4,512,640]{2,1,0:T(8,128)(2,1)S(1)} %copy-done.20), channel_id=1, source_target_pairs={{0,2},{1,3},{2,0},{3,1},{4,6},{5,7},{6,4},{7,5},{8,10},{9,11},{10,... | collective-permute-start | bytes 7864328 | tf_op jit(solution)/shard_map/ppermute | solution.py:853
  228.8 112.7 %collective-permute-start.1 = (bf16[512,2560]{1,0:T(8,128)(2,1)}, bf16[512,2560]{1,0:T(8,128)(2,1)}, u32[]{:S(2)}, u32[]{:S(2)}) collective-permute-start(bf16[512,2560]{1,0:T(8,128)(2,1)} %refs_4_.1), channel_id=1, source_target_pairs={{0,2},{1,3},{2,0},{3,1},{4,6},{5,7},{6,4},{7,5},{8,10},{9,11},{10,... | collective-permute-start | bytes 7864328 | tf_op jit(solution)/shard_map/ppermute | solution.py:853
  367.9 117.3 %reduce-scatter.6.cloned.1.call-start = ((), (), s32[]{:S(2)}) async-start(), calls=%async_computation.7 | async-start | bytes 6553600 | tf_op jit(solution)/shard_map/reduce_scatter | solution.py:852
  368.0 19.6 %collective-permute-start.4 = (bf16[512,2560]{1,0:T(8,128)(2,1)}, bf16[512,2560]{1,0:T(8,128)(2,1)}, u32[]{:S(2)}, u32[]{:S(2)}) collective-permute-start(bf16[512,2560]{1,0:T(8,128)(2,1)} %refs_4_.1), channel_id=1, source_target_pairs={{0,1},{1,0},{2,3},{3,2},{4,5},{5,4},{6,7},{7,6},{8,9},{9,8},{10,11... | collective-permute-start | bytes 7864328 | tf_op jit(solution)/shard_map/ppermute | solution.py:853
  368.5 19.1 %collective-permute-start.5 = (bf16[512,2560]{1,0:T(8,128)(2,1)}, bf16[512,2560]{1,0:T(8,128)(2,1)}, u32[]{:S(2)}, u32[]{:S(2)}) collective-permute-start(bf16[512,2560]{1,0:T(8,128)(2,1)} %collective-permute-done.1.dy.refs_6_), channel_id=1, source_target_pairs={{0,1},{1,0},{2,3},{3,2},{4,5},{5,4},{6,7},{7,6},{8,9},{9,8},{10,11... | collective-permute-start | bytes 7864328 | tf_op jit(solution)/shard_map/ppermute | solution.py:853
  372.1 15.5 %collective-permute-start.2 = (bf16[512,1792]{1,0:T(8,128)(2,1)}, bf16[512,1792]{1,0:T(8,128)(2,1)}, u32[]{:S(2)}, u32[]{:S(2)}) collective-permute-start(bf16[512,1792]{1,0:T(8,128)(2,1)} %get-tuple-element.87.refs_0_), channel_id=1, source_target_pairs={{0,1},{1,0},{2,3},{3,2},{4,5},{5,4},{6,7},{7,6},{8,9},{9,8},{10,11... | collective-permute-start | bytes 5505032 | tf_op jit(solution)/shard_map/ppermute | solution.py:853
  372.6 15.0 %collective-permute-start.3 = (bf16[512,1792]{1,0:T(8,128)(2,1)}, bf16[512,1792]{1,0:T(8,128)(2,1)}, u32[]{:S(2)}, u32[]{:S(2)}) collective-permute-start(bf16[512,1792]{1,0:T(8,128)(2,1)} %get-tuple-element.88.refs_2_), channel_id=1, source_target_pairs={{0,1},{1,0},{2,3},{3,2},{4,5},{5,4},{6,7},{7,6},{8,9},{9,8},{10,11... | collective-permute-start | bytes 5505032 | tf_op jit(solution)/shard_map/ppermute | solution.py:853
  374.7 11.9 %collective-permute-start.7 = (bf16[512,640]{1,0:T(8,128)(2,1)S(1)}, bf16[512,640]{1,0:T(8,128)(2,1)S(1)}, u32[]{:S(2)}, u32[]{:S(2)}) collective-permute-start(bf16[512,640]{1,0:T(8,128)(2,1)S(1)} %get-tuple-element.134.refs_2_), channel_id=1, source_target_pairs={{0,1},{1,0},{2,3},{3,2},{4,5},{5,4},{6,7},{7,6},{8,9},{9,8},{10,11... | collective-permute-start | bytes 1966088 | tf_op jit(solution)/shard_map/ppermute | solution.py:853
  424.2 122.1 %reduce-scatter.8.cloned.1.call-start = ((), (), s32[]{:S(2)}) async-start(), calls=%async_computation.8 | async-start | bytes 6553600 | tf_op jit(solution)/shard_map/reduce_scatter | solution.py:852
  487.9 177.5 %all-gather.12.cloned.1.call-start = ((), (), s32[]{:S(2)}) async-start(), calls=%async_computation.9 | async-start | bytes 23674880 | tf_op jit(solution)/shard_map/all_gather | solution.py:851
  487.9 11.5 %collective-permute-start.11 = (bf16[512,2560]{1,0:T(8,128)(2,1)}, bf16[512,2560]{1,0:T(8,128)(2,1)S(1)}, u32[]{:S(2)}, u32[]{:S(2)}) collective-permute-start(bf16[512,2560]{1,0:T(8,128)(2,1)} %get-tuple-element.76.act.refs_4_), channel_id=1, source_target_pairs={{0,1},{1,0},{2,3},{3,2},{4,5},{5,4},{6,7},{7,6},{8,9},{9,8},{10,11... | collective-permute-start | bytes 7864328 | tf_op jit(solution)/shard_map/ppermute | solution.py:853
  488.0 11.5 %collective-permute-start.12 = (bf16[512,2560]{1,0:T(8,128)(2,1)}, bf16[512,2560]{1,0:T(8,128)(2,1)}, u32[]{:S(2)}, u32[]{:S(2)}) collective-permute-start(bf16[512,2560]{1,0:T(8,128)(2,1)} %get-tuple-element.81.act.refs_6_), channel_id=1, source_target_pairs={{0,1},{1,0},{2,3},{3,2},{4,5},{5,4},{6,7},{7,6},{8,9},{9,8},{10,11... | collective-permute-start | bytes 7864328 | tf_op jit(solution)/shard_map/ppermute | solution.py:853
  488.5 11.0 %collective-permute-start.9 = (bf16[512,1792]{1,0:T(8,128)(2,1)}, bf16[512,1792]{1,0:T(8,128)(2,1)S(1)}, u32[]{:S(2)}, u32[]{:S(2)}) collective-permute-start(bf16[512,1792]{1,0:T(8,128)(2,1)} %get-tuple-element.96.refs_0_), channel_id=1, source_target_pairs={{0,1},{1,0},{2,3},{3,2},{4,5},{5,4},{6,7},{7,6},{8,9},{9,8},{10,11... | collective-permute-start | bytes 5505032 | tf_op jit(solution)/shard_map/ppermute | solution.py:853
  488.5 13.7 %collective-permute-start.10 = (bf16[512,1792]{1,0:T(8,128)(2,1)}, bf16[512,1792]{1,0:T(8,128)(2,1)}, u32[]{:S(2)}, u32[]{:S(2)}) collective-permute-start(bf16[512,1792]{1,0:T(8,128)(2,1)} %get-tuple-element.97.refs_2_), channel_id=1, source_target_pairs={{0,1},{1,0},{2,3},{3,2},{4,5},{5,4},{6,7},{7,6},{8,9},{9,8},{10,11... | collective-permute-start | bytes 5505032 | tf_op jit(solution)/shard_map/ppermute | solution.py:853
  489.2 55.4 %collective-permute-start.8 = (bf16[512,1920]{1,0:T(8,128)(2,1)}, bf16[512,1920]{1,0:T(8,128)(2,1)}, u32[]{:S(2)}, u32[]{:S(2)}) collective-permute-start(bf16[512,1920]{1,0:T(8,128)(2,1)} %attend_back.1.refs_4_), channel_id=1, source_target_pairs={{0,2},{1,3},{2,0},{3,1},{4,6},{5,7},{6,4},{7,5},{8,10},{9,11},{10,... | collective-permute-start | bytes 5898248 | tf_op jit(solution)/shard_map/ppermute | solution.py:853
  556.3 145.4 %all-gather.14.cloned.1.call-start = ((), (), s32[]{:S(2)}) async-start(), calls=%async_computation.10 | async-start | bytes 3276800 | tf_op jit(solution)/shard_map/all_gather | solution.py:851
  556.4 4.2 collective-permute-start.15
  556.4 6.7 collective-permute-start.16
  556.9 33.8 %collective-permute-start.13 = (bf16[512,1920]{1,0:T(8,128)(2,1)S(1)}, bf16[512,1920]{1,0:T(8,128)(2,1)}, u32[]{:S(2)}, u32[]{:S(2)}) collective-permute-start(bf16[512,1920]{1,0:T(8,128)(2,1)S(1)} %copy-done.12), channel_id=1, source_target_pairs={{0,1},{1,0},{2,3},{3,2},{4,5},{5,4},{6,7},{7,6},{8,9},{9,8},{10,11... | collective-permute-start | bytes 5898248 | tf_op jit(solution)/shard_map/ppermute | solution.py:853
  557.0 33.8 %collective-permute-start.14 = (bf16[512,1920]{1,0:T(8,128)(2,1)}, bf16[512,1920]{1,0:T(8,128)(2,1)}, u32[]{:S(2)}, u32[]{:S(2)}) collective-permute-start(bf16[512,1920]{1,0:T(8,128)(2,1)} %collective-permute-done.8.refs_6_), channel_id=1, source_target_pairs={{0,1},{1,0},{2,3},{3,2},{4,5},{5,4},{6,7},{7,6},{8,9},{9,8},{10,11... | collective-permute-start | bytes 5898248 | tf_op jit(solution)/shard_map/ppermute | solution.py:853
  (23 other events, 196.8 us)
Sparse Core Ops, SparseCore 0:
  10.4 34.8 all-gather.5
  100.7 57.5 all-gather.7
  226.1 57.2 reduce-scatter.3
  368.0 56.1 all-gather.9
  427.6 57.5 reduce-scatter.5
  488.5 57.7 reduce-scatter.7
  556.4 94.4 all-gather.11
  665.6 36.0 all-gather.13

commit v9 on v8

--- a/solution.py
+++ b/solution.py
@@ -487,63 +487,13 @@
     )(info, ids, *arrays, angles)
 
 
-def out_proj_kernel(info, x, att, a0, b0, a1, b1, gain, res, act, wide, abuf, bbuf, sems):
-    tp, _, width = att.shape
-    na, nb = a0.shape[1], b0.shape[1]
-    sets = ((a0, b0), (a1, b1))
-
-    def copies(i):
-        return (pltpu.make_async_copy(sets[i][0], abuf.at[i], sems.at[i, 0]), pltpu.make_async_copy(sets[i][1], bbuf.at[i], sems.at[i, 1]))
-
-    for i in range(2):
-        for c in copies(i):
-            c.start()
-    for t in range(tp):
-        wide[:, t * width:(t + 1) * width] = att[t]
-    for i in range(2):
-        start = (info[1] ^ i) * (na + nb)
-        first, second = copies(i)
-        first.wait()
-        cols = pl.ds(pl.multiple_of(start, 128), na)
-        res[:, cols] = x[:, cols].astype(F32) + nn(wide[:], abuf[i])
-        second.wait()
-        cols = pl.ds(pl.multiple_of(start + na, 128), nb)
-        res[:, cols] = x[:, cols].astype(F32) + nn(wide[:], bbuf[i])
-    h = res[:]
-    inv = lax.rsqrt(mean_row(h * h) + NORM_EPS)
-    act[:] = (h * inv * gain[:]).astype(BF16)
-
-
-def out_proj(info, flip, x_all, att, pieces, gain):
-    _, rows, _ = att.shape
-    dim = x_all.shape[1]
-    full = pl.BlockSpec((rows, dim), lambda i, info: (0, 0))
-    return pl.pallas_call(
-        out_proj_kernel,
-        out_shape=[jax.ShapeDtypeStruct((rows, dim), F32), jax.ShapeDtypeStruct((rows, dim), BF16)],
-        grid_spec=pltpu.PrefetchScalarGridSpec(
-            num_scalar_prefetch=1,
-            grid=(1,),
-            in_specs=[pl.BlockSpec((rows, dim), lambda i, info: (info[0] ^ flip, 0)), whole(att)] + [pl.BlockSpec(memory_space=pl.ANY)] * 4 + [whole(gain)],
-            out_specs=[full, full],
-            scratch_shapes=[pltpu.VMEM((rows, dim), BF16), pltpu.VMEM((2,) + pieces[0].shape, BF16), pltpu.VMEM((2,) + pieces[1].shape, BF16), pltpu.SemaphoreType.DMA((2, 2))],
-        ),
-        compiler_params=pltpu.CompilerParams(vmem_limit_bytes=FULL),
-        cost_estimate=cost(2 * rows * dim * dim),
-        name="out_proj",
-    )(info, x_all, att, *pieces, gain)
-
-
-def att_kernel(att, lse, x_all, a0, b0, gain, parts, lse_out, res, act, a1, b1, x, abuf, bbuf, send, recv, lse_send, lse_recv, load, swap_send, swap_recv):
+def att_kernel(att, lse, x_all, w, gain, lse_out, res, act, parts, x, wide, send, recv, lse_send, lse_recv, load, swap_send, swap_recv):
     place = Place()
     rows, width = att.shape
-    na, nb = a0.shape[1], b0.shape[1]
+    half = w.shape[1]
     mine = place.cp()
-    loads = [pltpu.make_async_copy(x_all.at[pl.ds(mine * rows, rows), :], x, load.at[4])]
-    for i, (src, dst) in enumerate(((a0, abuf.at[0]), (b0, bbuf.at[0]), (a1, abuf.at[1]), (b1, bbuf.at[1]))):
-        loads.append(pltpu.make_async_copy(src, dst, load.at[i]))
-    early, late = loads[:3], loads[3:]
-    for c in early:
+    loads = [pltpu.make_async_copy(src, dst, load.at[i]) for i, (src, dst) in enumerate(((x_all.at[pl.ds(mine * rows, rows), :], x), (w, wide.at[0])))]
+    for c in loads:
         c.start()
     place.meet(("y", "z", "x", "core"))
     started = []
@@ -567,47 +517,39 @@
         copy.start()
         started.append(copy)
 
-    swaps = [pltpu.make_async_remote_copy(src_ref=src, dst_ref=dst, send_sem=swap_send.at[i], recv_sem=swap_recv.at[i], device_id=place.device(("core",)), device_id_type=MESH) for i, (src, dst) in enumerate(((a0, a1), (b0, b1)))]
+    other = pltpu.make_async_remote_copy(src_ref=w, dst_ref=wide.at[1], send_sem=swap_send, recv_sem=swap_recv, device_id=place.device(("core",)), device_id_type=MESH)
     for step in range(2):
         for p in range(2):
             go(hop(p, (), near[(p + step) % 2]))
-    for c in swaps:
-        go(c)
+    go(other)
     go(lse_hop(0))
     go(lse_hop(1))
     lse_out[mine] = lse[:]
-    parts[place.tp()] = att[:]
-    for c in early:
+    for c in loads:
         c.wait()
 
-    def add(slot, halves=(0, 1), first=False):
+    def add(piece, slot, halves=(0, 1), first=False):
         for i in halves:
-            start = place.coord("core", ("core",) if i else ()) * (na + nb)
-            k = pl.ds(pl.multiple_of(slot * width, width), width)
-            for buf, at, n in ((abuf, 0, na), (bbuf, na, nb)):
-                cols = pl.ds(pl.multiple_of(start + at, 128), n)
-                t = nn(parts[slot], buf[i, k, :])
-                res[:, cols] = t + (x[:, cols].astype(F32) if first else res[:, cols])
-
-    add(place.tp(), (0,), True)
-    for c in swaps:
-        c.wait_recv()
-    for c in late:
-        c.start()
+            cols = pl.ds(pl.multiple_of(place.coord("core", ("core",) if i else ()) * half, 128), half)
+            t = nn(piece, wide[i, pl.ds(pl.multiple_of(slot * width, width), width), :])
+            res[:, cols] = t + (x[:, cols].astype(F32) if first else res[:, cols])
+
+    add(att[:], place.tp(), (0,), True)
     for p in range(2):
         hop(p, (), near[p]).wait_recv()
         go(hop(p, (near[p],), near[1 - p]))
     lse_hop(0).wait_recv()
     go(lse_hop(2))
-    for c in late:
-        c.wait()
-    add(place.tp(), (1,), True)
+    other.wait_recv()
+    add(att[:], place.tp(), (1,), True)
     for p in (1, 0):
         hop(p, (), near[1 - p]).wait_recv()
-        add(place.tp((near[1 - p],)))
+        slot = place.tp((near[1 - p],))
+        add(parts[slot], slot)
     for p in range(2):
         hop(p, (near[p],), near[1 - p]).wait_recv()
-    add(place.tp(near))
+    slot = place.tp(near)
+    add(parts[slot], slot)
     h = res[:]
     act[:] = (h * lax.rsqrt(mean_row(h * h) + NORM_EPS) * gain[:]).astype(BF16)
     lse_hop(1).wait_recv()
@@ -616,7 +558,7 @@
         c.wait_send()
 
 
-def att_project(att, lse, x_all, pieces, gain):
+def att_project(att, lse, x_all, w, gain):
     rows, width = att.shape
     dim = x_all.shape[1]
     dma = pltpu.SemaphoreType.DMA
@@ -624,16 +566,16 @@
     hbm = pl.BlockSpec(memory_space=pl.ANY)
     return pl.pallas_call(
         att_kernel,
-        out_shape=[jax.ShapeDtypeStruct((4, rows, width), BF16), jax.ShapeDtypeStruct((4,) + lse.shape, F32), jax.ShapeDtypeStruct((rows, dim), F32), jax.ShapeDtypeStruct((rows, dim), BF16)] + [jax.ShapeDtypeStruct(p.shape, BF16) for p in pieces],
-        in_specs=[vmem, vmem] + [hbm] * 3 + [vmem],
-        out_specs=[vmem] * 4 + [hbm, hbm],
+        out_shape=[jax.ShapeDtypeStruct((4,) + lse.shape, F32), jax.ShapeDtypeStruct((rows, dim), F32), jax.ShapeDtypeStruct((rows, dim), BF16)],
+        in_specs=[vmem, vmem, hbm, hbm, vmem],
+        out_specs=[vmem] * 3,
         scratch_shapes=[
-            pltpu.VMEM((rows, dim), BF16), pltpu.VMEM((2,) + pieces[0].shape, BF16), pltpu.VMEM((2,) + pieces[1].shape, BF16),
-            *[dma((n,)) for n in (6, 6, 3, 3, 5, 2, 2)],
+            pltpu.VMEM((4, rows, width), BF16), pltpu.VMEM((rows, dim), BF16), pltpu.VMEM((2,) + w.shape, BF16),
+            *[dma((n,)) for n in (6, 6, 3, 3, 2)], dma, dma,
         ],
         compiler_params=pltpu.CompilerParams(collective_id=1, has_side_effects=True, vmem_limit_bytes=FULL),
         name="att_project",
-    )(att, lse, x_all, *pieces, gain)
+    )(att, lse, x_all, w, gain)
 
 
 def weight_grad_kernel(info, *refs, pieces, splits):
@@ -857,9 +799,6 @@
         picked = jnp.where(owned[:, None], jnp.take(table, safe_ids, axis=0), 0).astype(BF16)
         info = jnp.stack([cp_rank, core]).astype(I32)
         half = dim // 2
-        near = 256
-        wo_half = lax.dynamic_slice_in_dim(w_o, core * half, half, 1)
-        wo_near = join(wo_half[:, :near], "tp")
         angle = pos.astype(F32)[:, None] * inv_freq[None, :]
         side_f = jnp.concatenate([jnp.cos(angle), jnp.sin(angle)], axis=1)
         side_i = jnp.stack([tokens, doc_id] * 4)
@@ -867,8 +806,8 @@
         angles = angles.reshape(total, head_dim)
         tok_all = ints[:, 0, :].reshape(total)
         doc_all = ints[:, 1, :].reshape(total)
-        wo_far = barrier((wo_half[:, near:], x_all))[0]
-        wo_rest = join(wo_far, "tp")
+        wo_half = barrier((lax.dynamic_slice_in_dim(w_o, core * half, half, 1), x_all))[0]
+        wo_half = join(wo_half, "tp")
 
         dy_x = swap(barrier((dy, x_all))[0], x_swap)
         act_a, query, key, value = project_qkv(x_all, gain_a[None, :], w_q, w_k, w_v, angles)
@@ -879,22 +818,32 @@
         doc_row = doc_all.reshape(blocks, 1, blk)
         attended, lse = attend(info, ints, query, key, value, doc_col, doc_row, head_dim, blk)
 
-        gain_row = gain_b[None, :]
-        att_parts, lse_all, residual, act_b, *wo_other = att_project(attended, lse, x_all, (wo_near, wo_rest), gain_row)
+        tok_all = barrier((tok_all, attended))[0]
+        slot_ids = jnp.arange(total, dtype=I32)
+        before = (tok_all[None, :] < tok_all[:, None]) | ((tok_all[None, :] == tok_all[:, None]) & (slot_ids[None, :] < slot_ids[:, None]))
+        rank = jnp.sum(before.astype(I32), axis=1)
+        count = jnp.sum((tok_all[None, :] == tok_all[:, None]).astype(I32), axis=1)
+        at_rank = rank[None, :] == slot_ids[:, None]
+        runs = jnp.sum(jnp.where(at_rank, count[None, :], 0), axis=1)
+        order = jnp.sum(jnp.where(at_rank, slot_ids[None, :], 0), axis=1)
+        sid = jnp.sum(jnp.where(at_rank, tok_all[None, :], 0), axis=1) - tp_rank * rows
+        order = order + 8 * (order // part)
+        bounds = jnp.stack([jnp.sum((tok_all < tp_rank * rows).astype(I32)), jnp.sum((tok_all < (tp_rank + 1) * rows).astype(I32))])
+        wo_half, runs, order, sid, bounds = barrier((wo_half, runs, order, sid, bounds))
+        heads_x = swap(attended, x_swap)
+        lse_all, residual, act_b = att_project(attended, lse, x_all, wo_half, gain_b[None, :])
         lse_all = lse_all.reshape(total, 8)
-        att_x = swap(att_parts, x_swap)
-
+        act_x = swap(act_b, x_swap)
         wg, wu = w_gate.T, w_up.T
         ffn = wg.shape[0]
         hidden, d_gate, d_up, d_act_b = mlp_block(act_b, dy, wg, wu, w_down, True)
         d_act_b = add_up(d_act_b)
-        act_x = out_proj(info, 2, x_all, att_x, (wo_near, wo_rest, *wo_other), gain_row)[1]
         hidden_x, d_gate_x, d_up_x = mlp_block(act_x, dy_x, wg, wu, w_down, False)
-        d_act_b, hidden_x, d_gate_x, d_up_x = barrier((d_act_b, hidden_x, d_gate_x, d_up_x))
+        out_part = nn(hidden[:, :ffn], w_down)
+        d_act_b, hidden_x, d_gate_x, d_up_x, out_part = barrier((d_act_b, hidden_x, d_gate_x, d_up_x, out_part))
         d_act_b = to_bf16(d_act_b)
         acts, dys, hiddens, d_gates, d_ups = [(a, swap(a, core_swap), b, swap(b, core_swap)) for a, b in (
             (act_b, act_x), (dy, dy_x), (hidden, hidden_x), (d_gate, d_gate_x), (d_up, d_up_x))]
-        heads_x = lax.dynamic_index_in_dim(att_x, tp_rank, 0, keepdims=False)
         head_parts = (attended, swap(attended, core_swap), heads_x, swap(heads_x, core_swap))
         att_heads = jnp.zeros((total, width), BF16)
         for k, piece in enumerate(head_parts):
@@ -911,7 +860,6 @@
         grad_gain_b = jnp.sum(d_act_b * normed_b, axis=0)
         d_resid = mine(dy).astype(F32) + rms_back(d_act_b * gain_b, normed_b, inv_b)
         d_resid_all = join(d_resid.astype(BF16), both)
-        out_part = nn(hidden[:, :ffn], w_down)
         d_resid_all, grad_down, att_heads, out_part = barrier((d_resid_all, grad_down, att_heads, out_part))
         out_slice = add_up(out_part)
         out_slice = (res_part + out_slice).astype(BF16)
@@ -940,21 +888,13 @@
         payload = jnp.concatenate([d_embed, jnp.stack([grad_gain_a, grad_gain_b] * 4)])
         gathered = join(payload, both)
         grad_qkv = weight_grad(info, [act_a.reshape(cp_count, span, dim)] * 4, dqkvs, splits=3)
-        tok_all = barrier((tok_all, d_act_a))[0]
-        slot_ids = jnp.arange(total, dtype=I32)
-        before = (tok_all[None, :] < tok_all[:, None]) | ((tok_all[None, :] == tok_all[:, None]) & (slot_ids[None, :] < slot_ids[:, None]))
-        rank = jnp.sum(before.astype(I32), axis=1)
-        count = jnp.sum((tok_all[None, :] == tok_all[:, None]).astype(I32), axis=1)
-        at_rank = rank[None, :] == slot_ids[:, None]
-        runs = jnp.sum(jnp.where(at_rank, count[None, :], 0), axis=1)
-        order = jnp.sum(jnp.where(at_rank, slot_ids[None, :], 0), axis=1)
-        sid = jnp.sum(jnp.where(at_rank, tok_all[None, :], 0), axis=1) - tp_rank * rows
-        order = order + 8 * (order // part)
-        bounds = jnp.stack([jnp.sum((tok_all < tp_rank * rows).astype(I32)), jnp.sum((tok_all < (tp_rank + 1) * rows).astype(I32))])
         base = zero_rows(barrier((bounds, d_act_a))[0], rows, dim)
-        gathered, grad_qkv, grad_gate, runs, order, sid, bounds, base = barrier((gathered, grad_qkv, grad_gate, runs, order, sid, bounds, base))
+        gathered, grad_qkv, grad_gate, base = barrier((gathered, grad_qkv, grad_gate, base))
         out_slice = barrier((out_slice, gathered))[0]
-        layer_out = join(out_slice, "tp")
+        layer_out = jnp.concatenate([out_slice] * tp_count)
+        for k in range(1, tp_count):
+            piece = swap(out_slice, [(i, i ^ k) for i in range(tp_count)], "tp")
+            layer_out = lax.dynamic_update_slice_in_dim(layer_out, piece, (tp_rank ^ k) * part, 0)
         gain_grads = jnp.sum(gathered.reshape(cp_count * tp_count, part + 8, dim)[:, part:part + 2], axis=0)
         grad_table = scatter_rows(order, sid, runs, bounds, gathered, base, total)
         return (layer_out, grad_table, *grad_qkv, grad_out, grad_gate.T, grad_up.T, grad_down, gain_grads[0], gain_grads[1])

time: 718 us -> 717 us (level)
  Pallas kernels: 431 us -> 411 us
  waiting for transfers between devices: 139 us -> 155 us
    ppermute x17 -> x21, waiting for transfers between devices: 110 us -> 139 us  [compute(): swap = lambda arr, pairs, axis='cp': lax.ppermute(arr, axis, pairs)]
    pallas_call x2 -> x1, Pallas kernels: 51.7 us -> 35.9 us  [att_project(): pl.pallas_call(att_kernel, out_shape=[jax.ShapeDtypeStruct((4,) + lse.sha...]
    all_gather x5 -> x3, waiting for transfers between devices: 22.3 us -> 10.5 us  [compute(): join = lambda arr, axis: lax.all_gather(arr, axis, axis=0, tiled=True)]
    pallas_call x1, Pallas kernels: 75.6 us -> 68.4 us  [embed_gather(): pl.pallas_call(embed_kernel, out_shape=[jax.ShapeDtypeStruct((16 * rows,...]
  transfers between devices with their start and end apart: 25 -> 27, of which waited for: 11 -> 10; matrix products, arithmetic and copies ran while one was open for 13% -> 11% of each run, Pallas kernels for 51% -> 38%
where the time goes in v9:
time: 717 us; the launch traced here: 711 us
  Pallas kernels  411 us (57%)
  waiting for transfers between devices  155 us (22%)
  matrix products  40.6 us (6%)
  other arithmetic  39.6 us (6%)
  local copies, waits for them, and re-layouts  36 us (5%)
  between operations  15 us (2%)
  starting transfers between devices  14.7 us (2%)
    ppermute x21, waiting for transfers between devices, compute(): swap = lambda arr, pairs, axis='cp': lax.ppermute(arr, axis, pairs)  139 us
    pallas_call x5, Pallas kernels, weight_grad(): pl.pallas_call(functools.partial(weight_grad_kernel, pieces=n, splits=spl...  129 us
    pallas_call x1, Pallas kernels, embed_gather(): pl.pallas_call(embed_kernel, out_shape=[jax.ShapeDtypeStruct((16 * rows,...  68.4 us
    pallas_call x2, Pallas kernels, mlp_block(): pl.pallas_call(functools.partial(mlp_kernel, limit=limit, tiles=tiles), o...  54.1 us
    dot_general x5, matrix products, contract(): lax.dot_general(a, b, (((ca,), (cb,)), ((), ())), preferred_element_type=...  36 us
    pallas_call x1, Pallas kernels, att_project(): pl.pallas_call(att_kernel, out_shape=[jax.ShapeDtypeStruct((4,) + lse.sha...  35.9 us
    pallas_call x1, Pallas kernels, project_qkv(): pl.pallas_call(functools.partial(qkv_kernel, head_dim=head_dim), out_shap...  32.6 us
    pallas_call x1, Pallas kernels, scatter_rows(): pl.pallas_call(scatter_kernel, out_shape=jax.ShapeDtypeStruct((rows, dim)...  30.7 us
  transfers between devices with their start and end apart: 27, of which 10 were waited for; matrix products, arithmetic and copies ran while one was open for 11% of the time, Pallas kernels for 38%

profile of v9, /device:TPU:0, one launch (start us, length us, event | category | flops | bytes accessed | tf_op | source)
XLA Modules:
  0.0 711.2 jit_solution(8310051382874421226)
XLA Ops:
  8.6 6.8 gather_fusion
  22.5 68.4 %embed_gather.1 = (bf16[2048,2560]{1,0:T(8,128)(2,1)}, bf16[128,2560]{1,0:T(8,128)(2,1)}, f32[4,512,128]{2,1,0:T(8,128)}, s32[4,8,512]{2,1,0:T(8,128)}) custom-call(bf16[4,128,2560]{2,1,0:T(8,128)(2,1)} %select_select_fusion.picked, f32[512,128]{1,0:T(8,128)} %pad_maximum_fusion.1.side_f, s32[8,512]{1,0:T(8,128)} %stack.50.side_i), custom_call_target="tpu_custom_call" | custom-call | tf_op jit(solution)/shard_map/embed_gather/pallas_call | solution.py:260
  94.8 32.6 %project_qkv.1 = (bf16[2048,2560]{1,0:T(8,128)(2,1)}, bf16[2048,640]{1,0:T(8,128)(2,1)}, bf16[2048,640]{1,0:T(8,128)(2,1)}, bf16[2048,640]{1,0:T(8,128)(2,1)}) custom-call(bf16[2048,2560]{1,0:T(8,128)(2,1)} %get-tuple-element.65.x.x_all, f32[1,2560]{1,0:T(1,128)} %broadcast_in_dim.88.gain, bf16[2560,640]{1,0:T(8,128)(2,1)} %wq.1, bf16[2560,640]{1,0:T(8,128)(2,1)} %wk.1, ...), custom_call_target="tpu_custom_call" | custom-call | flops 20132659200 | bytes 39321600 | tf_op jit(solution)/shard_map/project_qkv/pallas_call | solution.py:321
  127.4 10.2 %attend.1 = (bf16[512,640]{1,0:T(8,128)(2,1)}, f32[512,8]{1,0:T(8,128)}) custom-call(s32[2]{0:T(128)} %pad_add_fusion.info, s32[4,8,512]{2,1,0:T(8,128)} %get-tuple-element.64.ids, bf16[2048,640]{1,0:T(8,128)(2,1)} %get-tuple-element.67.q, bf16[2048,640]{1,0:T(8,128)(2,1)} %get-tuple-element.68.k, bf16[2048,640]{1,0:T(8,128)(2,1)} %get-tuple-element.69.v, ...), custom_call_target="tpu_custom_call" | custom-call | flops 2684354560 | bytes 5242880 | tf_op jit(solution)/shard_map/attend/pallas_call | solution.py:402
  145.5 8.2 %select_reduce_fusion = (s32[2048]{0:T(1024)S(1)}, s32[2048]{0:T(1024)S(1)}, s32[2048]{0:T(1024)S(1)}) fusion(s32[2048]{0:T(1024)S(1)} %convert_reduce_fusion, s32[2048]{0:T(1024)S(1)} %bitcast.62), kind=kLoop, calls=%fused_computation.4 | loop fusion | flops 33548288 | bytes 40960 | tf_op jit(solution)/shard_map/reduce_sum | solution.py:829
  159.5 35.9 %att_project.1 = (f32[4,512,8]{2,1,0:T(8,128)}, f32[512,2560]{1,0:T(8,128)}, bf16[512,2560]{1,0:T(8,128)(2,1)}) custom-call(bf16[512,640]{1,0:T(8,128)(2,1)} %get-tuple-element.70.att.refs_0_, f32[512,8]{1,0:T(8,128)} %get-tuple-element.71.lse, bf16[2048,2560]{1,0:T(8,128)(2,1)} %get-tuple-element.65.x.x_all, ...), custom_call_target="tpu_custom_call" | custom-call | tf_op jit(solution)/shard_map/att_project/pallas_call | solution.py:567
  195.4 32.8 %mlp_block.2 = (bf16[512,1792]{1,0:T(8,128)(2,1)}, bf16[512,1792]{1,0:T(8,128)(2,1)}, bf16[512,1792]{1,0:T(8,128)(2,1)}, f32[512,2560]{1,0:T(8,128)}) custom-call(bf16[512,2560]{1,0:T(8,128)(2,1)} %get-tuple-element.76.act.refs_4_, bf16[512,2560]{1,0:T(8,128)(2,1)} %refs_4_.1, bf16[1728,2560]{1,0:T(8,128)(2,1)} %bitcast.63, bf16[1728,2560]{1,0:T(8,128)(2,1)} %bitcast.65, ...), custom_call_target="tpu_custom_call" | custom-call | flops 22649241600 | bytes 44236800 | tf_op jit(solution)/shard_map/mlp_block/pallas_call | solution.py:661
  233.8 11.7 %fusion.6 = f32[512,2560]{1,0:T(8,128)} fusion(bf16[1728,2560]{1,0:T(8,128)(2,1)} %wd.3, bf16[512,1792]{1,0:T(8,128)(2,1)} %get-tuple-element.82.refs_0_), kind=kOutput, calls=%fused_computation.19 | convolution fusion | flops 4529848320 | bytes 15925248 | tf_op jit(solution)/shard_map/dot_general | solution.py:32
  245.5 44.6 %collective-permute-done.1.dy.refs_6_ = bf16[512,2560]{1,0:T(8,128)(2,1)} collective-permute-done((bf16[512,2560]{1,0:T(8,128)(2,1)S(1)}, bf16[512,2560]{1,0:T(8,128)(2,1)}, u32[]{:S(2)}, u32[]{:S(2)}) %collective-permute-start.1) | collective-permute-done | bytes 2621472 | tf_op jit(solution)/shard_map/ppermute | solution.py:795
  290.1 53.7 %collective-permute-done.act.refs_6_ = bf16[512,2560]{1,0:T(8,128)(2,1)} collective-permute-done((bf16[512,2560]{1,0:T(8,128)(2,1)}, bf16[512,2560]{1,0:T(8,128)(2,1)}, u32[]{:S(2)}, u32[]{:S(2)}) %collective-permute-start) | collective-permute-done | bytes 2621472 | tf_op jit(solution)/shard_map/ppermute | solution.py:795
  343.8 21.3 %mlp_block.3 = (bf16[512,1792]{1,0:T(8,128)(2,1)}, bf16[512,1792]{1,0:T(8,128)(2,1)}, bf16[512,1792]{1,0:T(8,128)(2,1)}) custom-call(bf16[512,2560]{1,0:T(8,128)(2,1)} %collective-permute-done.act.refs_6_, bf16[512,2560]{1,0:T(8,128)(2,1)} %collective-permute-done.1.dy.refs_6_, bf16[1728,2560]{1,0:T(8,128)(2,1)} %bitcast.64, bf16[1728,2560]{1,0:T(8,128)(2,1)} %bitcast.66, ...), custom_call_target="tpu_custom_call" | custom-call | flops 13589544960 | bytes 26542080 | tf_op jit(solution)/shard_map/mlp_block/pallas_call | solution.py:661
  371.4 8.7 %collective-permute-done.6.refs_1_ = bf16[512,640]{1,0:T(8,128)(2,1)S(1)} collective-permute-done((bf16[512,640]{1,0:T(8,128)(2,1)S(1)}, bf16[512,640]{1,0:T(8,128)(2,1)S(1)}, u32[]{:S(2)}, u32[]{:S(2)}) %collective-permute-start.6) | collective-permute-done | bytes 655392 | tf_op jit(solution)/shard_map/ppermute | solution.py:795
  381.9 22.2 %collective-permute-done.7.refs_2_ = bf16[512,640]{1,0:T(8,128)(2,1)S(1)} collective-permute-done((bf16[512,640]{1,0:T(8,128)(2,1)S(1)}, bf16[512,640]{1,0:T(8,128)(2,1)S(1)}, u32[]{:S(2)}, u32[]{:S(2)}) %collective-permute-start.7) | collective-permute-done | bytes 655392 | tf_op jit(solution)/shard_map/ppermute | solution.py:795
  410.5 28.8 %weight_grad.5 = f32[1728,2560]{1,0:T(8,128)} custom-call(s32[2]{0:T(128)} %pad_add_fusion.info, bf16[512,1792]{1,0:T(8,128)(2,1)} %get-tuple-element.82.refs_0_, bf16[512,1792]{1,0:T(8,128)(2,1)} %collective-permute-done.2.refs_1_, bf16[512,1792]{1,0:T(8,128)(2,1)} %get-tuple-element.84.refs_2_, bf16[512,1792]{1,0:T(8,128)(2,1)} %collective-permute-done.3.refs_3_, ...), custom_call_target="tpu_custom_call" | custom-call | flops 18119393280 | bytes 35389440 | tf_op jit(solution)/shard_map/weight_grad/pallas_call | solution.py:603
  441.4 12.9 %convolution_convert_fusion.do = bf16[2048,640]{1,0:T(8,128)(2,1)S(1)} fusion(bf16[2048,2560]{1,0:T(8,128)(2,1)} %all-gather.6.cloned.1.call-done, bf16[640,2560]{1,0:T(8,128)(2,1)} %param.23), kind=kOutput, calls=%fused_computation.16 | convolution fusion | flops 6712197120 | bytes 16384000 | tf_op jit(solution)/shard_map/dot_general | solution.py:32
  461.8 22.1 %attend_back.1.refs_4_ = bf16[512,1920]{1,0:T(8,128)(2,1)} custom-call(s32[2]{0:T(128)} %pad_add_fusion.info, s32[4,8,512]{2,1,0:T(8,128)} %get-tuple-element.64.ids, bf16[2048,640]{1,0:T(8,128)(2,1)} %get-tuple-element.67.q, bf16[2048,640]{1,0:T(8,128)(2,1)} %get-tuple-element.68.k, bf16[2048,640]{1,0:T(8,128)(2,1)} %get-tuple-element.69.v, ...), custom_call_target="tpu_custom_call" | custom-call | flops 4697620480 | bytes 9175040 | tf_op jit(solution)/shard_map/attend_back/pallas_call | solution.py:474
  503.9 6.9 collective-permute-done.10.refs_1_
  513.5 27.7 %weight_grad.7 = f32[1728,2560]{1,0:T(8,128)} custom-call(s32[2]{0:T(128)} %pad_add_fusion.info, bf16[512,1792]{1,0:T(8,128)(2,1)} %get-tuple-element.93.refs_0_, bf16[512,1792]{1,0:T(8,128)(2,1)} %copy-done.22, bf16[512,1792]{1,0:T(8,128)(2,1)} %get-tuple-element.94.refs_2_, bf16[512,1792]{1,0:T(8,128)(2,1)} %collective-permute-done.11.refs_3_, ...), custom_call_target="tpu_custom_call" | custom-call | flops 18119393280 | bytes 35389440 | tf_op jit(solution)/shard_map/weight_grad/pallas_call | solution.py:603
  541.2 15.5 %weight_grad.6 = f32[640,2560]{1,0:T(8,128)} custom-call(s32[2]{0:T(128)} %pad_add_fusion.info, bf16[512,640]{1,0:T(8,128)(2,1)} %get-tuple-element.70.att.refs_0_, bf16[512,640]{1,0:T(8,128)(2,1)} %copy-done.7, bf16[512,640]{1,0:T(8,128)(2,1)} %copy-done.8, bf16[512,640]{1,0:T(8,128)(2,1)} %collective-permute-done.8.refs_3_, ...), custom_call_target="tpu_custom_call" | custom-call | flops 6710886400 | bytes 13107200 | tf_op jit(solution)/shard_map/weight_grad/pallas_call | solution.py:603
  571.1 27.8 %zero_rows.1.base_hbm = f32[8000,2560]{1,0:T(8,128)} custom-call(s32[2]{0:T(128)S(1)} %pad_add_fusion.1.after.bounds), custom_call_target="tpu_custom_call" | custom-call | flops 20480000 | bytes 40000 | tf_op jit(solution)/shard_map/zero_rows/pallas_call | solution.py:692
  599.0 27.1 %weight_grad.9 = f32[1728,2560]{1,0:T(8,128)} custom-call(s32[2]{0:T(128)} %pad_add_fusion.info, bf16[512,1792]{1,0:T(8,128)(2,1)} %get-tuple-element.100.refs_0_, bf16[512,1792]{1,0:T(8,128)(2,1)} %collective-permute-done.16.refs_1_, bf16[512,1792]{1,0:T(8,128)(2,1)} %get-tuple-element.101.refs_2_, bf16[512,1792]{1,0:T(8,128)(2,1)} %collective-permute-done.17.refs_3_, ...), custom_call_target="tpu_custom_call" | custom-call | flops 18119393280 | bytes 35389440 | tf_op jit(solution)/shard_map/weight_grad/pallas_call | solution.py:603
  627.3 29.7 %weight_grad.8 = (f32[2560,640]{1,0:T(8,128)}, f32[2560,640]{1,0:T(8,128)}, f32[2560,640]{1,0:T(8,128)}) custom-call(s32[2]{0:T(128)} %pad_add_fusion.info, bf16[4,512,2560]{2,1,0:T(8,128)(2,1)} %bitcast.71, bf16[4,512,2560]{2,1,0:T(8,128)(2,1)} %bitcast.72, bf16[4,512,2560]{2,1,0:T(8,128)(2,1)} %bitcast.73, bf16[4,512,2560]{2,1,0:T(8,128)(2,1)} %bitcast.74, ...), custom_call_target="tpu_custom_call" | custom-call | flops 20132659200 | bytes 39321600 | tf_op jit(solution)/shard_map/weight_grad/pallas_call | solution.py:603
  657.1 7.6 %all-gather.8.cloned.1.call-done.rows = f32[2176,2560]{1,0:T(8,128)} async-done(((f32[136,2560]{1,0:T(8,128)}), f32[2176,2560]{1,0:T(8,128)}) %all-gather.8.cloned.1.call-update) | async-done | bytes 22282256 | tf_op jit(solution)/shard_map/all_gather | solution.py:793
  668.2 30.7 %scatter_rows.1 = f32[8000,2560]{1,0:T(8,128)} custom-call(s32[2048]{0:T(1024)} %get-tuple-element.106.order, s32[2048]{0:T(1024)} %get-tuple-element.107.sid, s32[2048]{0:T(1024)} %select_reduce_fusion.2.runs, s32[2]{0:T(128)} %copy-done, f32[2176,2560]{1,0:T(8,128)} %all-gather.8.cloned.1.call-done.rows, ...), custom_call_target="tpu_custom_call", output_to_operand_aliasing={{}: (5, {})} | custom-call | tf_op jit(solution)/shard_map/scatter_rows/pallas_call | solution.py:755
  (152 shorter events, 102.3 us)
Async XLA Ops:
  7.2 152.3 %all-gather.4.cloned.1.call-start = ((), (), s32[]{:S(2)}) async-start(), calls=%async_computation.3 | async-start | bytes 8192000 | tf_op jit(solution)/shard_map/all_gather | solution.py:793
  90.9 274.2 %reduce-scatter.4.cloned.1.call-start = ((), (), s32[]{:S(2)}) async-start(), calls=%async_computation.4 | async-start | bytes 6553600 | tf_op jit(solution)/shard_map/reduce_scatter | solution.py:794
  228.2 211.1 %all-gather.6.cloned.1.call-start = ((), (), s32[]{:S(2)}) async-start(), calls=%async_computation.5 | async-start | bytes 11141120 | tf_op jit(solution)/shard_map/all_gather | solution.py:793
  229.9 60.2 %collective-permute-start.1 = (bf16[512,2560]{1,0:T(8,128)(2,1)S(1)}, bf16[512,2560]{1,0:T(8,128)(2,1)}, u32[]{:S(2)}, u32[]{:S(2)}) collective-permute-start(bf16[512,2560]{1,0:T(8,128)(2,1)S(1)} %copy-done.10), channel_id=1, source_target_pairs={{0,2},{1,3},{2,0},{3,1},{4,6},{5,7},{6,4},{7,5},{8,10},{9,11},{10,... | collective-permute-start | bytes 7864328 | tf_op jit(solution)/shard_map/ppermute | solution.py:795
  232.3 111.5 %collective-permute-start = (bf16[512,2560]{1,0:T(8,128)(2,1)}, bf16[512,2560]{1,0:T(8,128)(2,1)}, u32[]{:S(2)}, u32[]{:S(2)}) collective-permute-start(bf16[512,2560]{1,0:T(8,128)(2,1)} %get-tuple-element.76.act.refs_4_), channel_id=1, source_target_pairs={{0,2},{1,3},{2,0},{3,1},{4,6},{5,7},{6,4},{7,5},{8,10},{9,11},{10,... | collective-permute-start | bytes 7864328 | tf_op jit(solution)/shard_map/ppermute | solution.py:795
  370.2 127.1 %reduce-scatter.6.cloned.1.call-start = ((), (), s32[]{:S(2)}) async-start(), calls=%async_computation.6 | async-start | bytes 6553600 | tf_op jit(solution)/shard_map/reduce_scatter | solution.py:794
  370.3 40.1 %collective-permute-start.4 = (bf16[512,2560]{1,0:T(8,128)(2,1)}, bf16[512,2560]{1,0:T(8,128)(2,1)}, u32[]{:S(2)}, u32[]{:S(2)}) collective-permute-start(bf16[512,2560]{1,0:T(8,128)(2,1)} %refs_4_.1), channel_id=1, source_target_pairs={{0,1},{1,0},{2,3},{3,2},{4,5},{5,4},{6,7},{7,6},{8,9},{9,8},{10,11... | collective-permute-start | bytes 7864328 | tf_op jit(solution)/shard_map/ppermute | solution.py:795
  370.3 40.1 %collective-permute-start.5 = (bf16[512,2560]{1,0:T(8,128)(2,1)}, bf16[512,2560]{1,0:T(8,128)(2,1)}, u32[]{:S(2)}, u32[]{:S(2)}) collective-permute-start(bf16[512,2560]{1,0:T(8,128)(2,1)} %collective-permute-done.1.dy.refs_6_), channel_id=1, source_target_pairs={{0,1},{1,0},{2,3},{3,2},{4,5},{5,4},{6,7},{7,6},{8,9},{9,8},{10,11... | collective-permute-start | bytes 7864328 | tf_op jit(solution)/shard_map/ppermute | solution.py:795
  370.9 39.6 %collective-permute-start.2 = (bf16[512,1792]{1,0:T(8,128)(2,1)}, bf16[512,1792]{1,0:T(8,128)(2,1)}, u32[]{:S(2)}, u32[]{:S(2)}) collective-permute-start(bf16[512,1792]{1,0:T(8,128)(2,1)} %get-tuple-element.82.refs_0_), channel_id=1, source_target_pairs={{0,1},{1,0},{2,3},{3,2},{4,5},{5,4},{6,7},{7,6},{8,9},{9,8},{10,11... | collective-permute-start | bytes 5505032 | tf_op jit(solution)/shard_map/ppermute | solution.py:795
  371.4 39.1 %collective-permute-start.3 = (bf16[512,1792]{1,0:T(8,128)(2,1)}, bf16[512,1792]{1,0:T(8,128)(2,1)}, u32[]{:S(2)}, u32[]{:S(2)}) collective-permute-start(bf16[512,1792]{1,0:T(8,128)(2,1)} %get-tuple-element.84.refs_2_), channel_id=1, source_target_pairs={{0,1},{1,0},{2,3},{3,2},{4,5},{5,4},{6,7},{7,6},{8,9},{9,8},{10,11... | collective-permute-start | bytes 5505032 | tf_op jit(solution)/shard_map/ppermute | solution.py:795
  380.1 23.9 %collective-permute-start.7 = (bf16[512,640]{1,0:T(8,128)(2,1)S(1)}, bf16[512,640]{1,0:T(8,128)(2,1)S(1)}, u32[]{:S(2)}, u32[]{:S(2)}) collective-permute-start(bf16[512,640]{1,0:T(8,128)(2,1)S(1)} %copy-done.3), channel_id=1, source_target_pairs={{0,2},{1,3},{2,0},{3,1},{4,6},{5,7},{6,4},{7,5},{8,10},{9,11},{10,... | collective-permute-start | bytes 1966088 | tf_op jit(solution)/shard_map/ppermute | solution.py:795
  439.3 120.8 %reduce-scatter.8.cloned.1.call-start = ((), (), s32[]{:S(2)}) async-start(), calls=%async_computation.7 | async-start | bytes 6553600 | tf_op jit(solution)/shard_map/reduce_scatter | solution.py:794
  499.2 165.5 %all-gather.8.cloned.1.call-start = ((), (), s32[]{:S(2)}) async-start(), calls=%async_computation.8 | async-start | bytes 23674880 | tf_op jit(solution)/shard_map/all_gather | solution.py:793
  499.2 11.5 %collective-permute-start.12 = (bf16[512,2560]{1,0:T(8,128)(2,1)}, bf16[512,2560]{1,0:T(8,128)(2,1)S(1)}, u32[]{:S(2)}, u32[]{:S(2)}) collective-permute-start(bf16[512,2560]{1,0:T(8,128)(2,1)} %get-tuple-element.76.act.refs_4_), channel_id=1, source_target_pairs={{0,1},{1,0},{2,3},{3,2},{4,5},{5,4},{6,7},{7,6},{8,9},{9,8},{10,11... | collective-permute-start | bytes 7864328 | tf_op jit(solution)/shard_map/ppermute | solution.py:795
  499.3 11.5 %collective-permute-start.13 = (bf16[512,2560]{1,0:T(8,128)(2,1)}, bf16[512,2560]{1,0:T(8,128)(2,1)}, u32[]{:S(2)}, u32[]{:S(2)}) collective-permute-start(bf16[512,2560]{1,0:T(8,128)(2,1)} %collective-permute-done.act.refs_6_), channel_id=1, source_target_pairs={{0,1},{1,0},{2,3},{3,2},{4,5},{5,4},{6,7},{7,6},{8,9},{9,8},{10,11... | collective-permute-start | bytes 7864328 | tf_op jit(solution)/shard_map/ppermute | solution.py:795
  499.8 13.7 %collective-permute-start.11 = (bf16[512,1792]{1,0:T(8,128)(2,1)}, bf16[512,1792]{1,0:T(8,128)(2,1)}, u32[]{:S(2)}, u32[]{:S(2)}) collective-permute-start(bf16[512,1792]{1,0:T(8,128)(2,1)} %get-tuple-element.94.refs_2_), channel_id=1, source_target_pairs={{0,1},{1,0},{2,3},{3,2},{4,5},{5,4},{6,7},{7,6},{8,9},{9,8},{10,11... | collective-permute-start | bytes 5505032 | tf_op jit(solution)/shard_map/ppermute | solution.py:795
  500.5 56.2 %collective-permute-start.9 = (bf16[512,1920]{1,0:T(8,128)(2,1)}, bf16[512,1920]{1,0:T(8,128)(2,1)}, u32[]{:S(2)}, u32[]{:S(2)}) collective-permute-start(bf16[512,1920]{1,0:T(8,128)(2,1)} %attend_back.1.refs_4_), channel_id=1, source_target_pairs={{0,2},{1,3},{2,0},{3,1},{4,6},{5,7},{6,4},{7,5},{8,10},{9,11},{10,... | collective-permute-start | bytes 5898248 | tf_op jit(solution)/shard_map/ppermute | solution.py:795
  570.1 28.9 %collective-permute-start.16 = (bf16[512,1792]{1,0:T(8,128)(2,1)}, bf16[512,1792]{1,0:T(8,128)(2,1)}, u32[]{:S(2)}, u32[]{:S(2)}) collective-permute-start(bf16[512,1792]{1,0:T(8,128)(2,1)} %get-tuple-element.100.refs_0_), channel_id=1, source_target_pairs={{0,1},{1,0},{2,3},{3,2},{4,5},{5,4},{6,7},{7,6},{8,9},{9,8},{10,11... | collective-permute-start | bytes 5505032 | tf_op jit(solution)/shard_map/ppermute | solution.py:795
  570.1 28.9 %collective-permute-start.17 = (bf16[512,1792]{1,0:T(8,128)(2,1)}, bf16[512,1792]{1,0:T(8,128)(2,1)}, u32[]{:S(2)}, u32[]{:S(2)}) collective-permute-start(bf16[512,1792]{1,0:T(8,128)(2,1)} %get-tuple-element.101.refs_2_), channel_id=1, source_target_pairs={{0,1},{1,0},{2,3},{3,2},{4,5},{5,4},{6,7},{7,6},{8,9},{9,8},{10,11... | collective-permute-start | bytes 5505032 | tf_op jit(solution)/shard_map/ppermute | solution.py:795
  570.6 55.4 %collective-permute-start.14 = (bf16[512,1920]{1,0:T(8,128)(2,1)}, bf16[512,1920]{1,0:T(8,128)(2,1)S(1)}, u32[]{:S(2)}, u32[]{:S(2)}) collective-permute-start(bf16[512,1920]{1,0:T(8,128)(2,1)} %attend_back.1.refs_4_), channel_id=1, source_target_pairs={{0,1},{1,0},{2,3},{3,2},{4,5},{5,4},{6,7},{7,6},{8,9},{9,8},{10,11... | collective-permute-start | bytes 5898248 | tf_op jit(solution)/shard_map/ppermute | solution.py:795
  570.7 55.4 %collective-permute-start.15 = (bf16[512,1920]{1,0:T(8,128)(2,1)}, bf16[512,1920]{1,0:T(8,128)(2,1)}, u32[]{:S(2)}, u32[]{:S(2)}) collective-permute-start(bf16[512,1920]{1,0:T(8,128)(2,1)} %collective-permute-done.9.refs_6_), channel_id=1, source_target_pairs={{0,1},{1,0},{2,3},{3,2},{4,5},{5,4},{6,7},{7,6},{8,9},{9,8},{10,11... | collective-permute-start | bytes 5898248 | tf_op jit(solution)/shard_map/ppermute | solution.py:795
  664.7 36.5 %collective-permute-start.18 = (bf16[128,2560]{1,0:T(8,128)(2,1)S(1)}, bf16[128,2560]{1,0:T(8,128)(2,1)}, u32[]{:S(2)}, u32[]{:S(2)}) collective-permute-start(bf16[128,2560]{1,0:T(8,128)(2,1)S(1)} %add_convert_fusion), channel_id=1, source_target_pairs={{0,4},{4,0},{8,12},{12,8},{1,5},{5,1},{9,13},{13,9},{2,6},{6,2},{1... | collective-permute-start | bytes 1966088 | tf_op jit(solution)/shard_map/ppermute | solution.py:795
  666.1 36.1 %collective-permute-start.19 = (bf16[128,2560]{1,0:T(8,128)(2,1)S(1)}, bf16[128,2560]{1,0:T(8,128)(2,1)S(1)}, u32[]{:S(2)}, u32[]{:S(2)}) collective-permute-start(bf16[128,2560]{1,0:T(8,128)(2,1)S(1)} %add_convert_fusion), channel_id=1, source_target_pairs={{0,8},{4,12},{8,0},{12,4},{1,9},{5,13},{9,1},{13,5},{2,10},{6,14},... | collective-permute-start | bytes 1966088 | tf_op jit(solution)/shard_map/ppermute | solution.py:795
  666.9 35.5 %collective-permute-start.20 = (bf16[128,2560]{1,0:T(8,128)(2,1)S(1)}, bf16[128,2560]{1,0:T(8,128)(2,1)S(1)}, u32[]{:S(2)}, u32[]{:S(2)}) collective-permute-start(bf16[128,2560]{1,0:T(8,128)(2,1)S(1)} %add_convert_fusion), channel_id=1, source_target_pairs={{0,12},{4,8},{8,4},{12,0},{1,13},{5,9},{9,5},{13,1},{2,14},{6,10},... | collective-permute-start | bytes 1966088 | tf_op jit(solution)/shard_map/ppermute | solution.py:795
  (26 other events, 656.4 us)
Sparse Core Ops, SparseCore 0:
  91.0 68.3 all-gather.3
  228.3 58.7 reduce-scatter.3
  370.4 65.5 all-gather.5
  439.4 57.8 reduce-scatter.5
  500.7 59.4 reduce-scatter.7
  570.2 94.4 all-gather.7

commit v10 on v9

--- a/solution.py
+++ b/solution.py
@@ -280,6 +280,32 @@
     )(picked, side_f, side_i)
 
 
+def spread_kernel(piece, out, buf, send, recv, core_send, core_recv, out_sem, load):
+    place = Place()
+    first = pltpu.make_async_copy(piece, buf.at[place.slot()], load)
+    first.start()
+    place.meet(("x", "y", "z", "core"))
+    first.wait()
+    gather = Gather(place, buf, send, recv, core_send, core_recv)
+    gather.run()
+    gather.finish(out, out_sem)
+
+
+def spread(piece):
+    rows, dim = piece.shape
+    dma = pltpu.SemaphoreType.DMA
+    hbm = pl.BlockSpec(memory_space=pltpu.HBM)
+    return pl.pallas_call(
+        spread_kernel,
+        out_shape=jax.ShapeDtypeStruct((16 * rows, dim), BF16),
+        in_specs=[hbm],
+        out_specs=hbm,
+        scratch_shapes=[pltpu.VMEM((16, rows, dim), BF16), *[dma((n,)) for n in (21, 21, 24, 24, 16)], dma],
+        compiler_params=pltpu.CompilerParams(collective_id=2, has_side_effects=True, vmem_limit_bytes=FULL),
+        name="spread",
+    )(piece)
+
+
 def slot_block(j):
     return jnp.where(j < 4, 2 * j, 15 - 2 * j)
 
@@ -840,14 +866,17 @@
         d_act_b = add_up(d_act_b)
         hidden_x, d_gate_x, d_up_x = mlp_block(act_x, dy_x, wg, wu, w_down, False)
         out_part = nn(hidden[:, :ffn], w_down)
-        d_act_b, hidden_x, d_gate_x, d_up_x, out_part = barrier((d_act_b, hidden_x, d_gate_x, d_up_x, out_part))
+        base = zero_rows(bounds, rows, dim)
+        heads_x = barrier((heads_x, act_b))[0]
+        head_parts = (attended, swap(attended, core_swap), heads_x, swap(heads_x, core_swap))
+        att_heads = jnp.concatenate([attended] * cp_count)
+        for k, piece in enumerate(head_parts):
+            if k:
+                att_heads = lax.dynamic_update_slice_in_dim(att_heads, piece, (cp_rank ^ k) * span, 0)
+        d_act_b, hidden_x, d_gate_x, d_up_x, out_part, base, att_heads = barrier((d_act_b, hidden_x, d_gate_x, d_up_x, out_part, base, att_heads))
         d_act_b = to_bf16(d_act_b)
         acts, dys, hiddens, d_gates, d_ups = [(a, swap(a, core_swap), b, swap(b, core_swap)) for a, b in (
             (act_b, act_x), (dy, dy_x), (hidden, hidden_x), (d_gate, d_gate_x), (d_up, d_up_x))]
-        head_parts = (attended, swap(attended, core_swap), heads_x, swap(heads_x, core_swap))
-        att_heads = jnp.zeros((total, width), BF16)
-        for k, piece in enumerate(head_parts):
-            att_heads = lax.dynamic_update_slice_in_dim(att_heads, piece, (cp_rank ^ k) * span, 0)
         grad_down = weight_grad(info, hiddens, dys, rows=ffn)
         grad_gate = weight_grad(info, d_gates, acts, rows=ffn)
         grad_up = weight_grad(info, d_ups, acts, rows=ffn)
@@ -859,8 +888,7 @@
         normed_b, inv_b = rms_stats(res_part)
         grad_gain_b = jnp.sum(d_act_b * normed_b, axis=0)
         d_resid = mine(dy).astype(F32) + rms_back(d_act_b * gain_b, normed_b, inv_b)
-        d_resid_all = join(d_resid.astype(BF16), both)
-        d_resid_all, grad_down, att_heads, out_part = barrier((d_resid_all, grad_down, att_heads, out_part))
+        d_resid_all, out_part = barrier((spread(d_resid.astype(BF16)), out_part))
         out_slice = add_up(out_part)
         out_slice = (res_part + out_slice).astype(BF16)
 
@@ -888,9 +916,8 @@
         payload = jnp.concatenate([d_embed, jnp.stack([grad_gain_a, grad_gain_b] * 4)])
         gathered = join(payload, both)
         grad_qkv = weight_grad(info, [act_a.reshape(cp_count, span, dim)] * 4, dqkvs, splits=3)
-        base = zero_rows(barrier((bounds, d_act_a))[0], rows, dim)
-        gathered, grad_qkv, grad_gate, base = barrier((gathered, grad_qkv, grad_gate, base))
-        out_slice = barrier((out_slice, gathered))[0]
+        gathered, grad_qkv, grad_gate, grad_down = barrier((gathered, grad_qkv, grad_gate, grad_down))
+        out_slice = barrier((out_slice, grad_qkv))[0]
         layer_out = jnp.concatenate([out_slice] * tp_count)
         for k in range(1, tp_count):
             piece = swap(out_slice, [(i, i ^ k) for i in range(tp_count)], "tp")

time: 717 us -> 708 us (0.987)
  waiting for transfers between devices: 155 us -> 96.3 us
  Pallas kernels: 411 us -> 449 us
    ppermute x21, waiting for transfers between devices: 139 us -> 83.4 us  [compute(): swap = lambda arr, pairs, axis='cp': lax.ppermute(arr, axis, pairs)]
    pallas_call x0 -> x1, Pallas kernels: none -> 42.4 us  [spread(): pl.pallas_call(spread_kernel, out_shape=jax.ShapeDtypeStruct((16 * rows,...]
    all_gather x3 -> x2, waiting for transfers between devices: 10.5 us -> 3.09 us  [compute(): join = lambda arr, axis: lax.all_gather(arr, axis, axis=0, tiled=True)]
  transfers between devices with their start and end apart: 27 -> 26, of which waited for: 10 -> 9; matrix products, arithmetic and copies ran while one was open for 11% -> 11% of each run, Pallas kernels for 38% -> 38%
where the time goes in v10:
time: 708 us; the launch traced here: 703 us
  Pallas kernels  449 us (63%)
  waiting for transfers between devices  96.3 us (14%)
  other arithmetic  46.3 us (7%)
  matrix products  40.1 us (6%)
  local copies, waits for them, and re-layouts  38.1 us (5%)
  starting transfers between devices  18.1 us (3%)
  between operations  14.4 us (2%)
    pallas_call x5, Pallas kernels, weight_grad(): pl.pallas_call(functools.partial(weight_grad_kernel, pieces=n, splits=spl...  127 us
    ppermute x21, waiting for transfers between devices, compute(): swap = lambda arr, pairs, axis='cp': lax.ppermute(arr, axis, pairs)  83.4 us
    pallas_call x1, Pallas kernels, embed_gather(): pl.pallas_call(embed_kernel, out_shape=[jax.ShapeDtypeStruct((16 * rows,...  68.6 us
    pallas_call x2, Pallas kernels, mlp_block(): pl.pallas_call(functools.partial(mlp_kernel, limit=limit, tiles=tiles), o...  54.1 us
    pallas_call x1, Pallas kernels, spread(): pl.pallas_call(spread_kernel, out_shape=jax.ShapeDtypeStruct((16 * rows,...  42.4 us
    dot_general x5, matrix products, contract(): lax.dot_general(a, b, (((ca,), (cb,)), ((), ())), preferred_element_type=...  35.4 us
    pallas_call x1, Pallas kernels, att_project(): pl.pallas_call(att_kernel, out_shape=[jax.ShapeDtypeStruct((4,) + lse.sha...  35.1 us
    pallas_call x1, Pallas kernels, project_qkv(): pl.pallas_call(functools.partial(qkv_kernel, head_dim=head_dim), out_shap...  32.6 us
  transfers between devices with their start and end apart: 26, of which 9 were waited for; matrix products, arithmetic and copies ran while one was open for 11% of the time, Pallas kernels for 38%

profile of v10, /device:TPU:0, one launch (start us, length us, event | category | flops | bytes accessed | tf_op | source)
XLA Modules:
  0.0 702.6 jit_solution(12425454557602499997)
XLA Ops:
  8.6 6.8 gather_fusion
  22.5 68.6 %embed_gather.1 = (bf16[2048,2560]{1,0:T(8,128)(2,1)}, bf16[128,2560]{1,0:T(8,128)(2,1)}, f32[4,512,128]{2,1,0:T(8,128)}, s32[4,8,512]{2,1,0:T(8,128)}) custom-call(bf16[4,128,2560]{2,1,0:T(8,128)(2,1)} %select_select_fusion.picked, f32[512,128]{1,0:T(8,128)} %pad_maximum_fusion.2.side_f, s32[8,512]{1,0:T(8,128)} %stack.50.side_i), custom_call_target="tpu_custom_call" | custom-call | tf_op jit(solution)/shard_map/embed_gather/pallas_call | solution.py:260
  95.1 32.6 %project_qkv.1 = (bf16[2048,2560]{1,0:T(8,128)(2,1)}, bf16[2048,640]{1,0:T(8,128)(2,1)}, bf16[2048,640]{1,0:T(8,128)(2,1)}, bf16[2048,640]{1,0:T(8,128)(2,1)}) custom-call(bf16[2048,2560]{1,0:T(8,128)(2,1)} %get-tuple-element.65.x.x_all, f32[1,2560]{1,0:T(1,128)} %broadcast_in_dim.85.gain, bf16[2560,640]{1,0:T(8,128)(2,1)} %wq.1, bf16[2560,640]{1,0:T(8,128)(2,1)} %wk.1, ...), custom_call_target="tpu_custom_call" | custom-call | flops 20132659200 | bytes 39321600 | tf_op jit(solution)/shard_map/project_qkv/pallas_call | solution.py:347
  127.7 10.1 %attend.1 = (bf16[512,640]{1,0:T(8,128)(2,1)}, f32[512,8]{1,0:T(8,128)}) custom-call(s32[2]{0:T(128)} %pad_add_fusion.info, s32[4,8,512]{2,1,0:T(8,128)} %get-tuple-element.64.ids, bf16[2048,640]{1,0:T(8,128)(2,1)} %get-tuple-element.67.q, bf16[2048,640]{1,0:T(8,128)(2,1)} %get-tuple-element.68.k, bf16[2048,640]{1,0:T(8,128)(2,1)} %get-tuple-element.69.v, ...), custom_call_target="tpu_custom_call" | custom-call | flops 2684354560 | bytes 5242880 | tf_op jit(solution)/shard_map/attend/pallas_call | solution.py:428
  145.7 8.0 %select_reduce_fusion = (s32[2048]{0:T(1024)S(1)}, s32[2048]{0:T(1024)S(1)}, s32[2048]{0:T(1024)S(1)}) fusion(s32[2048]{0:T(1024)S(1)} %convert_reduce_fusion, s32[2048]{0:T(1024)S(1)} %bitcast.62), kind=kLoop, calls=%fused_computation.4 | loop fusion | flops 33548288 | bytes 40960 | tf_op jit(solution)/shard_map/reduce_sum | solution.py:855
  159.7 35.1 %att_project.1 = (f32[4,512,8]{2,1,0:T(8,128)}, f32[512,2560]{1,0:T(8,128)}, bf16[512,2560]{1,0:T(8,128)(2,1)}) custom-call(bf16[512,640]{1,0:T(8,128)(2,1)} %get-tuple-element.70.att.refs_0_, f32[512,8]{1,0:T(8,128)} %get-tuple-element.71.lse, bf16[2048,2560]{1,0:T(8,128)(2,1)} %get-tuple-element.65.x.x_all, ...), custom_call_target="tpu_custom_call" | custom-call | tf_op jit(solution)/shard_map/att_project/pallas_call | solution.py:593
  194.8 32.8 %mlp_block.2 = (bf16[512,1792]{1,0:T(8,128)(2,1)}, bf16[512,1792]{1,0:T(8,128)(2,1)}, bf16[512,1792]{1,0:T(8,128)(2,1)}, f32[512,2560]{1,0:T(8,128)}) custom-call(bf16[512,2560]{1,0:T(8,128)(2,1)} %get-tuple-element.76.act.refs_4_, bf16[512,2560]{1,0:T(8,128)(2,1)} %refs_4_.1, bf16[1728,2560]{1,0:T(8,128)(2,1)} %bitcast.63, bf16[1728,2560]{1,0:T(8,128)(2,1)} %bitcast.65, ...), custom_call_target="tpu_custom_call" | custom-call | flops 22649241600 | bytes 44236800 | tf_op jit(solution)/shard_map/mlp_block/pallas_call | solution.py:687
  233.4 7.1 %pad_maximum_fusion = bf16[2048,640]{1,0:T(8,128)(2,1)} fusion(bf16[512,640]{1,0:T(8,128)(2,1)S(1)} %copy-done.3), kind=kLoop, calls=%fused_computation.17 | loop fusion | flops 10485760 | bytes 3276800 | tf_op jit(solution)/shard_map/concatenate | solution.py:872
  247.0 10.7 %fusion.6 = f32[512,2560]{1,0:T(8,128)} fusion(bf16[1728,2560]{1,0:T(8,128)(2,1)} %wd.3, bf16[512,1792]{1,0:T(8,128)(2,1)S(1)} %copy-done.26), kind=kOutput, calls=%fused_computation.20 | convolution fusion | flops 4529848320 | bytes 15925248 | tf_op jit(solution)/shard_map/dot_general | solution.py:32
  257.6 27.0 %zero_rows.1.base_hbm = f32[8000,2560]{1,0:T(8,128)} custom-call(s32[2]{0:T(128)S(1)} %pad_add_fusion.1.after.bounds), custom_call_target="tpu_custom_call" | custom-call | flops 20480000 | bytes 40000 | tf_op jit(solution)/shard_map/zero_rows/pallas_call | solution.py:718
  288.8 14.4 %collective-permute-done.1.dy.refs_6_ = bf16[512,2560]{1,0:T(8,128)(2,1)} collective-permute-done((bf16[512,2560]{1,0:T(8,128)(2,1)}, bf16[512,2560]{1,0:T(8,128)(2,1)}, u32[]{:S(2)}, u32[]{:S(2)}) %collective-permute-start.1) | collective-permute-done | bytes 2621472 | tf_op jit(solution)/shard_map/ppermute | solution.py:821
  303.3 56.0 %collective-permute-done.act.refs_6_ = bf16[512,2560]{1,0:T(8,128)(2,1)} collective-permute-done((bf16[512,2560]{1,0:T(8,128)(2,1)}, bf16[512,2560]{1,0:T(8,128)(2,1)}, u32[]{:S(2)}, u32[]{:S(2)}) %collective-permute-start) | collective-permute-done | bytes 2621472 | tf_op jit(solution)/shard_map/ppermute | solution.py:821
  359.2 21.3 %mlp_block.3 = (bf16[512,1792]{1,0:T(8,128)(2,1)}, bf16[512,1792]{1,0:T(8,128)(2,1)}, bf16[512,1792]{1,0:T(8,128)(2,1)}) custom-call(bf16[512,2560]{1,0:T(8,128)(2,1)} %collective-permute-done.act.refs_6_, bf16[512,2560]{1,0:T(8,128)(2,1)} %collective-permute-done.1.dy.refs_6_, bf16[1728,2560]{1,0:T(8,128)(2,1)} %bitcast.64, bf16[1728,2560]{1,0:T(8,128)(2,1)} %bitcast.66, ...), custom_call_target="tpu_custom_call" | custom-call | flops 13589544960 | bytes 26542080 | tf_op jit(solution)/shard_map/mlp_block/pallas_call | solution.py:687
  385.6 42.4 %spread.1 = bf16[2048,2560]{1,0:T(8,128)(2,1)} custom-call(bf16[128,2560]{1,0:T(8,128)(2,1)} %fusion.36.piece), custom_call_target="tpu_custom_call" | custom-call | tf_op jit(solution)/shard_map/spread/pallas_call | solution.py:298
  430.2 13.3 %convolution_convert_fusion.do = bf16[2048,640]{1,0:T(8,128)(2,1)S(1)} fusion(bf16[2048,2560]{1,0:T(8,128)(2,1)} %spread.1, bf16[640,2560]{1,0:T(8,128)(2,1)} %param.23), kind=kOutput, calls=%fused_computation.16 | convolution fusion | flops 6712197120 | bytes 16384000 | tf_op jit(solution)/shard_map/dot_general | solution.py:32
  451.0 22.1 %attend_back.1.refs_4_ = bf16[512,1920]{1,0:T(8,128)(2,1)} custom-call(s32[2]{0:T(128)} %pad_add_fusion.info, s32[4,8,512]{2,1,0:T(8,128)} %get-tuple-element.64.ids, bf16[2048,640]{1,0:T(8,128)(2,1)} %get-tuple-element.67.q, bf16[2048,640]{1,0:T(8,128)(2,1)} %get-tuple-element.68.k, bf16[2048,640]{1,0:T(8,128)(2,1)} %get-tuple-element.69.v, ...), custom_call_target="tpu_custom_call" | custom-call | flops 4697620480 | bytes 9175040 | tf_op jit(solution)/shard_map/attend_back/pallas_call | solution.py:500
  488.5 6.6 collective-permute-start.5
  495.1 15.4 %weight_grad.5 = f32[640,2560]{1,0:T(8,128)} custom-call(s32[2]{0:T(128)} %pad_add_fusion.info, bf16[512,640]{1,0:T(8,128)(2,1)} %get-tuple-element.70.att.refs_0_, bf16[512,640]{1,0:T(8,128)(2,1)} %copy-done.8, bf16[512,640]{1,0:T(8,128)(2,1)} %copy-done.9, bf16[512,640]{1,0:T(8,128)(2,1)} %copy-done.10, bf16[4,512,2560]{2,1,0:T(8,128)(2,1)} %bitcast.38, ...), custom_call_target="tpu_custom_call" | custom-call | flops 6710886400 | bytes 13107200 | tf_op jit(solution)/shard_map/weight_grad/pallas_call | solution.py:629
  512.6 27.4 %weight_grad.6 = f32[1728,2560]{1,0:T(8,128)} custom-call(s32[2]{0:T(128)} %pad_add_fusion.info, bf16[512,1792]{1,0:T(8,128)(2,1)} %get-tuple-element.94.refs_0_, bf16[512,1792]{1,0:T(8,128)(2,1)} %copy-done.28, bf16[512,1792]{1,0:T(8,128)(2,1)} %get-tuple-element.95.refs_2_, bf16[512,1792]{1,0:T(8,128)(2,1)} %collective-permute-done.7.refs_3_, ...), custom_call_target="tpu_custom_call" | custom-call | flops 18119393280 | bytes 35389440 | tf_op jit(solution)/shard_map/weight_grad/pallas_call | solution.py:629
  540.0 9.1 %reduce-scatter.8.cloned.1.call-done = f32[128,2560]{1,0:T(8,128)} async-done(((f32[512,2560]{1,0:T(8,128)}), f32[128,2560]{1,0:T(8,128)}) %reduce-scatter.8.cloned.1.call-update) | async-done | bytes 1310736 | tf_op jit(solution)/shard_map/reduce_scatter | solution.py:820
  569.6 27.0 %weight_grad.8 = f32[1728,2560]{1,0:T(8,128)} custom-call(s32[2]{0:T(128)} %pad_add_fusion.info, bf16[512,1792]{1,0:T(8,128)(2,1)} %get-tuple-element.101.refs_0_, bf16[512,1792]{1,0:T(8,128)(2,1)} %collective-permute-done.12.refs_1_, bf16[512,1792]{1,0:T(8,128)(2,1)} %get-tuple-element.102.refs_2_, bf16[512,1792]{1,0:T(8,128)(2,1)} %collective-permute-done.13.refs_3_, ...), custom_call_target="tpu_custom_call" | custom-call | flops 18119393280 | bytes 35389440 | tf_op jit(solution)/shard_map/weight_grad/pallas_call | solution.py:629
  597.9 27.0 %weight_grad.9 = f32[1728,2560]{1,0:T(8,128)} custom-call(s32[2]{0:T(128)} %pad_add_fusion.info, bf16[512,1792]{1,0:T(8,128)(2,1)} %get-tuple-element.82.refs_0_, bf16[512,1792]{1,0:T(8,128)(2,1)} %collective-permute-done.14.refs_1_, bf16[512,1792]{1,0:T(8,128)(2,1)} %get-tuple-element.103.refs_2_, bf16[512,1792]{1,0:T(8,128)(2,1)} %copy-done.27, ...), custom_call_target="tpu_custom_call" | custom-call | flops 18119393280 | bytes 35389440 | tf_op jit(solution)/shard_map/weight_grad/pallas_call | solution.py:629
  626.9 29.7 %weight_grad.7 = (f32[2560,640]{1,0:T(8,128)}, f32[2560,640]{1,0:T(8,128)}, f32[2560,640]{1,0:T(8,128)}) custom-call(s32[2]{0:T(128)} %pad_add_fusion.info, bf16[4,512,2560]{2,1,0:T(8,128)(2,1)} %bitcast.71, bf16[4,512,2560]{2,1,0:T(8,128)(2,1)} %bitcast.72, bf16[4,512,2560]{2,1,0:T(8,128)(2,1)} %bitcast.73, bf16[4,512,2560]{2,1,0:T(8,128)(2,1)} %bitcast.74, ...), custom_call_target="tpu_custom_call" | custom-call | flops 20132659200 | bytes 39321600 | tf_op jit(solution)/shard_map/weight_grad/pallas_call | solution.py:629
  660.2 30.7 %scatter_rows.1 = f32[8000,2560]{1,0:T(8,128)} custom-call(s32[2048]{0:T(1024)} %get-tuple-element.108.order, s32[2048]{0:T(1024)} %get-tuple-element.109.sid, s32[2048]{0:T(1024)} %select_reduce_fusion.2.runs, s32[2]{0:T(128)} %copy-done, f32[2176,2560]{1,0:T(8,128)} %all-gather.5.cloned.1.call-done.rows, ...), custom_call_target="tpu_custom_call", output_to_operand_aliasing={{}: (5, {})} | custom-call | tf_op jit(solution)/shard_map/scatter_rows/pallas_call | solution.py:781
  (161 shorter events, 106.9 us)
Async XLA Ops:
  7.2 152.5 %all-gather.3.cloned.1.call-start = ((), (), s32[]{:S(2)}) async-start(), calls=%async_computation.3 | async-start | bytes 8192000 | tf_op jit(solution)/shard_map/all_gather | solution.py:819
  91.1 289.5 %reduce-scatter.4.cloned.1.call-start = ((), (), s32[]{:S(2)}) async-start(), calls=%async_computation.4 | async-start | bytes 6553600 | tf_op jit(solution)/shard_map/reduce_scatter | solution.py:820
  227.6 257.6 %reduce-scatter.6.cloned.1.call-start = ((), (), s32[]{:S(2)}) async-start(), calls=%async_computation.5 | async-start | bytes 6553600 | tf_op jit(solution)/shard_map/reduce_scatter | solution.py:820
  228.7 11.8 %collective-permute-start.2 = (bf16[512,640]{1,0:T(8,128)(2,1)S(1)}, bf16[512,640]{1,0:T(8,128)(2,1)S(1)}, u32[]{:S(2)}, u32[]{:S(2)}) collective-permute-start(bf16[512,640]{1,0:T(8,128)(2,1)S(1)} %copy-done.3), channel_id=1, source_target_pairs={{0,1},{1,0},{2,3},{3,2},{4,5},{5,4},{6,7},{7,6},{8,9},{9,8},{10,11... | collective-permute-start | bytes 1966088 | tf_op jit(solution)/shard_map/ppermute | solution.py:821
  228.7 18.3 %collective-permute-start.3 = (bf16[512,640]{1,0:T(8,128)(2,1)S(1)}, bf16[512,640]{1,0:T(8,128)(2,1)S(1)}, u32[]{:S(2)}, u32[]{:S(2)}) collective-permute-start(bf16[512,640]{1,0:T(8,128)(2,1)S(1)} %copy-done.3), channel_id=1, source_target_pairs={{0,2},{1,3},{2,0},{3,1},{4,6},{5,7},{6,4},{7,5},{8,10},{9,11},{10,... | collective-permute-start | bytes 1966088 | tf_op jit(solution)/shard_map/ppermute | solution.py:821
  231.4 71.9 %collective-permute-start.1 = (bf16[512,2560]{1,0:T(8,128)(2,1)}, bf16[512,2560]{1,0:T(8,128)(2,1)}, u32[]{:S(2)}, u32[]{:S(2)}) collective-permute-start(bf16[512,2560]{1,0:T(8,128)(2,1)} %refs_4_.1), channel_id=1, source_target_pairs={{0,2},{1,3},{2,0},{3,1},{4,6},{5,7},{6,4},{7,5},{8,10},{9,11},{10,... | collective-permute-start | bytes 7864328 | tf_op jit(solution)/shard_map/ppermute | solution.py:821
  231.4 127.8 %collective-permute-start = (bf16[512,2560]{1,0:T(8,128)(2,1)}, bf16[512,2560]{1,0:T(8,128)(2,1)}, u32[]{:S(2)}, u32[]{:S(2)}) collective-permute-start(bf16[512,2560]{1,0:T(8,128)(2,1)} %get-tuple-element.76.act.refs_4_), channel_id=1, source_target_pairs={{0,2},{1,3},{2,0},{3,1},{4,6},{5,7},{6,4},{7,5},{8,10},{9,11},{10,... | collective-permute-start | bytes 7864328 | tf_op jit(solution)/shard_map/ppermute | solution.py:821
  247.0 40.1 %collective-permute-start.4 = (bf16[512,640]{1,0:T(8,128)(2,1)S(1)}, bf16[512,640]{1,0:T(8,128)(2,1)S(1)}, u32[]{:S(2)}, u32[]{:S(2)}) collective-permute-start(bf16[512,640]{1,0:T(8,128)(2,1)S(1)} %collective-permute-done.3.refs_2_), channel_id=1, source_target_pairs={{0,1},{1,0},{2,3},{3,2},{4,5},{5,4},{6,7},{7,6},{8,9},{9,8},{10,11... | collective-permute-start | bytes 1966088 | tf_op jit(solution)/shard_map/ppermute | solution.py:821
  428.0 121.0 %reduce-scatter.8.cloned.1.call-start = ((), (), s32[]{:S(2)}) async-start(), calls=%async_computation.6 | async-start | bytes 6553600 | tf_op jit(solution)/shard_map/reduce_scatter | solution.py:820
  487.1 169.5 %all-gather.5.cloned.1.call-start = ((), (), s32[]{:S(2)}) async-start(), calls=%async_computation.7 | async-start | bytes 23674880 | tf_op jit(solution)/shard_map/all_gather | solution.py:819
  487.2 23.4 %collective-permute-start.8 = (bf16[512,2560]{1,0:T(8,128)(2,1)}, bf16[512,2560]{1,0:T(8,128)(2,1)S(1)}, u32[]{:S(2)}, u32[]{:S(2)}) collective-permute-start(bf16[512,2560]{1,0:T(8,128)(2,1)} %get-tuple-element.76.act.refs_4_), channel_id=1, source_target_pairs={{0,1},{1,0},{2,3},{3,2},{4,5},{5,4},{6,7},{7,6},{8,9},{9,8},{10,11... | collective-permute-start | bytes 7864328 | tf_op jit(solution)/shard_map/ppermute | solution.py:821
  487.2 23.3 %collective-permute-start.9 = (bf16[512,2560]{1,0:T(8,128)(2,1)}, bf16[512,2560]{1,0:T(8,128)(2,1)}, u32[]{:S(2)}, u32[]{:S(2)}) collective-permute-start(bf16[512,2560]{1,0:T(8,128)(2,1)} %collective-permute-done.act.refs_6_), channel_id=1, source_target_pairs={{0,1},{1,0},{2,3},{3,2},{4,5},{5,4},{6,7},{7,6},{8,9},{9,8},{10,11... | collective-permute-start | bytes 7864328 | tf_op jit(solution)/shard_map/ppermute | solution.py:821
  487.7 22.8 %collective-permute-start.6 = (bf16[512,1792]{1,0:T(8,128)(2,1)}, bf16[512,1792]{1,0:T(8,128)(2,1)S(1)}, u32[]{:S(2)}, u32[]{:S(2)}) collective-permute-start(bf16[512,1792]{1,0:T(8,128)(2,1)} %get-tuple-element.94.refs_0_), channel_id=1, source_target_pairs={{0,1},{1,0},{2,3},{3,2},{4,5},{5,4},{6,7},{7,6},{8,9},{9,8},{10,11... | collective-permute-start | bytes 5505032 | tf_op jit(solution)/shard_map/ppermute | solution.py:821
  487.8 22.8 %collective-permute-start.7 = (bf16[512,1792]{1,0:T(8,128)(2,1)}, bf16[512,1792]{1,0:T(8,128)(2,1)}, u32[]{:S(2)}, u32[]{:S(2)}) collective-permute-start(bf16[512,1792]{1,0:T(8,128)(2,1)} %get-tuple-element.95.refs_2_), channel_id=1, source_target_pairs={{0,1},{1,0},{2,3},{3,2},{4,5},{5,4},{6,7},{7,6},{8,9},{9,8},{10,11... | collective-permute-start | bytes 5505032 | tf_op jit(solution)/shard_map/ppermute | solution.py:821
  488.5 51.6 %collective-permute-start.5 = (bf16[512,1920]{1,0:T(8,128)(2,1)}, bf16[512,1920]{1,0:T(8,128)(2,1)}, u32[]{:S(2)}, u32[]{:S(2)}) collective-permute-start(bf16[512,1920]{1,0:T(8,128)(2,1)} %attend_back.1.refs_4_), channel_id=1, source_target_pairs={{0,2},{1,3},{2,0},{3,1},{4,6},{5,7},{6,4},{7,5},{8,10},{9,11},{10,... | collective-permute-start | bytes 5898248 | tf_op jit(solution)/shard_map/ppermute | solution.py:821
  559.7 9.8 %collective-permute-start.13 = (bf16[512,1792]{1,0:T(8,128)(2,1)}, bf16[512,1792]{1,0:T(8,128)(2,1)}, u32[]{:S(2)}, u32[]{:S(2)}) collective-permute-start(bf16[512,1792]{1,0:T(8,128)(2,1)} %get-tuple-element.102.refs_2_), channel_id=1, source_target_pairs={{0,1},{1,0},{2,3},{3,2},{4,5},{5,4},{6,7},{7,6},{8,9},{9,8},{10,11... | collective-permute-start | bytes 5505032 | tf_op jit(solution)/shard_map/ppermute | solution.py:821
  559.8 36.9 %collective-permute-start.17 = (bf16[512,2560]{1,0:T(8,128)(2,1)}, bf16[512,2560]{1,0:T(8,128)(2,1)}, u32[]{:S(2)}, u32[]{:S(2)}) collective-permute-start(bf16[512,2560]{1,0:T(8,128)(2,1)} %collective-permute-done.1.dy.refs_6_), channel_id=1, source_target_pairs={{0,1},{1,0},{2,3},{3,2},{4,5},{5,4},{6,7},{7,6},{8,9},{9,8},{10,11... | collective-permute-start | bytes 7864328 | tf_op jit(solution)/shard_map/ppermute | solution.py:821
  560.2 36.5 %collective-permute-start.14 = (bf16[512,1792]{1,0:T(8,128)(2,1)}, bf16[512,1792]{1,0:T(8,128)(2,1)}, u32[]{:S(2)}, u32[]{:S(2)}) collective-permute-start(bf16[512,1792]{1,0:T(8,128)(2,1)} %get-tuple-element.82.refs_0_), channel_id=1, source_target_pairs={{0,1},{1,0},{2,3},{3,2},{4,5},{5,4},{6,7},{7,6},{8,9},{9,8},{10,11... | collective-permute-start | bytes 5505032 | tf_op jit(solution)/shard_map/ppermute | solution.py:821
  565.6 31.1 %collective-permute-start.15 = (bf16[512,1792]{1,0:T(8,128)(2,1)}, bf16[512,1792]{1,0:T(8,128)(2,1)S(1)}, u32[]{:S(2)}, u32[]{:S(2)}) collective-permute-start(bf16[512,1792]{1,0:T(8,128)(2,1)} %get-tuple-element.103.refs_2_), channel_id=1, source_target_pairs={{0,1},{1,0},{2,3},{3,2},{4,5},{5,4},{6,7},{7,6},{8,9},{9,8},{10,11... | collective-permute-start | bytes 5505032 | tf_op jit(solution)/shard_map/ppermute | solution.py:821
  566.9 58.1 %collective-permute-start.10 = (bf16[512,1920]{1,0:T(8,128)(2,1)}, bf16[512,1920]{1,0:T(8,128)(2,1)S(1)}, u32[]{:S(2)}, u32[]{:S(2)}) collective-permute-start(bf16[512,1920]{1,0:T(8,128)(2,1)} %attend_back.1.refs_4_), channel_id=1, source_target_pairs={{0,1},{1,0},{2,3},{3,2},{4,5},{5,4},{6,7},{7,6},{8,9},{9,8},{10,11... | collective-permute-start | bytes 5898248 | tf_op jit(solution)/shard_map/ppermute | solution.py:821
  569.5 55.5 %collective-permute-start.11 = (bf16[512,1920]{1,0:T(8,128)(2,1)}, bf16[512,1920]{1,0:T(8,128)(2,1)S(1)}, u32[]{:S(2)}, u32[]{:S(2)}) collective-permute-start(bf16[512,1920]{1,0:T(8,128)(2,1)} %collective-permute-done.5.refs_6_), channel_id=1, source_target_pairs={{0,1},{1,0},{2,3},{3,2},{4,5},{5,4},{6,7},{7,6},{8,9},{9,8},{10,11... | collective-permute-start | bytes 5898248 | tf_op jit(solution)/shard_map/ppermute | solution.py:821
  656.6 36.5 %collective-permute-start.18 = (bf16[128,2560]{1,0:T(8,128)(2,1)S(1)}, bf16[128,2560]{1,0:T(8,128)(2,1)}, u32[]{:S(2)}, u32[]{:S(2)}) collective-permute-start(bf16[128,2560]{1,0:T(8,128)(2,1)S(1)} %add_convert_fusion), channel_id=1, source_target_pairs={{0,4},{4,0},{8,12},{12,8},{1,5},{5,1},{9,13},{13,9},{2,6},{6,2},{1... | collective-permute-start | bytes 1966088 | tf_op jit(solution)/shard_map/ppermute | solution.py:821
  658.1 36.1 %collective-permute-start.19 = (bf16[128,2560]{1,0:T(8,128)(2,1)S(1)}, bf16[128,2560]{1,0:T(8,128)(2,1)S(1)}, u32[]{:S(2)}, u32[]{:S(2)}) collective-permute-start(bf16[128,2560]{1,0:T(8,128)(2,1)S(1)} %add_convert_fusion), channel_id=1, source_target_pairs={{0,8},{4,12},{8,0},{12,4},{1,9},{5,13},{9,1},{13,5},{2,10},{6,14},... | collective-permute-start | bytes 1966088 | tf_op jit(solution)/shard_map/ppermute | solution.py:821
  658.7 35.6 %collective-permute-start.20 = (bf16[128,2560]{1,0:T(8,128)(2,1)S(1)}, bf16[128,2560]{1,0:T(8,128)(2,1)S(1)}, u32[]{:S(2)}, u32[]{:S(2)}) collective-permute-start(bf16[128,2560]{1,0:T(8,128)(2,1)S(1)} %add_convert_fusion), channel_id=1, source_target_pairs={{0,12},{4,8},{8,4},{12,0},{1,13},{5,9},{9,5},{13,1},{2,14},{6,10},... | collective-permute-start | bytes 1966088 | tf_op jit(solution)/shard_map/ppermute | solution.py:821
  (31 other events, 375.8 us)
Sparse Core Ops, SparseCore 0:
  91.2 68.4 all-gather.2
  227.7 59.0 reduce-scatter.3
  428.2 57.0 reduce-scatter.5
  488.6 60.4 reduce-scatter.7
  559.3 94.4 all-gather.4

commit v11 on v10

--- a/solution.py
+++ b/solution.py
@@ -697,10 +697,10 @@
     )(act, dy, wg, wu, wd)
 
 
-def zero_kernel(after, out, zeros, sem):
+def zero_kernel(after, *refs, begin, end):
+    out, zeros, sem = refs[-3:]
     zeros[:] = jnp.zeros_like(zeros)
     step = zeros.shape[0]
-    count = out.shape[0] // step
 
     def send(i, c):
         pltpu.make_async_copy(zeros, out.at[pl.ds(pl.multiple_of(i * step, step), step), :], sem).start()
@@ -710,21 +710,22 @@
         pltpu.make_async_copy(zeros, out.at[pl.ds(0, step), :], sem).wait()
         return c
 
-    lax.fori_loop(0, count, send, 0)
-    lax.fori_loop(0, count, wait, 0)
-
-
-def zero_rows(after, rows, dim, step=200):
+    lax.fori_loop(begin // step, end // step, send, 0)
+    lax.fori_loop(begin // step, end // step, wait, 0)
+
+
+def zero_rows(after, shape, begin, end, base=(), step=200):
     return pl.pallas_call(
-        zero_kernel,
-        out_shape=jax.ShapeDtypeStruct((rows, dim), F32),
-        in_specs=[pl.BlockSpec(memory_space=pltpu.SMEM)],
+        functools.partial(zero_kernel, begin=begin, end=end),
+        out_shape=jax.ShapeDtypeStruct(shape, F32),
+        in_specs=[pl.BlockSpec(memory_space=pltpu.SMEM)] + [pl.BlockSpec(memory_space=pl.ANY)] * len(base),
         out_specs=pl.BlockSpec(memory_space=pl.ANY),
-        scratch_shapes=[pltpu.VMEM((step, dim), F32), pltpu.SemaphoreType.DMA],
+        scratch_shapes=[pltpu.VMEM((step, shape[1]), F32), pltpu.SemaphoreType.DMA],
+        input_output_aliases={1: 0} if base else {},
         compiler_params=pltpu.CompilerParams(vmem_limit_bytes=8 * MIB),
-        cost_estimate=cost(rows * dim),
+        cost_estimate=cost((end - begin) * shape[1]),
         name="zero_rows",
-    )(after)
+    )(after, *base)
 
 
 def scatter_kernel(order, sid, runs, bounds, rows, base_hbm, out_hbm, sums, row_sem, sum_sem):
@@ -866,13 +867,13 @@
         d_act_b = add_up(d_act_b)
         hidden_x, d_gate_x, d_up_x = mlp_block(act_x, dy_x, wg, wu, w_down, False)
         out_part = nn(hidden[:, :ffn], w_down)
-        base = zero_rows(bounds, rows, dim)
+        split = rows // 1000 * 600
+        base = zero_rows(bounds, (rows, dim), 0, split)
         heads_x = barrier((heads_x, act_b))[0]
         head_parts = (attended, swap(attended, core_swap), heads_x, swap(heads_x, core_swap))
-        att_heads = jnp.concatenate([attended] * cp_count)
+        att_heads = jnp.zeros((total, width), BF16)
         for k, piece in enumerate(head_parts):
-            if k:
-                att_heads = lax.dynamic_update_slice_in_dim(att_heads, piece, (cp_rank ^ k) * span, 0)
+            att_heads = lax.dynamic_update_slice_in_dim(att_heads, piece, (cp_rank ^ k) * span, 0)
         d_act_b, hidden_x, d_gate_x, d_up_x, out_part, base, att_heads = barrier((d_act_b, hidden_x, d_gate_x, d_up_x, out_part, base, att_heads))
         d_act_b = to_bf16(d_act_b)
         acts, dys, hiddens, d_gates, d_ups = [(a, swap(a, core_swap), b, swap(b, core_swap)) for a, b in (
@@ -908,7 +909,8 @@
         dqkv_x = swap(dqkv, x_swap)
         dqkvs = (dqkv, swap(dqkv, core_swap), dqkv_x, swap(dqkv_x, core_swap))
         grad_out = weight_grad(info, head_parts, [d_resid_all.reshape(cp_count, span, dim)] * 4)
-        d_act_a, dqkv_x, grad_out, grad_up = barrier((d_act_a, dqkv_x, grad_out, grad_up))
+        base = zero_rows(bounds, (rows, dim), split, rows, (barrier((base, dqkv))[0],))
+        d_act_a, dqkv_x, grad_out, grad_up, base = barrier((d_act_a, dqkv_x, grad_out, grad_up, base))
         d_act_a = to_bf16(d_act_a)
         normed_a, inv_a = rms_stats(x_slice.astype(F32))
         grad_gain_a = jnp.sum(d_act_a * normed_a, axis=0)

time: 708 us -> 710 us (level)
    ppermute x21, waiting for transfers between devices: 83.4 us -> 97.6 us  [compute(): swap = lambda arr, pairs, axis='cp': lax.ppermute(arr, axis, pairs)]
    reduce_scatter x3, waiting for transfers between devices: 9.75 us -> 1.21 us  [compute(): lax.psum_scatter(arr, 'tp', scatter_dimension=0, tiled=True)]
    pallas_call x1 -> x2, Pallas kernels: 27 us -> 28.2 us  [zero_rows(): pl.pallas_call(functools.partial(zero_kernel, begin=begin, end=end), out_...]
  transfers between devices with their start and end apart: 26 -> 26, of which waited for: 9 -> 8; matrix products, arithmetic and copies ran while one was open for 11% -> 11% of each run, Pallas kernels for 38% -> 39%
where the time goes in v11:
time: 710 us; the launch traced here: 705 us
  Pallas kernels  450 us (63%)
  waiting for transfers between devices  102 us (14%)
  local copies, waits for them, and re-layouts  40.6 us (6%)
  matrix products  39.7 us (6%)
  other arithmetic  39.3 us (6%)
  starting transfers between devices  17.9 us (3%)
  between operations  14.5 us (2%)
    pallas_call x5, Pallas kernels, weight_grad(): pl.pallas_call(functools.partial(weight_grad_kernel, pieces=n, splits=spl...  127 us
    ppermute x21, waiting for transfers between devices, compute(): swap = lambda arr, pairs, axis='cp': lax.ppermute(arr, axis, pairs)  97.6 us
    pallas_call x1, Pallas kernels, embed_gather(): pl.pallas_call(embed_kernel, out_shape=[jax.ShapeDtypeStruct((16 * rows,...  68.6 us
    pallas_call x2, Pallas kernels, mlp_block(): pl.pallas_call(functools.partial(mlp_kernel, limit=limit, tiles=tiles), o...  54.3 us
    pallas_call x1, Pallas kernels, spread(): pl.pallas_call(spread_kernel, out_shape=jax.ShapeDtypeStruct((16 * rows,...  42.4 us
    dot_general x5, matrix products, contract(): lax.dot_general(a, b, (((ca,), (cb,)), ((), ())), preferred_element_type=...  35.1 us
    pallas_call x1, Pallas kernels, att_project(): pl.pallas_call(att_kernel, out_shape=[jax.ShapeDtypeStruct((4,) + lse.sha...  34.9 us
    pallas_call x1, Pallas kernels, project_qkv(): pl.pallas_call(functools.partial(qkv_kernel, head_dim=head_dim), out_shap...  32.7 us
  transfers between devices with their start and end apart: 26, of which 8 were waited for; matrix products, arithmetic and copies ran while one was open for 11% of the time, Pallas kernels for 39%

profile of v11, /device:TPU:0, one launch (start us, length us, event | category | flops | bytes accessed | tf_op | source)
XLA Modules:
  0.0 704.6 jit_solution(7578038897559862056)
XLA Ops:
  8.6 6.8 gather_fusion
  22.5 68.6 %embed_gather.1 = (bf16[2048,2560]{1,0:T(8,128)(2,1)}, bf16[128,2560]{1,0:T(8,128)(2,1)}, f32[4,512,128]{2,1,0:T(8,128)}, s32[4,8,512]{2,1,0:T(8,128)}) custom-call(bf16[4,128,2560]{2,1,0:T(8,128)(2,1)} %select_select_fusion.picked, f32[512,128]{1,0:T(8,128)} %pad_maximum_fusion.1.side_f, s32[8,512]{1,0:T(8,128)} %stack.50.side_i), custom_call_target="tpu_custom_call" | custom-call | tf_op jit(solution)/shard_map/embed_gather/pallas_call | solution.py:260
  94.8 32.7 %project_qkv.1 = (bf16[2048,2560]{1,0:T(8,128)(2,1)}, bf16[2048,640]{1,0:T(8,128)(2,1)}, bf16[2048,640]{1,0:T(8,128)(2,1)}, bf16[2048,640]{1,0:T(8,128)(2,1)}) custom-call(bf16[2048,2560]{1,0:T(8,128)(2,1)} %get-tuple-element.67.x.x_all, f32[1,2560]{1,0:T(1,128)} %broadcast_in_dim.88.gain, bf16[2560,640]{1,0:T(8,128)(2,1)} %wq.1, bf16[2560,640]{1,0:T(8,128)(2,1)} %wk.1, ...), custom_call_target="tpu_custom_call" | custom-call | flops 20132659200 | bytes 39321600 | tf_op jit(solution)/shard_map/project_qkv/pallas_call | solution.py:347
  127.6 10.1 %attend.1 = (bf16[512,640]{1,0:T(8,128)(2,1)}, f32[512,8]{1,0:T(8,128)}) custom-call(s32[2]{0:T(128)} %pad_add_fusion.info, s32[4,8,512]{2,1,0:T(8,128)} %get-tuple-element.66.ids, bf16[2048,640]{1,0:T(8,128)(2,1)} %get-tuple-element.69.q, bf16[2048,640]{1,0:T(8,128)(2,1)} %get-tuple-element.70.k, bf16[2048,640]{1,0:T(8,128)(2,1)} %get-tuple-element.71.v, ...), custom_call_target="tpu_custom_call" | custom-call | flops 2684354560 | bytes 5242880 | tf_op jit(solution)/shard_map/attend/pallas_call | solution.py:428
  145.5 8.0 %select_reduce_fusion = (s32[2048]{0:T(1024)S(1)}, s32[2048]{0:T(1024)S(1)}, s32[2048]{0:T(1024)S(1)}) fusion(s32[2048]{0:T(1024)S(1)} %convert_reduce_fusion, s32[2048]{0:T(1024)S(1)} %bitcast.62), kind=kLoop, calls=%fused_computation.4 | loop fusion | flops 33548288 | bytes 40960 | tf_op jit(solution)/shard_map/reduce_sum | solution.py:856
  159.7 34.9 %att_project.1 = (f32[4,512,8]{2,1,0:T(8,128)}, f32[512,2560]{1,0:T(8,128)}, bf16[512,2560]{1,0:T(8,128)(2,1)}) custom-call(bf16[512,640]{1,0:T(8,128)(2,1)} %get-tuple-element.72.att.refs_0_, f32[512,8]{1,0:T(8,128)} %get-tuple-element.73.lse, bf16[2048,2560]{1,0:T(8,128)(2,1)} %get-tuple-element.67.x.x_all, ...), custom_call_target="tpu_custom_call" | custom-call | tf_op jit(solution)/shard_map/att_project/pallas_call | solution.py:593
  194.6 33.0 %mlp_block.2 = (bf16[512,1792]{1,0:T(8,128)(2,1)}, bf16[512,1792]{1,0:T(8,128)(2,1)}, bf16[512,1792]{1,0:T(8,128)(2,1)}, f32[512,2560]{1,0:T(8,128)}) custom-call(bf16[512,2560]{1,0:T(8,128)(2,1)} %get-tuple-element.78.act.refs_4_, bf16[512,2560]{1,0:T(8,128)(2,1)} %refs_4_.1, bf16[1728,2560]{1,0:T(8,128)(2,1)} %bitcast.63, bf16[1728,2560]{1,0:T(8,128)(2,1)} %bitcast.65, ...), custom_call_target="tpu_custom_call" | custom-call | flops 22649241600 | bytes 44236800 | tf_op jit(solution)/shard_map/mlp_block/pallas_call | solution.py:687
  236.8 10.0 %collective-permute-done.3.refs_2_ = bf16[512,640]{1,0:T(8,128)(2,1)S(1)} collective-permute-done((bf16[512,640]{1,0:T(8,128)(2,1)S(1)}, bf16[512,640]{1,0:T(8,128)(2,1)S(1)}, u32[]{:S(2)}, u32[]{:S(2)}) %collective-permute-start.3) | collective-permute-done | bytes 655392 | tf_op jit(solution)/shard_map/ppermute | solution.py:822
  246.8 10.7 %fusion.6 = f32[512,2560]{1,0:T(8,128)} fusion(bf16[1728,2560]{1,0:T(8,128)(2,1)} %wd.3, bf16[512,1792]{1,0:T(8,128)(2,1)S(1)} %copy-done.26), kind=kOutput, calls=%fused_computation.19 | convolution fusion | flops 4529848320 | bytes 15925248 | tf_op jit(solution)/shard_map/dot_general | solution.py:32
  257.5 16.8 %zero_rows.2.refs_0_ = f32[8000,2560]{1,0:T(8,128)} custom-call(s32[2]{0:T(128)S(1)} %pad_add_fusion.1.after.bounds), custom_call_target="tpu_custom_call" | custom-call | flops 12288000 | bytes 24000 | tf_op jit(solution)/shard_map/zero_rows/pallas_call | solution.py:718
  278.5 24.6 %collective-permute-done.1.dy.refs_6_ = bf16[512,2560]{1,0:T(8,128)(2,1)} collective-permute-done((bf16[512,2560]{1,0:T(8,128)(2,1)}, bf16[512,2560]{1,0:T(8,128)(2,1)}, u32[]{:S(2)}, u32[]{:S(2)}) %collective-permute-start.1) | collective-permute-done | bytes 2621472 | tf_op jit(solution)/shard_map/ppermute | solution.py:822
  303.1 56.0 %collective-permute-done.act.refs_6_ = bf16[512,2560]{1,0:T(8,128)(2,1)} collective-permute-done((bf16[512,2560]{1,0:T(8,128)(2,1)}, bf16[512,2560]{1,0:T(8,128)(2,1)}, u32[]{:S(2)}, u32[]{:S(2)}) %collective-permute-start) | collective-permute-done | bytes 2621472 | tf_op jit(solution)/shard_map/ppermute | solution.py:822
  359.1 21.3 %mlp_block.3 = (bf16[512,1792]{1,0:T(8,128)(2,1)}, bf16[512,1792]{1,0:T(8,128)(2,1)}, bf16[512,1792]{1,0:T(8,128)(2,1)}) custom-call(bf16[512,2560]{1,0:T(8,128)(2,1)} %collective-permute-done.act.refs_6_, bf16[512,2560]{1,0:T(8,128)(2,1)} %collective-permute-done.1.dy.refs_6_, bf16[1728,2560]{1,0:T(8,128)(2,1)} %bitcast.64, bf16[1728,2560]{1,0:T(8,128)(2,1)} %bitcast.66, ...), custom_call_target="tpu_custom_call" | custom-call | flops 13589544960 | bytes 26542080 | tf_op jit(solution)/shard_map/mlp_block/pallas_call | solution.py:687
  385.4 42.4 %spread.1 = bf16[2048,2560]{1,0:T(8,128)(2,1)} custom-call(bf16[128,2560]{1,0:T(8,128)(2,1)} %fusion.36.piece), custom_call_target="tpu_custom_call" | custom-call | tf_op jit(solution)/shard_map/spread/pallas_call | solution.py:298
  430.0 13.0 %convolution_convert_fusion.do = bf16[2048,640]{1,0:T(8,128)(2,1)S(1)} fusion(bf16[2048,2560]{1,0:T(8,128)(2,1)} %spread.1, bf16[640,2560]{1,0:T(8,128)(2,1)} %param.23), kind=kOutput, calls=%fused_computation.16 | convolution fusion | flops 6712197120 | bytes 16384000 | tf_op jit(solution)/shard_map/dot_general | solution.py:32
  450.5 22.0 %attend_back.1.refs_4_ = bf16[512,1920]{1,0:T(8,128)(2,1)} custom-call(s32[2]{0:T(128)} %pad_add_fusion.info, s32[4,8,512]{2,1,0:T(8,128)} %get-tuple-element.66.ids, bf16[2048,640]{1,0:T(8,128)(2,1)} %get-tuple-element.69.q, bf16[2048,640]{1,0:T(8,128)(2,1)} %get-tuple-element.70.k, bf16[2048,640]{1,0:T(8,128)(2,1)} %get-tuple-element.71.v, ...), custom_call_target="tpu_custom_call" | custom-call | flops 4697620480 | bytes 9175040 | tf_op jit(solution)/shard_map/attend_back/pallas_call | solution.py:500
  488.4 6.2 collective-permute-start.5
  494.6 15.4 %weight_grad.5 = f32[640,2560]{1,0:T(8,128)} custom-call(s32[2]{0:T(128)} %pad_add_fusion.info, bf16[512,640]{1,0:T(8,128)(2,1)} %get-tuple-element.72.att.refs_0_, bf16[512,640]{1,0:T(8,128)(2,1)} %copy-done.8, bf16[512,640]{1,0:T(8,128)(2,1)} %copy-done.9, bf16[512,640]{1,0:T(8,128)(2,1)} %copy-done.10, bf16[4,512,2560]{2,1,0:T(8,128)(2,1)} %bitcast.38, ...), custom_call_target="tpu_custom_call" | custom-call | flops 6710886400 | bytes 13107200 | tf_op jit(solution)/shard_map/weight_grad/pallas_call | solution.py:629
  510.0 11.4 %zero_rows.3.base_hbm = f32[8000,2560]{1,0:T(8,128)} custom-call(s32[2]{0:T(128)S(1)} %pad_add_fusion.1.after.bounds, f32[8000,2560]{1,0:T(8,128)} %zero_rows.2.refs_0_), custom_call_target="tpu_custom_call", output_to_operand_aliasing={{}: (1, {})} | custom-call | flops 8192000 | bytes 16000 | tf_op jit(solution)/shard_map/zero_rows/pallas_call | solution.py:718
  523.5 27.2 %weight_grad.6 = f32[1728,2560]{1,0:T(8,128)} custom-call(s32[2]{0:T(128)} %pad_add_fusion.info, bf16[512,1792]{1,0:T(8,128)(2,1)} %get-tuple-element.96.refs_0_, bf16[512,1792]{1,0:T(8,128)(2,1)} %copy-done.28, bf16[512,1792]{1,0:T(8,128)(2,1)} %get-tuple-element.97.refs_2_, bf16[512,1792]{1,0:T(8,128)(2,1)} %collective-permute-done.7.refs_3_, ...), custom_call_target="tpu_custom_call" | custom-call | flops 18119393280 | bytes 35389440 | tf_op jit(solution)/shard_map/weight_grad/pallas_call | solution.py:629
  571.4 27.0 %weight_grad.8 = f32[1728,2560]{1,0:T(8,128)} custom-call(s32[2]{0:T(128)} %pad_add_fusion.info, bf16[512,1792]{1,0:T(8,128)(2,1)} %get-tuple-element.105.refs_0_, bf16[512,1792]{1,0:T(8,128)(2,1)} %collective-permute-done.12.refs_1_, bf16[512,1792]{1,0:T(8,128)(2,1)} %get-tuple-element.106.refs_2_, bf16[512,1792]{1,0:T(8,128)(2,1)} %collective-permute-done.13.refs_3_, ...), custom_call_target="tpu_custom_call" | custom-call | flops 18119393280 | bytes 35389440 | tf_op jit(solution)/shard_map/weight_grad/pallas_call | solution.py:629
  599.7 27.0 %weight_grad.9 = f32[1728,2560]{1,0:T(8,128)} custom-call(s32[2]{0:T(128)} %pad_add_fusion.info, bf16[512,1792]{1,0:T(8,128)(2,1)} %get-tuple-element.84.refs_0_, bf16[512,1792]{1,0:T(8,128)(2,1)} %collective-permute-done.14.refs_1_, bf16[512,1792]{1,0:T(8,128)(2,1)} %get-tuple-element.107.refs_2_, bf16[512,1792]{1,0:T(8,128)(2,1)} %copy-done.27, ...), custom_call_target="tpu_custom_call" | custom-call | flops 18119393280 | bytes 35389440 | tf_op jit(solution)/shard_map/weight_grad/pallas_call | solution.py:629
  628.7 29.9 %weight_grad.7 = (f32[2560,640]{1,0:T(8,128)}, f32[2560,640]{1,0:T(8,128)}, f32[2560,640]{1,0:T(8,128)}) custom-call(s32[2]{0:T(128)} %pad_add_fusion.info, bf16[4,512,2560]{2,1,0:T(8,128)(2,1)} %bitcast.71, bf16[4,512,2560]{2,1,0:T(8,128)(2,1)} %bitcast.72, bf16[4,512,2560]{2,1,0:T(8,128)(2,1)} %bitcast.73, bf16[4,512,2560]{2,1,0:T(8,128)(2,1)} %bitcast.74, ...), custom_call_target="tpu_custom_call" | custom-call | flops 20132659200 | bytes 39321600 | tf_op jit(solution)/shard_map/weight_grad/pallas_call | solution.py:629
  662.1 30.7 %scatter_rows.1 = f32[8000,2560]{1,0:T(8,128)} custom-call(s32[2048]{0:T(1024)} %get-tuple-element.112.order, s32[2048]{0:T(1024)} %get-tuple-element.113.sid, s32[2048]{0:T(1024)} %select_reduce_fusion.2.runs, s32[2]{0:T(128)} %copy-done, f32[2176,2560]{1,0:T(8,128)} %all-gather.5.cloned.1.call-done.rows, ...), custom_call_target="tpu_custom_call", output_to_operand_aliasing={{}: (5, {})} | custom-call | tf_op jit(solution)/shard_map/scatter_rows/pallas_call | solution.py:782
  (163 shorter events, 104.3 us)
Async XLA Ops:
  7.2 152.5 %all-gather.3.cloned.1.call-start = ((), (), s32[]{:S(2)}) async-start(), calls=%async_computation.3 | async-start | bytes 8192000 | tf_op jit(solution)/shard_map/all_gather | solution.py:820
  91.1 289.3 %reduce-scatter.4.cloned.1.call-start = ((), (), s32[]{:S(2)}) async-start(), calls=%async_computation.4 | async-start | bytes 6553600 | tf_op jit(solution)/shard_map/reduce_scatter | solution.py:821
  227.6 257.6 %reduce-scatter.6.cloned.1.call-start = ((), (), s32[]{:S(2)}) async-start(), calls=%async_computation.5 | async-start | bytes 6553600 | tf_op jit(solution)/shard_map/reduce_scatter | solution.py:821
  228.7 18.2 %collective-permute-start.3 = (bf16[512,640]{1,0:T(8,128)(2,1)S(1)}, bf16[512,640]{1,0:T(8,128)(2,1)S(1)}, u32[]{:S(2)}, u32[]{:S(2)}) collective-permute-start(bf16[512,640]{1,0:T(8,128)(2,1)S(1)} %copy-done.3), channel_id=1, source_target_pairs={{0,2},{1,3},{2,0},{3,1},{4,6},{5,7},{6,4},{7,5},{8,10},{9,11},{10,... | collective-permute-start | bytes 1966088 | tf_op jit(solution)/shard_map/ppermute | solution.py:822
  231.3 71.9 %collective-permute-start.1 = (bf16[512,2560]{1,0:T(8,128)(2,1)}, bf16[512,2560]{1,0:T(8,128)(2,1)}, u32[]{:S(2)}, u32[]{:S(2)}) collective-permute-start(bf16[512,2560]{1,0:T(8,128)(2,1)} %refs_4_.1), channel_id=1, source_target_pairs={{0,2},{1,3},{2,0},{3,1},{4,6},{5,7},{6,4},{7,5},{8,10},{9,11},{10,... | collective-permute-start | bytes 7864328 | tf_op jit(solution)/shard_map/ppermute | solution.py:822
  231.3 127.8 %collective-permute-start = (bf16[512,2560]{1,0:T(8,128)(2,1)}, bf16[512,2560]{1,0:T(8,128)(2,1)}, u32[]{:S(2)}, u32[]{:S(2)}) collective-permute-start(bf16[512,2560]{1,0:T(8,128)(2,1)} %get-tuple-element.78.act.refs_4_), channel_id=1, source_target_pairs={{0,2},{1,3},{2,0},{3,1},{4,6},{5,7},{6,4},{7,5},{8,10},{9,11},{10,... | collective-permute-start | bytes 7864328 | tf_op jit(solution)/shard_map/ppermute | solution.py:822
  246.8 29.9 %collective-permute-start.4 = (bf16[512,640]{1,0:T(8,128)(2,1)S(1)}, bf16[512,640]{1,0:T(8,128)(2,1)S(1)}, u32[]{:S(2)}, u32[]{:S(2)}) collective-permute-start(bf16[512,640]{1,0:T(8,128)(2,1)S(1)} %collective-permute-done.3.refs_2_), channel_id=1, source_target_pairs={{0,1},{1,0},{2,3},{3,2},{4,5},{5,4},{6,7},{7,6},{8,9},{9,8},{10,11... | collective-permute-start | bytes 1966088 | tf_op jit(solution)/shard_map/ppermute | solution.py:822
  427.9 122.8 %reduce-scatter.8.cloned.1.call-start = ((), (), s32[]{:S(2)}) async-start(), calls=%async_computation.6 | async-start | bytes 6553600 | tf_op jit(solution)/shard_map/reduce_scatter | solution.py:821
  487.0 171.6 %all-gather.5.cloned.1.call-start = ((), (), s32[]{:S(2)}) async-start(), calls=%async_computation.7 | async-start | bytes 23674880 | tf_op jit(solution)/shard_map/all_gather | solution.py:820
  487.1 34.4 %collective-permute-start.8 = (bf16[512,2560]{1,0:T(8,128)(2,1)}, bf16[512,2560]{1,0:T(8,128)(2,1)S(1)}, u32[]{:S(2)}, u32[]{:S(2)}) collective-permute-start(bf16[512,2560]{1,0:T(8,128)(2,1)} %get-tuple-element.78.act.refs_4_), channel_id=1, source_target_pairs={{0,1},{1,0},{2,3},{3,2},{4,5},{5,4},{6,7},{7,6},{8,9},{9,8},{10,11... | collective-permute-start | bytes 7864328 | tf_op jit(solution)/shard_map/ppermute | solution.py:822
  487.1 34.3 %collective-permute-start.9 = (bf16[512,2560]{1,0:T(8,128)(2,1)}, bf16[512,2560]{1,0:T(8,128)(2,1)}, u32[]{:S(2)}, u32[]{:S(2)}) collective-permute-start(bf16[512,2560]{1,0:T(8,128)(2,1)} %collective-permute-done.act.refs_6_), channel_id=1, source_target_pairs={{0,1},{1,0},{2,3},{3,2},{4,5},{5,4},{6,7},{7,6},{8,9},{9,8},{10,11... | collective-permute-start | bytes 7864328 | tf_op jit(solution)/shard_map/ppermute | solution.py:822
  487.6 33.8 %collective-permute-start.6 = (bf16[512,1792]{1,0:T(8,128)(2,1)}, bf16[512,1792]{1,0:T(8,128)(2,1)S(1)}, u32[]{:S(2)}, u32[]{:S(2)}) collective-permute-start(bf16[512,1792]{1,0:T(8,128)(2,1)} %get-tuple-element.96.refs_0_), channel_id=1, source_target_pairs={{0,1},{1,0},{2,3},{3,2},{4,5},{5,4},{6,7},{7,6},{8,9},{9,8},{10,11... | collective-permute-start | bytes 5505032 | tf_op jit(solution)/shard_map/ppermute | solution.py:822
  487.7 33.8 %collective-permute-start.7 = (bf16[512,1792]{1,0:T(8,128)(2,1)}, bf16[512,1792]{1,0:T(8,128)(2,1)}, u32[]{:S(2)}, u32[]{:S(2)}) collective-permute-start(bf16[512,1792]{1,0:T(8,128)(2,1)} %get-tuple-element.97.refs_2_), channel_id=1, source_target_pairs={{0,1},{1,0},{2,3},{3,2},{4,5},{5,4},{6,7},{7,6},{8,9},{9,8},{10,11... | collective-permute-start | bytes 5505032 | tf_op jit(solution)/shard_map/ppermute | solution.py:822
  488.4 62.3 %collective-permute-start.5 = (bf16[512,1920]{1,0:T(8,128)(2,1)}, bf16[512,1920]{1,0:T(8,128)(2,1)}, u32[]{:S(2)}, u32[]{:S(2)}) collective-permute-start(bf16[512,1920]{1,0:T(8,128)(2,1)} %attend_back.1.refs_4_), channel_id=1, source_target_pairs={{0,2},{1,3},{2,0},{3,1},{4,6},{5,7},{6,4},{7,5},{8,10},{9,11},{10,... | collective-permute-start | bytes 5898248 | tf_op jit(solution)/shard_map/ppermute | solution.py:822
  561.1 7.4 %collective-permute-start.12 = (bf16[512,1792]{1,0:T(8,128)(2,1)}, bf16[512,1792]{1,0:T(8,128)(2,1)}, u32[]{:S(2)}, u32[]{:S(2)}) collective-permute-start(bf16[512,1792]{1,0:T(8,128)(2,1)} %get-tuple-element.105.refs_0_), channel_id=1, source_target_pairs={{0,1},{1,0},{2,3},{3,2},{4,5},{5,4},{6,7},{7,6},{8,9},{9,8},{10,11... | collective-permute-start | bytes 5505032 | tf_op jit(solution)/shard_map/ppermute | solution.py:822
  561.4 9.8 %collective-permute-start.13 = (bf16[512,1792]{1,0:T(8,128)(2,1)}, bf16[512,1792]{1,0:T(8,128)(2,1)}, u32[]{:S(2)}, u32[]{:S(2)}) collective-permute-start(bf16[512,1792]{1,0:T(8,128)(2,1)} %get-tuple-element.106.refs_2_), channel_id=1, source_target_pairs={{0,1},{1,0},{2,3},{3,2},{4,5},{5,4},{6,7},{7,6},{8,9},{9,8},{10,11... | collective-permute-start | bytes 5505032 | tf_op jit(solution)/shard_map/ppermute | solution.py:822
  561.7 36.8 %collective-permute-start.17 = (bf16[512,2560]{1,0:T(8,128)(2,1)}, bf16[512,2560]{1,0:T(8,128)(2,1)}, u32[]{:S(2)}, u32[]{:S(2)}) collective-permute-start(bf16[512,2560]{1,0:T(8,128)(2,1)} %collective-permute-done.1.dy.refs_6_), channel_id=1, source_target_pairs={{0,1},{1,0},{2,3},{3,2},{4,5},{5,4},{6,7},{7,6},{8,9},{9,8},{10,11... | collective-permute-start | bytes 7864328 | tf_op jit(solution)/shard_map/ppermute | solution.py:822
  561.9 36.6 %collective-permute-start.14 = (bf16[512,1792]{1,0:T(8,128)(2,1)}, bf16[512,1792]{1,0:T(8,128)(2,1)}, u32[]{:S(2)}, u32[]{:S(2)}) collective-permute-start(bf16[512,1792]{1,0:T(8,128)(2,1)} %get-tuple-element.84.refs_0_), channel_id=1, source_target_pairs={{0,1},{1,0},{2,3},{3,2},{4,5},{5,4},{6,7},{7,6},{8,9},{9,8},{10,11... | collective-permute-start | bytes 5505032 | tf_op jit(solution)/shard_map/ppermute | solution.py:822
  567.3 31.2 %collective-permute-start.15 = (bf16[512,1792]{1,0:T(8,128)(2,1)}, bf16[512,1792]{1,0:T(8,128)(2,1)S(1)}, u32[]{:S(2)}, u32[]{:S(2)}) collective-permute-start(bf16[512,1792]{1,0:T(8,128)(2,1)} %get-tuple-element.107.refs_2_), channel_id=1, source_target_pairs={{0,1},{1,0},{2,3},{3,2},{4,5},{5,4},{6,7},{7,6},{8,9},{9,8},{10,11... | collective-permute-start | bytes 5505032 | tf_op jit(solution)/shard_map/ppermute | solution.py:822
  568.5 58.2 %collective-permute-start.10 = (bf16[512,1920]{1,0:T(8,128)(2,1)}, bf16[512,1920]{1,0:T(8,128)(2,1)S(1)}, u32[]{:S(2)}, u32[]{:S(2)}) collective-permute-start(bf16[512,1920]{1,0:T(8,128)(2,1)} %attend_back.1.refs_4_), channel_id=1, source_target_pairs={{0,1},{1,0},{2,3},{3,2},{4,5},{5,4},{6,7},{7,6},{8,9},{9,8},{10,11... | collective-permute-start | bytes 5898248 | tf_op jit(solution)/shard_map/ppermute | solution.py:822
  571.2 55.6 %collective-permute-start.11 = (bf16[512,1920]{1,0:T(8,128)(2,1)}, bf16[512,1920]{1,0:T(8,128)(2,1)S(1)}, u32[]{:S(2)}, u32[]{:S(2)}) collective-permute-start(bf16[512,1920]{1,0:T(8,128)(2,1)} %collective-permute-done.5.refs_6_), channel_id=1, source_target_pairs={{0,1},{1,0},{2,3},{3,2},{4,5},{5,4},{6,7},{7,6},{8,9},{9,8},{10,11... | collective-permute-start | bytes 5898248 | tf_op jit(solution)/shard_map/ppermute | solution.py:822
  658.6 36.5 %collective-permute-start.18 = (bf16[128,2560]{1,0:T(8,128)(2,1)S(1)}, bf16[128,2560]{1,0:T(8,128)(2,1)}, u32[]{:S(2)}, u32[]{:S(2)}) collective-permute-start(bf16[128,2560]{1,0:T(8,128)(2,1)S(1)} %add_convert_fusion), channel_id=1, source_target_pairs={{0,4},{4,0},{8,12},{12,8},{1,5},{5,1},{9,13},{13,9},{2,6},{6,2},{1... | collective-permute-start | bytes 1966088 | tf_op jit(solution)/shard_map/ppermute | solution.py:822
  659.1 37.1 %collective-permute-start.19 = (bf16[128,2560]{1,0:T(8,128)(2,1)S(1)}, bf16[128,2560]{1,0:T(8,128)(2,1)S(1)}, u32[]{:S(2)}, u32[]{:S(2)}) collective-permute-start(bf16[128,2560]{1,0:T(8,128)(2,1)S(1)} %add_convert_fusion), channel_id=1, source_target_pairs={{0,8},{4,12},{8,0},{12,4},{1,9},{5,13},{9,1},{13,5},{2,10},{6,14},... | collective-permute-start | bytes 1966088 | tf_op jit(solution)/shard_map/ppermute | solution.py:822
  659.9 36.4 %collective-permute-start.20 = (bf16[128,2560]{1,0:T(8,128)(2,1)S(1)}, bf16[128,2560]{1,0:T(8,128)(2,1)S(1)}, u32[]{:S(2)}, u32[]{:S(2)}) collective-permute-start(bf16[128,2560]{1,0:T(8,128)(2,1)S(1)} %add_convert_fusion), channel_id=1, source_target_pairs={{0,12},{4,8},{8,4},{12,0},{1,13},{5,9},{9,5},{13,1},{2,14},{6,10},... | collective-permute-start | bytes 1966088 | tf_op jit(solution)/shard_map/ppermute | solution.py:822
  (31 other events, 621.9 us)
Sparse Core Ops, SparseCore 0:
  91.2 68.4 all-gather.2
  227.7 58.9 reduce-scatter.3
  428.0 57.1 reduce-scatter.5
  488.5 59.9 reduce-scatter.7
  561.0 93.1 all-gather.4

commit v12 on v11

--- a/solution.py
+++ b/solution.py
@@ -93,6 +93,7 @@
 
 MESH = pl.DeviceIdType.MESH
 ORDERS = (("x", "y", "z"), ("y", "z", "x"), ("z", "x", "y"))
+COUNTS = (21, 21, 24, 24, 48)
 FLIPS = tuple(tuple(d for i, d in enumerate(DIMS) if n >> i & 1) for n in range(8))
 
 
@@ -107,10 +108,11 @@
 
 
 class Gather:
-    def __init__(self, place, buf, send, recv, core_send, core_recv):
-        self.place, self.buf, self.send, self.recv, self.core_send, self.core_recv = place, buf, send, recv, core_send, core_recv
+    def __init__(self, place, buf, out, send, recv, core_send, core_recv, out_sem):
+        self.place, self.buf, self.out = place, buf, out
+        self.send, self.recv, self.core_send, self.core_recv, self.out_sem = send, recv, core_send, core_recv, out_sem
         self.parts = column_parts(buf.shape[2], 3)
-        self.started = []
+        self.started, self.stores = [], []
 
     def view(self, part, flip):
         start, size = self.parts[part]
@@ -139,46 +141,43 @@
         for dim in order[last + 1:]:
             self.go(self.hop(part, flip, dim))
         self.go(self.core_hop(part, flip))
+        self.store(part, flip)
+
+    def take(self, part, flip):
+        index = part * 8 + flip_code(flip)
+        there = flip + ("core",)
+        ref = self.view(part, there)
+        pltpu.make_async_remote_copy(src_ref=ref, dst_ref=ref, send_sem=self.core_send.at[index], recv_sem=self.core_recv.at[index], device_id=self.place.device(("core",)), device_id_type=MESH).wait_recv()
+        self.store(part, there)
+
+    def store(self, part, flip):
+        start, size = self.parts[part]
+        rows = self.buf.shape[1]
+        dst = self.out.at[pl.ds(self.place.slot(flip) * rows, rows), pl.ds(start, size)]
+        copy = pltpu.make_async_copy(self.view(part, flip), dst, self.out_sem.at[len(self.stores)])
+        copy.start()
+        self.stores.append(copy)
 
     def run(self):
         for step in range(3):
             for part, order in enumerate(ORDERS):
                 self.go(self.hop(part, (), order[step]))
-        for part in range(3):
-            self.go(self.core_hop(part, ()))
+        pending = [(part, ()) for part in range(3)]
+        for item in pending:
+            self.go(self.core_hop(*item))
+            self.store(*item)
         for step in range(3):
-            for flip in FLIPS[1:]:
-                for part, order in enumerate(ORDERS):
-                    if max(order.index(d) for d in flip) == step and len(flip) == 1:
-                        self.wait(part, flip)
-            for flip in FLIPS[1:]:
-                for part, order in enumerate(ORDERS):
-                    if max(order.index(d) for d in flip) == step and len(flip) > 1:
-                        self.wait(part, flip)
-
-    def finish(self, out, out_sem):
-        rows = self.buf.shape[1]
-        copies = []
-
-        def store(flip):
-            slot = self.place.slot(flip)
-            c = pltpu.make_async_copy(self.buf.at[slot], out.at[pl.ds(slot * rows, rows), :], out_sem.at[len(copies)])
-            c.start()
-            copies.append(c)
-
-        for flip in FLIPS:
-            store(flip)
-        for flip in FLIPS:
-            other = flip + ("core",)
-            for part in range(3):
-                start, size = self.parts[part]
-                ref = self.buf.at[self.place.slot(other), :, pl.ds(start, size)]
-                index = part * 8 + flip_code(flip)
-                pltpu.make_async_remote_copy(src_ref=ref, dst_ref=ref, send_sem=self.core_send.at[index], recv_sem=self.core_recv.at[index], device_id=self.place.device(("core",)), device_id_type=MESH).wait_recv()
-            store(other)
+            batch = [(part, flip) for flip in sorted(FLIPS[1:], key=len) for part, order in enumerate(ORDERS) if max(order.index(d) for d in flip) == step]
+            for item in batch:
+                self.wait(*item)
+            for item in pending:
+                self.take(*item)
+            pending = batch
+        for item in pending:
+            self.take(*item)
         for c in self.started:
             c.wait_send()
-        for c in copies:
+        for c in self.stores:
             c.wait()
 
 
@@ -237,11 +236,9 @@
         part = picked[place.tp(), :, cols] + r1[h, 0]
         second(h).wait_recv()
         buf[mine, :, cols] = part + r2[h]
-    gather = Gather(place, buf, send, recv, core_send, core_recv)
-    gather.run()
     keeps.append(pltpu.make_async_copy(buf.at[mine], slice_out, slice_sem.at[2]))
     keeps[-1].start()
-    gather.finish(out, out_sem)
+    Gather(place, buf, out, send, recv, core_send, core_recv, out_sem).run()
     for c in keeps:
         c.wait()
     for i in range(2):
@@ -272,7 +269,7 @@
             pltpu.VMEM((2, 2, rows, half), BF16),
             pltpu.VMEM((2, rows, half), BF16),
             pltpu.VMEM((2, rows, half), BF16),
-            dma((21,)), dma((21,)), dma((24,)), dma((24,)), dma((16,)),
+            *[dma((n,)) for n in COUNTS],
             *[dma((2, 3))] * 4, dma((3,)),
         ],
         compiler_params=pltpu.CompilerParams(collective_id=0, has_side_effects=True, vmem_limit_bytes=FULL),
@@ -280,30 +277,51 @@
     )(picked, side_f, side_i)
 
 
-def spread_kernel(piece, out, buf, send, recv, core_send, core_recv, out_sem, load):
+def spread_kernel(d_act, res, dy, gain, out, d_resid, d_gain, buf, send, recv, core_send, core_recv, out_sem):
     place = Place()
-    first = pltpu.make_async_copy(piece, buf.at[place.slot()], load)
-    first.start()
+    d = to_bf16(d_act[:])
+    normed, inv = rms_stats(res[:])
+    t = dy[:].astype(F32) + rms_back(d * gain[:], normed, inv)
+    d_resid[:] = t
+    d_gain[:] = jnp.sum(d * normed, 0, keepdims=True)
+    buf[place.slot()] = t.astype(BF16)
     place.meet(("x", "y", "z", "core"))
-    first.wait()
-    gather = Gather(place, buf, send, recv, core_send, core_recv)
-    gather.run()
-    gather.finish(out, out_sem)
-
-
-def spread(piece):
-    rows, dim = piece.shape
+    Gather(place, buf, out, send, recv, core_send, core_recv, out_sem).run()
+
+
+def spread(d_act, res, dy, gain):
+    rows, dim = res.shape
     dma = pltpu.SemaphoreType.DMA
-    hbm = pl.BlockSpec(memory_space=pltpu.HBM)
+    vmem = pl.BlockSpec(memory_space=pltpu.VMEM)
     return pl.pallas_call(
         spread_kernel,
-        out_shape=jax.ShapeDtypeStruct((16 * rows, dim), BF16),
-        in_specs=[hbm],
-        out_specs=hbm,
-        scratch_shapes=[pltpu.VMEM((16, rows, dim), BF16), *[dma((n,)) for n in (21, 21, 24, 24, 16)], dma],
+        out_shape=[jax.ShapeDtypeStruct((16 * rows, dim), BF16), jax.ShapeDtypeStruct((rows, dim), F32), jax.ShapeDtypeStruct((1, dim), F32)],
+        in_specs=[vmem] * 4,
+        out_specs=[pl.BlockSpec(memory_space=pltpu.HBM), vmem, vmem],
+        scratch_shapes=[pltpu.VMEM((16, rows, dim), BF16), *[dma((n,)) for n in COUNTS]],
         compiler_params=pltpu.CompilerParams(collective_id=2, has_side_effects=True, vmem_limit_bytes=FULL),
         name="spread",
-    )(piece)
+    )(d_act, res, dy, gain)
+
+
+def payload_kernel(d_act, x, d_resid, gain, d_gain_b, out):
+    rows = x.shape[0]
+    d = to_bf16(d_act[:])
+    normed, inv = rms_stats(x[:].astype(F32))
+    out[:rows] = d_resid[:] + rms_back(d * gain[:], normed, inv)
+    d_gain_a = jnp.sum(d * normed, 0, keepdims=True)
+    extra = (out.shape[0] - rows, out.shape[1])
+    out[rows:] = jnp.where(lax.broadcasted_iota(I32, extra, 0) == 0, d_gain_a, d_gain_b[:])
+
+
+def payload_rows(d_act, x, d_resid, gain, d_gain_b):
+    rows, dim = x.shape
+    return pl.pallas_call(
+        payload_kernel,
+        out_shape=jax.ShapeDtypeStruct((rows + 8, dim), F32),
+        compiler_params=pltpu.CompilerParams(vmem_limit_bytes=FULL),
+        name="payload_rows",
+    )(d_act, x, d_resid, gain, d_gain_b)
 
 
 def slot_block(j):
@@ -875,7 +893,6 @@
         for k, piece in enumerate(head_parts):
             att_heads = lax.dynamic_update_slice_in_dim(att_heads, piece, (cp_rank ^ k) * span, 0)
         d_act_b, hidden_x, d_gate_x, d_up_x, out_part, base, att_heads = barrier((d_act_b, hidden_x, d_gate_x, d_up_x, out_part, base, att_heads))
-        d_act_b = to_bf16(d_act_b)
         acts, dys, hiddens, d_gates, d_ups = [(a, swap(a, core_swap), b, swap(b, core_swap)) for a, b in (
             (act_b, act_x), (dy, dy_x), (hidden, hidden_x), (d_gate, d_gate_x), (d_up, d_up_x))]
         grad_down = weight_grad(info, hiddens, dys, rows=ffn)
@@ -886,10 +903,8 @@
             return lax.dynamic_slice_in_dim(arr, tp_rank * part, part, 0)
 
         res_part = mine(residual)
-        normed_b, inv_b = rms_stats(res_part)
-        grad_gain_b = jnp.sum(d_act_b * normed_b, axis=0)
-        d_resid = mine(dy).astype(F32) + rms_back(d_act_b * gain_b, normed_b, inv_b)
-        d_resid_all, out_part = barrier((spread(d_resid.astype(BF16)), out_part))
+        d_resid_all, d_resid, d_gain_b = spread(d_act_b, res_part, mine(dy), gain_b[None])
+        d_resid_all, out_part = barrier((d_resid_all, out_part))
         out_slice = add_up(out_part)
         out_slice = (res_part + out_slice).astype(BF16)
 
@@ -911,11 +926,7 @@
         grad_out = weight_grad(info, head_parts, [d_resid_all.reshape(cp_count, span, dim)] * 4)
         base = zero_rows(bounds, (rows, dim), split, rows, (barrier((base, dqkv))[0],))
         d_act_a, dqkv_x, grad_out, grad_up, base = barrier((d_act_a, dqkv_x, grad_out, grad_up, base))
-        d_act_a = to_bf16(d_act_a)
-        normed_a, inv_a = rms_stats(x_slice.astype(F32))
-        grad_gain_a = jnp.sum(d_act_a * normed_a, axis=0)
-        d_embed = d_resid + rms_back(d_act_a * gain_a, normed_a, inv_a)
-        payload = jnp.concatenate([d_embed, jnp.stack([grad_gain_a, grad_gain_b] * 4)])
+        payload = payload_rows(d_act_a, x_slice, d_resid, gain_a[None], d_gain_b)
         gathered = join(payload, both)
         grad_qkv = weight_grad(info, [act_a.reshape(cp_count, span, dim)] * 4, dqkvs, splits=3)
         gathered, grad_qkv, grad_gate, grad_down = barrier((gathered, grad_qkv, grad_gate, grad_down))

time: 710 us -> 700 us (0.986)
  other arithmetic: 39.3 us -> 27.3 us
    pallas_call x1 -> x2, Pallas kernels: 42.4 us -> 48.3 us  [the longest x1 44.3 us: spread(): pl.pallas_call(spread_kernel, out_shape=[jax.ShapeDtypeStruct((16 * rows,...]
where the time goes in v12:
time: 700 us; the launch traced here: 694 us
  Pallas kernels  457 us (65%)
  waiting for transfers between devices  102 us (15%)
  matrix products  39.7 us (6%)
  local copies, waits for them, and re-layouts  37.1 us (5%)
  other arithmetic  27.3 us (4%)
  starting transfers between devices  15.4 us (2%)
  between operations  14.5 us (2%)
    pallas_call x5, Pallas kernels, weight_grad(): pl.pallas_call(functools.partial(weight_grad_kernel, pieces=n, splits=spl...  127 us
    ppermute x21, waiting for transfers between devices, compute(): swap = lambda arr, pairs, axis='cp': lax.ppermute(arr, axis, pairs)  97.7 us
    pallas_call x1, Pallas kernels, embed_gather(): pl.pallas_call(embed_kernel, out_shape=[jax.ShapeDtypeStruct((16 * rows,...  66.9 us
    pallas_call x2, Pallas kernels, mlp_block(): pl.pallas_call(functools.partial(mlp_kernel, limit=limit, tiles=tiles), o...  54.3 us
    pallas_call x1, Pallas kernels, spread(): pl.pallas_call(spread_kernel, out_shape=[jax.ShapeDtypeStruct((16 * rows,...  44.3 us
    pallas_call x1, Pallas kernels, att_project(): pl.pallas_call(att_kernel, out_shape=[jax.ShapeDtypeStruct((4,) + lse.sha...  37.3 us
    dot_general x5, matrix products, contract(): lax.dot_general(a, b, (((ca,), (cb,)), ((), ())), preferred_element_type=...  35 us
    pallas_call x1, Pallas kernels, project_qkv(): pl.pallas_call(functools.partial(qkv_kernel, head_dim=head_dim), out_shap...  32.7 us
  transfers between devices with their start and end apart: 26, of which 8 were waited for; matrix products, arithmetic and copies ran while one was open for 11% of the time, Pallas kernels for 39%

profile of v12, /device:TPU:0, one launch (start us, length us, event | category | flops | bytes accessed | tf_op | source)
XLA Modules:
  0.0 693.8 jit_solution(7647538250086850482)
XLA Ops:
  8.6 6.8 gather_fusion
  22.5 66.9 %embed_gather.1 = (bf16[2048,2560]{1,0:T(8,128)(2,1)}, bf16[128,2560]{1,0:T(8,128)(2,1)}, f32[4,512,128]{2,1,0:T(8,128)}, s32[4,8,512]{2,1,0:T(8,128)}) custom-call(bf16[4,128,2560]{2,1,0:T(8,128)(2,1)} %select_select_fusion.picked, f32[512,128]{1,0:T(8,128)} %pad_maximum_fusion.1.side_f, s32[8,512]{1,0:T(8,128)} %stack.38.side_i), custom_call_target="tpu_custom_call" | custom-call | tf_op jit(solution)/shard_map/embed_gather/pallas_call | solution.py:257
  93.1 32.7 %project_qkv.1 = (bf16[2048,2560]{1,0:T(8,128)(2,1)}, bf16[2048,640]{1,0:T(8,128)(2,1)}, bf16[2048,640]{1,0:T(8,128)(2,1)}, bf16[2048,640]{1,0:T(8,128)(2,1)}) custom-call(bf16[2048,2560]{1,0:T(8,128)(2,1)} %get-tuple-element.70.x.x_all, f32[1,2560]{1,0:T(1,128)} %reshape.111.gain, bf16[2560,640]{1,0:T(8,128)(2,1)} %wq.1, bf16[2560,640]{1,0:T(8,128)(2,1)} %wk.1, ...), custom_call_target="tpu_custom_call" | custom-call | flops 20132659200 | bytes 39321600 | tf_op jit(solution)/shard_map/project_qkv/pallas_call | solution.py:365
  125.9 10.1 %attend.1 = (bf16[512,640]{1,0:T(8,128)(2,1)}, f32[512,8]{1,0:T(8,128)}) custom-call(s32[2]{0:T(128)} %pad_add_fusion.info, s32[4,8,512]{2,1,0:T(8,128)} %get-tuple-element.69.ids, bf16[2048,640]{1,0:T(8,128)(2,1)} %get-tuple-element.72.q, bf16[2048,640]{1,0:T(8,128)(2,1)} %get-tuple-element.73.k, bf16[2048,640]{1,0:T(8,128)(2,1)} %get-tuple-element.74.v, ...), custom_call_target="tpu_custom_call" | custom-call | flops 2684354560 | bytes 5242880 | tf_op jit(solution)/shard_map/attend/pallas_call | solution.py:446
  138.6 5.2 convert_reduce_fusion
  143.8 8.0 %select_reduce_fusion = (s32[2048]{0:T(1024)S(1)}, s32[2048]{0:T(1024)S(1)}, s32[2048]{0:T(1024)S(1)}) fusion(s32[2048]{0:T(1024)S(1)} %convert_reduce_fusion, s32[2048]{0:T(1024)S(1)} %bitcast.62), kind=kLoop, calls=%fused_computation.4 | loop fusion | flops 33548288 | bytes 40960 | tf_op jit(solution)/shard_map/reduce_sum | solution.py:874
  158.2 37.3 %att_project.1 = (f32[4,512,8]{2,1,0:T(8,128)}, f32[512,2560]{1,0:T(8,128)}, bf16[512,2560]{1,0:T(8,128)(2,1)}) custom-call(bf16[512,640]{1,0:T(8,128)(2,1)} %get-tuple-element.75.att.refs_0_, f32[512,8]{1,0:T(8,128)} %get-tuple-element.76.lse, bf16[2048,2560]{1,0:T(8,128)(2,1)} %get-tuple-element.70.x.x_all, ...), custom_call_target="tpu_custom_call" | custom-call | tf_op jit(solution)/shard_map/att_project/pallas_call | solution.py:611
  195.4 33.0 %mlp_block.2 = (bf16[512,1792]{1,0:T(8,128)(2,1)}, bf16[512,1792]{1,0:T(8,128)(2,1)}, bf16[512,1792]{1,0:T(8,128)(2,1)}, f32[512,2560]{1,0:T(8,128)}) custom-call(bf16[512,2560]{1,0:T(8,128)(2,1)} %get-tuple-element.80.act.refs_4_, bf16[512,2560]{1,0:T(8,128)(2,1)} %refs_4_.1, bf16[1728,2560]{1,0:T(8,128)(2,1)} %bitcast.63, bf16[1728,2560]{1,0:T(8,128)(2,1)} %bitcast.65, ...), custom_call_target="tpu_custom_call" | custom-call | flops 22649241600 | bytes 44236800 | tf_op jit(solution)/shard_map/mlp_block/pallas_call | solution.py:705
  238.9 8.2 %collective-permute-done.3.refs_2_ = bf16[512,640]{1,0:T(8,128)(2,1)S(1)} collective-permute-done((bf16[512,640]{1,0:T(8,128)(2,1)S(1)}, bf16[512,640]{1,0:T(8,128)(2,1)S(1)}, u32[]{:S(2)}, u32[]{:S(2)}) %collective-permute-start.3) | collective-permute-done | bytes 655392 | tf_op jit(solution)/shard_map/ppermute | solution.py:840
  247.1 10.6 %fusion.6 = f32[512,2560]{1,0:T(8,128)} fusion(bf16[1728,2560]{1,0:T(8,128)(2,1)} %wd.3, bf16[512,1792]{1,0:T(8,128)(2,1)S(1)} %copy-done.22), kind=kOutput, calls=%fused_computation.19 | convolution fusion | flops 4529848320 | bytes 15925248 | tf_op jit(solution)/shard_map/dot_general | solution.py:32
  257.7 16.8 %zero_rows.2.refs_0_ = f32[8000,2560]{1,0:T(8,128)} custom-call(s32[2]{0:T(128)S(1)} %pad_add_fusion.1.after.bounds), custom_call_target="tpu_custom_call" | custom-call | flops 12288000 | bytes 24000 | tf_op jit(solution)/shard_map/zero_rows/pallas_call | solution.py:736
  278.9 24.5 %collective-permute-done.1.dy.refs_6_ = bf16[512,2560]{1,0:T(8,128)(2,1)} collective-permute-done((bf16[512,2560]{1,0:T(8,128)(2,1)}, bf16[512,2560]{1,0:T(8,128)(2,1)}, u32[]{:S(2)}, u32[]{:S(2)}) %collective-permute-start.1) | collective-permute-done | bytes 2621472 | tf_op jit(solution)/shard_map/ppermute | solution.py:840
  303.4 55.7 %collective-permute-done.act.refs_6_ = bf16[512,2560]{1,0:T(8,128)(2,1)} collective-permute-done((bf16[512,2560]{1,0:T(8,128)(2,1)}, bf16[512,2560]{1,0:T(8,128)(2,1)}, u32[]{:S(2)}, u32[]{:S(2)}) %collective-permute-start) | collective-permute-done | bytes 2621472 | tf_op jit(solution)/shard_map/ppermute | solution.py:840
  359.1 21.3 %mlp_block.3 = (bf16[512,1792]{1,0:T(8,128)(2,1)}, bf16[512,1792]{1,0:T(8,128)(2,1)}, bf16[512,1792]{1,0:T(8,128)(2,1)}) custom-call(bf16[512,2560]{1,0:T(8,128)(2,1)} %collective-permute-done.act.refs_6_, bf16[512,2560]{1,0:T(8,128)(2,1)} %collective-permute-done.1.dy.refs_6_, bf16[1728,2560]{1,0:T(8,128)(2,1)} %bitcast.64, bf16[1728,2560]{1,0:T(8,128)(2,1)} %bitcast.66, ...), custom_call_target="tpu_custom_call" | custom-call | flops 13589544960 | bytes 26542080 | tf_op jit(solution)/shard_map/mlp_block/pallas_call | solution.py:705
  380.5 44.3 %spread.1 = (bf16[2048,2560]{1,0:T(8,128)(2,1)}, f32[128,2560]{1,0:T(8,128)}, f32[1,2560]{1,0:T(1,128)}) custom-call(f32[128,2560]{1,0:T(8,128)} %reduce-scatter.4.cloned.1.call-done.d_act, f32[128,2560]{1,0:T(8,128)} %constant_dynamic-slice_fusion.1.res, bf16[128,2560]{1,0:T(8,128)(2,1)} %constant_dynamic-slice_fusion.dy, f32[1,2560]{1,0:T(1,128)} %reshape.112.gain), custom_call_target="tpu_custom_call" | custom-call | tf_op jit(solution)/shard_map/spread/pallas_call | solution.py:296
  426.9 13.0 %convolution_convert_fusion.do = bf16[2048,640]{1,0:T(8,128)(2,1)S(1)} fusion(bf16[2048,2560]{1,0:T(8,128)(2,1)} %get-tuple-element.93, bf16[640,2560]{1,0:T(8,128)(2,1)} %param.23), kind=kOutput, calls=%fused_computation.16 | convolution fusion | flops 6712197120 | bytes 16384000 | tf_op jit(solution)/shard_map/dot_general | solution.py:32
  447.4 22.0 %attend_back.1.refs_4_ = bf16[512,1920]{1,0:T(8,128)(2,1)} custom-call(s32[2]{0:T(128)} %pad_add_fusion.info, s32[4,8,512]{2,1,0:T(8,128)} %get-tuple-element.69.ids, bf16[2048,640]{1,0:T(8,128)(2,1)} %get-tuple-element.72.q, bf16[2048,640]{1,0:T(8,128)(2,1)} %get-tuple-element.73.k, bf16[2048,640]{1,0:T(8,128)(2,1)} %get-tuple-element.74.v, ...), custom_call_target="tpu_custom_call" | custom-call | flops 4697620480 | bytes 9175040 | tf_op jit(solution)/shard_map/attend_back/pallas_call | solution.py:518
  490.2 16.0 %weight_grad.5 = f32[640,2560]{1,0:T(8,128)} custom-call(s32[2]{0:T(128)} %pad_add_fusion.info, bf16[512,640]{1,0:T(8,128)(2,1)} %get-tuple-element.75.att.refs_0_, bf16[512,640]{1,0:T(8,128)(2,1)} %copy-done.5, bf16[512,640]{1,0:T(8,128)(2,1)} %copy-done.6, bf16[512,640]{1,0:T(8,128)(2,1)} %copy-done.7, bf16[4,512,2560]{2,1,0:T(8,128)(2,1)} %bitcast.38, ...), custom_call_target="tpu_custom_call" | custom-call | flops 6710886400 | bytes 13107200 | tf_op jit(solution)/shard_map/weight_grad/pallas_call | solution.py:647
  506.3 11.4 %zero_rows.3.base_hbm = f32[8000,2560]{1,0:T(8,128)} custom-call(s32[2]{0:T(128)S(1)} %pad_add_fusion.1.after.bounds, f32[8000,2560]{1,0:T(8,128)} %zero_rows.2.refs_0_), custom_call_target="tpu_custom_call", output_to_operand_aliasing={{}: (1, {})} | custom-call | flops 8192000 | bytes 16000 | tf_op jit(solution)/shard_map/zero_rows/pallas_call | solution.py:736
  520.1 27.2 %weight_grad.6 = f32[1728,2560]{1,0:T(8,128)} custom-call(s32[2]{0:T(128)} %pad_add_fusion.info, bf16[512,1792]{1,0:T(8,128)(2,1)} %get-tuple-element.99.refs_0_, bf16[512,1792]{1,0:T(8,128)(2,1)} %collective-permute-done.6.refs_1_, bf16[512,1792]{1,0:T(8,128)(2,1)} %get-tuple-element.100.refs_2_, bf16[512,1792]{1,0:T(8,128)(2,1)} %collective-permute-done.7.refs_3_, ...), custom_call_target="tpu_custom_call" | custom-call | flops 18119393280 | bytes 35389440 | tf_op jit(solution)/shard_map/weight_grad/pallas_call | solution.py:647
  562.0 27.0 %weight_grad.8 = f32[1728,2560]{1,0:T(8,128)} custom-call(s32[2]{0:T(128)} %pad_add_fusion.info, bf16[512,1792]{1,0:T(8,128)(2,1)} %get-tuple-element.111.refs_0_, bf16[512,1792]{1,0:T(8,128)(2,1)} %collective-permute-done.12.refs_1_, bf16[512,1792]{1,0:T(8,128)(2,1)} %get-tuple-element.112.refs_2_, bf16[512,1792]{1,0:T(8,128)(2,1)} %collective-permute-done.13.refs_3_, ...), custom_call_target="tpu_custom_call" | custom-call | flops 18119393280 | bytes 35389440 | tf_op jit(solution)/shard_map/weight_grad/pallas_call | solution.py:647
  589.0 27.1 %weight_grad.9 = f32[1728,2560]{1,0:T(8,128)} custom-call(s32[2]{0:T(128)} %pad_add_fusion.info, bf16[512,1792]{1,0:T(8,128)(2,1)} %get-tuple-element.86.refs_0_, bf16[512,1792]{1,0:T(8,128)(2,1)} %collective-permute-done.14.refs_1_, bf16[512,1792]{1,0:T(8,128)(2,1)} %get-tuple-element.113.refs_2_, bf16[512,1792]{1,0:T(8,128)(2,1)} %collective-permute-done.15.refs_3_, ...), custom_call_target="tpu_custom_call" | custom-call | flops 18119393280 | bytes 35389440 | tf_op jit(solution)/shard_map/weight_grad/pallas_call | solution.py:647
  618.0 29.7 %weight_grad.7 = (f32[2560,640]{1,0:T(8,128)}, f32[2560,640]{1,0:T(8,128)}, f32[2560,640]{1,0:T(8,128)}) custom-call(s32[2]{0:T(128)} %pad_add_fusion.info, bf16[4,512,2560]{2,1,0:T(8,128)(2,1)} %bitcast.71, bf16[4,512,2560]{2,1,0:T(8,128)(2,1)} %bitcast.72, bf16[4,512,2560]{2,1,0:T(8,128)(2,1)} %bitcast.73, bf16[4,512,2560]{2,1,0:T(8,128)(2,1)} %bitcast.74, ...), custom_call_target="tpu_custom_call" | custom-call | flops 20132659200 | bytes 39321600 | tf_op jit(solution)/shard_map/weight_grad/pallas_call | solution.py:647
  651.3 30.7 %scatter_rows.1 = f32[8000,2560]{1,0:T(8,128)} custom-call(s32[2048]{0:T(1024)} %get-tuple-element.118.order, s32[2048]{0:T(1024)} %get-tuple-element.119.sid, s32[2048]{0:T(1024)} %select_reduce_fusion.2.runs, s32[2]{0:T(128)} %copy-done, f32[2176,2560]{1,0:T(8,128)} %all-gather.5.cloned.1.call-done.rows, ...), custom_call_target="tpu_custom_call", output_to_operand_aliasing={{}: (5, {})} | custom-call | tf_op jit(solution)/shard_map/scatter_rows/pallas_call | solution.py:800
  (139 shorter events, 93.8 us)
Async XLA Ops:
  7.2 151.0 %all-gather.3.cloned.1.call-start = ((), (), s32[]{:S(2)}) async-start(), calls=%async_computation.3 | async-start | bytes 8192000 | tf_op jit(solution)/shard_map/all_gather | solution.py:838
  89.4 291.1 %reduce-scatter.4.cloned.1.call-start = ((), (), s32[]{:S(2)}) async-start(), calls=%async_computation.4 | async-start | bytes 6553600 | tf_op jit(solution)/shard_map/reduce_scatter | solution.py:839
  228.4 253.7 %reduce-scatter.6.cloned.1.call-start = ((), (), s32[]{:S(2)}) async-start(), calls=%async_computation.5 | async-start | bytes 6553600 | tf_op jit(solution)/shard_map/reduce_scatter | solution.py:839
  229.5 8.4 %collective-permute-start.2 = (bf16[512,640]{1,0:T(8,128)(2,1)S(1)}, bf16[512,640]{1,0:T(8,128)(2,1)S(1)}, u32[]{:S(2)}, u32[]{:S(2)}) collective-permute-start(bf16[512,640]{1,0:T(8,128)(2,1)S(1)} %copy-done.1), channel_id=1, source_target_pairs={{0,1},{1,0},{2,3},{3,2},{4,5},{5,4},{6,7},{7,6},{8,9},{9,8},{10,11... | collective-permute-start | bytes 1966088 | tf_op jit(solution)/shard_map/ppermute | solution.py:840
  229.5 17.6 %collective-permute-start.3 = (bf16[512,640]{1,0:T(8,128)(2,1)S(1)}, bf16[512,640]{1,0:T(8,128)(2,1)S(1)}, u32[]{:S(2)}, u32[]{:S(2)}) collective-permute-start(bf16[512,640]{1,0:T(8,128)(2,1)S(1)} %copy-done.1), channel_id=1, source_target_pairs={{0,2},{1,3},{2,0},{3,1},{4,6},{5,7},{6,4},{7,5},{8,10},{9,11},{10,... | collective-permute-start | bytes 1966088 | tf_op jit(solution)/shard_map/ppermute | solution.py:840
  231.3 72.1 %collective-permute-start.1 = (bf16[512,2560]{1,0:T(8,128)(2,1)}, bf16[512,2560]{1,0:T(8,128)(2,1)}, u32[]{:S(2)}, u32[]{:S(2)}) collective-permute-start(bf16[512,2560]{1,0:T(8,128)(2,1)} %refs_4_.1), channel_id=1, source_target_pairs={{0,2},{1,3},{2,0},{3,1},{4,6},{5,7},{6,4},{7,5},{8,10},{9,11},{10,... | collective-permute-start | bytes 7864328 | tf_op jit(solution)/shard_map/ppermute | solution.py:840
  234.1 125.0 %collective-permute-start = (bf16[512,2560]{1,0:T(8,128)(2,1)}, bf16[512,2560]{1,0:T(8,128)(2,1)}, u32[]{:S(2)}, u32[]{:S(2)}) collective-permute-start(bf16[512,2560]{1,0:T(8,128)(2,1)} %get-tuple-element.80.act.refs_4_), channel_id=1, source_target_pairs={{0,2},{1,3},{2,0},{3,1},{4,6},{5,7},{6,4},{7,5},{8,10},{9,11},{10,... | collective-permute-start | bytes 7864328 | tf_op jit(solution)/shard_map/ppermute | solution.py:840
  247.1 30.8 %collective-permute-start.4 = (bf16[512,640]{1,0:T(8,128)(2,1)S(1)}, bf16[512,640]{1,0:T(8,128)(2,1)S(1)}, u32[]{:S(2)}, u32[]{:S(2)}) collective-permute-start(bf16[512,640]{1,0:T(8,128)(2,1)S(1)} %collective-permute-done.3.refs_2_), channel_id=1, source_target_pairs={{0,1},{1,0},{2,3},{3,2},{4,5},{5,4},{6,7},{7,6},{8,9},{9,8},{10,11... | collective-permute-start | bytes 1966088 | tf_op jit(solution)/shard_map/ppermute | solution.py:840
  424.8 122.5 %reduce-scatter.8.cloned.1.call-start = ((), (), s32[]{:S(2)}) async-start(), calls=%async_computation.6 | async-start | bytes 6553600 | tf_op jit(solution)/shard_map/reduce_scatter | solution.py:839
  484.0 163.8 %all-gather.5.cloned.1.call-start = ((), (), s32[]{:S(2)}) async-start(), calls=%async_computation.7 | async-start | bytes 23674880 | tf_op jit(solution)/shard_map/all_gather | solution.py:838
  484.0 33.7 %collective-permute-start.8 = (bf16[512,2560]{1,0:T(8,128)(2,1)}, bf16[512,2560]{1,0:T(8,128)(2,1)S(1)}, u32[]{:S(2)}, u32[]{:S(2)}) collective-permute-start(bf16[512,2560]{1,0:T(8,128)(2,1)} %get-tuple-element.80.act.refs_4_), channel_id=1, source_target_pairs={{0,1},{1,0},{2,3},{3,2},{4,5},{5,4},{6,7},{7,6},{8,9},{9,8},{10,11... | collective-permute-start | bytes 7864328 | tf_op jit(solution)/shard_map/ppermute | solution.py:840
  484.9 32.8 %collective-permute-start.9 = (bf16[512,2560]{1,0:T(8,128)(2,1)}, bf16[512,2560]{1,0:T(8,128)(2,1)S(1)}, u32[]{:S(2)}, u32[]{:S(2)}) collective-permute-start(bf16[512,2560]{1,0:T(8,128)(2,1)} %collective-permute-done.act.refs_6_), channel_id=1, source_target_pairs={{0,1},{1,0},{2,3},{3,2},{4,5},{5,4},{6,7},{7,6},{8,9},{9,8},{10,11... | collective-permute-start | bytes 7864328 | tf_op jit(solution)/shard_map/ppermute | solution.py:840
  484.9 32.8 %collective-permute-start.6 = (bf16[512,1792]{1,0:T(8,128)(2,1)}, bf16[512,1792]{1,0:T(8,128)(2,1)}, u32[]{:S(2)}, u32[]{:S(2)}) collective-permute-start(bf16[512,1792]{1,0:T(8,128)(2,1)} %get-tuple-element.99.refs_0_), channel_id=1, source_target_pairs={{0,1},{1,0},{2,3},{3,2},{4,5},{5,4},{6,7},{7,6},{8,9},{9,8},{10,11... | collective-permute-start | bytes 5505032 | tf_op jit(solution)/shard_map/ppermute | solution.py:840
  485.4 32.4 %collective-permute-start.7 = (bf16[512,1792]{1,0:T(8,128)(2,1)}, bf16[512,1792]{1,0:T(8,128)(2,1)}, u32[]{:S(2)}, u32[]{:S(2)}) collective-permute-start(bf16[512,1792]{1,0:T(8,128)(2,1)} %get-tuple-element.100.refs_2_), channel_id=1, source_target_pairs={{0,1},{1,0},{2,3},{3,2},{4,5},{5,4},{6,7},{7,6},{8,9},{9,8},{10,11... | collective-permute-start | bytes 5505032 | tf_op jit(solution)/shard_map/ppermute | solution.py:840
  485.4 61.8 %collective-permute-start.5 = (bf16[512,1920]{1,0:T(8,128)(2,1)}, bf16[512,1920]{1,0:T(8,128)(2,1)}, u32[]{:S(2)}, u32[]{:S(2)}) collective-permute-start(bf16[512,1920]{1,0:T(8,128)(2,1)} %attend_back.1.refs_4_), channel_id=1, source_target_pairs={{0,2},{1,3},{2,0},{3,1},{4,6},{5,7},{6,4},{7,5},{8,10},{9,11},{10,... | collective-permute-start | bytes 5898248 | tf_op jit(solution)/shard_map/ppermute | solution.py:840
  551.8 10.0 %collective-permute-start.13 = (bf16[512,1792]{1,0:T(8,128)(2,1)}, bf16[512,1792]{1,0:T(8,128)(2,1)}, u32[]{:S(2)}, u32[]{:S(2)}) collective-permute-start(bf16[512,1792]{1,0:T(8,128)(2,1)} %get-tuple-element.112.refs_2_), channel_id=1, source_target_pairs={{0,1},{1,0},{2,3},{3,2},{4,5},{5,4},{6,7},{7,6},{8,9},{9,8},{10,11... | collective-permute-start | bytes 5505032 | tf_op jit(solution)/shard_map/ppermute | solution.py:840
  551.9 37.1 %collective-permute-start.17 = (bf16[512,2560]{1,0:T(8,128)(2,1)}, bf16[512,2560]{1,0:T(8,128)(2,1)}, u32[]{:S(2)}, u32[]{:S(2)}) collective-permute-start(bf16[512,2560]{1,0:T(8,128)(2,1)} %collective-permute-done.1.dy.refs_6_), channel_id=1, source_target_pairs={{0,1},{1,0},{2,3},{3,2},{4,5},{5,4},{6,7},{7,6},{8,9},{9,8},{10,11... | collective-permute-start | bytes 7864328 | tf_op jit(solution)/shard_map/ppermute | solution.py:840
  552.3 36.7 %collective-permute-start.14 = (bf16[512,1792]{1,0:T(8,128)(2,1)}, bf16[512,1792]{1,0:T(8,128)(2,1)}, u32[]{:S(2)}, u32[]{:S(2)}) collective-permute-start(bf16[512,1792]{1,0:T(8,128)(2,1)} %get-tuple-element.86.refs_0_), channel_id=1, source_target_pairs={{0,1},{1,0},{2,3},{3,2},{4,5},{5,4},{6,7},{7,6},{8,9},{9,8},{10,11... | collective-permute-start | bytes 5505032 | tf_op jit(solution)/shard_map/ppermute | solution.py:840
  556.6 32.5 %collective-permute-start.15 = (bf16[512,1792]{1,0:T(8,128)(2,1)}, bf16[512,1792]{1,0:T(8,128)(2,1)}, u32[]{:S(2)}, u32[]{:S(2)}) collective-permute-start(bf16[512,1792]{1,0:T(8,128)(2,1)} %get-tuple-element.113.refs_2_), channel_id=1, source_target_pairs={{0,1},{1,0},{2,3},{3,2},{4,5},{5,4},{6,7},{7,6},{8,9},{9,8},{10,11... | collective-permute-start | bytes 5505032 | tf_op jit(solution)/shard_map/ppermute | solution.py:840
  559.2 56.9 %collective-permute-start.10 = (bf16[512,1920]{1,0:T(8,128)(2,1)}, bf16[512,1920]{1,0:T(8,128)(2,1)S(1)}, u32[]{:S(2)}, u32[]{:S(2)}) collective-permute-start(bf16[512,1920]{1,0:T(8,128)(2,1)} %attend_back.1.refs_4_), channel_id=1, source_target_pairs={{0,1},{1,0},{2,3},{3,2},{4,5},{5,4},{6,7},{7,6},{8,9},{9,8},{10,11... | collective-permute-start | bytes 5898248 | tf_op jit(solution)/shard_map/ppermute | solution.py:840
  561.8 54.3 %collective-permute-start.11 = (bf16[512,1920]{1,0:T(8,128)(2,1)}, bf16[512,1920]{1,0:T(8,128)(2,1)S(1)}, u32[]{:S(2)}, u32[]{:S(2)}) collective-permute-start(bf16[512,1920]{1,0:T(8,128)(2,1)} %collective-permute-done.5.refs_6_), channel_id=1, source_target_pairs={{0,1},{1,0},{2,3},{3,2},{4,5},{5,4},{6,7},{7,6},{8,9},{9,8},{10,11... | collective-permute-start | bytes 5898248 | tf_op jit(solution)/shard_map/ppermute | solution.py:840
  647.7 36.5 %collective-permute-start.18 = (bf16[128,2560]{1,0:T(8,128)(2,1)S(1)}, bf16[128,2560]{1,0:T(8,128)(2,1)}, u32[]{:S(2)}, u32[]{:S(2)}) collective-permute-start(bf16[128,2560]{1,0:T(8,128)(2,1)S(1)} %add_convert_fusion), channel_id=1, source_target_pairs={{0,4},{4,0},{8,12},{12,8},{1,5},{5,1},{9,13},{13,9},{2,6},{6,2},{1... | collective-permute-start | bytes 1966088 | tf_op jit(solution)/shard_map/ppermute | solution.py:840
  648.8 36.6 %collective-permute-start.19 = (bf16[128,2560]{1,0:T(8,128)(2,1)S(1)}, bf16[128,2560]{1,0:T(8,128)(2,1)S(1)}, u32[]{:S(2)}, u32[]{:S(2)}) collective-permute-start(bf16[128,2560]{1,0:T(8,128)(2,1)S(1)} %add_convert_fusion), channel_id=1, source_target_pairs={{0,8},{4,12},{8,0},{12,4},{1,9},{5,13},{9,1},{13,5},{2,10},{6,14},... | collective-permute-start | bytes 1966088 | tf_op jit(solution)/shard_map/ppermute | solution.py:840
  649.6 35.8 %collective-permute-start.20 = (bf16[128,2560]{1,0:T(8,128)(2,1)S(1)}, bf16[128,2560]{1,0:T(8,128)(2,1)S(1)}, u32[]{:S(2)}, u32[]{:S(2)}) collective-permute-start(bf16[128,2560]{1,0:T(8,128)(2,1)S(1)} %add_convert_fusion), channel_id=1, source_target_pairs={{0,12},{4,8},{8,4},{12,0},{1,13},{5,9},{9,5},{13,1},{2,14},{6,10},... | collective-permute-start | bytes 1966088 | tf_op jit(solution)/shard_map/ppermute | solution.py:840
  (25 other events, 707.1 us)
Sparse Core Ops, SparseCore 0:
  89.5 68.5 all-gather.2
  228.6 57.8 reduce-scatter.3
  424.9 57.1 reduce-scatter.5
  485.5 59.6 reduce-scatter.7
  551.4 93.3 all-gather.4

commit v13 on v12

--- a/solution.py
+++ b/solution.py
@@ -893,8 +893,9 @@
         for k, piece in enumerate(head_parts):
             att_heads = lax.dynamic_update_slice_in_dim(att_heads, piece, (cp_rank ^ k) * span, 0)
         d_act_b, hidden_x, d_gate_x, d_up_x, out_part, base, att_heads = barrier((d_act_b, hidden_x, d_gate_x, d_up_x, out_part, base, att_heads))
-        acts, dys, hiddens, d_gates, d_ups = [(a, swap(a, core_swap), b, swap(b, core_swap)) for a, b in (
-            (act_b, act_x), (dy, dy_x), (hidden, hidden_x), (d_gate, d_gate_x), (d_up, d_up_x))]
+        four = lambda a, b: (a, swap(a, core_swap), b, swap(b, core_swap))
+        acts, d_ups = four(act_b, act_x), four(d_up, d_up_x)
+        dys, hiddens, d_gates = four(dy, dy_x), four(hidden, hidden_x), four(d_gate, d_gate_x)
         grad_down = weight_grad(info, hiddens, dys, rows=ffn)
         grad_gate = weight_grad(info, d_gates, acts, rows=ffn)
         grad_up = weight_grad(info, d_ups, acts, rows=ffn)

time: 700 us -> 700 us (level)
  no operation moved by 1% of the time
where the time goes in v13:
time: 700 us; the launch traced here: 694 us
  Pallas kernels  457 us (65%)
  waiting for transfers between devices  102 us (15%)
  matrix products  39.7 us (6%)
  local copies, waits for them, and re-layouts  37.1 us (5%)
  other arithmetic  27.3 us (4%)
  starting transfers between devices  15.4 us (2%)
  between operations  14.5 us (2%)
    pallas_call x5, Pallas kernels, weight_grad(): pl.pallas_call(functools.partial(weight_grad_kernel, pieces=n, splits=spl...  127 us
    ppermute x21, waiting for transfers between devices, compute(): swap = lambda arr, pairs, axis='cp': lax.ppermute(arr, axis, pairs)  97.7 us
    pallas_call x1, Pallas kernels, embed_gather(): pl.pallas_call(embed_kernel, out_shape=[jax.ShapeDtypeStruct((16 * rows,...  66.9 us
    pallas_call x2, Pallas kernels, mlp_block(): pl.pallas_call(functools.partial(mlp_kernel, limit=limit, tiles=tiles), o...  54.3 us
    pallas_call x1, Pallas kernels, spread(): pl.pallas_call(spread_kernel, out_shape=[jax.ShapeDtypeStruct((16 * rows,...  44.3 us
    pallas_call x1, Pallas kernels, att_project(): pl.pallas_call(att_kernel, out_shape=[jax.ShapeDtypeStruct((4,) + lse.sha...  37.3 us
    dot_general x5, matrix products, contract(): lax.dot_general(a, b, (((ca,), (cb,)), ((), ())), preferred_element_type=...  35 us
    pallas_call x1, Pallas kernels, project_qkv(): pl.pallas_call(functools.partial(qkv_kernel, head_dim=head_dim), out_shap...  32.7 us
  transfers between devices with their start and end apart: 26, of which 8 were waited for; matrix products, arithmetic and copies ran while one was open for 11% of the time, Pallas kernels for 39%

profile of v13, /device:TPU:0, one launch (start us, length us, event | category | flops | bytes accessed | tf_op | source)
XLA Modules:
  0.0 693.8 jit_solution(7647538250086850482)
XLA Ops:
  8.6 6.8 gather_fusion
  22.5 66.9 %embed_gather.1 = (bf16[2048,2560]{1,0:T(8,128)(2,1)}, bf16[128,2560]{1,0:T(8,128)(2,1)}, f32[4,512,128]{2,1,0:T(8,128)}, s32[4,8,512]{2,1,0:T(8,128)}) custom-call(bf16[4,128,2560]{2,1,0:T(8,128)(2,1)} %select_select_fusion.picked, f32[512,128]{1,0:T(8,128)} %pad_maximum_fusion.1.side_f, s32[8,512]{1,0:T(8,128)} %stack.38.side_i), custom_call_target="tpu_custom_call" | custom-call | tf_op jit(solution)/shard_map/embed_gather/pallas_call | solution.py:257
  93.1 32.7 %project_qkv.1 = (bf16[2048,2560]{1,0:T(8,128)(2,1)}, bf16[2048,640]{1,0:T(8,128)(2,1)}, bf16[2048,640]{1,0:T(8,128)(2,1)}, bf16[2048,640]{1,0:T(8,128)(2,1)}) custom-call(bf16[2048,2560]{1,0:T(8,128)(2,1)} %get-tuple-element.70.x.x_all, f32[1,2560]{1,0:T(1,128)} %reshape.111.gain, bf16[2560,640]{1,0:T(8,128)(2,1)} %wq.1, bf16[2560,640]{1,0:T(8,128)(2,1)} %wk.1, ...), custom_call_target="tpu_custom_call" | custom-call | flops 20132659200 | bytes 39321600 | tf_op jit(solution)/shard_map/project_qkv/pallas_call | solution.py:365
  125.9 10.1 %attend.1 = (bf16[512,640]{1,0:T(8,128)(2,1)}, f32[512,8]{1,0:T(8,128)}) custom-call(s32[2]{0:T(128)} %pad_add_fusion.info, s32[4,8,512]{2,1,0:T(8,128)} %get-tuple-element.69.ids, bf16[2048,640]{1,0:T(8,128)(2,1)} %get-tuple-element.72.q, bf16[2048,640]{1,0:T(8,128)(2,1)} %get-tuple-element.73.k, bf16[2048,640]{1,0:T(8,128)(2,1)} %get-tuple-element.74.v, ...), custom_call_target="tpu_custom_call" | custom-call | flops 2684354560 | bytes 5242880 | tf_op jit(solution)/shard_map/attend/pallas_call | solution.py:446
  138.6 5.2 convert_reduce_fusion
  143.8 8.0 %select_reduce_fusion = (s32[2048]{0:T(1024)S(1)}, s32[2048]{0:T(1024)S(1)}, s32[2048]{0:T(1024)S(1)}) fusion(s32[2048]{0:T(1024)S(1)} %convert_reduce_fusion, s32[2048]{0:T(1024)S(1)} %bitcast.62), kind=kLoop, calls=%fused_computation.4 | loop fusion | flops 33548288 | bytes 40960 | tf_op jit(solution)/shard_map/reduce_sum | solution.py:874
  158.2 37.3 %att_project.1 = (f32[4,512,8]{2,1,0:T(8,128)}, f32[512,2560]{1,0:T(8,128)}, bf16[512,2560]{1,0:T(8,128)(2,1)}) custom-call(bf16[512,640]{1,0:T(8,128)(2,1)} %get-tuple-element.75.att.refs_0_, f32[512,8]{1,0:T(8,128)} %get-tuple-element.76.lse, bf16[2048,2560]{1,0:T(8,128)(2,1)} %get-tuple-element.70.x.x_all, ...), custom_call_target="tpu_custom_call" | custom-call | tf_op jit(solution)/shard_map/att_project/pallas_call | solution.py:611
  195.4 33.0 %mlp_block.2 = (bf16[512,1792]{1,0:T(8,128)(2,1)}, bf16[512,1792]{1,0:T(8,128)(2,1)}, bf16[512,1792]{1,0:T(8,128)(2,1)}, f32[512,2560]{1,0:T(8,128)}) custom-call(bf16[512,2560]{1,0:T(8,128)(2,1)} %get-tuple-element.80.act.refs_4_, bf16[512,2560]{1,0:T(8,128)(2,1)} %refs_4_.1, bf16[1728,2560]{1,0:T(8,128)(2,1)} %bitcast.63, bf16[1728,2560]{1,0:T(8,128)(2,1)} %bitcast.65, ...), custom_call_target="tpu_custom_call" | custom-call | flops 22649241600 | bytes 44236800 | tf_op jit(solution)/shard_map/mlp_block/pallas_call | solution.py:705
  238.9 8.2 %collective-permute-done.3.refs_2_ = bf16[512,640]{1,0:T(8,128)(2,1)S(1)} collective-permute-done((bf16[512,640]{1,0:T(8,128)(2,1)S(1)}, bf16[512,640]{1,0:T(8,128)(2,1)S(1)}, u32[]{:S(2)}, u32[]{:S(2)}) %collective-permute-start.3) | collective-permute-done | bytes 655392 | tf_op jit(solution)/shard_map/ppermute | solution.py:840
  247.1 10.6 %fusion.6 = f32[512,2560]{1,0:T(8,128)} fusion(bf16[1728,2560]{1,0:T(8,128)(2,1)} %wd.3, bf16[512,1792]{1,0:T(8,128)(2,1)S(1)} %copy-done.22), kind=kOutput, calls=%fused_computation.19 | convolution fusion | flops 4529848320 | bytes 15925248 | tf_op jit(solution)/shard_map/dot_general | solution.py:32
  257.7 16.8 %zero_rows.2.refs_0_ = f32[8000,2560]{1,0:T(8,128)} custom-call(s32[2]{0:T(128)S(1)} %pad_add_fusion.1.after.bounds), custom_call_target="tpu_custom_call" | custom-call | flops 12288000 | bytes 24000 | tf_op jit(solution)/shard_map/zero_rows/pallas_call | solution.py:736
  278.9 24.5 %collective-permute-done.1.dy.refs_6_ = bf16[512,2560]{1,0:T(8,128)(2,1)} collective-permute-done((bf16[512,2560]{1,0:T(8,128)(2,1)}, bf16[512,2560]{1,0:T(8,128)(2,1)}, u32[]{:S(2)}, u32[]{:S(2)}) %collective-permute-start.1) | collective-permute-done | bytes 2621472 | tf_op jit(solution)/shard_map/ppermute | solution.py:840
  303.4 55.7 %collective-permute-done.act.refs_6_ = bf16[512,2560]{1,0:T(8,128)(2,1)} collective-permute-done((bf16[512,2560]{1,0:T(8,128)(2,1)}, bf16[512,2560]{1,0:T(8,128)(2,1)}, u32[]{:S(2)}, u32[]{:S(2)}) %collective-permute-start) | collective-permute-done | bytes 2621472 | tf_op jit(solution)/shard_map/ppermute | solution.py:840
  359.1 21.3 %mlp_block.3 = (bf16[512,1792]{1,0:T(8,128)(2,1)}, bf16[512,1792]{1,0:T(8,128)(2,1)}, bf16[512,1792]{1,0:T(8,128)(2,1)}) custom-call(bf16[512,2560]{1,0:T(8,128)(2,1)} %collective-permute-done.act.refs_6_, bf16[512,2560]{1,0:T(8,128)(2,1)} %collective-permute-done.1.dy.refs_6_, bf16[1728,2560]{1,0:T(8,128)(2,1)} %bitcast.64, bf16[1728,2560]{1,0:T(8,128)(2,1)} %bitcast.66, ...), custom_call_target="tpu_custom_call" | custom-call | flops 13589544960 | bytes 26542080 | tf_op jit(solution)/shard_map/mlp_block/pallas_call | solution.py:705
  380.5 44.3 %spread.1 = (bf16[2048,2560]{1,0:T(8,128)(2,1)}, f32[128,2560]{1,0:T(8,128)}, f32[1,2560]{1,0:T(1,128)}) custom-call(f32[128,2560]{1,0:T(8,128)} %reduce-scatter.4.cloned.1.call-done.d_act, f32[128,2560]{1,0:T(8,128)} %constant_dynamic-slice_fusion.1.res, bf16[128,2560]{1,0:T(8,128)(2,1)} %constant_dynamic-slice_fusion.dy, f32[1,2560]{1,0:T(1,128)} %reshape.112.gain), custom_call_target="tpu_custom_call" | custom-call | tf_op jit(solution)/shard_map/spread/pallas_call | solution.py:296
  426.9 13.0 %convolution_convert_fusion.do = bf16[2048,640]{1,0:T(8,128)(2,1)S(1)} fusion(bf16[2048,2560]{1,0:T(8,128)(2,1)} %get-tuple-element.93, bf16[640,2560]{1,0:T(8,128)(2,1)} %param.23), kind=kOutput, calls=%fused_computation.16 | convolution fusion | flops 6712197120 | bytes 16384000 | tf_op jit(solution)/shard_map/dot_general | solution.py:32
  447.4 22.0 %attend_back.1.refs_4_ = bf16[512,1920]{1,0:T(8,128)(2,1)} custom-call(s32[2]{0:T(128)} %pad_add_fusion.info, s32[4,8,512]{2,1,0:T(8,128)} %get-tuple-element.69.ids, bf16[2048,640]{1,0:T(8,128)(2,1)} %get-tuple-element.72.q, bf16[2048,640]{1,0:T(8,128)(2,1)} %get-tuple-element.73.k, bf16[2048,640]{1,0:T(8,128)(2,1)} %get-tuple-element.74.v, ...), custom_call_target="tpu_custom_call" | custom-call | flops 4697620480 | bytes 9175040 | tf_op jit(solution)/shard_map/attend_back/pallas_call | solution.py:518
  490.2 16.0 %weight_grad.5 = f32[640,2560]{1,0:T(8,128)} custom-call(s32[2]{0:T(128)} %pad_add_fusion.info, bf16[512,640]{1,0:T(8,128)(2,1)} %get-tuple-element.75.att.refs_0_, bf16[512,640]{1,0:T(8,128)(2,1)} %copy-done.5, bf16[512,640]{1,0:T(8,128)(2,1)} %copy-done.6, bf16[512,640]{1,0:T(8,128)(2,1)} %copy-done.7, bf16[4,512,2560]{2,1,0:T(8,128)(2,1)} %bitcast.38, ...), custom_call_target="tpu_custom_call" | custom-call | flops 6710886400 | bytes 13107200 | tf_op jit(solution)/shard_map/weight_grad/pallas_call | solution.py:647
  506.3 11.4 %zero_rows.3.base_hbm = f32[8000,2560]{1,0:T(8,128)} custom-call(s32[2]{0:T(128)S(1)} %pad_add_fusion.1.after.bounds, f32[8000,2560]{1,0:T(8,128)} %zero_rows.2.refs_0_), custom_call_target="tpu_custom_call", output_to_operand_aliasing={{}: (1, {})} | custom-call | flops 8192000 | bytes 16000 | tf_op jit(solution)/shard_map/zero_rows/pallas_call | solution.py:736
  520.1 27.2 %weight_grad.6 = f32[1728,2560]{1,0:T(8,128)} custom-call(s32[2]{0:T(128)} %pad_add_fusion.info, bf16[512,1792]{1,0:T(8,128)(2,1)} %get-tuple-element.99.refs_0_, bf16[512,1792]{1,0:T(8,128)(2,1)} %collective-permute-done.6.refs_1_, bf16[512,1792]{1,0:T(8,128)(2,1)} %get-tuple-element.100.refs_2_, bf16[512,1792]{1,0:T(8,128)(2,1)} %collective-permute-done.7.refs_3_, ...), custom_call_target="tpu_custom_call" | custom-call | flops 18119393280 | bytes 35389440 | tf_op jit(solution)/shard_map/weight_grad/pallas_call | solution.py:647
  562.0 27.0 %weight_grad.8 = f32[1728,2560]{1,0:T(8,128)} custom-call(s32[2]{0:T(128)} %pad_add_fusion.info, bf16[512,1792]{1,0:T(8,128)(2,1)} %get-tuple-element.111.refs_0_, bf16[512,1792]{1,0:T(8,128)(2,1)} %collective-permute-done.12.refs_1_, bf16[512,1792]{1,0:T(8,128)(2,1)} %get-tuple-element.112.refs_2_, bf16[512,1792]{1,0:T(8,128)(2,1)} %collective-permute-done.13.refs_3_, ...), custom_call_target="tpu_custom_call" | custom-call | flops 18119393280 | bytes 35389440 | tf_op jit(solution)/shard_map/weight_grad/pallas_call | solution.py:647
  589.0 27.1 %weight_grad.9 = f32[1728,2560]{1,0:T(8,128)} custom-call(s32[2]{0:T(128)} %pad_add_fusion.info, bf16[512,1792]{1,0:T(8,128)(2,1)} %get-tuple-element.86.refs_0_, bf16[512,1792]{1,0:T(8,128)(2,1)} %collective-permute-done.14.refs_1_, bf16[512,1792]{1,0:T(8,128)(2,1)} %get-tuple-element.113.refs_2_, bf16[512,1792]{1,0:T(8,128)(2,1)} %collective-permute-done.15.refs_3_, ...), custom_call_target="tpu_custom_call" | custom-call | flops 18119393280 | bytes 35389440 | tf_op jit(solution)/shard_map/weight_grad/pallas_call | solution.py:647
  618.0 29.7 %weight_grad.7 = (f32[2560,640]{1,0:T(8,128)}, f32[2560,640]{1,0:T(8,128)}, f32[2560,640]{1,0:T(8,128)}) custom-call(s32[2]{0:T(128)} %pad_add_fusion.info, bf16[4,512,2560]{2,1,0:T(8,128)(2,1)} %bitcast.71, bf16[4,512,2560]{2,1,0:T(8,128)(2,1)} %bitcast.72, bf16[4,512,2560]{2,1,0:T(8,128)(2,1)} %bitcast.73, bf16[4,512,2560]{2,1,0:T(8,128)(2,1)} %bitcast.74, ...), custom_call_target="tpu_custom_call" | custom-call | flops 20132659200 | bytes 39321600 | tf_op jit(solution)/shard_map/weight_grad/pallas_call | solution.py:647
  651.3 30.7 %scatter_rows.1 = f32[8000,2560]{1,0:T(8,128)} custom-call(s32[2048]{0:T(1024)} %get-tuple-element.118.order, s32[2048]{0:T(1024)} %get-tuple-element.119.sid, s32[2048]{0:T(1024)} %select_reduce_fusion.2.runs, s32[2]{0:T(128)} %copy-done, f32[2176,2560]{1,0:T(8,128)} %all-gather.5.cloned.1.call-done.rows, ...), custom_call_target="tpu_custom_call", output_to_operand_aliasing={{}: (5, {})} | custom-call | tf_op jit(solution)/shard_map/scatter_rows/pallas_call | solution.py:800
  (139 shorter events, 93.8 us)
Async XLA Ops:
  7.2 151.0 %all-gather.3.cloned.1.call-start = ((), (), s32[]{:S(2)}) async-start(), calls=%async_computation.3 | async-start | bytes 8192000 | tf_op jit(solution)/shard_map/all_gather | solution.py:838
  89.4 291.1 %reduce-scatter.4.cloned.1.call-start = ((), (), s32[]{:S(2)}) async-start(), calls=%async_computation.4 | async-start | bytes 6553600 | tf_op jit(solution)/shard_map/reduce_scatter | solution.py:839
  228.4 253.7 %reduce-scatter.6.cloned.1.call-start = ((), (), s32[]{:S(2)}) async-start(), calls=%async_computation.5 | async-start | bytes 6553600 | tf_op jit(solution)/shard_map/reduce_scatter | solution.py:839
  229.5 8.4 %collective-permute-start.2 = (bf16[512,640]{1,0:T(8,128)(2,1)S(1)}, bf16[512,640]{1,0:T(8,128)(2,1)S(1)}, u32[]{:S(2)}, u32[]{:S(2)}) collective-permute-start(bf16[512,640]{1,0:T(8,128)(2,1)S(1)} %copy-done.1), channel_id=1, source_target_pairs={{0,1},{1,0},{2,3},{3,2},{4,5},{5,4},{6,7},{7,6},{8,9},{9,8},{10,11... | collective-permute-start | bytes 1966088 | tf_op jit(solution)/shard_map/ppermute | solution.py:840
  229.5 17.6 %collective-permute-start.3 = (bf16[512,640]{1,0:T(8,128)(2,1)S(1)}, bf16[512,640]{1,0:T(8,128)(2,1)S(1)}, u32[]{:S(2)}, u32[]{:S(2)}) collective-permute-start(bf16[512,640]{1,0:T(8,128)(2,1)S(1)} %copy-done.1), channel_id=1, source_target_pairs={{0,2},{1,3},{2,0},{3,1},{4,6},{5,7},{6,4},{7,5},{8,10},{9,11},{10,... | collective-permute-start | bytes 1966088 | tf_op jit(solution)/shard_map/ppermute | solution.py:840
  231.3 72.1 %collective-permute-start.1 = (bf16[512,2560]{1,0:T(8,128)(2,1)}, bf16[512,2560]{1,0:T(8,128)(2,1)}, u32[]{:S(2)}, u32[]{:S(2)}) collective-permute-start(bf16[512,2560]{1,0:T(8,128)(2,1)} %refs_4_.1), channel_id=1, source_target_pairs={{0,2},{1,3},{2,0},{3,1},{4,6},{5,7},{6,4},{7,5},{8,10},{9,11},{10,... | collective-permute-start | bytes 7864328 | tf_op jit(solution)/shard_map/ppermute | solution.py:840
  234.1 125.0 %collective-permute-start = (bf16[512,2560]{1,0:T(8,128)(2,1)}, bf16[512,2560]{1,0:T(8,128)(2,1)}, u32[]{:S(2)}, u32[]{:S(2)}) collective-permute-start(bf16[512,2560]{1,0:T(8,128)(2,1)} %get-tuple-element.80.act.refs_4_), channel_id=1, source_target_pairs={{0,2},{1,3},{2,0},{3,1},{4,6},{5,7},{6,4},{7,5},{8,10},{9,11},{10,... | collective-permute-start | bytes 7864328 | tf_op jit(solution)/shard_map/ppermute | solution.py:840
  247.1 30.8 %collective-permute-start.4 = (bf16[512,640]{1,0:T(8,128)(2,1)S(1)}, bf16[512,640]{1,0:T(8,128)(2,1)S(1)}, u32[]{:S(2)}, u32[]{:S(2)}) collective-permute-start(bf16[512,640]{1,0:T(8,128)(2,1)S(1)} %collective-permute-done.3.refs_2_), channel_id=1, source_target_pairs={{0,1},{1,0},{2,3},{3,2},{4,5},{5,4},{6,7},{7,6},{8,9},{9,8},{10,11... | collective-permute-start | bytes 1966088 | tf_op jit(solution)/shard_map/ppermute | solution.py:840
  424.8 122.5 %reduce-scatter.8.cloned.1.call-start = ((), (), s32[]{:S(2)}) async-start(), calls=%async_computation.6 | async-start | bytes 6553600 | tf_op jit(solution)/shard_map/reduce_scatter | solution.py:839
  484.0 163.8 %all-gather.5.cloned.1.call-start = ((), (), s32[]{:S(2)}) async-start(), calls=%async_computation.7 | async-start | bytes 23674880 | tf_op jit(solution)/shard_map/all_gather | solution.py:838
  484.0 33.7 %collective-permute-start.8 = (bf16[512,2560]{1,0:T(8,128)(2,1)}, bf16[512,2560]{1,0:T(8,128)(2,1)S(1)}, u32[]{:S(2)}, u32[]{:S(2)}) collective-permute-start(bf16[512,2560]{1,0:T(8,128)(2,1)} %get-tuple-element.80.act.refs_4_), channel_id=1, source_target_pairs={{0,1},{1,0},{2,3},{3,2},{4,5},{5,4},{6,7},{7,6},{8,9},{9,8},{10,11... | collective-permute-start | bytes 7864328 | tf_op jit(solution)/shard_map/ppermute | solution.py:840
  484.9 32.8 %collective-permute-start.9 = (bf16[512,2560]{1,0:T(8,128)(2,1)}, bf16[512,2560]{1,0:T(8,128)(2,1)S(1)}, u32[]{:S(2)}, u32[]{:S(2)}) collective-permute-start(bf16[512,2560]{1,0:T(8,128)(2,1)} %collective-permute-done.act.refs_6_), channel_id=1, source_target_pairs={{0,1},{1,0},{2,3},{3,2},{4,5},{5,4},{6,7},{7,6},{8,9},{9,8},{10,11... | collective-permute-start | bytes 7864328 | tf_op jit(solution)/shard_map/ppermute | solution.py:840
  484.9 32.8 %collective-permute-start.6 = (bf16[512,1792]{1,0:T(8,128)(2,1)}, bf16[512,1792]{1,0:T(8,128)(2,1)}, u32[]{:S(2)}, u32[]{:S(2)}) collective-permute-start(bf16[512,1792]{1,0:T(8,128)(2,1)} %get-tuple-element.99.refs_0_), channel_id=1, source_target_pairs={{0,1},{1,0},{2,3},{3,2},{4,5},{5,4},{6,7},{7,6},{8,9},{9,8},{10,11... | collective-permute-start | bytes 5505032 | tf_op jit(solution)/shard_map/ppermute | solution.py:840
  485.4 32.4 %collective-permute-start.7 = (bf16[512,1792]{1,0:T(8,128)(2,1)}, bf16[512,1792]{1,0:T(8,128)(2,1)}, u32[]{:S(2)}, u32[]{:S(2)}) collective-permute-start(bf16[512,1792]{1,0:T(8,128)(2,1)} %get-tuple-element.100.refs_2_), channel_id=1, source_target_pairs={{0,1},{1,0},{2,3},{3,2},{4,5},{5,4},{6,7},{7,6},{8,9},{9,8},{10,11... | collective-permute-start | bytes 5505032 | tf_op jit(solution)/shard_map/ppermute | solution.py:840
  485.4 61.8 %collective-permute-start.5 = (bf16[512,1920]{1,0:T(8,128)(2,1)}, bf16[512,1920]{1,0:T(8,128)(2,1)}, u32[]{:S(2)}, u32[]{:S(2)}) collective-permute-start(bf16[512,1920]{1,0:T(8,128)(2,1)} %attend_back.1.refs_4_), channel_id=1, source_target_pairs={{0,2},{1,3},{2,0},{3,1},{4,6},{5,7},{6,4},{7,5},{8,10},{9,11},{10,... | collective-permute-start | bytes 5898248 | tf_op jit(solution)/shard_map/ppermute | solution.py:840
  551.8 10.0 %collective-permute-start.13 = (bf16[512,1792]{1,0:T(8,128)(2,1)}, bf16[512,1792]{1,0:T(8,128)(2,1)}, u32[]{:S(2)}, u32[]{:S(2)}) collective-permute-start(bf16[512,1792]{1,0:T(8,128)(2,1)} %get-tuple-element.112.refs_2_), channel_id=1, source_target_pairs={{0,1},{1,0},{2,3},{3,2},{4,5},{5,4},{6,7},{7,6},{8,9},{9,8},{10,11... | collective-permute-start | bytes 5505032 | tf_op jit(solution)/shard_map/ppermute | solution.py:840
  551.9 37.1 %collective-permute-start.17 = (bf16[512,2560]{1,0:T(8,128)(2,1)}, bf16[512,2560]{1,0:T(8,128)(2,1)}, u32[]{:S(2)}, u32[]{:S(2)}) collective-permute-start(bf16[512,2560]{1,0:T(8,128)(2,1)} %collective-permute-done.1.dy.refs_6_), channel_id=1, source_target_pairs={{0,1},{1,0},{2,3},{3,2},{4,5},{5,4},{6,7},{7,6},{8,9},{9,8},{10,11... | collective-permute-start | bytes 7864328 | tf_op jit(solution)/shard_map/ppermute | solution.py:840
  552.3 36.7 %collective-permute-start.14 = (bf16[512,1792]{1,0:T(8,128)(2,1)}, bf16[512,1792]{1,0:T(8,128)(2,1)}, u32[]{:S(2)}, u32[]{:S(2)}) collective-permute-start(bf16[512,1792]{1,0:T(8,128)(2,1)} %get-tuple-element.86.refs_0_), channel_id=1, source_target_pairs={{0,1},{1,0},{2,3},{3,2},{4,5},{5,4},{6,7},{7,6},{8,9},{9,8},{10,11... | collective-permute-start | bytes 5505032 | tf_op jit(solution)/shard_map/ppermute | solution.py:840
  556.6 32.5 %collective-permute-start.15 = (bf16[512,1792]{1,0:T(8,128)(2,1)}, bf16[512,1792]{1,0:T(8,128)(2,1)}, u32[]{:S(2)}, u32[]{:S(2)}) collective-permute-start(bf16[512,1792]{1,0:T(8,128)(2,1)} %get-tuple-element.113.refs_2_), channel_id=1, source_target_pairs={{0,1},{1,0},{2,3},{3,2},{4,5},{5,4},{6,7},{7,6},{8,9},{9,8},{10,11... | collective-permute-start | bytes 5505032 | tf_op jit(solution)/shard_map/ppermute | solution.py:840
  559.2 56.9 %collective-permute-start.10 = (bf16[512,1920]{1,0:T(8,128)(2,1)}, bf16[512,1920]{1,0:T(8,128)(2,1)S(1)}, u32[]{:S(2)}, u32[]{:S(2)}) collective-permute-start(bf16[512,1920]{1,0:T(8,128)(2,1)} %attend_back.1.refs_4_), channel_id=1, source_target_pairs={{0,1},{1,0},{2,3},{3,2},{4,5},{5,4},{6,7},{7,6},{8,9},{9,8},{10,11... | collective-permute-start | bytes 5898248 | tf_op jit(solution)/shard_map/ppermute | solution.py:840
  561.8 54.3 %collective-permute-start.11 = (bf16[512,1920]{1,0:T(8,128)(2,1)}, bf16[512,1920]{1,0:T(8,128)(2,1)S(1)}, u32[]{:S(2)}, u32[]{:S(2)}) collective-permute-start(bf16[512,1920]{1,0:T(8,128)(2,1)} %collective-permute-done.5.refs_6_), channel_id=1, source_target_pairs={{0,1},{1,0},{2,3},{3,2},{4,5},{5,4},{6,7},{7,6},{8,9},{9,8},{10,11... | collective-permute-start | bytes 5898248 | tf_op jit(solution)/shard_map/ppermute | solution.py:840
  647.7 36.5 %collective-permute-start.18 = (bf16[128,2560]{1,0:T(8,128)(2,1)S(1)}, bf16[128,2560]{1,0:T(8,128)(2,1)}, u32[]{:S(2)}, u32[]{:S(2)}) collective-permute-start(bf16[128,2560]{1,0:T(8,128)(2,1)S(1)} %add_convert_fusion), channel_id=1, source_target_pairs={{0,4},{4,0},{8,12},{12,8},{1,5},{5,1},{9,13},{13,9},{2,6},{6,2},{1... | collective-permute-start | bytes 1966088 | tf_op jit(solution)/shard_map/ppermute | solution.py:840
  648.8 36.6 %collective-permute-start.19 = (bf16[128,2560]{1,0:T(8,128)(2,1)S(1)}, bf16[128,2560]{1,0:T(8,128)(2,1)S(1)}, u32[]{:S(2)}, u32[]{:S(2)}) collective-permute-start(bf16[128,2560]{1,0:T(8,128)(2,1)S(1)} %add_convert_fusion), channel_id=1, source_target_pairs={{0,8},{4,12},{8,0},{12,4},{1,9},{5,13},{9,1},{13,5},{2,10},{6,14},... | collective-permute-start | bytes 1966088 | tf_op jit(solution)/shard_map/ppermute | solution.py:840
  649.6 35.8 %collective-permute-start.20 = (bf16[128,2560]{1,0:T(8,128)(2,1)S(1)}, bf16[128,2560]{1,0:T(8,128)(2,1)S(1)}, u32[]{:S(2)}, u32[]{:S(2)}) collective-permute-start(bf16[128,2560]{1,0:T(8,128)(2,1)S(1)} %add_convert_fusion), channel_id=1, source_target_pairs={{0,12},{4,8},{8,4},{12,0},{1,13},{5,9},{9,5},{13,1},{2,14},{6,10},... | collective-permute-start | bytes 1966088 | tf_op jit(solution)/shard_map/ppermute | solution.py:840
  (25 other events, 707.1 us)
Sparse Core Ops, SparseCore 0:
  89.5 68.5 all-gather.2
  228.6 57.8 reduce-scatter.3
  424.9 57.1 reduce-scatter.5
  485.5 59.6 reduce-scatter.7
  551.4 93.3 all-gather.4
